TPU v7x, 32 devices: a whole 2x2x4 slice. The times are simulated.
32 devices in a mesh: dp: 8 (over y, x, core), seq: 4 (over z).
Axes of the slice: x: 2, y: 2, z: 4, core: 2. Of those that a mesh axis runs over, the one named last changes fastest.
Arguments:
- block_input: bfloat16 [16, 512, 2048], P('dp', 'seq'), may hold values from -12 to 12
- segment_ids: int32 [16, 512], P('dp'), may hold values from 0 to 3, never falling along the last dimension, each value on 1 to 256 neighbouring positions
- cotangent: bfloat16 [16, 512, 2048], P('dp', 'seq'), may hold values from -6 to 6
- attn_gain: float32 [2048], P(('dp', 'seq')), may hold values from 0.5 to 1.5
- qkv_weight: float32 [2048, 3072], P('dp', 'seq'), may hold values from -1 to 1
- out_weight: float32 [2048, 2048], P('seq', 'dp'), may hold values from -0.75 to 0.75
- mlp_gain: float32 [2048], P(('dp', 'seq')), may hold values from 0.5 to 1.5
- gate_up_weight: float32 [2048, 2, 8192], P('dp', None, 'seq'), may hold values from -0.125 to 0.125
- down_weight: float32 [8192, 2048], P('seq', 'dp'), may hold values from -0.125 to 0.125
- first_attn_gain: float32 [2048], P(('dp', 'seq')), may hold values from -30 to 30
- first_qkv: float32 [2048, 3072], P('dp', 'seq'), may hold values from -30 to 30
- first_out: float32 [2048, 2048], P('seq', 'dp'), may hold values from -30 to 30
- first_mlp_gain: float32 [2048], P(('dp', 'seq')), may hold values from -30 to 30
- first_gate_up: float32 [2048, 2, 8192], P('dp', None, 'seq'), may hold values from -30 to 30
- first_down: float32 [8192, 2048], P('seq', 'dp'), may hold values from -30 to 30
- second_attn_gain: float32 [2048], P(('dp', 'seq')), may hold values from 100 to 300000
- second_qkv: float32 [2048, 3072], P('dp', 'seq'), may hold values from 100 to 30000
- second_out: float32 [2048, 2048], P('seq', 'dp'), may hold values from 50 to 500
- second_mlp_gain: float32 [2048], P(('dp', 'seq')), may hold values from 50 to 500
- second_gate_up: float32 [2048, 2, 8192], P('dp', None, 'seq'), may hold values from 50 to 500
- second_down: float32 [8192, 2048], P('seq', 'dp'), may hold values from 50 to 500
Outputs:
- output: bfloat16 [16, 512, 2048], P('dp', 'seq')
- input_grad: bfloat16 [16, 512, 2048], P('dp', 'seq')
- grad_attn_gain: float32 [2048], P(('dp', 'seq'))
- grad_qkv: float32 [2048, 3072], P('dp', 'seq')
- grad_out: float32 [2048, 2048], P('seq', 'dp')
- grad_mlp_gain: float32 [2048], P(('dp', 'seq'))
- grad_gate_up: float32 [2048, 2, 8192], P('dp', None, 'seq')
- grad_down: float32 [8192, 2048], P('seq', 'dp')
- new_attn_gain: float32 [2048], P(('dp', 'seq'))
- new_qkv: float32 [2048, 3072], P('dp', 'seq')
- new_out: float32 [2048, 2048], P('seq', 'dp')
- new_mlp_gain: float32 [2048], P(('dp', 'seq'))
- new_gate_up: float32 [2048, 2, 8192], P('dp', None, 'seq')
- new_down: float32 [8192, 2048], P('seq', 'dp')
- new_first_attn_gain: float32 [2048], P(('dp', 'seq'))
- new_first_qkv: float32 [2048, 3072], P('dp', 'seq')
- new_first_out: float32 [2048, 2048], P('seq', 'dp')
- new_first_mlp_gain: float32 [2048], P(('dp', 'seq'))
- new_first_gate_up: float32 [2048, 2, 8192], P('dp', None, 'seq')
- new_first_down: float32 [8192, 2048], P('seq', 'dp')
- new_second_attn_gain: float32 [2048], P(('dp', 'seq'))
- new_second_qkv: float32 [2048, 3072], P('dp', 'seq')
- new_second_out: float32 [2048, 2048], P('seq', 'dp')
- new_second_mlp_gain: float32 [2048], P(('dp', 'seq'))
- new_second_gate_up: float32 [2048, 2, 8192], P('dp', None, 'seq')
- new_second_down: float32 [8192, 2048], P('seq', 'dp')
Inputs may be any that keep to these rules, and one draw needn't show every extreme that they name: `segment_ids`: in each sequence the numbers never fall, and each segment holds 1 to 256 consecutive positions, one of them exactly that many.
All inputs are finite; a program needn't handle non-finite values.
Results may differ from a plain program's by a relative error of at most 0.023.
Values may be sent and summed in bfloat16 or wider, within the bound.
A program may use at most 320 MiB of HBM per device.

v0:
```python
import jax
import jax.numpy as jnp
from jax import lax
from jax.sharding import PartitionSpec as P

HEADS = 32
KV_HEADS = 8
HEAD_DIM = 64


norm_eps = 1e-05
rope_base = 500000.0
beta_one = 0.9
beta_two = 0.95
learn_rate = 0.01
weight_decay = 0.1
adam_eps = 1e-08
step_count = 10.0
masked_score = -1e30


def segment_positions(segments):
    length_here = segments.shape[-1]
    earlier = (segments[..., None, :] < segments[..., :, None]).astype(jnp.int32)
    return jnp.arange(length_here, dtype=jnp.int32) - jnp.sum(earlier, axis=-1, dtype=jnp.int32)


def rope_tables(positions, head_size):
    half_size = head_size // 2
    inverse = rope_base ** (-2.0 * jnp.arange(half_size, dtype=jnp.float32) / head_size)
    angles = positions.astype(jnp.float32)[..., None] * inverse
    return (jnp.cos(angles), jnp.sin(angles))


def rotate(vectors, cosine, sine):
    half_size = vectors.shape[-1] // 2
    first_half = vectors[..., :half_size]
    second_half = vectors[..., half_size:]
    cos_wide = cosine[..., None, :]
    sin_wide = sine[..., None, :]
    return jnp.concatenate(
        [
            first_half * cos_wide - second_half * sin_wide,
            second_half * cos_wide + first_half * sin_wide,
        ],
        -1,
    )


def unrotate(vectors, cosine, sine):
    half_size = vectors.shape[-1] // 2
    first_half = vectors[..., :half_size]
    second_half = vectors[..., half_size:]
    cos_wide = cosine[..., None, :]
    sin_wide = sine[..., None, :]
    return jnp.concatenate(
        [
            first_half * cos_wide + second_half * sin_wide,
            second_half * cos_wide - first_half * sin_wide,
        ],
        -1,
    )


def rms_forward(values, gain_wide):
    inverse = lax.rsqrt(jnp.mean(values * values, axis=-1, keepdims=True) + norm_eps)
    scaled = values * inverse
    return (scaled, inverse, (scaled * gain_wide).astype(jnp.bfloat16))


def rms_backward(d_normed, scaled, inverse, gain_wide):
    d_scaled = d_normed * gain_wide
    d_values = inverse * (d_scaled - scaled * jnp.mean(d_scaled * scaled, axis=-1, keepdims=True))
    return (d_values, jnp.sum(d_normed * scaled, axis=0))


def adam_update(weight, grad, first, second):
    new_first = beta_one * first + (1.0 - beta_one) * grad
    new_second = beta_two * second + (1.0 - beta_two) * grad * grad
    first_hat = new_first / (1.0 - beta_one**step_count)
    second_hat = new_second / (1.0 - beta_two**step_count)
    new_weight = weight - learn_rate * (
        first_hat / (jnp.sqrt(second_hat) + adam_eps) + weight_decay * weight
    )
    return (new_weight, new_first, new_second)


def contract_rows(left, right):
    return lax.dot_general(
        left, right, (((0,), (0,)), ((), ())), preferred_element_type=jnp.float32
    )


def times_transpose(left, right):
    return lax.dot_general(
        left, right, (((1,), (1,)), ((), ())), preferred_element_type=jnp.float32
    )


def per_device(
    block_input,
    segment_ids,
    cotangent,
    attn_gain,
    qkv_weight,
    out_weight,
    mlp_gain,
    gate_up_weight,
    down_weight,
    first_attn_gain,
    first_qkv,
    first_out,
    first_mlp_gain,
    first_gate_up,
    first_down,
    second_attn_gain,
    second_qkv,
    second_out,
    second_mlp_gain,
    second_gate_up,
    second_down,
):
    seqs_here, local_len, width = block_input.shape
    full_len = segment_ids.shape[1]
    total_rows = seqs_here * full_len
    groups = HEADS // KV_HEADS
    slot_count = groups + 2
    kv_local = qkv_weight.shape[1] // (slot_count * HEAD_DIM)
    query_cols = kv_local * groups * HEAD_DIM
    unit_count = down_weight.shape[0]
    score_scale = HEAD_DIM ** (-0.5)
    gain_pair = jnp.stack([attn_gain, mlp_gain]).astype(jnp.bfloat16)
    rows_all, cot_all, gain_block = (
        lax.all_gather(block_input, "seq", axis=1, tiled=True),
        lax.all_gather(cotangent, "seq", axis=1, tiled=True),
        lax.all_gather(gain_pair, "seq", axis=1, tiled=True),
    )
    attn_cast = (qkv_weight.astype(jnp.bfloat16), out_weight.astype(jnp.bfloat16))
    qkv_cols, out_rows, gain_full = (
        lax.all_gather(attn_cast[0], "dp", axis=0, tiled=True),
        lax.all_gather(attn_cast[1], "dp", axis=1, tiled=True),
        lax.all_gather(gain_block, "dp", axis=1, tiled=True),
    )
    gain_one = gain_full[0].astype(jnp.float32)
    gain_two = gain_full[1].astype(jnp.float32)
    positions = segment_positions(segment_ids)
    cosine, sine = rope_tables(positions, HEAD_DIM)
    index_line = jnp.arange(full_len, dtype=jnp.int32)
    allowed = (segment_ids[:, :, None] == segment_ids[:, None, :]) & (
        index_line[None, None, :] <= index_line[None, :, None]
    )
    allowed = allowed[:, None, None, :, :]
    wide_input = rows_all.reshape(total_rows, width).astype(jnp.float32)
    scaled_one, inverse_one, normed_one = rms_forward(wide_input, gain_one)
    qkv = jnp.dot(normed_one, qkv_cols, preferred_element_type=jnp.float32)
    qkv = qkv.reshape(seqs_here, full_len, kv_local, slot_count, HEAD_DIM)
    query = qkv[:, :, :, :groups].reshape(seqs_here, full_len, kv_local * groups, HEAD_DIM)
    query_groups = (
        rotate(query, cosine, sine)
        .astype(jnp.bfloat16)
        .reshape(seqs_here, full_len, kv_local, groups, HEAD_DIM)
    )
    key16 = rotate(qkv[:, :, :, groups], cosine, sine).astype(jnp.bfloat16)
    value16 = qkv[:, :, :, groups + 1].astype(jnp.bfloat16)

    def masked_scores():
        raw_scores = (
            jnp.einsum("sqgjd,skgd->sgjqk", query_groups, key16, preferred_element_type=jnp.float32)
            * score_scale
        )
        return jnp.where(allowed, raw_scores, masked_score)

    scores = masked_scores()
    top_score = jnp.max(scores, axis=-1, keepdims=True)
    log_total = top_score + jnp.log(jnp.sum(jnp.exp(scores - top_score), axis=-1, keepdims=True))
    probs16 = jnp.exp(scores - log_total).astype(jnp.bfloat16)
    attended16 = jnp.einsum(
        "sgjqk,skgd->sqgjd", probs16, value16, preferred_element_type=jnp.float32
    )
    attended16 = attended16.reshape(total_rows, query_cols).astype(jnp.bfloat16)
    attn_total = lax.psum(jnp.dot(attended16, out_rows, preferred_element_type=jnp.float32), "seq")
    resid = wide_input + attn_total
    mlp_cast = (gate_up_weight.astype(jnp.bfloat16), down_weight.astype(jnp.bfloat16))
    gate_up_cols, down_rows = (
        lax.all_gather(mlp_cast[0], "dp", axis=0, tiled=True),
        lax.all_gather(mlp_cast[1], "dp", axis=1, tiled=True),
    )
    scaled_two, inverse_two, normed_two = rms_forward(resid, gain_two)
    gate_up = jnp.dot(
        normed_two, gate_up_cols.reshape(width, 2 * unit_count), preferred_element_type=jnp.float32
    )
    gate_part = gate_up[:, :unit_count]
    up_part = gate_up[:, unit_count:]
    sigmoid_gate = jax.nn.sigmoid(gate_part)
    active = gate_part * sigmoid_gate
    hidden16 = (active * up_part).astype(jnp.bfloat16)
    down_part = jnp.dot(hidden16, down_rows, preferred_element_type=jnp.float32).reshape(
        seqs_here, full_len, width
    )
    down_here = lax.psum_scatter(
        down_part.astype(jnp.bfloat16), "seq", scatter_dimension=1, tiled=True
    ).astype(jnp.float32)
    offset = lax.axis_index("seq") * local_len
    resid_here = lax.dynamic_slice_in_dim(
        resid.reshape(seqs_here, full_len, width), offset, local_len, 1
    )
    output = (resid_here + down_here).astype(jnp.bfloat16)
    gate_up_cols, down_rows = (
        lax.all_gather(mlp_cast[0], "dp", axis=0, tiled=True),
        lax.all_gather(mlp_cast[1], "dp", axis=1, tiled=True),
    )
    cot_rows = cot_all.reshape(total_rows, width)
    d_hidden = times_transpose(cot_rows, down_rows)
    d_gate = d_hidden * up_part * sigmoid_gate * (1.0 + gate_part * (1.0 - sigmoid_gate))
    d_up = d_hidden * active
    d_gate_up16 = jnp.concatenate([d_gate, d_up], 1).astype(jnp.bfloat16)
    down_term = contract_rows(cot_rows, hidden16)
    gate_up_term = contract_rows(normed_two, d_gate_up16).reshape(width, 2, unit_count)
    down_sum, grad_gate_up = (
        lax.psum_scatter(
            down_term.astype(jnp.bfloat16), "dp", scatter_dimension=0, tiled=True
        ).astype(jnp.float32),
        lax.psum_scatter(
            gate_up_term.astype(jnp.bfloat16), "dp", scatter_dimension=0, tiled=True
        ).astype(jnp.float32),
    )
    grad_down = down_sum.T
    d_normed_two = times_transpose(d_gate_up16, gate_up_cols.reshape(width, 2 * unit_count))
    resid_part, gain_two_term = rms_backward(d_normed_two, scaled_two, inverse_two, gain_two)
    d_resid = cot_rows.astype(jnp.float32) + lax.psum(resid_part, "seq")
    d_resid16 = d_resid.astype(jnp.bfloat16)
    qkv_cols, out_rows = (
        lax.all_gather(attn_cast[0], "dp", axis=0, tiled=True),
        lax.all_gather(attn_cast[1], "dp", axis=1, tiled=True),
    )
    d_attended = times_transpose(d_resid16, out_rows).astype(jnp.bfloat16)
    d_attended = d_attended.reshape(seqs_here, full_len, kv_local, groups, HEAD_DIM)
    scores = masked_scores()
    probs = jnp.exp(scores - log_total)
    d_probs = jnp.einsum(
        "sqgjd,skgd->sgjqk", d_attended, value16, preferred_element_type=jnp.float32
    )
    delta = jnp.sum(probs * d_probs, axis=-1, keepdims=True)
    d_scores16 = (probs * (d_probs - delta) * score_scale).astype(jnp.bfloat16)
    d_query = jnp.einsum("sgjqk,skgd->sqgjd", d_scores16, key16, preferred_element_type=jnp.float32)
    d_key = jnp.einsum(
        "sgjqk,sqgjd->skgd", d_scores16, query_groups, preferred_element_type=jnp.float32
    )
    d_value = jnp.einsum(
        "sgjqk,sqgjd->skgd", probs16, d_attended, preferred_element_type=jnp.float32
    )
    d_query = unrotate(
        d_query.reshape(seqs_here, full_len, kv_local * groups, HEAD_DIM), cosine, sine
    )
    d_query = d_query.reshape(seqs_here, full_len, kv_local, groups, HEAD_DIM)
    d_key = unrotate(d_key, cosine, sine)
    d_qkv16 = jnp.concatenate([d_query, d_key[:, :, :, None], d_value[:, :, :, None]], 3)
    d_qkv16 = d_qkv16.reshape(total_rows, qkv_cols.shape[1]).astype(jnp.bfloat16)
    qkv_term = contract_rows(normed_one, d_qkv16)
    out_term = contract_rows(d_resid16, attended16)
    d_normed_one = times_transpose(d_qkv16, qkv_cols)
    input_part, gain_one_term = rms_backward(d_normed_one, scaled_one, inverse_one, gain_one)
    gain_terms = jnp.stack([gain_one_term, gain_two_term], 1)
    grad_qkv, out_sum, gain_sum = (
        lax.psum_scatter(
            qkv_term.astype(jnp.bfloat16), "dp", scatter_dimension=0, tiled=True
        ).astype(jnp.float32),
        lax.psum_scatter(
            out_term.astype(jnp.bfloat16), "dp", scatter_dimension=0, tiled=True
        ).astype(jnp.float32),
        lax.psum_scatter(
            gain_terms.astype(jnp.bfloat16), "dp", scatter_dimension=0, tiled=True
        ).astype(jnp.float32),
    )
    grad_out = out_sum.T
    input_here, gain_grads = (
        lax.psum_scatter(
            input_part.reshape(seqs_here, full_len, width).astype(jnp.bfloat16),
            "seq",
            scatter_dimension=1,
            tiled=True,
        ).astype(jnp.float32),
        lax.psum_scatter(
            gain_sum[None].astype(jnp.bfloat16), "seq", scatter_dimension=1, tiled=True
        ).astype(jnp.float32),
    )
    d_resid_here = lax.dynamic_slice_in_dim(
        d_resid.reshape(seqs_here, full_len, width), offset, local_len, 1
    )
    input_grad = (d_resid_here + input_here).astype(jnp.bfloat16)
    grad_gain_one = gain_grads[0, :, 0]
    grad_gain_two = gain_grads[0, :, 1]
    w_one, m_one, v_one = adam_update(attn_gain, grad_gain_one, first_attn_gain, second_attn_gain)
    w_qkv, m_qkv, v_qkv = adam_update(qkv_weight, grad_qkv, first_qkv, second_qkv)
    w_out, m_out, v_out = adam_update(out_weight, grad_out, first_out, second_out)
    w_two, m_two, v_two = adam_update(mlp_gain, grad_gain_two, first_mlp_gain, second_mlp_gain)
    w_gu, m_gu, v_gu = adam_update(gate_up_weight, grad_gate_up, first_gate_up, second_gate_up)
    w_down, m_down, v_down = adam_update(down_weight, grad_down, first_down, second_down)
    return (
        output,
        input_grad,
        grad_gain_one,
        grad_qkv,
        grad_out,
        grad_gain_two,
        grad_gate_up,
        grad_down,
        w_one,
        w_qkv,
        w_out,
        w_two,
        w_gu,
        w_down,
        m_one,
        m_qkv,
        m_out,
        m_two,
        m_gu,
        m_down,
        v_one,
        v_qkv,
        v_out,
        v_two,
        v_gu,
        v_down,
    )


def solution(mesh):
    in_specs = (
        P("dp", "seq", None),
        P("dp", None),
        P("dp", "seq", None),
        P(("dp", "seq")),
        P("dp", "seq"),
        P("seq", "dp"),
        P(("dp", "seq")),
        P("dp", None, "seq"),
        P("seq", "dp"),
        P(("dp", "seq")),
        P("dp", "seq"),
        P("seq", "dp"),
        P(("dp", "seq")),
        P("dp", None, "seq"),
        P("seq", "dp"),
        P(("dp", "seq")),
        P("dp", "seq"),
        P("seq", "dp"),
        P(("dp", "seq")),
        P("dp", None, "seq"),
        P("seq", "dp"),
    )
    out_specs = (
        P("dp", "seq", None),
        P("dp", "seq", None),
        P(("dp", "seq")),
        P("dp", "seq"),
        P("seq", "dp"),
        P(("dp", "seq")),
        P("dp", None, "seq"),
        P("seq", "dp"),
        P(("dp", "seq")),
        P("dp", "seq"),
        P("seq", "dp"),
        P(("dp", "seq")),
        P("dp", None, "seq"),
        P("seq", "dp"),
        P(("dp", "seq")),
        P("dp", "seq"),
        P("seq", "dp"),
        P(("dp", "seq")),
        P("dp", None, "seq"),
        P("seq", "dp"),
        P(("dp", "seq")),
        P("dp", "seq"),
        P("seq", "dp"),
        P(("dp", "seq")),
        P("dp", None, "seq"),
        P("seq", "dp"),
    )
    return jax.shard_map(
        per_device, mesh=mesh, in_specs=in_specs, out_specs=out_specs, check_vma=False
    )
```

profile of v0, /device:TPU:0, one launch (start us, length us, event | category | flops | bytes accessed | tf_op | source)
XLA Modules:
  0.0 1747.8 jit_solution(4317944858245214601)
XLA Ops:
  7.2 1.9 convert_element_type.159
  10.0 1.8 convert_element_type.167
  12.6 12.6 all-gather
  25.4 8.9 all_gather.30
  35.4 2.0 compare_and_fusion
  37.9 7.5 all-gather.10.cloned.1.call-done
  45.4 4.6 copy.86
  50.1 77.7 %all-gather.8.cloned.1.call-done = bf16[2,512,2048]{2,1,0:T(8,128)(2,1)} async-done(((bf16[2,128,2048]{2,1,0:T(8,128)(2,1)}), bf16[2,512,2048]{2,1,0:T(8,128)(2,1)}) %all-gather.8.cloned.1.call-update) | async-done | bytes 4194320 | tf_op jit(solution)/shard_map/all_gather | solution.py:134
  127.8 3.2 fusion.14
  131.6 3.2 fusion.16
  134.8 3.5 fusion.20
  139.7 7.2 fusion.5
  147.0 9.4 exponential_reduce_fusion
  156.4 8.4 fusion.32
  164.9 1.1 copy.88
  166.2 7.6 fusion.68
  173.9 5.7 convert_element_type.169
  180.2 1.1 convert_element_type.171
  181.3 282.2 %all-reduce.5.cloned.1.call-done = f32[1024,2048]{1,0:T(8,128)} async-done(((f32[1024,2048]{1,0:T(8,128)}), f32[1024,2048]{1,0:T(8,128)}) %all-reduce.5.cloned.1.call-update) | async-done | bytes 8388624 | tf_op jit(solution)/shard_map/psum | solution.py:181
  463.6 9.5 multiply_reduce_fusion.2
  473.0 81.6 %all-gather.14.cloned.1.call-done = bf16[2048,2,2048]{2,1,0:T(2,128)(2,1)} async-done(((bf16[256,2,2048]{2,1,0:T(2,128)(2,1)}), bf16[2048,2,2048]{2,1,0:T(2,128)(2,1)}) %all-gather.14.cloned.1.call-update) | async-done | bytes 16777232 | tf_op jit(solution)/shard_map/all_gather | solution.py:185
  554.6 13.5 copy.123
  568.1 5.7 copy-done.2
  573.8 21.0 %fusion.61 = f32[1024,4096]{1,0:T(8,128)} fusion(bf16[2048,4096]{1,0:T(8,128)(2,1)S(1)} %bitcast.211, f32[1024,2048]{1,0:T(8,128)S(1)} %copy-done.1, f32[2048]{0:T(1024)S(1)} %bitcast.240, f32[1024]{0:T(1024)S(1)} %add_rsqrt_fusion), kind=kOutput, calls=%fused_computation.138 | convolution fusion | flops 17186160640 | bytes 41955328 | tf_op jit(solution)/shard_map/dot_general | solution.py:189
  594.9 41.9 %all-gather.18.cloned.1.call-done = bf16[2,512,2048]{2,1,0:T(8,128)(2,1)} async-done(((bf16[2,128,2048]{2,1,0:T(8,128)(2,1)}), bf16[2,512,2048]{2,1,0:T(8,128)(2,1)}) %all-gather.18.cloned.1.call-update) | async-done | bytes 4194320 | tf_op jit(solution)/shard_map/all_gather | solution.py:135
  636.8 56.8 %all-gather.16.cloned.1.call-done = bf16[2048,2048]{1,0:T(8,128)(2,1)} async-done(((bf16[2048,256]{1,0:T(8,128)(2,1)}), bf16[2048,2048]{1,0:T(8,128)(2,1)}) %all-gather.16.cloned.1.call-update) | async-done | bytes 8388624 | tf_op jit(solution)/shard_map/all_gather | solution.py:186
  693.6 21.7 %multiply_convert_fusion.1 = (bf16[1024,2048]{1,0:T(8,128)(2,1)}, bf16[1024,2048]{1,0:T(8,128)(2,1)}, bf16[1024,2048]{1,0:T(8,128)(2,1)}) fusion(f32[1024,4096]{1,0:T(8,128)} %fusion.61, bf16[1024,2048]{1,0:T(8,128)(2,1)} %bitcast.216, bf16[2048,2048]{1,0:T(8,128)(2,1)} %all-gather.16.cloned.1.call-done), kind=kOutput, calls=%fused_computation.33 | convolution fusion | flops 8621391872 | bytes 41943040 | tf_op jit(solution)/shard_map/dot_general | solution.py:95
  715.4 24.8 %multiply_reduce_fusion = (bf16[2048]{0:T(1024)(128)(2,1)S(1)}, f32[1024]{0:T(1024)S(1)}, f32[1024,2048]{1,0:T(8,128)S(1)}) fusion(f32[1024,2048]{1,0:T(8,128)} %get-tuple-element.132, f32[1024]{0:T(1024)S(1)} %add_rsqrt_fusion, f32[2048]{0:T(1024)S(1)} %bitcast.241, bf16[2048,4096]{1,0:T(8,128)(2,1)} %bitcast.212, ...), kind=kOutput, calls=%fused_computation.29 | convolution fusion | flops 17209225216 | bytes 41963520 | tf_op jit(solution)/shard_map/dot_general | solution.py:95
  740.2 6.4 subtract_multiply_fusion
  747.2 290.3 %all-reduce.7.cloned.1.call-done = f32[1024,2048]{1,0:T(8,128)} async-done(((f32[1024,2048]{1,0:T(8,128)}), f32[1024,2048]{1,0:T(8,128)}) %all-reduce.7.cloned.1.call-update) | async-done | bytes 8388624 | tf_op jit(solution)/shard_map/psum | solution.py:230
  1037.5 5.8 convert_add_fusion
  1043.4 3.2 copy-done.3
  1046.6 2.4 fusion.29
  1049.0 1.3 reshape.232
  1050.3 1.8 copy.90
  1052.2 8.0 convolution_bitcast_fusion
  1060.2 9.2 fusion.38
  1069.5 23.5 %fusion.33 = f32[2,512,2,64]{1,3,2,0:T(8,128)S(1)} fusion(f32[2,2,512,512,4]{3,2,4,1,0:T(8,128)} %fusion.38, f32[2,2,512,512,4]{3,2,4,1,0:T(8,128)} %get-tuple-element.155, f32[2,2,4,512]{3,2,1,0:T(4,128)S(1)} %bitcast.246, pred[2,512,512]{1,2,0:T(8,128)(4,1)} %compare_and_fusion, bf16[2,512,2,4,32]{1,4,3,2,0:T(8,128)(2,1)S(1)} %bitcast.233, ...), kind=kOutput, calls=%fused_computation.71 | convolution fusion | flops 585114112 | bytes 35684352 | tf_op jit(solution)/shard_map/sgjqk,sqgjd->skgd/dot_general | solution.py:246
  1093.0 23.8 %fusion.24 = f32[2,2,64,4,512]{4,2,3,1,0:T(8,128)S(1)} fusion(f32[2,2,512,512,4]{3,2,4,1,0:T(8,128)} %fusion.38, f32[2,2,512,512,4]{3,2,4,1,0:T(8,128)} %get-tuple-element.155, f32[2,2,4,512]{3,2,1,0:T(4,128)S(1)} %bitcast.247, pred[2,512,512]{1,2,0:T(8,128)(4,1)} %compare_and_fusion, bf16[2,512,2,32]{1,3,2,0:T(8,128)(2,1)S(1)} %copy-done.28, ...), kind=kOutput, calls=%fused_computation.53 | convolution fusion | flops 583541248 | bytes 36470784 | tf_op jit(solution)/shard_map/sgjqk,skgd->sqgjd/dot_general | solution.py:245
  1118.1 1.1 copy.92
  1119.2 6.1 maximum_convert_fusion
  1125.7 7.9 fusion.13
  1133.7 1.1 copy.115
  1134.8 13.8 convolution_convert_fusion.1
  1148.7 25.1 %convolution_convert_fusion = bf16[2048,4096]{1,0:T(8,128)(2,1)} fusion(bf16[1024,2048]{1,0:T(8,128)(2,1)} %get-tuple-element.134, bf16[1024,2048]{1,0:T(8,128)(2,1)} %get-tuple-element.133, f32[1024,2048]{1,0:T(8,128)} %get-tuple-element.132, f32[2048]{0:T(1024)S(1)} %bitcast.243, f32[1024]{0:T(1024)S(1)} %add_rsqrt_fusion), kind=kOutput, calls=%fused_computation.9 | convolution fusion | flops 17211326464 | bytes 33566720 | tf_op jit(solution)/shard_map/dot_general | solution.py:89
  1173.8 28.0 %convert_element_type.193 = bf16[2048,2,2048]{2,1,0:T(2,128)(2,1)} reshape(bf16[2048,4096]{1,0:T(8,128)(2,1)} %convolution_convert_fusion) | data formatting | bytes 33554432 | tf_op jit(solution)/shard_map/convert_element_type | solution.py:224
  1203.7 7.2 convolution_convert_fusion.3
  1211.0 14.2 convert_bitcast_fusion
  1225.4 7.4 convolution_convert_fusion.2
  1233.0 7.1 fusion.12
  1243.6 3.9 reduce-scatter.12.cloned.1.call-done
  1247.5 3.2 add_convert_fusion.1
  1250.8 218.9 %all-reduce.9.cloned.1.call-done = bf16[2048,2,2048]{2,1,0:T(2,128)(2,1)} async-done(((bf16[2048,2,2048]{2,1,0:T(2,128)(2,1)}), bf16[2048,2,2048]{2,1,0:T(2,128)(2,1)}) %all-reduce.9.cloned.1.call-update) | async-done | bytes 16777232
  1469.6 21.3 %multiply_subtract_fusion = (f32[256,2,2048]{2,1,0:T(2,128)}, f32[256,2,2048]{2,1,0:T(2,128)}, f32[256,2,2048]{2,1,0:T(2,128)}, f32[256,2,2048]{2,1,0:T(2,128)}) fusion(f32[256,2,2048]{2,1,0:T(2,128)} %param.28, f32[256,2,2048]{2,1,0:T(2,128)} %param.34, f32[256,2,2048]{2,1,0:T(2,128)} %param.40, bf16[2048,2,2048]{2,1,0:T(2,128)(2,1)} %all-reduce.9.cloned.1.call-done, ...), kind=kLoop, calls=%fused_computation.45 | loop fusion | flops 16777216 | bytes 31457284 | tf_op jit(solution)/shard_map/sub | solution.py:82
  1493.1 41.7 %reduce-scatter.18.cloned.1.call-done = bf16[256,512]{1,0:T(8,128)(2,1)} async-done(((bf16[2048,512]{1,0:T(8,128)(2,1)}), bf16[256,512]{1,0:T(8,128)(2,1)}) %reduce-scatter.18.cloned.1.call-update) | async-done | bytes 262160 | tf_op jit(solution)/shard_map/reduce_scatter | solution.py:268
  1536.8 2.6 multiply_subtract_fusion.4
  1539.5 2.0 copy.103
  1542.5 2.2 copy.105
  1544.7 64.7 %reduce-scatter.20.cloned.1.call-done = bf16[256,2048]{0,1:T(8,128)(2,1)} async-done(((bf16[2048,2048]{0,1:T(8,128)(2,1)}), bf16[256,2048]{0,1:T(8,128)(2,1)}) %reduce-scatter.20.cloned.1.call-update) | async-done | bytes 1048592 | tf_op jit(solution)/shard_map/reduce_scatter | solution.py:220
  1609.4 6.3 multiply_subtract_fusion.1
  1615.7 43.0 %reduce-scatter.16.cloned.1.call-done = bf16[256,768]{1,0:T(8,128)(2,1)} async-done(((bf16[2048,768]{1,0:T(8,128)(2,1)}), bf16[256,768]{1,0:T(8,128)(2,1)}) %reduce-scatter.16.cloned.1.call-update) | async-done | bytes 393232 | tf_op jit(solution)/shard_map/reduce_scatter | solution.py:265
  1658.7 3.3 multiply_subtract_fusion.3
  1662.0 75.7 %reduce-scatter.14.cloned.1.call-done = bf16[2,128,2048]{2,1,0:T(8,128)(2,1)} async-done(((bf16[2,512,2048]{2,1,0:T(8,128)(2,1)}), bf16[2,128,2048]{2,1,0:T(8,128)(2,1)}) %reduce-scatter.14.cloned.1.call-update) | async-done | bytes 1048592 | tf_op jit(solution)/shard_map/reduce_scatter | solution.py:277
  1737.7 3.2 add_convert_fusion
  (162 shorter events, 19.0 us)
Async XLA Ops:
  7.2 38.2 %all-gather.10.cloned.1.call-start = ((), (), s32[]{:S(2)}) async-start(), calls=%async_computation.8 | async-start | bytes 3538944 | tf_op jit(solution)/shard_map/all_gather | solution.py:140
  9.2 118.6 %all-gather.8.cloned.1.call-start = ((), (), s32[]{:S(2)}) async-start(), calls=%async_computation.7 | async-start | bytes 5242880 | tf_op jit(solution)/shard_map/all_gather | solution.py:134
  9.9 156.3 %all-gather.12.cloned.1.call-start = ((), (), s32[]{:S(2)}) async-start(), calls=%async_computation.9 | async-start | bytes 2359296 | tf_op jit(solution)/shard_map/all_gather | solution.py:141
  11.8 451.8 %all-reduce.5.cloned.1.call-start = ((), (), s32[]{:S(2)}) async-start(), calls=%async_computation.10 | async-start | bytes 16777216 | tf_op jit(solution)/shard_map/psum | solution.py:181
  34.3 100.5 %copy-start.29 = (f32[1,2048]{1,0:T(1,128)}, f32[1,2048]{1,0:T(1,128)S(1)}, u32[]{:S(2)}) copy-start(f32[1,2048]{1,0:T(1,128)S(1)} %get-tuple-element.145) | copy-start | bytes 24580
  37.9 100.8 %copy-start.7 = (f32[2,512,32]{1,2,0:T(8,128)}, f32[2,512,32]{1,2,0:T(8,128)S(1)}, u32[]{:S(2)}) copy-start(f32[2,512,32]{1,2,0:T(8,128)S(1)} %get-tuple-element.146) | copy-start | bytes 393220
  37.9 100.8 %copy-start.9 = (f32[2,512,32]{1,2,0:T(8,128)}, f32[2,512,32]{1,2,0:T(8,128)S(1)}, u32[]{:S(2)}) copy-start(f32[2,512,32]{1,2,0:T(8,128)S(1)} %get-tuple-element.147) | copy-start | bytes 393220
  127.8 7.1 copy-start.13
  134.8 3.5 copy-start.6
  138.3 18.1 %copy-start.12 = (f32[2,512,2,6,64]{1,4,3,2,0:T(8,128)}, f32[2,512,2,6,64]{1,4,3,2,0:T(8,128)S(1)}, u32[]{:S(2)}) copy-start(f32[2,512,2,6,64]{1,4,3,2,0:T(8,128)S(1)} %fusion.20) | copy-start | bytes 9437188
  138.3 1.4 copy-start.15
  138.5 8.5 copy-start.25
  138.5 8.5 copy-start.27
  139.1 7.9 copy-start.21
  139.1 7.9 copy-start.23
  156.4 8.4 copy-start.31
  166.2 7.6 copy-start.17
  173.8 6.4 copy-start.4
  173.8 380.8 %all-gather.14.cloned.1.call-start = ((), (), s32[]{:S(2)}) async-start(), calls=%async_computation.11 | async-start | bytes 18874368 | tf_op jit(solution)/shard_map/all_gather | solution.py:185
  179.6 457.2 %all-gather.18.cloned.1.call-start = ((), (), s32[]{:S(2)}) async-start(), calls=%async_computation.14 | async-start | bytes 5242880 | tf_op jit(solution)/shard_map/all_gather | solution.py:135
  180.1 513.5 %all-gather.16.cloned.1.call-start = ((), (), s32[]{:S(2)}) async-start(), calls=%async_computation.12 | async-start | bytes 9437184 | tf_op jit(solution)/shard_map/all_gather | solution.py:186
  181.3 856.2 %all-reduce.7.cloned.1.call-start = ((), (), s32[]{:S(2)}) async-start(), calls=%async_computation.15 | async-start | bytes 16777216 | tf_op jit(solution)/shard_map/psum | solution.py:230
  554.6 19.2 %copy-start.1 = (f32[1024,2048]{1,0:T(8,128)S(1)}, f32[1024,2048]{1,0:T(8,128)}, u32[]{:S(2)}) copy-start(f32[1024,2048]{1,0:T(8,128)} %get-tuple-element.132) | copy-start | bytes 25165828
  568.1 5.7 copy-start.2
  746.5 0.7 copy-start.33
  746.6 455.2 %reduce-scatter.22.cloned.1.call-start = ((), (), s32[]{:S(2)}) async-start(), calls=%async_computation.20 | async-start | bytes 589824
  747.2 299.4 %copy-start.40 = (bf16[512,2048]{1,0:T(8,128)(2,1)S(1)}, bf16[512,2048]{1,0:T(8,128)(2,1)}, u32[]{:S(2)}) copy-start(bf16[512,2048]{1,0:T(8,128)(2,1)} %all-gather.12.cloned.1.call-done) | copy-start | bytes 6291460
  1043.4 3.2 copy-start.3
  1046.6 5.5 copy-start.32
  1060.2 9.3 copy-start.22
  1060.2 9.3 copy-start.24
  1069.5 23.5 %copy-start.26 = (bf16[2,512,2,32]{1,3,2,0:T(8,128)(2,1)S(1)}, bf16[2,512,2,32]{1,3,2,0:T(8,128)(2,1)}, u32[]{:S(2)}) copy-start(bf16[2,512,2,32]{1,3,2,0:T(8,128)(2,1)} %copy-done.25) | copy-start | bytes 393220
  1069.5 23.5 %copy-start.28 = (bf16[2,512,2,32]{1,3,2,0:T(8,128)(2,1)S(1)}, bf16[2,512,2,32]{1,3,2,0:T(8,128)(2,1)}, u32[]{:S(2)}) copy-start(bf16[2,512,2,32]{1,3,2,0:T(8,128)(2,1)} %copy-done.27) | copy-start | bytes 393220
  1093.0 24.2 %copy-start.8 = (f32[2,512,32]{1,2,0:T(8,128)S(1)}, f32[2,512,32]{1,2,0:T(8,128)}, u32[]{:S(2)}) copy-start(f32[2,512,32]{1,2,0:T(8,128)} %copy-done.7) | copy-start | bytes 393220
  1093.0 24.2 %copy-start.10 = (f32[2,512,32]{1,2,0:T(8,128)S(1)}, f32[2,512,32]{1,2,0:T(8,128)}, u32[]{:S(2)}) copy-start(f32[2,512,32]{1,2,0:T(8,128)} %copy-done.9) | copy-start | bytes 393220
  1116.9 8.8 copy-start
  1116.9 8.8 copy-start.11
  1116.9 8.8 copy-start.30
  1134.8 112.8 %reduce-scatter.12.cloned.1.call-start = ((), (), s32[]{:S(2)}) async-start(), calls=%async_computation.13 | async-start | bytes 5242880 | tf_op jit(solution)/shard_map/reduce_scatter | solution.py:200
  1148.6 321.0 %all-reduce.9.cloned.1.call-start = ((), (), s32[]{:S(2)}) async-start(), calls=%async_computation.22 | async-start | bytes 33554432
  1201.7 2.0 copy-start.18
  1201.7 289.9 %reduce-scatter.24.cloned.1.call-start = ((), (), s32[]{:S(2)}) async-start(), calls=%async_computation.21 | async-start | bytes 81920
  1203.7 331.1 %reduce-scatter.18.cloned.1.call-start = ((), (), s32[]{:S(2)}) async-start(), calls=%async_computation.18 | async-start | bytes 2359296 | tf_op jit(solution)/shard_map/reduce_scatter | solution.py:268
  1211.0 398.5 %reduce-scatter.20.cloned.1.call-start = ((), (), s32[]{:S(2)}) async-start(), calls=%async_computation.19 | async-start | bytes 9437184 | tf_op jit(solution)/shard_map/reduce_scatter | solution.py:220
  1225.2 433.6 %reduce-scatter.16.cloned.1.call-start = ((), (), s32[]{:S(2)}) async-start(), calls=%async_computation.17 | async-start | bytes 3538944 | tf_op jit(solution)/shard_map/reduce_scatter | solution.py:265
  1232.9 504.8 %reduce-scatter.14.cloned.1.call-start = ((), (), s32[]{:S(2)}) async-start(), calls=%async_computation.16 | async-start | bytes 5242880 | tf_op jit(solution)/shard_map/reduce_scatter | solution.py:277
  1232.9 7.2 copy-start.16
  1233.0 7.4 copy-start.19
  1233.0 8.4 copy-start.20
  1233.0 9.4 copy-start.41
  1250.7 241.8 %copy-start.34 = (f32[64]{0:T(128)S(1)}, f32[64]{0:T(128)}, u32[]{:S(2)}) copy-start(f32[64]{0:T(128)} %param.27) | copy-start | bytes 772
  1250.7 241.8 %copy-start.35 = (f32[64]{0:T(128)S(1)}, f32[64]{0:T(128)}, u32[]{:S(2)}) copy-start(f32[64]{0:T(128)} %param.24) | copy-start | bytes 772
  1250.7 241.8 %copy-start.36 = (f32[64]{0:T(128)S(1)}, f32[64]{0:T(128)}, u32[]{:S(2)}) copy-start(f32[64]{0:T(128)} %param.33) | copy-start | bytes 772
  1250.7 241.8 %copy-start.37 = (f32[64]{0:T(128)S(1)}, f32[64]{0:T(128)}, u32[]{:S(2)}) copy-start(f32[64]{0:T(128)} %param.39) | copy-start | bytes 772
  1250.7 241.8 %copy-start.38 = (f32[64]{0:T(128)S(1)}, f32[64]{0:T(128)}, u32[]{:S(2)}) copy-start(f32[64]{0:T(128)} %param.36) | copy-start | bytes 772
  1250.7 241.8 %copy-start.39 = (f32[64]{0:T(128)S(1)}, f32[64]{0:T(128)}, u32[]{:S(2)}) copy-start(f32[64]{0:T(128)} %param.30) | copy-start | bytes 772
  1490.9 118.5 %copy-start.5 = (f32[2048,256]{1,0:T(8,128)S(1)}, f32[2048,256]{1,0:T(8,128)}, u32[]{:S(2)}) copy-start(f32[2048,256]{1,0:T(8,128)} %param.29) | copy-start | bytes 6291460
  1542.5 116.2 %copy-start.14 = (f32[256,768]{1,0:T(8,128)S(1)}, f32[256,768]{1,0:T(8,128)}, u32[]{:S(2)}) copy-start(f32[256,768]{1,0:T(8,128)} %param.25) | copy-start | bytes 2359300
Sparse Core Ops, SparseCore 0:
  10.5 34.9 all-gather.9
  47.0 80.7 all-gather.7
  130.2 26.5 all-gather.11
  174.0 289.5 all-reduce.4
  465.9 88.6 all-gather.13
  556.0 80.7 all-gather.17
  639.3 54.3 all-gather.15
  746.7 290.8 all-reduce.6
  1134.9 33.0 reduce-scatter.21
  1170.7 76.7 reduce-scatter.11
  1251.3 218.2 all-reduce.8
  1472.3 19.2 reduce-scatter.23
  1495.5 39.2 reduce-scatter.17
  1538.1 71.2 reduce-scatter.19
  1612.7 46.0 reduce-scatter.15
  1660.9 76.7 reduce-scatter.13
where the time goes:
time: 1760 us; the launch traced here: 1750 us
  waiting for transfers between devices  1290 us (73%)
  matrix products  237 us (13%)
  other arithmetic  109 us (6%)
  local copies, waits for them, and re-layouts  76.1 us (4%)
  blocking collectives  21.6 us (1%)
    psum x1, waiting for transfers between devices, per_device(): d_resid = cot_rows.astype(jnp.float32) + lax.psum(resid_part, 'seq')  290 us
    psum x1, waiting for transfers between devices, per_device(): lax.psum(jnp.dot(attended16, out_rows, preferred_element_type=jnp.float32...  282 us
    unnamed x19, waiting for transfers between devices  221 us
    all_gather x1, waiting for transfers between devices, per_device(): lax.all_gather(mlp_cast[0], 'dp', axis=0, tiled=True)  81.6 us
    all_gather x1, waiting for transfers between devices, per_device(): lax.all_gather(block_input, 'seq', axis=1, tiled=True)  77.7 us
    reduce_scatter x1, waiting for transfers between devices, per_device(): lax.psum_scatter(input_part.reshape(seqs_here, full_len, width).astype(jn...  75.7 us
    reduce_scatter x1, waiting for transfers between devices, per_device(): lax.psum_scatter(down_term.astype(jnp.bfloat16), 'dp', scatter_dimension=...  64.7 us
    all_gather x1, waiting for transfers between devices, per_device(): lax.all_gather(mlp_cast[1], 'dp', axis=1, tiled=True)  56.8 us
  transfers between devices with their start and end apart: 16, of which 14 were waited for; matrix products, arithmetic and copies ran while one was open for 14% of the time, Pallas kernels for 0%

commit v1 on v0

--- a/solution.py
+++ b/solution.py
@@ -129,20 +129,23 @@
     query_cols = kv_local * groups * HEAD_DIM
     unit_count = down_weight.shape[0]
     score_scale = HEAD_DIM ** (-0.5)
+    local_rows = seqs_here * local_len
     gain_pair = jnp.stack([attn_gain, mlp_gain]).astype(jnp.bfloat16)
-    rows_all, cot_all, gain_block = (
-        lax.all_gather(block_input, "seq", axis=1, tiled=True),
-        lax.all_gather(cotangent, "seq", axis=1, tiled=True),
-        lax.all_gather(gain_pair, "seq", axis=1, tiled=True),
-    )
-    attn_cast = (qkv_weight.astype(jnp.bfloat16), out_weight.astype(jnp.bfloat16))
-    qkv_cols, out_rows, gain_full = (
-        lax.all_gather(attn_cast[0], "dp", axis=0, tiled=True),
-        lax.all_gather(attn_cast[1], "dp", axis=1, tiled=True),
-        lax.all_gather(gain_block, "dp", axis=1, tiled=True),
-    )
-    gain_one = gain_full[0].astype(jnp.float32)
-    gain_two = gain_full[1].astype(jnp.float32)
+    gain_block = lax.all_gather(gain_pair, ("dp", "seq"), axis=1, tiled=True)
+    gain_one = gain_block[0].astype(jnp.float32)
+    gain_two = gain_block[1].astype(jnp.float32)
+    local_input = block_input.reshape(local_rows, width).astype(jnp.float32)
+    scaled_one, inverse_one, normed_here = rms_forward(local_input, gain_one)
+    normed_one = lax.all_gather(
+        normed_here.reshape(seqs_here, local_len, width), "seq", axis=1, tiled=True
+    ).reshape(total_rows, width)
+    qkv_cols = lax.all_gather(qkv_weight.astype(jnp.bfloat16), "dp", axis=0, tiled=True)
+    out_rows = lax.all_gather(out_weight.astype(jnp.bfloat16), "dp", axis=1, tiled=True)
+    gate_up_cols = lax.all_gather(
+        gate_up_weight.astype(jnp.bfloat16).reshape(-1, 2 * unit_count), "dp", axis=0, tiled=True
+    )
+    cot_all = lax.all_gather(cotangent, "seq", axis=1, tiled=True)
+    down_rows = lax.all_gather(down_weight.astype(jnp.bfloat16), "dp", axis=1, tiled=True)
     positions = segment_positions(segment_ids)
     cosine, sine = rope_tables(positions, HEAD_DIM)
     index_line = jnp.arange(full_len, dtype=jnp.int32)
@@ -150,8 +153,6 @@
         index_line[None, None, :] <= index_line[None, :, None]
     )
     allowed = allowed[:, None, None, :, :]
-    wide_input = rows_all.reshape(total_rows, width).astype(jnp.float32)
-    scaled_one, inverse_one, normed_one = rms_forward(wide_input, gain_one)
     qkv = jnp.dot(normed_one, qkv_cols, preferred_element_type=jnp.float32)
     qkv = qkv.reshape(seqs_here, full_len, kv_local, slot_count, HEAD_DIM)
     query = qkv[:, :, :, :groups].reshape(seqs_here, full_len, kv_local * groups, HEAD_DIM)
@@ -178,61 +179,58 @@
         "sgjqk,skgd->sqgjd", probs16, value16, preferred_element_type=jnp.float32
     )
     attended16 = attended16.reshape(total_rows, query_cols).astype(jnp.bfloat16)
-    attn_total = lax.psum(jnp.dot(attended16, out_rows, preferred_element_type=jnp.float32), "seq")
-    resid = wide_input + attn_total
-    mlp_cast = (gate_up_weight.astype(jnp.bfloat16), down_weight.astype(jnp.bfloat16))
-    gate_up_cols, down_rows = (
-        lax.all_gather(mlp_cast[0], "dp", axis=0, tiled=True),
-        lax.all_gather(mlp_cast[1], "dp", axis=1, tiled=True),
-    )
-    scaled_two, inverse_two, normed_two = rms_forward(resid, gain_two)
-    gate_up = jnp.dot(
-        normed_two, gate_up_cols.reshape(width, 2 * unit_count), preferred_element_type=jnp.float32
-    )
+    attn_part = jnp.dot(attended16, out_rows, preferred_element_type=jnp.float32)
+
+    def to_local(part):
+        return (
+            lax.psum_scatter(
+                part.astype(jnp.bfloat16).reshape(seqs_here, full_len, width),
+                "seq",
+                scatter_dimension=1,
+                tiled=True,
+            )
+            .astype(jnp.float32)
+            .reshape(local_rows, width)
+        )
+
+    resid = local_input + to_local(attn_part)
+    scaled_two, inverse_two, normed_two_here = rms_forward(resid, gain_two)
+    normed_two = lax.all_gather(
+        normed_two_here.reshape(seqs_here, local_len, width), "seq", axis=1, tiled=True
+    ).reshape(total_rows, width)
+    gate_up = jnp.dot(normed_two, gate_up_cols, preferred_element_type=jnp.float32)
     gate_part = gate_up[:, :unit_count]
     up_part = gate_up[:, unit_count:]
     sigmoid_gate = jax.nn.sigmoid(gate_part)
     active = gate_part * sigmoid_gate
     hidden16 = (active * up_part).astype(jnp.bfloat16)
-    down_part = jnp.dot(hidden16, down_rows, preferred_element_type=jnp.float32).reshape(
-        seqs_here, full_len, width
-    )
-    down_here = lax.psum_scatter(
-        down_part.astype(jnp.bfloat16), "seq", scatter_dimension=1, tiled=True
-    ).astype(jnp.float32)
-    offset = lax.axis_index("seq") * local_len
-    resid_here = lax.dynamic_slice_in_dim(
-        resid.reshape(seqs_here, full_len, width), offset, local_len, 1
-    )
-    output = (resid_here + down_here).astype(jnp.bfloat16)
-    gate_up_cols, down_rows = (
-        lax.all_gather(mlp_cast[0], "dp", axis=0, tiled=True),
-        lax.all_gather(mlp_cast[1], "dp", axis=1, tiled=True),
-    )
+    down_part = jnp.dot(hidden16, down_rows, preferred_element_type=jnp.float32)
+    output = (resid + to_local(down_part)).astype(jnp.bfloat16).reshape(block_input.shape)
     cot_rows = cot_all.reshape(total_rows, width)
     d_hidden = times_transpose(cot_rows, down_rows)
     d_gate = d_hidden * up_part * sigmoid_gate * (1.0 + gate_part * (1.0 - sigmoid_gate))
     d_up = d_hidden * active
     d_gate_up16 = jnp.concatenate([d_gate, d_up], 1).astype(jnp.bfloat16)
+    d_normed_two = to_local(times_transpose(d_gate_up16, gate_up_cols))
     down_term = contract_rows(cot_rows, hidden16)
-    gate_up_term = contract_rows(normed_two, d_gate_up16).reshape(width, 2, unit_count)
-    down_sum, grad_gate_up = (
-        lax.psum_scatter(
-            down_term.astype(jnp.bfloat16), "dp", scatter_dimension=0, tiled=True
-        ).astype(jnp.float32),
-        lax.psum_scatter(
-            gate_up_term.astype(jnp.bfloat16), "dp", scatter_dimension=0, tiled=True
-        ).astype(jnp.float32),
+    gate_up_term = contract_rows(normed_two, d_gate_up16)
+    down_sum = lax.psum_scatter(
+        down_term.astype(jnp.bfloat16), "dp", scatter_dimension=0, tiled=True
+    ).astype(jnp.float32)
+    grad_gate_up = (
+        lax.psum_scatter(gate_up_term.astype(jnp.bfloat16), "dp", scatter_dimension=0, tiled=True)
+        .reshape(gate_up_weight.shape)
+        .astype(jnp.float32)
     )
     grad_down = down_sum.T
-    d_normed_two = times_transpose(d_gate_up16, gate_up_cols.reshape(width, 2 * unit_count))
     resid_part, gain_two_term = rms_backward(d_normed_two, scaled_two, inverse_two, gain_two)
-    d_resid = cot_rows.astype(jnp.float32) + lax.psum(resid_part, "seq")
-    d_resid16 = d_resid.astype(jnp.bfloat16)
-    qkv_cols, out_rows = (
-        lax.all_gather(attn_cast[0], "dp", axis=0, tiled=True),
-        lax.all_gather(attn_cast[1], "dp", axis=1, tiled=True),
-    )
+    d_resid = cotangent.reshape(local_rows, width).astype(jnp.float32) + resid_part
+    d_resid16 = lax.all_gather(
+        d_resid.astype(jnp.bfloat16).reshape(seqs_here, local_len, width),
+        "seq",
+        axis=1,
+        tiled=True,
+    ).reshape(total_rows, width)
     d_attended = times_transpose(d_resid16, out_rows).astype(jnp.bfloat16)
     d_attended = d_attended.reshape(seqs_here, full_len, kv_local, groups, HEAD_DIM)
     scores = masked_scores()
@@ -256,40 +254,23 @@
     d_key = unrotate(d_key, cosine, sine)
     d_qkv16 = jnp.concatenate([d_query, d_key[:, :, :, None], d_value[:, :, :, None]], 3)
     d_qkv16 = d_qkv16.reshape(total_rows, qkv_cols.shape[1]).astype(jnp.bfloat16)
+    d_normed_one = to_local(times_transpose(d_qkv16, qkv_cols))
     qkv_term = contract_rows(normed_one, d_qkv16)
     out_term = contract_rows(d_resid16, attended16)
-    d_normed_one = times_transpose(d_qkv16, qkv_cols)
+    grad_qkv = lax.psum_scatter(
+        qkv_term.astype(jnp.bfloat16), "dp", scatter_dimension=0, tiled=True
+    ).astype(jnp.float32)
+    out_sum = lax.psum_scatter(
+        out_term.astype(jnp.bfloat16), "dp", scatter_dimension=0, tiled=True
+    ).astype(jnp.float32)
+    grad_out = out_sum.T
     input_part, gain_one_term = rms_backward(d_normed_one, scaled_one, inverse_one, gain_one)
-    gain_terms = jnp.stack([gain_one_term, gain_two_term], 1)
-    grad_qkv, out_sum, gain_sum = (
-        lax.psum_scatter(
-            qkv_term.astype(jnp.bfloat16), "dp", scatter_dimension=0, tiled=True
-        ).astype(jnp.float32),
-        lax.psum_scatter(
-            out_term.astype(jnp.bfloat16), "dp", scatter_dimension=0, tiled=True
-        ).astype(jnp.float32),
-        lax.psum_scatter(
-            gain_terms.astype(jnp.bfloat16), "dp", scatter_dimension=0, tiled=True
-        ).astype(jnp.float32),
-    )
-    grad_out = out_sum.T
-    input_here, gain_grads = (
-        lax.psum_scatter(
-            input_part.reshape(seqs_here, full_len, width).astype(jnp.bfloat16),
-            "seq",
-            scatter_dimension=1,
-            tiled=True,
-        ).astype(jnp.float32),
-        lax.psum_scatter(
-            gain_sum[None].astype(jnp.bfloat16), "seq", scatter_dimension=1, tiled=True
-        ).astype(jnp.float32),
-    )
-    d_resid_here = lax.dynamic_slice_in_dim(
-        d_resid.reshape(seqs_here, full_len, width), offset, local_len, 1
-    )
-    input_grad = (d_resid_here + input_here).astype(jnp.bfloat16)
-    grad_gain_one = gain_grads[0, :, 0]
-    grad_gain_two = gain_grads[0, :, 1]
+    input_grad = (d_resid + input_part).astype(jnp.bfloat16).reshape(block_input.shape)
+    gain_grads = lax.psum_scatter(
+        jnp.stack([gain_one_term, gain_two_term], 1), ("dp", "seq"), scatter_dimension=0, tiled=True
+    )
+    grad_gain_one = gain_grads[:, 0]
+    grad_gain_two = gain_grads[:, 1]
     w_one, m_one, v_one = adam_update(attn_gain, grad_gain_one, first_attn_gain, second_attn_gain)
     w_qkv, m_qkv, v_qkv = adam_update(qkv_weight, grad_qkv, first_qkv, second_qkv)
     w_out, m_out, v_out = adam_update(out_weight, grad_out, first_out, second_out)

time: 1760 us -> 1520 us (0.86)
  waiting for transfers between devices: 1290 us -> 1050 us
  blocking collectives: 21.6 us -> 69.8 us
  local copies, waits for them, and re-layouts: 76.1 us -> 43.9 us
  other arithmetic: 109 us -> 81.3 us
    psum x2 -> x0, waiting for transfers between devices: 573 us -> none  [the longest x1 290 us: per_device(): d_resid = cot_rows.astype(jnp.float32) + lax.psum(resid_part, 'seq')]
    reduce_scatter x2 -> x5, waiting for transfers between devices: 79.6 us -> 373 us  [the longest x4 260 us: to_local(): lax.psum_scatter(part.astype(jnp.bfloat16).reshape(seqs_here, full_len, w...]
    all_gather x6 -> x8, waiting for transfers between devices: 266 us -> 430 us  [the longest x1 90.6 us: per_device(): lax.all_gather(gate_up_weight.astype(jnp.bfloat16).reshape(-1, 2 * unit_c...]
    unnamed x19 -> x18, waiting for transfers between devices: 221 us -> 136 us
    all_gather x2 -> x1, blocking collectives: 21.6 us -> 69.8 us  [per_device(): gain_block = lax.all_gather(gain_pair, ('dp', 'seq'), axis=1, tiled=True)]
    reduce_scatter x1, waiting for transfers between devices: 64.7 us -> 40.1 us  [per_device(): lax.psum_scatter(down_term.astype(jnp.bfloat16), 'dp', scatter_dimension=...]
    convert_element_type x1, local copies, waits for them, and re-layouts: 28 us -> 6.56 us  [per_device(): grad_gate_up = lax.psum_scatter(gate_up_term.astype(jnp.bfloat16), 'dp',...]
    unnamed x103 -> x78, local copies, waits for them, and re-layouts: 37.3 us -> 20 us
  transfers between devices with their start and end apart: 16 -> 17, of which waited for: 14 -> 15; matrix products, arithmetic and copies ran while one was open for 14% -> 12% of each run, Pallas kernels for 0% -> 0%
where the time goes in v1:
time: 1520 us; the launch traced here: 1510 us
  waiting for transfers between devices  1050 us (69%)
  matrix products  248 us (16%)
  other arithmetic  81.3 us (5%)
  blocking collectives  69.8 us (5%)
  local copies, waits for them, and re-layouts  43.9 us (3%)
    reduce_scatter x4, waiting for transfers between devices, to_local(): lax.psum_scatter(part.astype(jnp.bfloat16).reshape(seqs_here, full_len, w...  260 us
    unnamed x18, waiting for transfers between devices  136 us
    reduce_scatter x1, waiting for transfers between devices, per_device(): lax.psum_scatter(gate_up_term.astype(jnp.bfloat16), 'dp', scatter_dimensi...  114 us
    all_gather x1, waiting for transfers between devices, per_device(): lax.all_gather(gate_up_weight.astype(jnp.bfloat16).reshape(-1, 2 * unit_c...  90.6 us
    all_gather x1, waiting for transfers between devices, per_device(): lax.all_gather(d_resid.astype(jnp.bfloat16).reshape(seqs_here, local_len,...  81.3 us
    all_gather x1, waiting for transfers between devices, per_device(): lax.all_gather(normed_two_here.reshape(seqs_here, local_len, width), 'seq...  72.9 us
    all_gather x1, waiting for transfers between devices, per_device(): lax.all_gather(normed_here.reshape(seqs_here, local_len, width), 'seq', a...  70 us
    all_gather x1, blocking collectives, per_device(): gain_block = lax.all_gather(gain_pair, ('dp', 'seq'), axis=1, tiled=True)  69.8 us
  transfers between devices with their start and end apart: 17, of which 15 were waited for; matrix products, arithmetic and copies ran while one was open for 12% of the time, Pallas kernels for 0%

profile of v1, /device:TPU:0, one launch (start us, length us, event | category | flops | bytes accessed | tf_op | source)
XLA Modules:
  0.0 1514.0 jit_solution(13102967327842110868)
XLA Ops:
  7.3 2.0 convert_element_type.162
  10.0 69.8 %all-gather = bf16[32,64,2]{1,2,0:T(2,128)(2,1)S(1)} all-gather(bf16[1,64,2]{1,2,0:T(2,128)(2,1)S(1)} %maximum_bitcast_fusion.4), channel_id=1, replica_groups=mesh['dp'=8,'seq'=4] {'dp','seq'}, dimensions={0}, use_global_device_ids=true | all-gather | bytes 8448 | tf_op jit(solution)/shard_map/all_gather | solution.py:134
  79.9 1.5 fusion.32
  81.5 2.5 fusion.29
  86.3 4.8 copy.86
  91.1 70.0 %all-gather.10.cloned.1.call-done = bf16[2,512,2048]{2,1,0:T(8,128)(2,1)} async-done(((bf16[2,128,2048]{2,1,0:T(8,128)(2,1)}), bf16[2,512,2048]{2,1,0:T(8,128)(2,1)}) %all-gather.10.cloned.1.call-update) | async-done | bytes 4194320 | tf_op jit(solution)/shard_map/all_gather | solution.py:139
  161.2 6.3 fusion.9
  169.2 7.4 fusion.5
  176.6 9.6 exponential_reduce_fusion
  186.2 10.3 fusion.35
  196.5 1.1 copy.88
  197.9 6.4 convolution_convert_fusion.2
  204.3 75.1 %reduce-scatter.12.cloned.1.call-done = bf16[2,128,2048]{2,1,0:T(8,128)(2,1)} async-done(((bf16[2,512,2048]{2,1,0:T(8,128)(2,1)}), bf16[2,128,2048]{2,1,0:T(8,128)(2,1)}) %reduce-scatter.12.cloned.1.call-update) | async-done | bytes 1048592 | tf_op jit(solution)/shard_map/reduce_scatter | solution.py:186
  279.4 1.6 multiply_reduce_fusion
  281.0 2.6 multiply_convert_fusion.3
  283.7 4.2 convert_element_type.174
  287.9 2.2 copy.122
  292.1 72.9 %all-gather.16.cloned.1.call-done = bf16[2,512,2048]{2,1,0:T(8,128)(2,1)} async-done(((bf16[2,128,2048]{2,1,0:T(8,128)(2,1)}), bf16[2,512,2048]{2,1,0:T(8,128)(2,1)}) %all-gather.16.cloned.1.call-update) | async-done | bytes 4194320 | tf_op jit(solution)/shard_map/all_gather | solution.py:198
  365.0 90.6 %all-gather.18.cloned.1.call-done = bf16[2048,4096]{1,0:T(8,128)(2,1)} async-done(((bf16[256,4096]{1,0:T(8,128)(2,1)}), bf16[2048,4096]{1,0:T(8,128)(2,1)}) %all-gather.18.cloned.1.call-update) | async-done | bytes 16777232 | tf_op jit(solution)/shard_map/all_gather | solution.py:144
  455.6 23.9 %fusion.71 = f32[1024,4096]{1,0:T(8,128)} fusion(bf16[1024,2048]{1,0:T(8,128)(2,1)} %bitcast.221, bf16[2048,4096]{1,0:T(8,128)(2,1)} %all-gather.18.cloned.1.call-done), kind=kOutput, calls=%fused_computation.139 | convolution fusion | flops 17179869184 | bytes 37748736 | tf_op jit(solution)/shard_map/dot_general | solution.py:201
  479.5 58.4 %all-gather.22.cloned.1.call-done = bf16[2,512,2048]{2,1,0:T(8,128)(2,1)} async-done(((bf16[2,128,2048]{2,1,0:T(8,128)(2,1)}), bf16[2,512,2048]{2,1,0:T(8,128)(2,1)}) %all-gather.22.cloned.1.call-update) | async-done | bytes 4194320 | tf_op jit(solution)/shard_map/all_gather | solution.py:147
  538.0 56.8 %all-gather.20.cloned.1.call-done = bf16[2048,2048]{1,0:T(8,128)(2,1)} async-done(((bf16[2048,256]{1,0:T(8,128)(2,1)}), bf16[2048,2048]{1,0:T(8,128)(2,1)}) %all-gather.20.cloned.1.call-update) | async-done | bytes 8388624 | tf_op jit(solution)/shard_map/all_gather | solution.py:148
  594.8 21.7 %multiply_convert_fusion.1 = (bf16[1024,2048]{1,0:T(8,128)(2,1)}, bf16[1024,2048]{1,0:T(8,128)(2,1)}, bf16[1024,2048]{1,0:T(8,128)(2,1)}) fusion(f32[1024,4096]{1,0:T(8,128)} %fusion.71, bf16[1024,2048]{1,0:T(8,128)(2,1)} %bitcast.223, bf16[2048,2048]{1,0:T(8,128)(2,1)} %all-gather.20.cloned.1.call-done), kind=kOutput, calls=%fused_computation.15 | convolution fusion | flops 8621391872 | bytes 41943040 | tf_op jit(solution)/shard_map/dot_general | solution.py:95
  616.5 23.8 %fusion.11 = bf16[1024,2048]{1,0:T(8,128)(2,1)} fusion(bf16[2048,4096]{1,0:T(8,128)(2,1)} %all-gather.18.cloned.1.call-done, bf16[1024,2048]{1,0:T(8,128)(2,1)} %get-tuple-element.129, bf16[1024,2048]{1,0:T(8,128)(2,1)} %get-tuple-element.128), kind=kOutput, calls=%fused_computation.26 | convolution fusion | flops 17198743552 | bytes 29360128 | tf_op jit(solution)/shard_map/dot_general | solution.py:95
  640.6 76.7 %reduce-scatter.16.cloned.1.call-done = bf16[2,128,2048]{2,1,0:T(8,128)(2,1)} async-done(((bf16[2,512,2048]{2,1,0:T(8,128)(2,1)}), bf16[2,128,2048]{2,1,0:T(8,128)(2,1)}) %reduce-scatter.16.cloned.1.call-update) | async-done | bytes 1048592 | tf_op jit(solution)/shard_map/reduce_scatter | solution.py:186
  717.3 2.0 fusion.28
  719.4 3.2 fusion.38
  722.7 81.3 %all-gather.24.cloned.1.call-done = bf16[2,512,2048]{2,1,0:T(8,128)(2,1)} async-done(((bf16[2,128,2048]{2,1,0:T(8,128)(2,1)}), bf16[2,512,2048]{2,1,0:T(8,128)(2,1)}) %all-gather.24.cloned.1.call-update) | async-done | bytes 4194320 | tf_op jit(solution)/shard_map/all_gather | solution.py:228
  804.0 6.2 convolution_convert_fusion.7
  810.2 4.6 reshape.347
  814.8 4.0 copy.90
  818.9 9.5 fusion.42
  828.4 24.6 %fusion.18 = f32[2,2,64,4,512]{4,2,3,1,0:T(8,128)} fusion(f32[2,2,512,512,4]{3,2,4,1,0:T(8,128)} %fusion.42, f32[2,2,512,512,4]{3,2,4,1,0:T(8,128)} %get-tuple-element.148, f32[2,2,4,512]{3,2,1,0:T(4,128)S(1)} %bitcast.215, pred[2,512,512]{1,2,0:T(8,128)(4,1)} %copy-done.10, bf16[2,512,2,32]{1,3,2,0:T(8,128)(2,1)S(1)} %get-tuple-element.140, ...), kind=kOutput, calls=%fused_computation.42 | convolution fusion | flops 583541248 | bytes 36470784 | tf_op jit(solution)/shard_map/sgjqk,skgd->sqgjd/dot_general | solution.py:243
  853.0 24.9 %fusion.36 = f32[2,512,2,64]{1,3,2,0:T(8,128)} fusion(f32[2,2,512,512,4]{3,2,4,1,0:T(8,128)} %fusion.42, f32[2,2,512,512,4]{3,2,4,1,0:T(8,128)} %get-tuple-element.148, f32[2,2,4,512]{3,2,1,0:T(4,128)S(1)} %bitcast.216, pred[2,512,512]{1,2,0:T(8,128)(4,1)} %copy-done.10, bf16[2,512,2,4,32]{1,4,3,2,0:T(8,128)(2,1)} %bitcast.201, ...), kind=kOutput, calls=%fused_computation.75 | convolution fusion | flops 585114112 | bytes 35684352 | tf_op jit(solution)/shard_map/sgjqk,sqgjd->skgd/dot_general | solution.py:244
  877.9 10.3 convolution_bitcast_fusion
  890.5 6.1 maximum_convert_fusion
  897.1 5.0 convolution_convert_fusion.3
  902.2 14.5 convert_bitcast_fusion
  916.8 6.2 convolution_convert_fusion.5
  923.1 7.9 convolution_convert_fusion.4
  931.1 14.0 convolution_convert_fusion.1
  945.2 32.4 %reduce-scatter.18.cloned.1.call-done = bf16[2,128,2048]{2,1,0:T(8,128)(2,1)} async-done(((bf16[2,512,2048]{2,1,0:T(8,128)(2,1)}), bf16[2,128,2048]{2,1,0:T(8,128)(2,1)}) %reduce-scatter.18.cloned.1.call-update) | async-done | bytes 1048592 | tf_op jit(solution)/shard_map/reduce_scatter | solution.py:186
  977.6 1.9 fusion.31
  979.6 1.3 copy.115
  981.0 25.4 %convolution_convert_fusion = bf16[2048,4096]{1,0:T(8,128)(2,1)} fusion(bf16[1024,2048]{1,0:T(8,128)(2,1)} %bitcast.222, bf16[1024,2048]{1,0:T(8,128)(2,1)} %get-tuple-element.129, bf16[1024,2048]{1,0:T(8,128)(2,1)} %get-tuple-element.128), kind=kOutput, calls=%fused_computation.9 | convolution fusion | flops 17205035008 | bytes 29360128 | tf_op jit(solution)/shard_map/dot_general | solution.py:89
  1006.4 2.2 copy.101
  1008.6 2.0 copy.98
  1010.7 2.0 copy.99
  1012.7 40.1 %reduce-scatter.26.cloned.1.call-done = bf16[256,2048]{0,1:T(8,128)(2,1)} async-done(((bf16[2048,2048]{0,1:T(8,128)(2,1)}), bf16[256,2048]{0,1:T(8,128)(2,1)}) %reduce-scatter.26.cloned.1.call-update) | async-done | bytes 1048592 | tf_op jit(solution)/shard_map/reduce_scatter | solution.py:217
  1052.8 6.9 multiply_subtract_fusion.1
  1059.6 37.5 %reduce-scatter.22.cloned.1.call-done = bf16[256,512]{1,0:T(8,128)(2,1)} async-done(((bf16[2048,512]{1,0:T(8,128)(2,1)}), bf16[256,512]{1,0:T(8,128)(2,1)}) %reduce-scatter.22.cloned.1.call-update) | async-done | bytes 262160 | tf_op jit(solution)/shard_map/reduce_scatter | solution.py:263
  1097.2 2.9 multiply_subtract_fusion.4
  1100.1 2.0 copy.103
  1102.1 2.0 copy.104
  1104.2 2.0 copy.105
  1107.0 2.1 copy.102
  1109.1 37.4 %reduce-scatter.20.cloned.1.call-done = bf16[256,768]{1,0:T(8,128)(2,1)} async-done(((bf16[2048,768]{1,0:T(8,128)(2,1)}), bf16[256,768]{1,0:T(8,128)(2,1)}) %reduce-scatter.20.cloned.1.call-update) | async-done | bytes 393232 | tf_op jit(solution)/shard_map/reduce_scatter | solution.py:260
  1146.5 3.5 multiply_subtract_fusion.3
  1150.1 75.4 %reduce-scatter.14.cloned.1.call-done = bf16[2,128,2048]{2,1,0:T(8,128)(2,1)} async-done(((bf16[2,512,2048]{2,1,0:T(8,128)(2,1)}), bf16[2,128,2048]{2,1,0:T(8,128)(2,1)}) %reduce-scatter.14.cloned.1.call-update) | async-done | bytes 1048592 | tf_op jit(solution)/shard_map/reduce_scatter | solution.py:186
  1225.5 4.9 fusion.24
  1230.4 135.3 %reduce-scatter.28.cloned.1.call-done = f32[64,2]{1,0:T(8,128)} async-done(((f32[2048,2]{1,0:T(8,128)}), f32[64,2]{1,0:T(8,128)}) %reduce-scatter.28.cloned.1.call-update) | async-done | bytes 528
  1367.9 113.8 %reduce-scatter.24.cloned.1.call-done = bf16[256,4096]{1,0:T(8,128)(2,1)} async-done(((bf16[2048,4096]{1,0:T(8,128)(2,1)}), bf16[256,4096]{1,0:T(8,128)(2,1)}) %reduce-scatter.24.cloned.1.call-update) | async-done | bytes 2097168 | tf_op jit(solution)/shard_map/reduce_scatter | solution.py:221
  1481.7 6.6 reshape.336
  1488.3 18.9 %multiply_subtract_fusion = (f32[256,2,2048]{2,1,0:T(2,128)}, f32[256,2,2048]{2,1,0:T(2,128)}, f32[256,2,2048]{2,1,0:T(2,128)}) fusion(f32[256,2,2048]{2,1,0:T(2,128)} %param.28, f32[256,2,2048]{2,1,0:T(2,128)} %reshape.336, f32[256,2,2048]{2,1,0:T(2,128)} %param.34, f32[256,2,2048]{2,1,0:T(2,128)} %param.40), kind=kLoop, calls=%fused_computation.24 | loop fusion | flops 15728640 | bytes 29360128 | tf_op jit(solution)/shard_map/sub | solution.py:82
  (138 shorter events, 13.5 us)
Async XLA Ops:
  7.2 76.8 %copy-start.11 = (f32[512,256]{1,0:T(8,128)S(1)}, f32[512,256]{1,0:T(8,128)}, u32[]{:S(2)}) copy-start(f32[512,256]{1,0:T(8,128)} %param.26) | copy-start | bytes 1572868
  7.2 77.8 %copy-start.21 = (s32[2,512]{1,0:T(2,128)S(1)}, s32[2,512]{1,0:T(2,128)}, u32[]{:S(2)}) copy-start(s32[2,512]{1,0:T(2,128)} %param.22) | copy-start | bytes 12292
  7.2 79.1 %all-gather.12.cloned.1.call-start = ((), (), s32[]{:S(2)}) async-start(), calls=%async_computation.10 | async-start | bytes 3538944 | tf_op jit(solution)/shard_map/all_gather | solution.py:142
  9.3 151.9 %all-gather.10.cloned.1.call-start = ((), (), s32[]{:S(2)}) async-start(), calls=%async_computation.9 | async-start | bytes 5242880 | tf_op jit(solution)/shard_map/all_gather | solution.py:139
  81.4 3.8 copy-start.22
  81.5 3.8 copy-start.19
  84.0 113.9 %all-gather.14.cloned.1.call-start = ((), (), s32[]{:S(2)}) async-start(), calls=%async_computation.11 | async-start | bytes 2359296 | tf_op jit(solution)/shard_map/all_gather | solution.py:143
  84.8 194.6 %reduce-scatter.12.cloned.1.call-start = ((), (), s32[]{:S(2)}) async-start(), calls=%async_computation.12 | async-start | bytes 5242880 | tf_op jit(solution)/shard_map/reduce_scatter | solution.py:186
  85.7 100.4 %copy-start.10 = (pred[2,512,512]{1,2,0:T(8,128)(4,1)}, pred[2,512,512]{1,2,0:T(8,128)(4,1)S(1)}, u32[]{:S(2)}) copy-start(pred[2,512,512]{1,2,0:T(8,128)(4,1)S(1)} %compare_and_fusion) | copy-start | bytes 1572868
  86.3 81.5 %copy-start.4 = (f32[2,512,32]{1,2,0:T(8,128)}, f32[2,512,32]{1,2,0:T(8,128)S(1)}, u32[]{:S(2)}) copy-start(f32[2,512,32]{1,2,0:T(8,128)S(1)} %get-tuple-element.145) | copy-start | bytes 393220
  86.3 81.5 %copy-start.6 = (f32[2,512,32]{1,2,0:T(8,128)}, f32[2,512,32]{1,2,0:T(8,128)S(1)}, u32[]{:S(2)}) copy-start(f32[2,512,32]{1,2,0:T(8,128)S(1)} %get-tuple-element.146) | copy-start | bytes 393220
  167.5 1.7 copy-start.9
  169.2 7.4 copy-start.17
  169.2 7.4 copy-start.18
  197.9 6.4 copy-start.14
  204.2 75.1 %copy-start = (bf16[2,128,2048]{2,1,0:T(8,128)(2,1)S(1)}, bf16[2,128,2048]{2,1,0:T(8,128)(2,1)}, u32[]{:S(2)}) copy-start(bf16[2,128,2048]{2,1,0:T(8,128)(2,1)} %param.21) | copy-start | bytes 3145732
  204.3 160.8 %all-gather.16.cloned.1.call-start = ((), (), s32[]{:S(2)}) async-start(), calls=%async_computation.13 | async-start | bytes 5242880 | tf_op jit(solution)/shard_map/all_gather | solution.py:198
  283.7 172.0 %all-gather.18.cloned.1.call-start = ((), (), s32[]{:S(2)}) async-start(), calls=%async_computation.14 | async-start | bytes 18874368 | tf_op jit(solution)/shard_map/all_gather | solution.py:144
  287.9 3.1 copy-start.3
  290.2 247.8 %all-gather.22.cloned.1.call-start = ((), (), s32[]{:S(2)}) async-start(), calls=%async_computation.17 | async-start | bytes 5242880 | tf_op jit(solution)/shard_map/all_gather | solution.py:147
  290.9 303.9 %all-gather.20.cloned.1.call-start = ((), (), s32[]{:S(2)}) async-start(), calls=%async_computation.15 | async-start | bytes 9437184 | tf_op jit(solution)/shard_map/all_gather | solution.py:148
  292.1 425.2 %reduce-scatter.16.cloned.1.call-start = ((), (), s32[]{:S(2)}) async-start(), calls=%async_computation.18 | async-start | bytes 5242880 | tf_op jit(solution)/shard_map/reduce_scatter | solution.py:186
  640.3 77.0 %copy-start.1 = (bf16[2,128,2048]{2,1,0:T(8,128)(2,1)S(1)}, bf16[2,128,2048]{2,1,0:T(8,128)(2,1)}, u32[]{:S(2)}) copy-start(bf16[2,128,2048]{2,1,0:T(8,128)(2,1)} %reduce-scatter.12.cloned.1.call-done) | copy-start | bytes 3145732
  640.3 79.0 %copy-start.2 = (bf16[2,128,2048]{2,1,0:T(8,128)(2,1)S(1)}, bf16[2,128,2048]{2,1,0:T(8,128)(2,1)}, u32[]{:S(2)}) copy-start(bf16[2,128,2048]{2,1,0:T(8,128)(2,1)} %param.23) | copy-start | bytes 3145732
  640.4 163.6 %all-gather.24.cloned.1.call-start = ((), (), s32[]{:S(2)}) async-start(), calls=%async_computation.19 | async-start | bytes 5242880 | tf_op jit(solution)/shard_map/all_gather | solution.py:228
  722.6 255.0 %reduce-scatter.18.cloned.1.call-start = ((), (), s32[]{:S(2)}) async-start(), calls=%async_computation.20 | async-start | bytes 5242880 | tf_op jit(solution)/shard_map/reduce_scatter | solution.py:186
  877.9 10.4 copy-start.5
  877.9 10.4 copy-start.7
  877.9 10.3 copy-start.12
  888.2 1.6 copy-start.16
  889.9 7.2 copy-start.8
  897.1 5.1 copy-start.13
  902.2 150.6 %reduce-scatter.26.cloned.1.call-start = ((), (), s32[]{:S(2)}) async-start(), calls=%async_computation.24 | async-start | bytes 9437184 | tf_op jit(solution)/shard_map/reduce_scatter | solution.py:217
  916.8 180.4 %reduce-scatter.22.cloned.1.call-start = ((), (), s32[]{:S(2)}) async-start(), calls=%async_computation.22 | async-start | bytes 2359296 | tf_op jit(solution)/shard_map/reduce_scatter | solution.py:263
  923.0 223.5 %reduce-scatter.20.cloned.1.call-start = ((), (), s32[]{:S(2)}) async-start(), calls=%async_computation.21 | async-start | bytes 3538944 | tf_op jit(solution)/shard_map/reduce_scatter | solution.py:260
  931.0 294.5 %reduce-scatter.14.cloned.1.call-start = ((), (), s32[]{:S(2)}) async-start(), calls=%async_computation.16 | async-start | bytes 5242880 | tf_op jit(solution)/shard_map/reduce_scatter | solution.py:186
  945.1 32.5 %copy-start.20 = (f32[1,2048]{1,0:T(1,128)S(1)}, f32[1,2048]{1,0:T(1,128)}, u32[]{:S(2)}) copy-start(f32[1,2048]{1,0:T(1,128)} %copy-done.19) | copy-start | bytes 24580
  945.1 32.5 %copy-start.23 = (f32[2,128]{1,0:T(2,128)S(1)}, f32[2,128]{1,0:T(2,128)}, u32[]{:S(2)}) copy-start(f32[2,128]{1,0:T(2,128)} %copy-done.22) | copy-start | bytes 3076
  945.1 420.6 %reduce-scatter.28.cloned.1.call-start = ((), (), s32[]{:S(2)}) async-start(), calls=%async_computation.25 | async-start | bytes 1081344
  981.0 500.8 %reduce-scatter.24.cloned.1.call-start = ((), (), s32[]{:S(2)}) async-start(), calls=%async_computation.23 | async-start | bytes 18874368 | tf_op jit(solution)/shard_map/reduce_scatter | solution.py:221
  1097.2 9.0 copy-start.15
  1150.0 216.7 %copy-start.26 = (f32[64]{0:T(128)S(1)}, f32[64]{0:T(128)}, u32[]{:S(2)}) copy-start(f32[64]{0:T(128)} %param.27) | copy-start | bytes 772
  1150.0 216.7 %copy-start.28 = (f32[64]{0:T(128)S(1)}, f32[64]{0:T(128)}, u32[]{:S(2)}) copy-start(f32[64]{0:T(128)} %param.33) | copy-start | bytes 772
  1150.0 216.7 %copy-start.29 = (f32[64]{0:T(128)S(1)}, f32[64]{0:T(128)}, u32[]{:S(2)}) copy-start(f32[64]{0:T(128)} %param.39) | copy-start | bytes 772
  1150.0 217.3 %copy-start.27 = (f32[64]{0:T(128)S(1)}, f32[64]{0:T(128)}, u32[]{:S(2)}) copy-start(f32[64]{0:T(128)} %param.24) | copy-start | bytes 772
  1150.1 217.3 %copy-start.30 = (f32[64]{0:T(128)S(1)}, f32[64]{0:T(128)}, u32[]{:S(2)}) copy-start(f32[64]{0:T(128)} %param.30) | copy-start | bytes 772
  1150.1 217.3 %copy-start.31 = (f32[64]{0:T(128)S(1)}, f32[64]{0:T(128)}, u32[]{:S(2)}) copy-start(f32[64]{0:T(128)} %param.36) | copy-start | bytes 772
  1366.7 140.5 %copy-start.24 = (f32[64,1]{0,1:T(1,128)}, f32[64,1]{0,1:T(1,128)S(1)}, u32[]{:S(2)}) copy-start(f32[64,1]{0,1:T(1,128)S(1)} %copy.120) | copy-start | bytes 772
  1366.8 140.4 %copy-start.25 = (f32[64,1]{0,1:T(1,128)}, f32[64,1]{0,1:T(1,128)S(1)}, u32[]{:S(2)}) copy-start(f32[64,1]{0,1:T(1,128)S(1)} %copy.119) | copy-start | bytes 772
Sparse Core Ops, SparseCore 0:
  10.5 34.9 all-gather.11
  84.1 76.9 all-gather.9
  163.6 26.5 all-gather.13
  204.4 74.9 reduce-scatter.11
  283.8 81.2 all-gather.15
  367.4 88.2 all-gather.17
  457.2 80.7 all-gather.21
  540.4 54.3 all-gather.19
  640.5 76.7 reduce-scatter.15
  722.7 81.2 all-gather.23
  902.3 75.2 reduce-scatter.17
  980.9 71.7 reduce-scatter.25
  1056.1 41.0 reduce-scatter.21
  1100.4 46.0 reduce-scatter.19
  1148.6 76.7 reduce-scatter.13
  1228.1 137.5 reduce-scatter.27
  1369.1 112.5 reduce-scatter.23

commit v2 on v1

v2 whole, which is shorter than its diff:
```python
import functools

import jax
import jax.numpy as jnp
from jax import lax
from jax.experimental import pallas as pl
from jax.experimental.pallas import tpu as pltpu
from jax.sharding import PartitionSpec as P

HEADS = 32
KV_HEADS = 8
norm_eps = 1e-05
rope_base = 500000.0
beta_one = 0.9
beta_two = 0.95
learn_rate = 0.01
weight_decay = 0.1
adam_eps = 1e-08
step_count = 10.0
masked_score = -1e30


HEAD_DIM = 64
LANES = 128


def dot_t(a, b):
    return lax.dot_general(a, b, (((1,), (1,)), ((), ())), preferred_element_type=jnp.float32)


def dot_n(a, b):
    return lax.dot_general(a, b, (((1,), (0,)), ((), ())), preferred_element_type=jnp.float32)


def dot_c(a, b):
    return lax.dot_general(a, b, (((0,), (0,)), ((), ())), preferred_element_type=jnp.float32)


def swap_halves(u):
    lane = lax.broadcasted_iota(jnp.int32, u.shape, 1)
    return jnp.where(lane % 64 < 32, pltpu.roll(u, 96, 1), pltpu.roll(u, 32, 1))


def turn(u, cos_wide, sin_wide):
    return u * cos_wide + swap_halves(u) * sin_wide


def key_start(block, q_rows, reach):
    return max(0, (block * q_rows - reach + 1) // q_rows * q_rows)


def attn_forward_kernel(pairs, q_rows, reach, qkv_ref, cos_ref, sin_ref, seg_col_ref, seg_row_ref,
                        turned_ref, lse_ref, out_ref):
    full_len = qkv_ref.shape[0]
    lane = lax.broadcasted_iota(jnp.int32, (full_len, LANES), 1)
    low = lane < HEAD_DIM
    cos_q = cos_ref[...]
    sin_q = sin_ref[...]
    kv = qkv_ref[:, pairs * LANES:].astype(jnp.float32)
    kv16 = turn(kv, jnp.where(low, cos_q, 1.0), jnp.where(low, sin_q, 0.0)).astype(jnp.bfloat16)
    turned_ref[:, pairs * LANES:] = kv16
    kv32 = kv16.astype(jnp.float32)
    rolled = pltpu.roll(kv32, HEAD_DIM, 1)
    zero = jnp.zeros_like(kv32)
    keys = (jnp.where(low, kv32, zero).astype(jnp.bfloat16), jnp.where(low, zero, rolled).astype(jnp.bfloat16))
    vals = (jnp.where(low, rolled, zero).astype(jnp.bfloat16), jnp.where(low, zero, kv32).astype(jnp.bfloat16))
    for pair in range(pairs):
        cols = slice(pair * LANES, (pair + 1) * LANES)
        query = turn(qkv_ref[:, cols].astype(jnp.float32), cos_q, sin_q) .astype(jnp.bfloat16)
        turned_ref[:, cols] = query
    for block in range(full_len // q_rows):
        first = key_start(block, q_rows, reach)
        last = (block + 1) * q_rows
        rows = slice(block * q_rows, last)
        span = slice(first, last)
        i = lax.broadcasted_iota(jnp.int32, (q_rows, last - first), 0) + block * q_rows
        j = lax.broadcasted_iota(jnp.int32, (q_rows, last - first), 1) + first
        allowed = (j <= i) & (seg_col_ref[rows, :1] == seg_row_ref[:1, span])
        for pair in range(pairs):
            cols = slice(pair * LANES, (pair + 1) * LANES)
            query = turned_ref[rows, cols]
            total = None
            for half in range(2):
                scores = dot_t(query, keys[half][span]) * (HEAD_DIM ** -0.5)
                scores = jnp.where(allowed, scores, masked_score)
                top = jnp.max(scores, axis=1, keepdims=True)
                lse = top + jnp.log(jnp.sum(jnp.exp(scores - top), axis=1, keepdims=True))
                probs = jnp.exp(scores - lse).astype(jnp.bfloat16)
                part = dot_n(probs, vals[half][span])
                total = part if total is None else total + part
                head = 2 * pair + half
                lse_ref[rows, head:head + 1] = lse
            out_ref[rows, cols] = total.astype(jnp.bfloat16)


def attn_backward_kernel(pairs, q_rows, reach, turned_ref, d_out_ref, lse_ref, cos_ref, sin_ref, seg_col_ref,
                         seg_row_ref, grad_ref, dk_ref, dv_ref):
    full_len = turned_ref.shape[0]
    lane = lax.broadcasted_iota(jnp.int32, (full_len, LANES), 1)
    low = lane < HEAD_DIM
    kv32 = turned_ref[:, pairs * LANES:].astype(jnp.float32)
    rolled = pltpu.roll(kv32, HEAD_DIM, 1)
    zero = jnp.zeros_like(kv32)
    keys = (jnp.where(low, kv32, zero).astype(jnp.bfloat16), jnp.where(low, zero, rolled).astype(jnp.bfloat16))
    vals = (jnp.where(low, rolled, zero).astype(jnp.bfloat16), jnp.where(low, zero, kv32).astype(jnp.bfloat16))
    dk_ref[...] = jnp.zeros_like(dk_ref)
    dv_ref[...] = jnp.zeros_like(dv_ref)
    low_rows = low[:q_rows]
    scale = HEAD_DIM ** -0.5
    for block in range(full_len // q_rows):
        first = key_start(block, q_rows, reach)
        last = (block + 1) * q_rows
        rows = slice(block * q_rows, last)
        span = slice(first, last)
        i = lax.broadcasted_iota(jnp.int32, (q_rows, last - first), 0) + block * q_rows
        j = lax.broadcasted_iota(jnp.int32, (q_rows, last - first), 1) + first
        allowed = (j <= i) & (seg_col_ref[rows, :1] == seg_row_ref[:1, span])
        cos_q = cos_ref[rows]
        sin_q = sin_ref[rows]
        for pair in range(pairs):
            cols = slice(pair * LANES, (pair + 1) * LANES)
            query = turned_ref[rows, cols]
            d_out = d_out_ref[rows, cols]
            q32 = query.astype(jnp.float32)
            o32 = d_out.astype(jnp.float32)
            d_query = None
            d_key = None
            d_val = None
            for half in range(2):
                keep = low_rows if half == 0 else ~low_rows
                q_only = jnp.where(keep, q32, 0.0).astype(jnp.bfloat16)
                o_only = jnp.where(keep, o32, 0.0).astype(jnp.bfloat16)
                head = 2 * pair + half
                scores = dot_t(query, keys[half][span]) * scale
                scores = jnp.where(allowed, scores, masked_score)
                probs = jnp.exp(scores - lse_ref[rows, head:head + 1])
                d_probs = dot_t(d_out, vals[half][span])
                delta = jnp.sum(probs * d_probs, axis=1, keepdims=True)
                d_scores = (probs * (d_probs - delta) * scale).astype(jnp.bfloat16)
                probs16 = probs.astype(jnp.bfloat16)
                dq = dot_n(d_scores, keys[half][span])
                dk = dot_c(d_scores, q_only)
                dv = dot_c(probs16, o_only)
                d_query = dq if d_query is None else d_query + dq
                d_key = dk if d_key is None else d_key + dk
                d_val = dv if d_val is None else d_val + dv
            dk_ref[span] = dk_ref[span] + d_key
            dv_ref[span] = dv_ref[span] + d_val
            grad_ref[rows, cols] = turn(d_query, cos_q, -sin_q).astype(jnp.bfloat16)
    d_key = dk_ref[...]
    d_val = dv_ref[...]
    d_key = d_key + pltpu.roll(d_key, HEAD_DIM, 1)
    d_val = d_val + pltpu.roll(d_val, HEAD_DIM, 1)
    d_key = turn(d_key, cos_ref[...], -sin_ref[...])
    grad_ref[:, pairs * LANES:] = jnp.where(low, d_key, d_val).astype(jnp.bfloat16)


def attn_specs(full_len, width):
    line = pl.BlockSpec((full_len, width), lambda s, g: (s, g))
    table = pl.BlockSpec((full_len, LANES), lambda s, g: (s, 0))
    row = pl.BlockSpec((8, full_len), lambda s, g: (s, 0))
    return line, table, row


Q_ROWS = 128
REACH = 256


def attn_forward(qkv, cos, sin, seg_col, seg_row, full_len, groups):
    pairs = groups // 2
    width = (groups + 2) * HEAD_DIM
    seqs = qkv.shape[0] // full_len
    kv = qkv.shape[1] // width
    line, table, row = attn_specs(full_len, width)
    outw = pl.BlockSpec((full_len, groups * HEAD_DIM), lambda s, g: (s, g))
    rows = seqs * full_len
    return pl.pallas_call(
        functools.partial(attn_forward_kernel, pairs, Q_ROWS, REACH),
        grid=(seqs, kv),
        in_specs=[line, table, table, table, row],
        out_specs=[line, pl.BlockSpec((full_len, LANES), lambda s, g: (s, g)), outw],
        out_shape=[
            jax.ShapeDtypeStruct((rows, kv * width), jnp.bfloat16),
            jax.ShapeDtypeStruct((rows, kv * LANES), jnp.float32),
            jax.ShapeDtypeStruct((rows, kv * groups * HEAD_DIM), jnp.bfloat16),
        ],
        cost_estimate=pl.CostEstimate(flops=4 * rows * full_len * kv * LANES * groups, bytes_accessed=rows * kv * width * 6, transcendentals=0),
        name="attn_forward",
    )(qkv, cos, sin, seg_col, seg_row)


def attn_backward(turned, d_out, lse, cos, sin, seg_col, seg_row, full_len, groups):
    pairs = groups // 2
    width = (groups + 2) * HEAD_DIM
    seqs = turned.shape[0] // full_len
    kv = turned.shape[1] // width
    line, table, row = attn_specs(full_len, width)
    outw = pl.BlockSpec((full_len, groups * HEAD_DIM), lambda s, g: (s, g))
    rows = seqs * full_len
    return pl.pallas_call(
        functools.partial(attn_backward_kernel, pairs, Q_ROWS, REACH),
        grid=(seqs, kv),
        in_specs=[line, outw, pl.BlockSpec((full_len, LANES), lambda s, g: (s, g)), table, table, table, row],
        out_specs=line,
        out_shape=jax.ShapeDtypeStruct((rows, kv * width), jnp.bfloat16),
        scratch_shapes=[pltpu.VMEM((full_len, LANES), jnp.float32)] * 2,
        cost_estimate=pl.CostEstimate(flops=10 * rows * full_len * kv * LANES * groups, bytes_accessed=rows * kv * width * 6, transcendentals=0),
        name="attn_backward",
    )(turned, d_out, lse, cos, sin, seg_col, seg_row)


def attn_tables(segment_ids):
    seqs, full_len = segment_ids.shape
    earlier = (segment_ids[..., None, :] < segment_ids[..., :, None]).astype(jnp.int32)
    positions = jnp.arange(full_len, dtype=jnp.int32) - jnp.sum(earlier, axis=-1, dtype=jnp.int32)
    inverse = 500000.0 ** (-2.0 * jnp.arange(HEAD_DIM // 2, dtype=jnp.float32) / HEAD_DIM)
    angles = positions.astype(jnp.float32)[..., None] * inverse
    cos = jnp.cos(angles)
    sin = jnp.sin(angles)
    cos = jnp.concatenate([cos] * 4, -1).reshape(seqs * full_len, LANES)
    sin = jnp.concatenate([-sin, sin] * 2, -1).reshape(seqs * full_len, LANES)
    seg_col = jnp.broadcast_to(segment_ids[:, :, None], (seqs, full_len, LANES)).reshape(seqs * full_len, LANES)
    seg_row = jnp.broadcast_to(segment_ids[:, None, :], (seqs, 8, full_len)).reshape(seqs * 8, full_len)
    return cos, sin, seg_col, seg_row


MESH = pl.DeviceIdType.MESH
VMEM_SPEC = pl.BlockSpec(memory_space=pltpu.VMEM)
ANY_SPEC = pl.BlockSpec(memory_space=pl.ANY)
DMA = pltpu.SemaphoreType.DMA


def place():
    d = lax.axis_index("dp")
    z = lax.axis_index("seq")
    return d, z, d // 2, d % 2


def remote(src, dst, send, recv, dev):
    return pltpu.make_async_remote_copy(
        src_ref=src, dst_ref=dst, send_sem=send, recv_sem=recv, device_id=dev, device_id_type=MESH
    )


def greet_all(n_dp, n_z, d, z):
    barrier = pltpu.get_barrier_semaphore()
    me = d * n_z + z

    def one(o, carry):
        other = lax.rem(me + o, n_dp * n_z)
        pl.semaphore_signal(barrier, inc=1, device_id=(other // n_z, lax.rem(other, n_z)), device_id_type=MESH)
        return carry

    lax.fori_loop(1, n_dp * n_z, one, 0)
    pl.semaphore_wait(barrier, n_dp * n_z - 1)


def greet_line(n_z, d, z, extra=()):
    barrier = pltpu.get_barrier_semaphore()
    c = d % 2
    for o in range(n_z):
        zz = lax.rem(z + o, n_z)
        for core in range(2):
            if o == 0 and core == 0:
                continue
            pl.semaphore_signal(barrier, inc=1, device_id=(d - c + lax.rem(c + core, 2), zz), device_id_type=MESH)
    for dev in extra:
        pl.semaphore_signal(barrier, inc=1, device_id=dev, device_id_type=MESH)
    pl.semaphore_wait(barrier, 2 * n_z - 1 + len(extra))


def block_at(ref, shape, row, col):
    return ref.at[pl.ds(pl.multiple_of(row * shape[0], shape[0]), shape[0]),
                  pl.ds(pl.multiple_of(col * shape[1], shape[1]), shape[1])]


def gather_in_kernel(n_dp, n_z, x_ref, w_ref, g_ref, s_ref, xs, wq, ga, sg,
                     x_s, x_r, f_s, f_r, w_s, w_r, d_s, d_r, g_s, g_r, s_s, s_r, loc):
    d, z, pair, c = place()
    n_d = n_dp // 2
    me = d * n_z + z
    total = n_dp * n_z
    rows = x_ref.shape[1]
    half = rows // 2
    shape = w_ref.shape
    cz = z // 2
    greet_all(n_dp, n_z, d, z)

    my_block = block_at(wq, shape, d, z % 2)
    for o in range(n_z):
        zz = lax.rem(z + o, n_z)
        copy = remote(w_ref, my_block, w_s.at[o], w_r.at[c, z % 2], (2 * pair + cz, zz))
        if o == 0:
            pl.when(c != cz)(copy.start)
            pl.when(c == cz)(lambda: pltpu.make_async_copy(w_ref, my_block, loc.at[0]).start())
        else:
            copy.start()

    for i in range(2):
        for h in range(2):
            src = x_ref.at[i, pl.ds(h * half, half)]
            dst = xs.at[pl.ds(pl.multiple_of(z * rows + h * half, half), half)]
            zz = 2 * c + i
            mine = (h == c) & (zz == z)
            copy = remote(src, dst, x_s.at[i, h], x_r.at[z], (2 * pair + h, zz))
            pl.when(jnp.logical_not(mine))(copy.start)
            pl.when(mine)(lambda src=src, dst=dst: pltpu.make_async_copy(src, dst, loc.at[1]).start())

    seg_copy = remote(s_ref, sg.at[c], s_s, s_r, (2 * pair + 1 - c, z))
    seg_copy.start()
    own_seg = pltpu.make_async_copy(s_ref, sg.at[c], loc.at[2])
    own_seg.start()
    own_gain = pltpu.make_async_copy(g_ref, ga.at[me], loc.at[3])
    own_gain.start()

    def send_gain(o, carry):
        other = lax.rem(me + o, total)
        remote(g_ref, ga.at[me], g_s, g_r, (other // n_z, lax.rem(other, n_z))).start()
        return carry

    lax.fori_loop(1, total, send_gain, 0)

    first = jnp.where(c == cz, z % 2, 1 - c)
    for t in range(4):
        b = first if t < 2 else 1 - first
        core = t % 2
        blk = block_at(wq, shape, 2 * pair + core, b)
        mine = (core == c) & (2 * c + b == z)
        arrive = remote(w_ref, blk, w_s.at[0], w_r.at[core, b], (d, z))
        pl.when(jnp.logical_not(mine))(arrive.wait_recv)
        pl.when(mine)(lambda blk=blk: pltpu.make_async_copy(w_ref, blk, loc.at[0]).wait())
        for k in range(1, n_d):
            remote(blk, blk, d_s.at[k - 1, t], d_r.at[k - 1], (2 * (pair ^ k) + c, z)).start()

    for o in range(n_z):
        zs = lax.rem(z + o, n_z)
        src = xs.at[pl.ds(pl.multiple_of(zs * rows + c * half, half), half)]
        mine = (cz == c) & (zs == z)
        arrive = remote(src, src, x_s.at[0, 0], x_r.at[zs], (d, z))
        pl.when(jnp.logical_not(mine))(arrive.wait_recv)
        pl.when(mine)(lambda src=src: pltpu.make_async_copy(src, src, loc.at[1]).wait())
        remote(src, src, f_s.at[zs], f_r.at[zs], (2 * pair + 1 - c, z)).start()

    for o in range(n_z):
        copy = remote(w_ref, my_block, w_s.at[o], w_r.at[0, 0], (d, z))
        if o == 0:
            pl.when(c != cz)(copy.wait_send)
        else:
            copy.wait_send()
    for i in range(2):
        for h in range(2):
            src = x_ref.at[i, pl.ds(h * half, half)]
            mine = (h == c) & (2 * c + i == z)
            copy = remote(src, src, x_s.at[i, h], x_r.at[0], (d, z))
            pl.when(jnp.logical_not(mine))(copy.wait_send)
    for zs in range(n_z):
        src = xs.at[pl.ds(zs * rows, half)]
        copy = remote(src, src, f_s.at[zs], f_r.at[zs], (d, z))
        copy.wait_send()
        copy.wait_recv()
    seg_copy.wait_send()
    remote(s_ref, sg.at[1 - c], s_s, s_r, (d, z)).wait_recv()
    own_seg.wait()
    own_gain.wait()
    many = ga.at[pl.ds(0, total - 1)]
    gains = remote(many, many, g_s, g_r, (d, z))
    gains.wait_send()
    gains.wait_recv()
    blk = block_at(wq, shape, 0, 0)
    for k in range(1, n_d):
        for t in range(4):
            remote(blk, blk, d_s.at[k - 1, t], d_r.at[k - 1], (d, z)).wait_send()
        region = wq.at[pl.ds(0, 2 * shape[0])]
        remote(region, region, d_s.at[k - 1, 0], d_r.at[k - 1], (d, z)).wait_recv()


def gather_in(x_loc, w, gain_tile, seg_tile, n_dp, n_z):
    seqs, rows, width = x_loc.shape
    n_d = n_dp // 2
    total = n_dp * n_z
    return pl.pallas_call(
        functools.partial(gather_in_kernel, n_dp, n_z),
        in_specs=[VMEM_SPEC] * 4,
        out_specs=[ANY_SPEC] * 4,
        out_shape=[
            jax.ShapeDtypeStruct((rows * n_z, width), x_loc.dtype),
            jax.ShapeDtypeStruct((w.shape[0] * n_dp, 2 * w.shape[1]), w.dtype),
            jax.ShapeDtypeStruct((total,) + gain_tile.shape, gain_tile.dtype),
            jax.ShapeDtypeStruct((2,) + seg_tile.shape, seg_tile.dtype),
        ],
        scratch_shapes=[
            DMA((2, 2)), DMA((n_z,)), DMA((n_z,)), DMA((n_z,)), DMA((n_z,)), DMA((2, 2)),
            DMA((n_d - 1, 4)), DMA((n_d - 1,)), DMA, DMA, DMA, DMA, DMA((4,)),
        ],
        compiler_params=pltpu.CompilerParams(collective_id=1, has_side_effects=True),
        cost_estimate=pl.CostEstimate(flops=0, bytes_accessed=200_000_000, transcendentals=0),
        name="gather_in",
    )(x_loc, w, gain_tile, seg_tile)


def share_resid_kernel(n_z, part_ref, x_ref, out, got, buf, p_s, p_r, u_s, u_r, loc):
    d, z, pair, c = place()
    cz = z // 2
    full = x_ref.shape[0]
    half = full // 2
    unit = half // 2
    greet_line(n_z, d, z)
    mine = pl.ds(pl.multiple_of(c * half, half), half)
    theirs = pl.ds(pl.multiple_of((1 - c) * half, half), half)
    swap = remote(part_ref.at[theirs], got, p_s, p_r, (2 * pair + 1 - c, z))
    swap.start()
    swap.wait_recv()

    def add(r, carry):
        at = pl.ds(pl.multiple_of(r * 16, 16), 16)
        src = pl.ds(pl.multiple_of(c * half + r * 16, 16), 16)
        total = x_ref[src].astype(jnp.float32) + part_ref[src].astype(jnp.float32) + got[at].astype(jnp.float32)
        buf[at] = total.astype(jnp.bfloat16)
        return carry

    def spot(jl, h, k):
        return out.at[jl, pl.ds(pl.multiple_of(h * half + k * unit, unit), unit)]

    def sends(k, wait):
        src = buf.at[pl.ds(k * unit, unit)]
        dst = spot(z % 2, c, k)
        for o, zz in ((0, z), (1, z - 1), (2, z + 1)):
            copy = remote(src, dst, u_s.at[o, k], u_r.at[z % 2, c, k], (2 * pair + cz, zz))
            act = copy.wait_send if wait else copy.start
            if o == 0:
                keep = pltpu.make_async_copy(src, dst, loc.at[k])
                pl.when(c != cz)(act)
                pl.when(c == cz)(keep.wait if wait else keep.start)
            elif o == 1:
                pl.when(z > 0)(act)
            else:
                pl.when(z < n_z - 1)(act)

    per = unit // 16
    lax.fori_loop(0, per, add, 0)
    lax.fori_loop(per, per + per // 2, add, 0)
    sends(0, False)
    lax.fori_loop(per + per // 2, 2 * per, add, 0)
    swap.wait_send()
    sends(1, False)

    def relay(dist, sign, jl_wait):
        j = z + sign * dist
        ok = (j >= 2 * c) & (j <= 2 * c + 1)
        to = z - sign
        more = (to >= 0) & (to <= n_z - 1)
        jl = lax.rem(j + n_z, 2)

        @pl.when(ok)
        def _():
            for k in range(2):
                for h in range(2):
                    at = spot(jl, h, k)
                    copy = remote(at, at, u_s.at[3 + (0 if sign < 0 else 1), 4 * jl + 2 * h + k], u_r.at[jl, h, k], (2 * pair + c, to))
                    if jl_wait:
                        copy.wait_recv()
                        pl.when(more)(copy.start)
                    else:
                        pl.when(more)(copy.wait_send)

    order = [(dist, sign) for dist in range(1, n_z) for sign in (-1, 1)]
    for dist, sign in order:
        relay(dist, sign, True)
    @pl.when(c == cz)
    def _():
        for k in range(2):
            at = spot(z % 2, 1 - c, k)
            remote(at, at, u_s.at[0, 0], u_r.at[z % 2, 1 - c, k], (d, z)).wait_recv()
    for dist, sign in order:
        relay(dist, sign, False)
    sends(0, True)
    sends(1, True)


def share_resid(part, x, n_z):
    full, width = x.shape
    return pl.pallas_call(
        functools.partial(share_resid_kernel, n_z),
        in_specs=[VMEM_SPEC] * 2,
        out_specs=ANY_SPEC,
        out_shape=jax.ShapeDtypeStruct((2, full, width), jnp.bfloat16),
        scratch_shapes=[
            pltpu.VMEM((full // 2, width), jnp.bfloat16), pltpu.VMEM((full // 2, width), jnp.bfloat16),
            DMA, DMA, DMA((5, 8)), DMA((2, 2, 2)), DMA((2,)),
        ],
        compiler_params=pltpu.CompilerParams(collective_id=2, has_side_effects=True),
        cost_estimate=pl.CostEstimate(flops=0, bytes_accessed=200_000_000, transcendentals=0),
        name="share_resid",
    )(part, x)


CHUNKS = 8


def sum_line_kernel(n_z, part_ref, resid_all, cot_all, gain_ref, d_out, gain_out, got, buf, resid_ref, cot_ref,
                    s_s, s_r, p_s, p_r, loc, rows_sem):
    d, z, pair, c = place()
    cz = z // 2
    full, width = buf.shape
    rows = full // CHUNKS
    fetch = (
        pltpu.make_async_copy(resid_all.at[z % 2], resid_ref, rows_sem.at[0]),
        pltpu.make_async_copy(cot_all.at[z % 2], cot_ref, rows_sem.at[1]),
    )
    for one in fetch:
        one.start()
    greet_line(n_z, d, z)
    gain_out[...] = jnp.zeros_like(gain_out)
    own = c == cz
    steps = [(k, t) for k in range(CHUNKS) for t in range(2)]

    def where_is(k, t):
        jl = jnp.bitwise_xor(c, t)
        return jl, 2 * c + jl, pl.ds(k * rows, rows)

    def copy_on(k, t, side, src):
        jl, j, at = where_is(k, t)
        to = z + 1 if side == 0 else z - 1
        return remote(src, got.at[side, jl, at], s_s.at[t, k], s_r.at[side, jl, k], (2 * pair + c, to))

    def arrived(side, jl, k):
        at = got.at[side, jl, pl.ds(k * rows, rows)]
        return remote(at, at, s_s.at[0, 0], s_r.at[side, jl, k], (d, z))

    def add_in(side, jl, k):
        def one(r, carry):
            at = pl.ds(pl.multiple_of(k * rows + r * 16, 16), 16)
            got[side, jl, at] = (got[side, jl, at].astype(jnp.float32) + part_ref[jl, at].astype(jnp.float32)).astype(jnp.bfloat16)
            return carry
        lax.fori_loop(0, rows // 16, one, 0)

    def finish(jl, k):
        def one(r, carry):
            at = pl.ds(pl.multiple_of(k * rows + r * 16, 16), 16)
            total = part_ref[jl, at].astype(jnp.float32)
            left = got[0, jl, at].astype(jnp.float32)
            right = got[1, jl, at].astype(jnp.float32)
            total = total + jnp.where(z > 0, left, 0.0) + jnp.where(z < n_z - 1, right, 0.0)
            value = resid_ref[at].astype(jnp.float32)
            inverse = lax.rsqrt(jnp.mean(value * value, axis=-1, keepdims=True) + norm_eps)
            scaled = value * inverse
            d_scaled = total * gain_ref[...]
            mean = jnp.mean(d_scaled * scaled, axis=-1, keepdims=True)
            d_resid = cot_ref[at].astype(jnp.float32) + inverse * (d_scaled - scaled * mean)
            buf[at] = d_resid.astype(jnp.bfloat16)
            prod = total * scaled
            gain_out[...] = gain_out[...] + prod[:8] + prod[8:]
            return carry
        lax.fori_loop(0, rows // 16, one, 0)

    def to_partner(k):
        at = pl.ds(k * rows, rows)
        return remote(buf.at[at], d_out.at[at], p_s.at[k], p_r.at[k], (2 * pair + 1 - c, z))

    def keep(k):
        at = pl.ds(k * rows, rows)
        return pltpu.make_async_copy(buf.at[at], d_out.at[at], loc.at[k])

    def send_step(k, t, wait):
        jl, j, at = where_is(k, t)
        for side in range(2):
            going = (z < j) if side == 0 else (z > j)
            edge = (z == 0) if side == 0 else (z == n_z - 1)
            edge_copy = copy_on(k, t, side, part_ref.at[jl, at])
            inner_copy = copy_on(k, t, side, got.at[side, jl, at])
            pl.when(going & edge)(edge_copy.wait_send if wait else edge_copy.start)
            pl.when(going & jnp.logical_not(edge))(inner_copy.wait_send if wait else inner_copy.start)

    def publish(k, wait):
        @pl.when(own)
        def _():
            if wait:
                to_partner(k).wait_send()
                keep(k).wait()
            else:
                to_partner(k).start()
                keep(k).start()

    for n, (k, t) in enumerate(steps):
        jl, j, at = where_is(k, t)
        for side in range(2):
            going = (z < j) if side == 0 else (z > j)
            inner = (z > 0) if side == 0 else (z < n_z - 1)

            @pl.when(going & inner)
            def _():
                arrived(side, jl, k).wait_recv()
                add_in(side, jl, k)

        if n > 0:
            send_step(*steps[n - 1], False)
    send_step(*steps[-1], False)

    for one in fetch:
        one.wait()

    @pl.when(own)
    def _():
        jl = z % 2
        for k in range(CHUNKS):
            pl.when(z > 0)(arrived(0, jl, k).wait_recv)
            pl.when(z < n_z - 1)(arrived(1, jl, k).wait_recv)
            finish(jl, k)
            if k > 0:
                to_partner(k - 1).start()
                keep(k - 1).start()
        to_partner(CHUNKS - 1).start()
        keep(CHUNKS - 1).start()

    for k, t in steps:
        send_step(k, t, True)
    for k in range(CHUNKS):
        publish(k, True)
        at = d_out.at[pl.ds(k * rows, rows)]
        pl.when(jnp.logical_not(own))(remote(at, at, p_s.at[k], p_r.at[k], (d, z)).wait_recv)


def sum_line(part, resid, cot, gain, n_z):
    _, full, width = part.shape
    return pl.pallas_call(
        functools.partial(sum_line_kernel, n_z),
        in_specs=[VMEM_SPEC, ANY_SPEC, ANY_SPEC, VMEM_SPEC],
        out_specs=[ANY_SPEC, VMEM_SPEC],
        out_shape=[jax.ShapeDtypeStruct((full, width), jnp.bfloat16), jax.ShapeDtypeStruct((8, width), jnp.float32)],
        scratch_shapes=[
            pltpu.VMEM((2, 2, full, width), jnp.bfloat16), pltpu.VMEM((full, width), jnp.bfloat16),
            pltpu.VMEM((full, width), jnp.bfloat16), pltpu.VMEM((full, width), jnp.bfloat16),
            DMA((2, CHUNKS)), DMA((2, 2, CHUNKS)), DMA((CHUNKS,)), DMA((CHUNKS,)), DMA((CHUNKS,)), DMA((2,)),
        ],
        compiler_params=pltpu.CompilerParams(collective_id=3, has_side_effects=True, vmem_limit_bytes=56 * 1024 * 1024),
        cost_estimate=pl.CostEstimate(flops=0, bytes_accessed=200_000_000, transcendentals=0),
        name="sum_line",
    )(part, resid, cot, gain)


def gather_out_kernel(n_dp, n_z, w_ref, wo, w_s, w_r, d_s, d_r, loc):
    d, z, pair, c = place()
    n_d = n_dp // 2
    cz = z // 2
    shape = w_ref.shape
    greet_line(n_z, d, z, [(2 * (pair ^ k) + c, z) for k in range(1, n_d)])
    my_block = block_at(wo, shape, d, z % 2)
    for o in range(n_z):
        copy = remote(w_ref, my_block, w_s.at[o], w_r.at[c, z % 2], (2 * pair + cz, lax.rem(z + o, n_z)))
        if o == 0:
            pl.when(c != cz)(copy.start)
            pl.when(c == cz)(lambda: pltpu.make_async_copy(w_ref, my_block, loc).start())
        else:
            copy.start()
    first = jnp.where(c == cz, z % 2, 1 - c)
    for t in range(4):
        b = first if t < 2 else 1 - first
        core = t % 2
        blk = block_at(wo, shape, 2 * pair + core, b)
        mine = (core == c) & (2 * c + b == z)
        arrive = remote(w_ref, blk, w_s.at[0], w_r.at[core, b], (d, z))
        pl.when(jnp.logical_not(mine))(arrive.wait_recv)
        pl.when(mine)(lambda blk=blk: pltpu.make_async_copy(w_ref, blk, loc).wait())
        for k in range(1, n_d):
            remote(blk, blk, d_s.at[k - 1, t], d_r.at[k - 1], (2 * (pair ^ k) + c, z)).start()
    for o in range(n_z):
        copy = remote(w_ref, my_block, w_s.at[o], w_r.at[0, 0], (d, z))
        if o == 0:
            pl.when(c != cz)(copy.wait_send)
        else:
            copy.wait_send()
    blk = block_at(wo, shape, 0, 0)
    for k in range(1, n_d):
        for t in range(4):
            remote(blk, blk, d_s.at[k - 1, t], d_r.at[k - 1], (d, z)).wait_send()
        region = wo.at[pl.ds(0, 2 * shape[0])]
        remote(region, region, d_s.at[k - 1, 0], d_r.at[k - 1], (d, z)).wait_recv()


def gather_out(w, n_dp, n_z):
    n_d = n_dp // 2
    return pl.pallas_call(
        functools.partial(gather_out_kernel, n_dp, n_z),
        in_specs=[VMEM_SPEC],
        out_specs=ANY_SPEC,
        out_shape=jax.ShapeDtypeStruct((n_dp * w.shape[0], 2 * w.shape[1]), w.dtype),
        scratch_shapes=[DMA((n_z,)), DMA((2, 2)), DMA((n_d - 1, 4)), DMA((n_d - 1,)), DMA],
        compiler_params=pltpu.CompilerParams(collective_id=4, has_side_effects=True),
        cost_estimate=pl.CostEstimate(flops=0, bytes_accessed=100_000_000, transcendentals=0),
        name="gather_out",
    )(w)


def hand_out_kernel(n_dp, n_z, dn_ref, x_ref, dr_ref, gain_ref, gain2_ref, qt_ref, ot_ref,
                    ig, gq, go, gains, got, buf, q_got, q_own, q_put, q_fin, o_got, o_own, o_put, o_fin, g_src, g_all,
                    p_s, p_r, i_s, i_r, q_s, q_r, qf_s, qf_r, o_s, o_r, of_s, of_r, g_s, g_r, loc):
    d, z, pair, c = place()
    n_d = n_dp // 2
    total = n_dp * n_z
    me = d * n_z + z
    cz = z // 2
    full, width = x_ref.shape
    half = full // 2
    quarter = half // 2
    q_rows, q_cols = q_fin.shape[1:]
    o_rows, o_cols = o_fin.shape[1:]
    q_load = pltpu.make_async_copy(qt_ref.at[pl.ds(pl.multiple_of(pair * 2 * q_rows, 2 * q_rows), 2 * q_rows)], q_own, loc.at[0])
    o_load = pltpu.make_async_copy(ot_ref.at[pl.ds(pl.multiple_of(pair * 2 * o_rows, 2 * o_rows), 2 * o_rows)], o_own, loc.at[1])
    q_load.start()
    o_load.start()
    greet_all(n_dp, n_z, d, z)

    def q_send(k, b):
        other = pair ^ k
        src = qt_ref.at[pl.ds(pl.multiple_of(other * 2 * q_rows, 2 * q_rows), 2 * q_rows), pl.ds(b * q_cols, q_cols)]
        return remote(src, q_got.at[k - 1, :, pl.ds(b * q_cols, q_cols)], q_s.at[k - 1, b], q_r.at[k - 1, b], (2 * other + c, z))

    def o_send(k, b):
        other = pair ^ k
        src = ot_ref.at[pl.ds(pl.multiple_of(other * 2 * o_rows, 2 * o_rows), 2 * o_rows), pl.ds(b * o_cols, o_cols)]
        return remote(src, o_got.at[k - 1, :, pl.ds(b * o_cols, o_cols)], o_s.at[k - 1, b], o_r.at[k - 1, b], (2 * other + c, z))

    mine = pl.ds(pl.multiple_of(c * half, half), half)
    theirs = pl.ds(pl.multiple_of((1 - c) * half, half), half)
    swap = remote(dn_ref.at[theirs], got, p_s, p_r, (2 * pair + 1 - c, z))
    swap.start()
    for b in range(2):
        for k in range(1, n_d):
            o_send(k, b).start()
    for b in range(2):
        for k in range(1, n_d):
            q_send(k, b).start()

    g_src[pl.ds(0, 8)] = jnp.zeros((8, width), jnp.float32)
    g_src[pl.ds(8, 8)] = gain2_ref[...]
    swap.wait_recv()

    def rows_of(r, carry):
        at = pl.ds(pl.multiple_of(r * 16, 16), 16)
        src = pl.ds(pl.multiple_of(c * half + r * 16, 16), 16)
        d_normed = dn_ref[src].astype(jnp.float32) + got[at].astype(jnp.float32)
        value = x_ref[src].astype(jnp.float32)
        inverse = lax.rsqrt(jnp.mean(value * value, axis=-1, keepdims=True) + norm_eps)
        scaled = value * inverse
        d_scaled = d_normed * gain_ref[...]
        mean = jnp.mean(d_scaled * scaled, axis=-1, keepdims=True)
        out = dr_ref[src].astype(jnp.float32) + inverse * (d_scaled - scaled * mean)
        buf[at] = out.astype(jnp.bfloat16)
        prod = d_normed * scaled
        g_src[pl.ds(0, 8)] = g_src[pl.ds(0, 8)] + prod[:8] + prod[8:]
        return carry

    def row_send(b, wait):
        src = buf.at[pl.ds(b * quarter, quarter)]
        dst = ig.at[z % 2]
        zz = 2 * c + b
        here = (cz == c) & (zz == z)
        copy = remote(src, dst, i_s.at[b], i_r.at[z % 2], (2 * pair + cz, zz))
        keep = pltpu.make_async_copy(src, dst, loc.at[2])
        pl.when(jnp.logical_not(here))(copy.wait_send if wait else copy.start)
        pl.when(here)(keep.wait if wait else keep.start)

    per = quarter // 16
    lax.fori_loop(0, per, rows_of, 0)
    lax.fori_loop(per, per + per // 2, rows_of, 0)
    row_send(0, False)
    lax.fori_loop(per + per // 2, 2 * per, rows_of, 0)
    q_load.wait()
    o_load.wait()
    row_send(1, False)

    each = width // total

    def gain_tile(o):
        return g_src.at[:, pl.ds(pl.multiple_of(o * each // 128 * 128, 128), 128)]

    own_gain = pltpu.make_async_copy(gain_tile(me), g_all.at[me], loc.at[3])
    own_gain.start()

    def send_gain(o, carry):
        other = lax.rem(me + o, total)
        remote(gain_tile(other), g_all.at[me], g_s, g_r, (other // n_z, lax.rem(other, n_z))).start()
        return carry

    lax.fori_loop(1, total, send_gain, 0)

    def second(b, rows, own_ref, got_ref, put_ref, cut):
        for core in range(2):

            def add(r, carry):
                at = pl.ds(pl.multiple_of(r * 16, 16), 16)
                src, lanes = cut(core, b, r)
                value = own_ref[src, lanes].astype(jnp.float32)
                for k in range(n_d - 1):
                    value = value + got_ref[k, src, lanes].astype(jnp.float32)
                put_ref[core, b, at] = value.astype(jnp.bfloat16)
                return carry

            lax.fori_loop(0, rows // 16, add, 0)

    def second_send(b, put_ref, fin_ref, f_s, f_r, spare, wait):
        for core in range(2):
            here = (core == c) & (2 * c + b == z)
            src = put_ref.at[core, b]
            copy = remote(src, fin_ref.at[z], f_s.at[core, b], f_r.at[z], (2 * pair + core, 2 * c + b))
            keep = pltpu.make_async_copy(src, fin_ref.at[z], loc.at[spare])
            pl.when(jnp.logical_not(here))(copy.wait_send if wait else copy.start)
            pl.when(here)(keep.wait if wait else keep.start)

    def q_cut(core, b, r):
        return pl.ds(pl.multiple_of(core * q_rows + r * 16, 16), 16), pl.ds(b * q_cols, q_cols)

    def o_cut(core, b, r):
        return pl.ds(pl.multiple_of(core * o_rows + r * 16, 16), 16), pl.ds(b * o_cols, o_cols)

    def last(rows, fin_ref, out_ref):
        def add(r, carry):
            at = pl.ds(pl.multiple_of(r * 16, 16), 16)
            value = fin_ref[0, at].astype(jnp.float32)
            for zs in range(1, n_z):
                value = value + fin_ref[zs, at].astype(jnp.float32)
            out_ref[at] = value
            return carry

        lax.fori_loop(0, rows // 16, add, 0)

    o_args = (o_put, o_fin, of_s, of_r, 4)
    q_args = (q_put, q_fin, qf_s, qf_r, 5)
    for b in range(2):
        for k in range(1, n_d):
            o_send(k, b).wait_recv()
        second(b, o_rows, o_own, o_got, o_put, o_cut)
        if b:
            second_send(0, *o_args, False)
    for b in range(2):
        for k in range(1, n_d):
            q_send(k, b).wait_recv()
        second(b, q_rows, q_own, q_got, q_put, q_cut)
        if b:
            second_send(0, *q_args, False)
        else:
            second_send(1, *o_args, False)

    def arrived(fin_ref, f_s, f_r):
        for zs in range(n_z):
            at = fin_ref.at[zs]
            from_here = (cz == c) & (zs == z)
            pl.when(jnp.logical_not(from_here))(remote(at, at, f_s.at[0, 0], f_r.at[zs], (d, z)).wait_recv)

    def own_done(args):
        for b in range(2):
            second_send(b, *args, True)

    own_done(o_args)
    arrived(o_fin, of_s, of_r)
    value = o_fin[0].astype(jnp.float32)
    for zs in range(1, n_z):
        value = value + o_fin[zs].astype(jnp.float32)
    go[...] = value.T
    second_send(1, *q_args, False)
    own_done(q_args)
    arrived(q_fin, qf_s, qf_r)
    last(q_rows, q_fin, gq)

    many = g_all.at[pl.ds(0, total - 1)]
    gain_copy = remote(many, many, g_s, g_r, (d, z))
    gain_copy.wait_send()
    gain_copy.wait_recv()
    own_gain.wait()
    gains[...] = jnp.zeros_like(gains)

    def add_gain(o, carry):
        gains[...] = gains[...] + g_all[o]
        return carry

    lax.fori_loop(0, total, add_gain, 0)

    swap.wait_send()
    for b in range(2):
        row_send(b, True)
        for k in range(1, n_d):
            o_send(k, b).wait_send()
            q_send(k, b).wait_send()
    for i in range(2):
        from_here = (cz == c) & (2 * c + i == z)
        at = ig.at[i]
        pl.when(jnp.logical_not(from_here))(remote(at, at, i_s.at[0], i_r.at[i], (d, z)).wait_recv)


def hand_out(dn, x, dr, gain, gain2, qt, ot, n_dp, n_z):
    full, width = x.shape
    n_d = n_dp // 2
    total = n_dp * n_z
    q_rows, q_cols = qt.shape[0] // n_dp, qt.shape[1] // 2
    o_rows, o_cols = ot.shape[0] // n_dp, ot.shape[1] // 2
    b16 = jnp.bfloat16
    return pl.pallas_call(
        functools.partial(hand_out_kernel, n_dp, n_z),
        in_specs=[VMEM_SPEC] * 5 + [ANY_SPEC] * 2,
        out_specs=[ANY_SPEC] + [VMEM_SPEC] * 3,
        out_shape=[
            jax.ShapeDtypeStruct((2, full // 4, width), b16),
            jax.ShapeDtypeStruct((q_rows, q_cols), jnp.float32),
            jax.ShapeDtypeStruct((o_cols, o_rows), jnp.float32),
            jax.ShapeDtypeStruct((16, 128), jnp.float32),
        ],
        scratch_shapes=[
            pltpu.VMEM((full // 2, width), b16), pltpu.VMEM((full // 2, width), b16),
            pltpu.VMEM((n_d - 1, 2 * q_rows, 2 * q_cols), b16), pltpu.VMEM((2 * q_rows, 2 * q_cols), b16),
            pltpu.VMEM((2, 2, q_rows, q_cols), b16), pltpu.VMEM((n_z, q_rows, q_cols), b16),
            pltpu.VMEM((n_d - 1, 2 * o_rows, 2 * o_cols), b16), pltpu.VMEM((2 * o_rows, 2 * o_cols), b16),
            pltpu.VMEM((2, 2, o_rows, o_cols), b16), pltpu.VMEM((n_z, o_rows, o_cols), b16),
            pltpu.VMEM((16, width), jnp.float32), pltpu.VMEM((total, 16, 128), jnp.float32),
            DMA, DMA, DMA((2,)), DMA((2,)), DMA((n_d - 1, 2)), DMA((n_d - 1, 2)), DMA((2, 2)), DMA((n_z,)),
            DMA((n_d - 1, 2)), DMA((n_d - 1, 2)), DMA((2, 2)), DMA((n_z,)), DMA, DMA, DMA((6,)),
        ],
        compiler_params=pltpu.CompilerParams(collective_id=5, has_side_effects=True, vmem_limit_bytes=56 * 1024 * 1024),
        cost_estimate=pl.CostEstimate(flops=0, bytes_accessed=300_000_000, transcendentals=0),
        name="hand_out",
    )(dn, x, dr, gain, gain2, qt, ot)


def rms_forward(values, gain_wide):
    inverse = lax.rsqrt(jnp.mean(values * values, axis=-1, keepdims=True) + norm_eps)
    scaled = values * inverse
    return (scaled, inverse, (scaled * gain_wide).astype(jnp.bfloat16))


def rms_backward(d_normed, scaled, inverse, gain_wide):
    d_scaled = d_normed * gain_wide
    d_values = inverse * (d_scaled - scaled * jnp.mean(d_scaled * scaled, axis=-1, keepdims=True))
    return (d_values, jnp.sum(d_normed * scaled, axis=0))


def adam_update(weight, grad, first, second):
    new_first = beta_one * first + (1.0 - beta_one) * grad
    new_second = beta_two * second + (1.0 - beta_two) * grad * grad
    first_hat = new_first / (1.0 - beta_one**step_count)
    second_hat = new_second / (1.0 - beta_two**step_count)
    new_weight = weight - learn_rate * (
        first_hat / (jnp.sqrt(second_hat) + adam_eps) + weight_decay * weight
    )
    return (new_weight, new_first, new_second)


def contract_rows(left, right):
    return lax.dot_general(
        left, right, (((0,), (0,)), ((), ())), preferred_element_type=jnp.float32
    )


def times_transpose(left, right):
    return lax.dot_general(
        left, right, (((1,), (1,)), ((), ())), preferred_element_type=jnp.float32
    )


def per_device(
    block_input,
    segment_ids,
    cotangent,
    attn_gain,
    qkv_weight,
    out_weight,
    mlp_gain,
    gate_up_weight,
    down_weight,
    first_attn_gain,
    first_qkv,
    first_out,
    first_mlp_gain,
    first_gate_up,
    first_down,
    second_attn_gain,
    second_qkv,
    second_out,
    second_mlp_gain,
    second_gate_up,
    second_down,
):
    seqs_here, local_len, width = block_input.shape
    full_len = segment_ids.shape[1]
    n_dp = lax.axis_size("dp")
    n_z = lax.axis_size("seq")
    groups = HEADS // KV_HEADS
    unit_count = down_weight.shape[0]
    z_here = lax.axis_index("seq")
    owned = attn_gain.shape[0]
    gain_line = jnp.concatenate([attn_gain, mlp_gain]).astype(jnp.bfloat16).astype(jnp.float32)
    gain_tile = jnp.pad(gain_line[None], ((0, 7), (0, LANES - 2 * owned)))
    seg_tile = jnp.pad(segment_ids, ((0, 8 - seqs_here), (0, 0)))
    gate_up_cols = lax.all_gather(
        gate_up_weight.astype(jnp.bfloat16).reshape(-1, 2 * unit_count), "dp", axis=0, tiled=True
    )
    down_rows = lax.all_gather(down_weight.astype(jnp.bfloat16), "dp", axis=1, tiled=True)
    cot_all = lax.all_gather(cotangent, "seq", axis=1, tiled=True)
    rows_in, qkv_cols, gain_all, seg_all = gather_in(
        block_input, qkv_weight.astype(jnp.bfloat16), gain_tile, seg_tile, n_dp, n_z
    )
    gain_one = gain_all[:, 0, :owned].reshape(1, width)
    gain_two = gain_all[:, 0, owned : 2 * owned].reshape(1, width)
    seg_here = lax.dynamic_slice(seg_all, (z_here // 2, z_here % 2, 0), (1, 1, full_len))[0]
    tables = attn_tables(seg_here)
    scaled_one, inverse_one, normed_one = rms_forward(rows_in.astype(jnp.float32), gain_one)
    qkv = jnp.dot(normed_one, qkv_cols, preferred_element_type=jnp.float32)
    turned, lse, attended16 = attn_forward(qkv, *tables, full_len, groups)
    out_rows = gather_out(out_weight.astype(jnp.bfloat16).T, n_dp, n_z)
    attn_part = times_transpose(attended16, out_rows)
    resid_all = share_resid(attn_part.astype(jnp.bfloat16), rows_in, n_z)
    total_rows = seqs_here * full_len
    resid = resid_all.reshape(total_rows, width).astype(jnp.float32)
    scaled_two, inverse_two, normed_two = rms_forward(resid, gain_two)
    gate_up = jnp.dot(normed_two, gate_up_cols, preferred_element_type=jnp.float32)
    gate_part = gate_up[:, :unit_count]
    up_part = gate_up[:, unit_count:]
    sigmoid_gate = jax.nn.sigmoid(gate_part)
    active = gate_part * sigmoid_gate
    hidden16 = (active * up_part).astype(jnp.bfloat16)
    cot_rows = cot_all.reshape(total_rows, width)
    d_hidden = times_transpose(cot_rows, down_rows)
    d_gate = d_hidden * up_part * sigmoid_gate * (1.0 + gate_part * (1.0 - sigmoid_gate))
    d_up = d_hidden * active
    d_gate_up16 = jnp.concatenate([d_gate, d_up], 1).astype(jnp.bfloat16)
    down_term = contract_rows(cot_rows, hidden16)
    down_sum = lax.psum_scatter(
        down_term.astype(jnp.bfloat16), "dp", scatter_dimension=0, tiled=True
    ).astype(jnp.float32)
    grad_down = down_sum.T
    d_normed_two = times_transpose(d_gate_up16, gate_up_cols).astype(jnp.bfloat16)
    d_resid16, gain_two_part = sum_line(
        d_normed_two.reshape(resid_all.shape), resid_all, cot_all, gain_two, n_z
    )
    gate_up_term = contract_rows(normed_two, d_gate_up16)
    grad_gate_up = (
        lax.psum_scatter(gate_up_term.astype(jnp.bfloat16), "dp", scatter_dimension=0, tiled=True)
        .reshape(gate_up_weight.shape)
        .astype(jnp.float32)
    )
    down_part = jnp.dot(hidden16, down_rows, preferred_element_type=jnp.float32)
    down_here = lax.psum_scatter(
        down_part.astype(jnp.bfloat16).reshape(resid_all.shape), "seq", scatter_dimension=1, tiled=True
    ).astype(jnp.float32)
    resid_here = lax.dynamic_slice_in_dim(resid_all, z_here * local_len, local_len, 1)
    output = (resid_here.astype(jnp.float32) + down_here).astype(jnp.bfloat16)
    d_attended = jnp.dot(d_resid16, out_rows, preferred_element_type=jnp.float32).astype(jnp.bfloat16)
    d_qkv16 = attn_backward(turned, d_attended, lse, *tables, full_len, groups)
    d_normed_one = times_transpose(d_qkv16, qkv_cols).astype(jnp.bfloat16)
    qkv_term = contract_rows(normed_one, d_qkv16).astype(jnp.bfloat16)
    out_term = contract_rows(d_resid16, attended16).astype(jnp.bfloat16)
    input_grad, grad_qkv, grad_out, gain_sums = hand_out(
        d_normed_one, rows_in, d_resid16, gain_one, gain_two_part, qkv_term, out_term, n_dp, n_z
    )
    flat = lax.axis_index("dp") * n_z + z_here
    gain_sums = lax.dynamic_slice(
        jnp.sum(gain_sums.reshape(2, 8, LANES), axis=1), (0, flat * owned % LANES), (2, owned)
    )
    grad_gain_one = gain_sums[0]
    grad_gain_two = gain_sums[1]
    w_one, m_one, v_one = adam_update(attn_gain, grad_gain_one, first_attn_gain, second_attn_gain)
    w_qkv, m_qkv, v_qkv = adam_update(qkv_weight, grad_qkv, first_qkv, second_qkv)
    w_out, m_out, v_out = adam_update(out_weight, grad_out, first_out, second_out)
    w_two, m_two, v_two = adam_update(mlp_gain, grad_gain_two, first_mlp_gain, second_mlp_gain)
    w_gu, m_gu, v_gu = adam_update(gate_up_weight, grad_gate_up, first_gate_up, second_gate_up)
    w_down, m_down, v_down = adam_update(down_weight, grad_down, first_down, second_down)
    return (
        output,
        input_grad,
        grad_gain_one,
        grad_qkv,
        grad_out,
        grad_gain_two,
        grad_gate_up,
        grad_down,
        w_one,
        w_qkv,
        w_out,
        w_two,
        w_gu,
        w_down,
        m_one,
        m_qkv,
        m_out,
        m_two,
        m_gu,
        m_down,
        v_one,
        v_qkv,
        v_out,
        v_two,
        v_gu,
        v_down,
    )


def solution(mesh):
    in_specs = (
        P("dp", "seq", None),
        P("dp", None),
        P("dp", "seq", None),
        P(("dp", "seq")),
        P("dp", "seq"),
        P("seq", "dp"),
        P(("dp", "seq")),
        P("dp", None, "seq"),
        P("seq", "dp"),
        P(("dp", "seq")),
        P("dp", "seq"),
        P("seq", "dp"),
        P(("dp", "seq")),
        P("dp", None, "seq"),
        P("seq", "dp"),
        P(("dp", "seq")),
        P("dp", "seq"),
        P("seq", "dp"),
        P(("dp", "seq")),
        P("dp", None, "seq"),
        P("seq", "dp"),
    )
    out_specs = (
        P("dp", "seq", None),
        P("dp", "seq", None),
        P(("dp", "seq")),
        P("dp", "seq"),
        P("seq", "dp"),
        P(("dp", "seq")),
        P("dp", None, "seq"),
        P("seq", "dp"),
        P(("dp", "seq")),
        P("dp", "seq"),
        P("seq", "dp"),
        P(("dp", "seq")),
        P("dp", None, "seq"),
        P("seq", "dp"),
        P(("dp", "seq")),
        P("dp", "seq"),
        P("seq", "dp"),
        P(("dp", "seq")),
        P("dp", None, "seq"),
        P("seq", "dp"),
        P(("dp", "seq")),
        P("dp", "seq"),
        P("seq", "dp"),
        P(("dp", "seq")),
        P("dp", None, "seq"),
        P("seq", "dp"),
    )
    return jax.shard_map(
        per_device, mesh=mesh, in_specs=in_specs, out_specs=out_specs, check_vma=False
    )
```

time: 1520 us -> 892 us (0.59)
  waiting for transfers between devices: 1050 us -> 28.9 us
  Pallas kernels: 0 us -> 601 us
  matrix products: 248 us -> 162 us
  blocking collectives: 69.8 us -> 0 us
  other arithmetic: 81.3 us -> 52.2 us
  local copies, waits for them, and re-layouts: 43.9 us -> 18.2 us
    pallas_call x0 -> x7, Pallas kernels: none -> 601 us  [the longest x1 204 us: hand_out(): pl.pallas_call(functools.partial(hand_out_kernel, n_dp, n_z), in_specs=[V...]
    reduce_scatter x6 -> x1, waiting for transfers between devices: 335 us -> 0.01 us  [per_device(): lax.psum_scatter(down_part.astype(jnp.bfloat16).reshape(resid_all.shape),...]
    all_gather x5 -> x0, waiting for transfers between devices: 224 us -> none  [the longest x1 81.3 us: per_device(): lax.all_gather(d_resid.astype(jnp.bfloat16).reshape(seqs_here, local_len,...]
    unnamed x18 -> x6, waiting for transfers between devices: 136 us -> 0.78 us
    reduce_scatter x1, waiting for transfers between devices: 114 us -> 0.01 us  [per_device(): lax.psum_scatter(gate_up_term.astype(jnp.bfloat16), 'dp', scatter_dimensi...]
    all_gather x1, waiting for transfers between devices: 90.6 us -> 0.01 us  [per_device(): lax.all_gather(gate_up_weight.astype(jnp.bfloat16).reshape(-1, 2 * unit_c...]
    dot_general x7 -> x1, matrix products: 93.4 us -> 3.3 us  [per_device(): jnp.dot(d_resid16, out_rows, preferred_element_type=jnp.float32)]
    all_gather x1 -> x0, blocking collectives: 69.8 us -> none  [per_device(): gain_block = lax.all_gather(gain_pair, ('dp', 'seq'), axis=1, tiled=True)]
  transfers between devices with their start and end apart: 17 -> 6, of which waited for: 15 -> 1; matrix products, arithmetic and copies ran while one was open for 12% -> 18% of each run, Pallas kernels for 0% -> 68%
where the time goes in v2:
time: 892 us; the launch traced here: 877 us
  Pallas kernels  601 us (67%)
  matrix products  162 us (18%)
  other arithmetic  52.2 us (6%)
  waiting for transfers between devices  28.9 us (3%)
  local copies, waits for them, and re-layouts  18.2 us (2%)
  between operations  14.7 us (2%)
    pallas_call x1, Pallas kernels, hand_out(): pl.pallas_call(functools.partial(hand_out_kernel, n_dp, n_z), in_specs=[V...  204 us
    pallas_call x1, Pallas kernels, sum_line(): pl.pallas_call(functools.partial(sum_line_kernel, n_z), in_specs=[VMEM_SP...  111 us
    pallas_call x1, Pallas kernels, gather_in(): pl.pallas_call(functools.partial(gather_in_kernel, n_dp, n_z), in_specs=[...  110 us
    pallas_call x1, Pallas kernels, gather_out(): pl.pallas_call(functools.partial(gather_out_kernel, n_dp, n_z), in_specs=...  73 us
    pallas_call x1, Pallas kernels, share_resid(): pl.pallas_call(functools.partial(share_resid_kernel, n_z), in_specs=[VMEM...  62.2 us
    dot_general x4, matrix products, times_transpose(): lax.dot_general(left, right, (((1,), (1,)), ((), ())), preferred_element_...  59.7 us
    dot_general x4, matrix products, contract_rows(): lax.dot_general(left, right, (((0,), (0,)), ((), ())), preferred_element_...  52.7 us
    sub x5, other arithmetic, adam_update(): weight - learn_rate * (first_hat / (jnp.sqrt(second_hat) + adam_eps) + we...  30.1 us
  transfers between devices with their start and end apart: 6, of which 1 were waited for; matrix products, arithmetic and copies ran while one was open for 18% of the time, Pallas kernels for 68%

profile of v2, /device:TPU:0, one launch (start us, length us, event | category | flops | bytes accessed | tf_op | source)
XLA Modules:
  0.0 877.2 jit_solution(13336181294840141128)
XLA Ops:
  7.2 0.0 all-gather.4.cloned.1.call-start
  7.2 4.2 convert_element_type.130
  11.5 2.2 copy.52
  13.7 0.0 all-gather.4.cloned.1.call-update
  13.7 0.0 all-gather.8.cloned.1.call-start
  13.8 0.7 all-gather.8.cloned.1.call-update
  14.5 0.0 all-gather.6.cloned.1.call-start
  14.5 1.1 convert_element_type.132
  15.6 0.0 all-gather.6.cloned.1.call-update
  15.6 0.3 reduce-scatter.4.cloned.1.call-start
  16.0 0.6 pad.12.s_ref
  16.6 0.8 copy.50
  17.5 0.8 convert_element_type.118.w_ref
  18.3 73.0 %gather_out.1 = bf16[2048,1024]{1,0:T(8,128)(2,1)} custom-call(bf16[256,512]{1,0:T(8,128)(2,1)} %bitcast.67), custom_call_target="tpu_custom_call" | custom-call | bytes 100000000 | tf_op jit(solution)/shard_map/gather_out/pallas_call | solution.py:682
  91.3 0.7 fusion.19.g_ref
  92.0 110.3 %gather_in.1 = (bf16[512,2048]{1,0:T(8,128)(2,1)}, bf16[2048,1536]{1,0:T(8,128)(2,1)}, f32[32,8,128]{2,1,0:T(8,128)}, s32[2,8,512]{2,1,0:T(8,128)}) custom-call(bf16[2,128,2048]{2,1,0:T(8,128)(2,1)} %x_ref.1, bf16[256,768]{1,0:T(8,128)(2,1)} %convert_element_type.118.w_ref, f32[8,128]{1,0:T(8,128)} %fusion.19.g_ref, s32[8,512]{1,0:T(8,128)} %pad.12.s_ref), custom_call_target="tpu_custom_call" | custom-call | bytes 200000000 | tf_op jit(solution)/shard_map/gather_in/pallas_call | solution.py:381
  202.4 1.2 slice_reduce_fusion.1
  203.6 0.1 mul.282
  203.7 0.1 mul.292
  203.8 0.7 constant_dynamic-slice_fusion.1
  204.5 0.2 convert_reduce_fusion
  204.7 1.0 fusion.15
  205.8 1.0 maximum_bitcast_fusion.cos_ref
  206.7 1.0 maximum_bitcast_fusion.1.sin_ref
  207.7 2.1 fusion.4
  209.8 8.3 fusion.12.qkv_ref
  218.2 0.6 reshape.377.seg_row_ref
  218.8 0.8 reshape.376.seg_col_ref
  219.6 18.4 %attn_forward.1 = (bf16[512,1536]{1,0:T(8,128)(2,1)}, f32[512,512]{1,0:T(8,128)}, bf16[512,1024]{1,0:T(8,128)(2,1)}) custom-call(f32[512,1536]{1,0:T(8,128)} %fusion.12.qkv_ref, f32[512,128]{1,0:T(8,128)} %maximum_bitcast_fusion.cos_ref, f32[512,128]{1,0:T(8,128)} %maximum_bitcast_fusion.1.sin_ref, s32[512,128]{1,0:T(8,128)} %reshape.376.seg_col_ref, ...), custom_call_target="tpu_custom_call" | custom-call | flops 2147483648 | bytes 4718592 | tf_op jit(solution)/shard_map/attn_forward/pallas_call | solution.py:177
  238.0 6.2 convolution_convert_fusion.4.part_ref
  244.2 62.2 %share_resid.1.resid_all = bf16[2,512,2048]{2,1,0:T(8,128)(2,1)} custom-call(bf16[512,2048]{1,0:T(8,128)(2,1)} %convolution_convert_fusion.4.part_ref, bf16[512,2048]{1,0:T(8,128)(2,1)} %get-tuple-element.39.x_ref), custom_call_target="tpu_custom_call" | custom-call | bytes 200000000 | tf_op jit(solution)/shard_map/share_resid/pallas_call | solution.py:482
  306.3 3.2 multiply_reduce_fusion
  309.6 0.2 copy-done
  309.8 3.0 fusion.1
  312.8 23.8 %fusion.30 = f32[1024,4096]{1,0:T(8,128)} fusion(bf16[1024,2048]{1,0:T(8,128)(2,1)} %fusion.1, bf16[2048,4096]{1,0:T(8,128)(2,1)} %all-gather.4.cloned.1.call-done), kind=kOutput, calls=%fused_computation.79 | convolution fusion | flops 17179869184 | bytes 37748736 | tf_op jit(solution)/shard_map/dot_general | solution.py:1013
  336.6 28.1 %all-gather.6.cloned.1.call-done = bf16[2048,2048]{1,0:T(8,128)(2,1)} async-done(((bf16[2048,256]{1,0:T(8,128)(2,1)}), bf16[2048,2048]{1,0:T(8,128)(2,1)}) %all-gather.6.cloned.1.call-update) | async-done | bytes 8388624 | tf_op jit(solution)/shard_map/all_gather | solution.py:995
  364.8 21.7 %multiply_convert_fusion.1 = (bf16[1024,2048]{1,0:T(8,128)(2,1)}, bf16[1024,2048]{1,0:T(8,128)(2,1)}, bf16[1024,2048]{1,0:T(8,128)(2,1)}) fusion(f32[1024,4096]{1,0:T(8,128)} %fusion.30, bf16[1024,2048]{1,0:T(8,128)(2,1)} %bitcast.64, bf16[2048,2048]{1,0:T(8,128)(2,1)} %all-gather.6.cloned.1.call-done), kind=kOutput, calls=%fused_computation.7 | convolution fusion | flops 8621391872 | bytes 41943040 | tf_op jit(solution)/shard_map/dot_general | solution.py:953
  386.5 14.1 %convolution_convert_fusion.3 = bf16[1024,2048]{1,0:T(8,128)(2,1)} fusion(bf16[1024,2048]{1,0:T(8,128)(2,1)} %get-tuple-element.77, bf16[2048,2048]{1,0:T(8,128)(2,1)} %all-gather.6.cloned.1.call-done), kind=kOutput, calls=%fused_computation.25 | convolution fusion | flops 8592031744 | bytes 16777216 | tf_op jit(solution)/shard_map/dot_general | solution.py:1039
  400.6 0.0 reduce-scatter.8.cloned.1.call-start
  400.7 14.0 %convert_bitcast_fusion = bf16[2048,2048]{0,1:T(8,128)(2,1)} fusion(bf16[1024,2048]{1,0:T(8,128)(2,1)} %get-tuple-element.77, bf16[1024,2048]{1,0:T(8,128)(2,1)} %bitcast.65), kind=kOutput, calls=%fused_computation.5 | convolution fusion | flops 8594128896 | bytes 16777216 | tf_op jit(solution)/shard_map/dot_general | solution.py:947
  414.7 0.0 reduce-scatter.6.cloned.1.call-start
  414.8 25.4 %convolution_convert_fusion = bf16[2048,4096]{1,0:T(8,128)(2,1)} fusion(bf16[1024,2048]{1,0:T(8,128)(2,1)} %fusion.1, bf16[1024,2048]{1,0:T(8,128)(2,1)} %get-tuple-element.76, bf16[1024,2048]{1,0:T(8,128)(2,1)} %get-tuple-element.75), kind=kOutput, calls=%fused_computation | convolution fusion | flops 17205035008 | bytes 29360128 | tf_op jit(solution)/shard_map/dot_general | solution.py:947
  440.3 0.7 reshape_squeeze.7.gain_ref
  440.9 0.7 reshape_squeeze.6.gain_ref
  441.6 24.1 %fusion.8 = bf16[1024,2048]{1,0:T(8,128)(2,1)} fusion(bf16[2048,4096]{1,0:T(8,128)(2,1)} %all-gather.4.cloned.1.call-done, bf16[1024,2048]{1,0:T(8,128)(2,1)} %get-tuple-element.76, bf16[1024,2048]{1,0:T(8,128)(2,1)} %get-tuple-element.75), kind=kOutput, calls=%fused_computation.23 | convolution fusion | flops 17198743552 | bytes 29360128 | tf_op jit(solution)/shard_map/dot_general | solution.py:953
  465.7 110.5 %sum_line.1 = (bf16[512,2048]{1,0:T(8,128)(2,1)}, f32[8,2048]{1,0:T(8,128)}) custom-call(bf16[2,512,2048]{2,1,0:T(8,128)(2,1)} %bitcast.66, bf16[2,512,2048]{2,1,0:T(8,128)(2,1)} %share_resid.1.resid_all, bf16[2,512,2048]{2,1,0:T(8,128)(2,1)} %all-gather.8.cloned.1.call-done.cot_all, f32[1,2048]{1,0:T(1,128)} %reshape_squeeze.6.gain_ref), custom_call_target="tpu_custom_call" | custom-call | bytes 200000000 | tf_op jit(solution)/shard_map/sum_line/pallas_call | solution.py:625
  576.3 6.1 convolution_convert_fusion.2.ot_ref
  582.4 3.3 convolution_convert_fusion.6.d_out_ref
  585.7 21.9 %attn_backward.1 = bf16[512,1536]{1,0:T(8,128)(2,1)} custom-call(bf16[512,1536]{1,0:T(8,128)(2,1)} %get-tuple-element.44.turned_ref, bf16[512,1024]{1,0:T(8,128)(2,1)} %convolution_convert_fusion.6.d_out_ref, f32[512,512]{1,0:T(8,128)} %get-tuple-element.46.lse_ref, f32[512,128]{1,0:T(8,128)} %maximum_bitcast_fusion.cos_ref, ...), custom_call_target="tpu_custom_call" | custom-call | flops 5368709120 | bytes 4718592 | tf_op jit(solution)/shard_map/attn_backward/pallas_call | solution.py:200
  607.7 7.1 convolution_convert_fusion.1.qt_ref
  614.8 7.7 convolution_convert_fusion.5.dn_ref
  622.5 204.4 %hand_out.1 = (bf16[2,128,2048]{2,1,0:T(8,128)(2,1)}, f32[256,768]{1,0:T(8,128)}, f32[512,256]{1,0:T(8,128)}, f32[16,128]{1,0:T(8,128)}) custom-call(bf16[512,2048]{1,0:T(8,128)(2,1)} %convolution_convert_fusion.5.dn_ref, bf16[512,2048]{1,0:T(8,128)(2,1)} %get-tuple-element.39.x_ref, bf16[512,2048]{1,0:T(8,128)(2,1)} %get-tuple-element.45.dr_ref, ...), custom_call_target="tpu_custom_call" | custom-call | bytes 300000000 | tf_op jit(solution)/shard_map/hand_out/pallas_call | solution.py:897
  826.9 0.9 bitcast_reduce_fusion
  827.8 0.1 constant_dynamic-slice_fusion
  827.9 0.6 multiply_subtract_fusion.4
  828.5 2.4 multiply_subtract_fusion.3
  830.9 1.8 multiply_subtract_fusion.2
  832.7 2.9 add_convert_fusion
  835.7 6.3 multiply_subtract_fusion.1
  841.9 6.6 reshape.384
  848.5 19.0 %multiply_subtract_fusion = (f32[256,2,2048]{2,1,0:T(2,128)}, f32[256,2,2048]{2,1,0:T(2,128)}, f32[256,2,2048]{2,1,0:T(2,128)}) fusion(f32[256,2,2048]{2,1,0:T(2,128)} %param.28, f32[256,2,2048]{2,1,0:T(2,128)} %reshape.384, f32[256,2,2048]{2,1,0:T(2,128)} %param.34, f32[256,2,2048]{2,1,0:T(2,128)} %param.40), kind=kLoop, calls=%fused_computation.21 | loop fusion | flops 15728640 | bytes 29360128 | tf_op jit(solution)/shard_map/sub | solution.py:940
  867.5 1.0 copy.56
  868.5 0.9 copy.57
  869.4 0.8 copy.58
  (79 shorter events, 0.3 us)
Async XLA Ops:
  7.2 305.6 %all-gather.4.cloned.1.call-start = ((), (), s32[]{:S(2)}) async-start(), calls=%async_computation.3 | async-start | bytes 18874368 | tf_op jit(solution)/shard_map/all_gather | solution.py:992
  11.5 3.1 copy-start.3
  13.7 2.3 copy-start.20
  13.7 2.9 copy-start.9
  13.7 3.8 copy-start.6
  13.7 322.9 %all-gather.8.cloned.1.call-start = ((), (), s32[]{:S(2)}) async-start(), calls=%async_computation.6 | async-start | bytes 5242880 | tf_op jit(solution)/shard_map/all_gather | solution.py:996
  14.5 350.3 %all-gather.6.cloned.1.call-start = ((), (), s32[]{:S(2)}) async-start(), calls=%async_computation.4 | async-start | bytes 9437184 | tf_op jit(solution)/shard_map/all_gather | solution.py:995
  15.6 75.7 %copy-start.23 = (f32[64]{0:T(128)S(1)}, f32[64]{0:T(128)}, u32[]{:S(2)}) copy-start(f32[64]{0:T(128)} %param.27) | copy-start | bytes 772
  15.6 75.7 %copy-start.25 = (f32[64]{0:T(128)S(1)}, f32[64]{0:T(128)}, u32[]{:S(2)}) copy-start(f32[64]{0:T(128)} %param.24) | copy-start | bytes 772
  15.6 817.1 %reduce-scatter.4.cloned.1.call-start = ((), (), s32[]{:S(2)}) async-start(), calls=%async_computation.5 | async-start | bytes 5242880 | tf_op jit(solution)/shard_map/reduce_scatter | solution.py:1040
  202.4 7.5 copy-start.1
  203.7 14.5 %copy-start.18 = (f32[2048]{0:T(1024)}, f32[2048]{0:T(1024)S(1)}, u32[]{:S(2)}) copy-start(f32[2048]{0:T(1024)S(1)} %mul.282) | copy-start | bytes 24580
  209.8 8.4 copy-start.21
  306.3 3.5 copy-start
  400.6 435.0 %reduce-scatter.8.cloned.1.call-start = ((), (), s32[]{:S(2)}) async-start(), calls=%async_computation.8 | async-start | bytes 9437184 | tf_op jit(solution)/shard_map/reduce_scatter | solution.py:1025
  414.7 427.2 %reduce-scatter.6.cloned.1.call-start = ((), (), s32[]{:S(2)}) async-start(), calls=%async_computation.7 | async-start | bytes 18874368 | tf_op jit(solution)/shard_map/reduce_scatter | solution.py:1035
  465.7 110.5 %copy-start.31 = (bf16[512,1024]{1,0:T(8,128)(2,1)S(1)}, bf16[512,1024]{1,0:T(8,128)(2,1)}, u32[]{:S(2)}) copy-start(bf16[512,1024]{1,0:T(8,128)(2,1)} %get-tuple-element.43) | copy-start | bytes 3145732
  576.3 6.2 copy-start.5
  576.3 6.2 copy-start.12
  585.7 21.9 %copy-start.2 = (bf16[512,2048]{1,0:T(8,128)(2,1)S(1)}, bf16[512,2048]{1,0:T(8,128)(2,1)}, u32[]{:S(2)}) copy-start(bf16[512,2048]{1,0:T(8,128)(2,1)} %get-tuple-element.39.x_ref) | copy-start | bytes 6291460
  585.7 21.9 %copy-start.19 = (f32[2048]{0:T(1024)S(1)}, f32[2048]{0:T(1024)}, u32[]{:S(2)}) copy-start(f32[2048]{0:T(1024)} %copy-done.18) | copy-start | bytes 24580
  585.7 21.9 %copy-start.22 = (f32[512]{0:T(512)S(1)}, f32[512]{0:T(512)}, u32[]{:S(2)}) copy-start(f32[512]{0:T(512)} %copy-done.21) | copy-start | bytes 6148
  607.6 7.1 copy-start.32
  622.5 205.4 %copy-start.24 = (f32[64]{0:T(128)S(1)}, f32[64]{0:T(128)}, u32[]{:S(2)}) copy-start(f32[64]{0:T(128)} %param.27) | copy-start | bytes 772
  622.5 205.4 %copy-start.26 = (f32[64]{0:T(128)S(1)}, f32[64]{0:T(128)}, u32[]{:S(2)}) copy-start(f32[64]{0:T(128)} %param.24) | copy-start | bytes 772
  622.5 205.4 %copy-start.27 = (f32[64]{0:T(128)S(1)}, f32[64]{0:T(128)}, u32[]{:S(2)}) copy-start(f32[64]{0:T(128)} %param.33) | copy-start | bytes 772
  622.5 205.4 %copy-start.28 = (f32[64]{0:T(128)S(1)}, f32[64]{0:T(128)}, u32[]{:S(2)}) copy-start(f32[64]{0:T(128)} %param.39) | copy-start | bytes 772
  622.5 205.4 %copy-start.29 = (f32[64]{0:T(128)S(1)}, f32[64]{0:T(128)}, u32[]{:S(2)}) copy-start(f32[64]{0:T(128)} %param.36) | copy-start | bytes 772
  622.5 205.4 %copy-start.30 = (f32[64]{0:T(128)S(1)}, f32[64]{0:T(128)}, u32[]{:S(2)}) copy-start(f32[64]{0:T(128)} %param.30) | copy-start | bytes 772
  622.5 206.0 %copy-start.10 = (f32[512,256]{1,0:T(8,128)S(1)}, f32[512,256]{1,0:T(8,128)}, u32[]{:S(2)}) copy-start(f32[512,256]{1,0:T(8,128)} %param.26) | copy-start | bytes 1572868
  622.5 206.0 %copy-start.16 = (f32[512,256]{1,0:T(8,128)S(1)}, f32[512,256]{1,0:T(8,128)}, u32[]{:S(2)}) copy-start(f32[512,256]{1,0:T(8,128)} %param.32) | copy-start | bytes 1572868
  622.5 206.0 %copy-start.17 = (f32[512,256]{1,0:T(8,128)S(1)}, f32[512,256]{1,0:T(8,128)}, u32[]{:S(2)}) copy-start(f32[512,256]{1,0:T(8,128)} %param.38) | copy-start | bytes 1572868
  826.9 4.0 copy-start.7
  826.9 4.0 copy-start.8
  826.9 4.0 copy-start.14
  826.9 4.0 copy-start.15
  830.9 4.7 copy-start.4
  848.5 19.0 %copy-start.13 = (bf16[2,128,2048]{2,1,0:T(8,128)(2,1)S(1)}, bf16[2,128,2048]{2,1,0:T(8,128)(2,1)}, u32[]{:S(2)}) copy-start(bf16[2,128,2048]{2,1,0:T(8,128)(2,1)} %get-tuple-element.116) | copy-start | bytes 3145732
  848.5 20.9 %copy-start.11 = (f32[512,256]{1,0:T(8,128)S(1)}, f32[512,256]{1,0:T(8,128)}, u32[]{:S(2)}) copy-start(f32[512,256]{1,0:T(8,128)} %get-tuple-element.119) | copy-start | bytes 1572868
Sparse Core Ops, SparseCore 0:
  13.8 180.6 all-gather.3
  196.1 105.4 all-gather.7
  304.0 60.7 all-gather.5
  400.7 96.3 reduce-scatter.3
  500.4 74.6 reduce-scatter.7
  578.5 205.2 reduce-scatter.5

commit v3 on v2

--- a/solution.py
+++ b/solution.py
@@ -7,10 +7,10 @@
 from jax.experimental.pallas import tpu as pltpu
 from jax.sharding import PartitionSpec as P
 
+
 HEADS = 32
 KV_HEADS = 8
 norm_eps = 1e-05
-rope_base = 500000.0
 beta_one = 0.9
 beta_two = 0.95
 learn_rate = 0.01
@@ -166,27 +166,70 @@
 REACH = 256
 
 
-def attn_forward(qkv, cos, sin, seg_col, seg_row, full_len, groups):
+def attn_gather_kernel(n_dp, pairs, q_rows, reach, qkv_ref, cos_ref, sin_ref, seg_col_ref, seg_row_ref, vo_ref,
+                       turned_ref, lse_ref, out_ref, wo, d_s, d_r, loc):
+    _, z, pair, c = place()
+    n_d = n_dp // 2
+    step = pl.program_id(1)
+    steps = pl.num_programs(1)
+    rows = vo_ref.shape[0]
+    parts = 2
+    part = rows // parts // 2
+
+    def spot(owner, t, h):
+        return wo.at[pl.ds(pl.multiple_of(owner * rows + (2 * t + h) * part, part), part)]
+
+    spread = Spread(n_d, pair, c, z, parts, spot, d_s, d_r)
+    keep = pltpu.make_async_copy(vo_ref, wo.at[pl.ds(pl.multiple_of(pair * rows, rows), rows)], loc)
+
+    @pl.when(step == 0)
+    def _():
+        keep.start()
+        barrier = pltpu.get_barrier_semaphore()
+        for k in range(1, n_d):
+            pl.semaphore_signal(barrier, inc=1, device_id=(2 * (pair ^ k) + c, z), device_id_type=MESH)
+        pl.semaphore_wait(barrier, n_d - 1)
+        keep.wait()
+        for t in range(parts):
+            spread.own(t)
+
+    attn_forward_kernel(pairs, q_rows, reach, qkv_ref, cos_ref, sin_ref, seg_col_ref, seg_row_ref, turned_ref, lse_ref, out_ref)
+
+    @pl.when(step == steps - 2)
+    def _():
+        spread.pass_on(0)
+
+    @pl.when(step == steps - 1)
+    def _():
+        spread.pass_on(1)
+        spread.finish()
+
+
+def attn_forward(qkv, cos, sin, seg_col, seg_row, vo, full_len, groups, n_dp):
     pairs = groups // 2
     width = (groups + 2) * HEAD_DIM
     seqs = qkv.shape[0] // full_len
     kv = qkv.shape[1] // width
+    n_d = n_dp // 2
     line, table, row = attn_specs(full_len, width)
     outw = pl.BlockSpec((full_len, groups * HEAD_DIM), lambda s, g: (s, g))
     rows = seqs * full_len
     return pl.pallas_call(
-        functools.partial(attn_forward_kernel, pairs, Q_ROWS, REACH),
+        functools.partial(attn_gather_kernel, n_dp, pairs, Q_ROWS, REACH),
         grid=(seqs, kv),
-        in_specs=[line, table, table, table, row],
-        out_specs=[line, pl.BlockSpec((full_len, LANES), lambda s, g: (s, g)), outw],
+        in_specs=[line, table, table, table, row, VMEM_SPEC],
+        out_specs=[line, pl.BlockSpec((full_len, LANES), lambda s, g: (s, g)), outw, ANY_SPEC],
         out_shape=[
             jax.ShapeDtypeStruct((rows, kv * width), jnp.bfloat16),
             jax.ShapeDtypeStruct((rows, kv * LANES), jnp.float32),
             jax.ShapeDtypeStruct((rows, kv * groups * HEAD_DIM), jnp.bfloat16),
+            jax.ShapeDtypeStruct((n_d * vo.shape[0], vo.shape[1]), jnp.bfloat16),
         ],
-        cost_estimate=pl.CostEstimate(flops=4 * rows * full_len * kv * LANES * groups, bytes_accessed=rows * kv * width * 6, transcendentals=0),
+        scratch_shapes=[DMA((n_d - 1, 2, 2)), DMA((n_d - 1, 2, 2)), DMA],
+        compiler_params=pltpu.CompilerParams(collective_id=4, has_side_effects=True),
+        cost_estimate=pl.CostEstimate(flops=4 * rows * full_len * kv * LANES * groups, bytes_accessed=150_000_000, transcendentals=0),
         name="attn_forward",
-    )(qkv, cos, sin, seg_col, seg_row)
+    )(qkv, cos, sin, seg_col, seg_row, vo)
 
 
 def attn_backward(turned, d_out, lse, cos, sin, seg_col, seg_row, full_len, groups):
@@ -274,8 +317,51 @@
                   pl.ds(pl.multiple_of(col * shape[1], shape[1]), shape[1])]
 
 
-def gather_in_kernel(n_dp, n_z, x_ref, w_ref, g_ref, s_ref, xs, wq, ga, sg,
-                     x_s, x_r, f_s, f_r, w_s, w_r, d_s, d_r, g_s, g_r, s_s, s_r, loc):
+class Spread:
+    def __init__(self, n_d, pair, c, z, parts, spot, send, recv):
+        self.n_d, self.pair, self.parts, self.spot = n_d, pair, parts, spot
+        self.send, self.recv = send, recv
+        self.dev = lambda k: (2 * (pair ^ k) + c, z)
+
+    def copy(self, slot, owner, t, h, to):
+        at = self.spot(owner, t, h)
+        return remote(at, at, self.send.at[slot, t, h], self.recv.at[slot, t, h], self.dev(to))
+
+    def own(self, t):
+        if self.n_d == 4:
+            for h in range(2):
+                self.copy(0, self.pair, t, h, 1).start()
+                self.copy(1, self.pair, t, 1 - h, 2).start()
+        else:
+            for k in range(1, self.n_d):
+                for h in range(2):
+                    self.copy(k - 1, self.pair, t, h, k).start()
+
+    def pass_on(self, t):
+        if self.n_d == 4:
+            self.copy(0, self.pair ^ 1, t, 0, 1).wait_recv()
+            self.copy(2, self.pair ^ 1, t, 0, 2).start()
+            self.copy(1, self.pair ^ 2, t, 1, 2).wait_recv()
+            self.copy(2, self.pair ^ 2, t, 1, 1).start()
+
+    def finish(self):
+        for t in range(self.parts):
+            if self.n_d == 4:
+                self.copy(0, self.pair ^ 1, t, 1, 1).wait_recv()
+                self.copy(1, self.pair ^ 2, t, 0, 2).wait_recv()
+                for h in range(2):
+                    self.copy(2, self.pair ^ 3, t, h, 1).wait_recv()
+                    for slot in range(3):
+                        self.copy(slot, self.pair, t, h, 1).wait_send()
+            else:
+                for k in range(1, self.n_d):
+                    for h in range(2):
+                        self.copy(k - 1, self.pair ^ k, t, h, k).wait_recv()
+                        self.copy(k - 1, self.pair, t, h, k).wait_send()
+
+
+def gather_in_kernel(n_dp, n_z, x_ref, w_ref, v_ref, g_ref, s_ref, xs, wq, vo, ga, sg,
+                     x_s, x_r, f_s, f_r, w_s, w_r, v_s, v_r, d_s, d_r, g_s, g_r, s_s, s_r, loc):
     d, z, pair, c = place()
     n_d = n_dp // 2
     me = d * n_z + z
@@ -286,15 +372,19 @@
     cz = z // 2
     greet_all(n_dp, n_z, d, z)
 
+    def line_stage(src, dst, send, recv, spare, wait):
+        for o in range(n_z):
+            copy = remote(src, dst, send.at[o], recv.at[c, z % 2], (2 * pair + cz, lax.rem(z + o, n_z)))
+            act = copy.wait_send if wait else copy.start
+            if o == 0:
+                pl.when(c != cz)(act)
+                if not wait:
+                    pl.when(c == cz)(pltpu.make_async_copy(src, dst, loc.at[spare]).start)
+            else:
+                act()
+
     my_block = block_at(wq, shape, d, z % 2)
-    for o in range(n_z):
-        zz = lax.rem(z + o, n_z)
-        copy = remote(w_ref, my_block, w_s.at[o], w_r.at[c, z % 2], (2 * pair + cz, zz))
-        if o == 0:
-            pl.when(c != cz)(copy.start)
-            pl.when(c == cz)(lambda: pltpu.make_async_copy(w_ref, my_block, loc.at[0]).start())
-        else:
-            copy.start()
+    line_stage(w_ref, my_block, w_s, w_r, 0, False)
 
     for i in range(2):
         for h in range(2):
@@ -321,16 +411,29 @@
     lax.fori_loop(1, total, send_gain, 0)
 
     first = jnp.where(c == cz, z % 2, 1 - c)
+
+    def turn_of(t):
+        return t % 2, (first if t < 2 else 1 - first)
+
+    def spot(owner, t, h):
+        core, b = turn_of(t)
+        part = shape[0] // 2
+        return wq.at[pl.ds(pl.multiple_of((2 * owner + core) * shape[0] + h * part, part), part),
+                     pl.ds(pl.multiple_of(b * shape[1], shape[1]), shape[1])]
+
+    spread = Spread(n_d, pair, c, z, 4, spot, d_s, d_r)
     for t in range(4):
-        b = first if t < 2 else 1 - first
-        core = t % 2
+        core, b = turn_of(t)
         blk = block_at(wq, shape, 2 * pair + core, b)
         mine = (core == c) & (2 * c + b == z)
         arrive = remote(w_ref, blk, w_s.at[0], w_r.at[core, b], (d, z))
         pl.when(jnp.logical_not(mine))(arrive.wait_recv)
         pl.when(mine)(lambda blk=blk: pltpu.make_async_copy(w_ref, blk, loc.at[0]).wait())
-        for k in range(1, n_d):
-            remote(blk, blk, d_s.at[k - 1, t], d_r.at[k - 1], (2 * (pair ^ k) + c, z)).start()
+        spread.own(t)
+        if t == 1:
+            line_stage(v_ref, block_at(vo, v_ref.shape, c, z % 2), v_s, v_r, 4, False)
+        if t > 0:
+            spread.pass_on(t - 1)
 
     for o in range(n_z):
         zs = lax.rem(z + o, n_z)
@@ -340,13 +443,10 @@
         pl.when(jnp.logical_not(mine))(arrive.wait_recv)
         pl.when(mine)(lambda src=src: pltpu.make_async_copy(src, src, loc.at[1]).wait())
         remote(src, src, f_s.at[zs], f_r.at[zs], (2 * pair + 1 - c, z)).start()
-
-    for o in range(n_z):
-        copy = remote(w_ref, my_block, w_s.at[o], w_r.at[0, 0], (d, z))
-        if o == 0:
-            pl.when(c != cz)(copy.wait_send)
-        else:
-            copy.wait_send()
+    spread.pass_on(3)
+
+    line_stage(w_ref, my_block, w_s, w_r, 0, True)
+    line_stage(v_ref, block_at(vo, v_ref.shape, c, z % 2), v_s, v_r, 4, True)
     for i in range(2):
         for h in range(2):
             src = x_ref.at[i, pl.ds(h * half, half)]
@@ -358,6 +458,12 @@
         copy = remote(src, src, f_s.at[zs], f_r.at[zs], (d, z))
         copy.wait_send()
         copy.wait_recv()
+    for core in range(2):
+        for b in range(2):
+            blk = block_at(vo, v_ref.shape, core, b)
+            mine = (core == c) & (2 * c + b == z)
+            pl.when(jnp.logical_not(mine))(remote(blk, blk, v_s.at[0], v_r.at[core, b], (d, z)).wait_recv)
+            pl.when(mine)(pltpu.make_async_copy(v_ref, blk, loc.at[4]).wait)
     seg_copy.wait_send()
     remote(s_ref, sg.at[1 - c], s_s, s_r, (d, z)).wait_recv()
     own_seg.wait()
@@ -366,36 +472,32 @@
     gains = remote(many, many, g_s, g_r, (d, z))
     gains.wait_send()
     gains.wait_recv()
-    blk = block_at(wq, shape, 0, 0)
-    for k in range(1, n_d):
-        for t in range(4):
-            remote(blk, blk, d_s.at[k - 1, t], d_r.at[k - 1], (d, z)).wait_send()
-        region = wq.at[pl.ds(0, 2 * shape[0])]
-        remote(region, region, d_s.at[k - 1, 0], d_r.at[k - 1], (d, z)).wait_recv()
-
-
-def gather_in(x_loc, w, gain_tile, seg_tile, n_dp, n_z):
-    seqs, rows, width = x_loc.shape
+    spread.finish()
+
+
+def gather_in(x_loc, w, v, gain_tile, seg_tile, n_dp, n_z):
+    _, rows, width = x_loc.shape
     n_d = n_dp // 2
     total = n_dp * n_z
     return pl.pallas_call(
         functools.partial(gather_in_kernel, n_dp, n_z),
-        in_specs=[VMEM_SPEC] * 4,
-        out_specs=[ANY_SPEC] * 4,
+        in_specs=[VMEM_SPEC] * 5,
+        out_specs=[ANY_SPEC] * 5,
         out_shape=[
             jax.ShapeDtypeStruct((rows * n_z, width), x_loc.dtype),
             jax.ShapeDtypeStruct((w.shape[0] * n_dp, 2 * w.shape[1]), w.dtype),
+            jax.ShapeDtypeStruct((v.shape[0] * 2, 2 * v.shape[1]), v.dtype),
             jax.ShapeDtypeStruct((total,) + gain_tile.shape, gain_tile.dtype),
             jax.ShapeDtypeStruct((2,) + seg_tile.shape, seg_tile.dtype),
         ],
         scratch_shapes=[
-            DMA((2, 2)), DMA((n_z,)), DMA((n_z,)), DMA((n_z,)), DMA((n_z,)), DMA((2, 2)),
-            DMA((n_d - 1, 4)), DMA((n_d - 1,)), DMA, DMA, DMA, DMA, DMA((4,)),
+            DMA((2, 2)), DMA((n_z,)), DMA((n_z,)), DMA((n_z,)), DMA((n_z,)), DMA((2, 2)), DMA((n_z,)), DMA((2, 2)),
+            DMA((n_d - 1, 4, 2)), DMA((n_d - 1, 4, 2)), DMA, DMA, DMA, DMA, DMA((5,)),
         ],
         compiler_params=pltpu.CompilerParams(collective_id=1, has_side_effects=True),
         cost_estimate=pl.CostEstimate(flops=0, bytes_accessed=200_000_000, transcendentals=0),
         name="gather_in",
-    )(x_loc, w, gain_tile, seg_tile)
+    )(x_loc, w, v, gain_tile, seg_tile)
 
 
 def share_resid_kernel(n_z, part_ref, x_ref, out, got, buf, p_s, p_r, u_s, u_r, loc):
@@ -466,11 +568,13 @@
     order = [(dist, sign) for dist in range(1, n_z) for sign in (-1, 1)]
     for dist, sign in order:
         relay(dist, sign, True)
+
     @pl.when(c == cz)
     def _():
         for k in range(2):
             at = spot(z % 2, 1 - c, k)
             remote(at, at, u_s.at[0, 0], u_r.at[z % 2, 1 - c, k], (d, z)).wait_recv()
+
     for dist, sign in order:
         relay(dist, sign, False)
     sends(0, True)
@@ -501,7 +605,7 @@
                     s_s, s_r, p_s, p_r, loc, rows_sem):
     d, z, pair, c = place()
     cz = z // 2
-    full, width = buf.shape
+    full, _ = buf.shape
     rows = full // CHUNKS
     fetch = (
         pltpu.make_async_copy(resid_all.at[z % 2], resid_ref, rows_sem.at[0]),
@@ -519,7 +623,7 @@
         return jl, 2 * c + jl, pl.ds(k * rows, rows)
 
     def copy_on(k, t, side, src):
-        jl, j, at = where_is(k, t)
+        jl, _, at = where_is(k, t)
         to = z + 1 if side == 0 else z - 1
         return remote(src, got.at[side, jl, at], s_s.at[t, k], s_r.at[side, jl, k], (2 * pair + c, to))
 
@@ -532,6 +636,7 @@
             at = pl.ds(pl.multiple_of(k * rows + r * 16, 16), 16)
             got[side, jl, at] = (got[side, jl, at].astype(jnp.float32) + part_ref[jl, at].astype(jnp.float32)).astype(jnp.bfloat16)
             return carry
+
         lax.fori_loop(0, rows // 16, one, 0)
 
     def finish(jl, k):
@@ -551,6 +656,7 @@
             prod = total * scaled
             gain_out[...] = gain_out[...] + prod[:8] + prod[8:]
             return carry
+
         lax.fori_loop(0, rows // 16, one, 0)
 
     def to_partner(k):
@@ -581,34 +687,45 @@
                 to_partner(k).start()
                 keep(k).start()
 
-    for n, (k, t) in enumerate(steps):
-        jl, j, at = where_is(k, t)
-        for side in range(2):
-            going = (z < j) if side == 0 else (z > j)
-            inner = (z > 0) if side == 0 else (z < n_z - 1)
-
-            @pl.when(going & inner)
-            def _():
-                arrived(side, jl, k).wait_recv()
-                add_in(side, jl, k)
-
-        if n > 0:
-            send_step(*steps[n - 1], False)
-    send_step(*steps[-1], False)
-
-    for one in fetch:
-        one.wait()
-
-    @pl.when(own)
-    def _():
-        jl = z % 2
-        for k in range(CHUNKS):
+    def own_chunk(k):
+        @pl.when(own)
+        def _():
+            if k == 0:
+                for one in fetch:
+                    one.wait()
+            jl = z % 2
             pl.when(z > 0)(arrived(0, jl, k).wait_recv)
             pl.when(z < n_z - 1)(arrived(1, jl, k).wait_recv)
             finish(jl, k)
             if k > 0:
                 to_partner(k - 1).start()
                 keep(k - 1).start()
+
+    for n, (k, t) in enumerate(steps):
+        jl, j, at = where_is(k, t)
+        for side in range(2):
+            going = (z < j) if side == 0 else (z > j)
+            inner = (z > 0) if side == 0 else (z < n_z - 1)
+
+            @pl.when(going & inner)
+            def _():
+                arrived(side, jl, k).wait_recv()
+                add_in(side, jl, k)
+
+        if n > 0:
+            send_step(*steps[n - 1], False)
+        if t == 1 and k > 0:
+            own_chunk(k - 1)
+    send_step(*steps[-1], False)
+    own_chunk(CHUNKS - 1)
+
+    @pl.when(jnp.logical_not(own))
+    def _():
+        for one in fetch:
+            one.wait()
+
+    @pl.when(own)
+    def _():
         to_partner(CHUNKS - 1).start()
         keep(CHUNKS - 1).start()
 
@@ -638,61 +755,8 @@
     )(part, resid, cot, gain)
 
 
-def gather_out_kernel(n_dp, n_z, w_ref, wo, w_s, w_r, d_s, d_r, loc):
-    d, z, pair, c = place()
-    n_d = n_dp // 2
-    cz = z // 2
-    shape = w_ref.shape
-    greet_line(n_z, d, z, [(2 * (pair ^ k) + c, z) for k in range(1, n_d)])
-    my_block = block_at(wo, shape, d, z % 2)
-    for o in range(n_z):
-        copy = remote(w_ref, my_block, w_s.at[o], w_r.at[c, z % 2], (2 * pair + cz, lax.rem(z + o, n_z)))
-        if o == 0:
-            pl.when(c != cz)(copy.start)
-            pl.when(c == cz)(lambda: pltpu.make_async_copy(w_ref, my_block, loc).start())
-        else:
-            copy.start()
-    first = jnp.where(c == cz, z % 2, 1 - c)
-    for t in range(4):
-        b = first if t < 2 else 1 - first
-        core = t % 2
-        blk = block_at(wo, shape, 2 * pair + core, b)
-        mine = (core == c) & (2 * c + b == z)
-        arrive = remote(w_ref, blk, w_s.at[0], w_r.at[core, b], (d, z))
-        pl.when(jnp.logical_not(mine))(arrive.wait_recv)
-        pl.when(mine)(lambda blk=blk: pltpu.make_async_copy(w_ref, blk, loc).wait())
-        for k in range(1, n_d):
-            remote(blk, blk, d_s.at[k - 1, t], d_r.at[k - 1], (2 * (pair ^ k) + c, z)).start()
-    for o in range(n_z):
-        copy = remote(w_ref, my_block, w_s.at[o], w_r.at[0, 0], (d, z))
-        if o == 0:
-            pl.when(c != cz)(copy.wait_send)
-        else:
-            copy.wait_send()
-    blk = block_at(wo, shape, 0, 0)
-    for k in range(1, n_d):
-        for t in range(4):
-            remote(blk, blk, d_s.at[k - 1, t], d_r.at[k - 1], (d, z)).wait_send()
-        region = wo.at[pl.ds(0, 2 * shape[0])]
-        remote(region, region, d_s.at[k - 1, 0], d_r.at[k - 1], (d, z)).wait_recv()
-
-
-def gather_out(w, n_dp, n_z):
-    n_d = n_dp // 2
-    return pl.pallas_call(
-        functools.partial(gather_out_kernel, n_dp, n_z),
-        in_specs=[VMEM_SPEC],
-        out_specs=ANY_SPEC,
-        out_shape=jax.ShapeDtypeStruct((n_dp * w.shape[0], 2 * w.shape[1]), w.dtype),
-        scratch_shapes=[DMA((n_z,)), DMA((2, 2)), DMA((n_d - 1, 4)), DMA((n_d - 1,)), DMA],
-        compiler_params=pltpu.CompilerParams(collective_id=4, has_side_effects=True),
-        cost_estimate=pl.CostEstimate(flops=0, bytes_accessed=100_000_000, transcendentals=0),
-        name="gather_out",
-    )(w)
-
-
 def hand_out_kernel(n_dp, n_z, dn_ref, x_ref, dr_ref, gain_ref, gain2_ref, qt_ref, ot_ref,
-                    ig, gq, go, gains, got, buf, q_got, q_own, q_put, q_fin, o_got, o_own, o_put, o_fin, g_src, g_all,
+                    ig, gq, go, gains, got, buf, q_got, q_own, q_mid, q_put, q_fin, o_got, o_own, o_mid, o_put, o_fin, g_src, g_all,
                     p_s, p_r, i_s, i_r, q_s, q_r, qf_s, qf_r, o_s, o_r, of_s, of_r, g_s, g_r, loc):
     d, z, pair, c = place()
     n_d = n_dp // 2
@@ -704,32 +768,93 @@
     quarter = half // 2
     q_rows, q_cols = q_fin.shape[1:]
     o_rows, o_cols = o_fin.shape[1:]
-    q_load = pltpu.make_async_copy(qt_ref.at[pl.ds(pl.multiple_of(pair * 2 * q_rows, 2 * q_rows), 2 * q_rows)], q_own, loc.at[0])
-    o_load = pltpu.make_async_copy(ot_ref.at[pl.ds(pl.multiple_of(pair * 2 * o_rows, 2 * o_rows), 2 * o_rows)], o_own, loc.at[1])
-    q_load.start()
-    o_load.start()
+    relay = n_d == 4
+
+    def region(ref, rows, cols, owner, b):
+        return ref.at[pl.ds(pl.multiple_of(owner * 2 * rows, 2 * rows), 2 * rows), pl.ds(b * cols, cols)]
+
+    class First:
+        def __init__(self, src, rows, cols, got_ref, own_ref, mid_ref, put_ref, send, recv, spare):
+            self.src, self.rows, self.cols, self.got, self.own, self.mid = src, rows, cols, got_ref, own_ref, mid_ref
+            self.put, self.send, self.recv, self.spare = put_ref, send, recv, spare
+
+        def slot(self, n, b):
+            return self.got.at[n, :, pl.ds(b * self.cols, self.cols)]
+
+        def copy(self, n, b, owner, to):
+            src = region(self.src, self.rows, self.cols, owner, b)
+            return remote(src, self.slot(n, b), self.send.at[n, b], self.recv.at[n, b], (2 * (pair ^ to) + c, z))
+
+        def load(self, b):
+            yield pltpu.make_async_copy(region(self.src, self.rows, self.cols, pair, b), self.own.at[:, pl.ds(b * self.cols, self.cols)], loc.at[self.spare + b])
+            if relay:
+                yield pltpu.make_async_copy(region(self.src, self.rows, self.cols, pair ^ (2 >> b), b), self.mid.at[:, pl.ds(b * self.cols, self.cols)], loc.at[self.spare + 2 + b])
+
+        def begin(self, b):
+            if relay:
+                near = 1 + b
+                self.copy(1, b, pair ^ 3, near).start()
+                self.copy(0, b, pair ^ near, near).start()
+            else:
+                for k in range(1, n_d):
+                    self.copy(k - 1, b, pair ^ k, k).start()
+
+        def arrived(self, n, b):
+            remote(self.slot(n, b), self.slot(n, b), self.send.at[n, b], self.recv.at[n, b], (d, z)).wait_recv()
+
+        def middle(self, b):
+            if not relay:
+                return
+            self.arrived(1, b)
+            lanes = pl.ds(b * self.cols, self.cols)
+
+            def add(r, carry):
+                at = pl.ds(pl.multiple_of(r * 16, 16), 16)
+                self.mid[at, lanes] = (self.mid[at, lanes].astype(jnp.float32) + self.got[1, at, lanes].astype(jnp.float32)).astype(jnp.bfloat16)
+                return carry
+
+            lax.fori_loop(0, 2 * self.rows // 16, add, 0)
+
+        def middle_copy(self, b):
+            src = self.mid.at[:, pl.ds(b * self.cols, self.cols)]
+            return remote(src, self.slot(2, b), self.send.at[2, b], self.recv.at[2, b], (2 * (pair ^ (2 >> b)) + c, z))
+
+        def total(self, b):
+            slots = (0, 2) if relay else range(n_d - 1)
+            for n in slots:
+                self.arrived(n, b)
+            lanes = pl.ds(b * self.cols, self.cols)
+            for core in range(2):
+
+                def add(r, carry):
+                    at = pl.ds(pl.multiple_of(r * 16, 16), 16)
+                    src = pl.ds(pl.multiple_of(core * self.rows + r * 16, 16), 16)
+                    value = self.own[src, lanes].astype(jnp.float32)
+                    for n in slots:
+                        value = value + self.got[n, src, lanes].astype(jnp.float32)
+                    self.put[core, b, at] = value.astype(jnp.bfloat16)
+                    return carry
+
+                lax.fori_loop(0, self.rows // 16, add, 0)
+
+        def sent(self, b):
+            for n in range(n_d - 1):
+                remote(self.slot(n, b), self.slot(n, b), self.send.at[n, b], self.recv.at[n, b], (d, z)).wait_send()
+
+    o_first = First(ot_ref, o_rows, o_cols, o_got, o_own, o_mid, o_put, o_s, o_r, 6)
+    q_first = First(qt_ref, q_rows, q_cols, q_got, q_own, q_mid, q_put, q_s, q_r, 10)
+    firsts = [(o_first, 0), (o_first, 1), (q_first, 0), (q_first, 1)]
+    for one, b in firsts:
+        for copy in one.load(b):
+            copy.start()
     greet_all(n_dp, n_z, d, z)
-
-    def q_send(k, b):
-        other = pair ^ k
-        src = qt_ref.at[pl.ds(pl.multiple_of(other * 2 * q_rows, 2 * q_rows), 2 * q_rows), pl.ds(b * q_cols, q_cols)]
-        return remote(src, q_got.at[k - 1, :, pl.ds(b * q_cols, q_cols)], q_s.at[k - 1, b], q_r.at[k - 1, b], (2 * other + c, z))
-
-    def o_send(k, b):
-        other = pair ^ k
-        src = ot_ref.at[pl.ds(pl.multiple_of(other * 2 * o_rows, 2 * o_rows), 2 * o_rows), pl.ds(b * o_cols, o_cols)]
-        return remote(src, o_got.at[k - 1, :, pl.ds(b * o_cols, o_cols)], o_s.at[k - 1, b], o_r.at[k - 1, b], (2 * other + c, z))
 
     mine = pl.ds(pl.multiple_of(c * half, half), half)
     theirs = pl.ds(pl.multiple_of((1 - c) * half, half), half)
     swap = remote(dn_ref.at[theirs], got, p_s, p_r, (2 * pair + 1 - c, z))
     swap.start()
-    for b in range(2):
-        for k in range(1, n_d):
-            o_send(k, b).start()
-    for b in range(2):
-        for k in range(1, n_d):
-            q_send(k, b).start()
+    for one, b in firsts:
+        one.begin(b)
 
     g_src[pl.ds(0, 8)] = jnp.zeros((8, width), jnp.float32)
     g_src[pl.ds(8, 8)] = gain2_ref[...]
@@ -765,8 +890,9 @@
     lax.fori_loop(per, per + per // 2, rows_of, 0)
     row_send(0, False)
     lax.fori_loop(per + per // 2, 2 * per, rows_of, 0)
-    q_load.wait()
-    o_load.wait()
+    for one, b in firsts:
+        for copy in one.load(b):
+            copy.wait()
     row_send(1, False)
 
     each = width // total
@@ -783,20 +909,6 @@
         return carry
 
     lax.fori_loop(1, total, send_gain, 0)
-
-    def second(b, rows, own_ref, got_ref, put_ref, cut):
-        for core in range(2):
-
-            def add(r, carry):
-                at = pl.ds(pl.multiple_of(r * 16, 16), 16)
-                src, lanes = cut(core, b, r)
-                value = own_ref[src, lanes].astype(jnp.float32)
-                for k in range(n_d - 1):
-                    value = value + got_ref[k, src, lanes].astype(jnp.float32)
-                put_ref[core, b, at] = value.astype(jnp.bfloat16)
-                return carry
-
-            lax.fori_loop(0, rows // 16, add, 0)
 
     def second_send(b, put_ref, fin_ref, f_s, f_r, spare, wait):
         for core in range(2):
@@ -807,12 +919,6 @@
             pl.when(jnp.logical_not(here))(copy.wait_send if wait else copy.start)
             pl.when(here)(keep.wait if wait else keep.start)
 
-    def q_cut(core, b, r):
-        return pl.ds(pl.multiple_of(core * q_rows + r * 16, 16), 16), pl.ds(b * q_cols, q_cols)
-
-    def o_cut(core, b, r):
-        return pl.ds(pl.multiple_of(core * o_rows + r * 16, 16), 16), pl.ds(b * o_cols, o_cols)
-
     def last(rows, fin_ref, out_ref):
         def add(r, carry):
             at = pl.ds(pl.multiple_of(r * 16, 16), 16)
@@ -826,20 +932,21 @@
 
     o_args = (o_put, o_fin, of_s, of_r, 4)
     q_args = (q_put, q_fin, qf_s, qf_r, 5)
-    for b in range(2):
-        for k in range(1, n_d):
-            o_send(k, b).wait_recv()
-        second(b, o_rows, o_own, o_got, o_put, o_cut)
-        if b:
-            second_send(0, *o_args, False)
-    for b in range(2):
-        for k in range(1, n_d):
-            q_send(k, b).wait_recv()
-        second(b, q_rows, q_own, q_got, q_put, q_cut)
-        if b:
-            second_send(0, *q_args, False)
-        else:
-            second_send(1, *o_args, False)
+    if relay:
+        for n, (one, b) in enumerate(firsts):
+            one.middle(b)
+            if n:
+                last_one, last_b = firsts[n - 1]
+                last_one.middle_copy(last_b).start()
+    o_first.total(0)
+    if relay:
+        q_first.middle_copy(1).start()
+    o_first.total(1)
+    second_send(0, *o_args, False)
+    q_first.total(0)
+    second_send(1, *o_args, False)
+    q_first.total(1)
+    second_send(0, *q_args, False)
 
     def arrived(fin_ref, f_s, f_r):
         for zs in range(n_z):
@@ -878,9 +985,8 @@
     swap.wait_send()
     for b in range(2):
         row_send(b, True)
-        for k in range(1, n_d):
-            o_send(k, b).wait_send()
-            q_send(k, b).wait_send()
+        o_first.sent(b)
+        q_first.sent(b)
     for i in range(2):
         from_here = (cz == c) & (2 * c + i == z)
         at = ig.at[i]
@@ -907,12 +1013,14 @@
         scratch_shapes=[
             pltpu.VMEM((full // 2, width), b16), pltpu.VMEM((full // 2, width), b16),
             pltpu.VMEM((n_d - 1, 2 * q_rows, 2 * q_cols), b16), pltpu.VMEM((2 * q_rows, 2 * q_cols), b16),
+            pltpu.VMEM((2 * q_rows, 2 * q_cols), b16),
             pltpu.VMEM((2, 2, q_rows, q_cols), b16), pltpu.VMEM((n_z, q_rows, q_cols), b16),
             pltpu.VMEM((n_d - 1, 2 * o_rows, 2 * o_cols), b16), pltpu.VMEM((2 * o_rows, 2 * o_cols), b16),
+            pltpu.VMEM((2 * o_rows, 2 * o_cols), b16),
             pltpu.VMEM((2, 2, o_rows, o_cols), b16), pltpu.VMEM((n_z, o_rows, o_cols), b16),
             pltpu.VMEM((16, width), jnp.float32), pltpu.VMEM((total, 16, 128), jnp.float32),
             DMA, DMA, DMA((2,)), DMA((2,)), DMA((n_d - 1, 2)), DMA((n_d - 1, 2)), DMA((2, 2)), DMA((n_z,)),
-            DMA((n_d - 1, 2)), DMA((n_d - 1, 2)), DMA((2, 2)), DMA((n_z,)), DMA, DMA, DMA((6,)),
+            DMA((n_d - 1, 2)), DMA((n_d - 1, 2)), DMA((2, 2)), DMA((n_z,)), DMA, DMA, DMA((14,)),
         ],
         compiler_params=pltpu.CompilerParams(collective_id=5, has_side_effects=True, vmem_limit_bytes=56 * 1024 * 1024),
         cost_estimate=pl.CostEstimate(flops=0, bytes_accessed=300_000_000, transcendentals=0),
@@ -924,12 +1032,6 @@
     inverse = lax.rsqrt(jnp.mean(values * values, axis=-1, keepdims=True) + norm_eps)
     scaled = values * inverse
     return (scaled, inverse, (scaled * gain_wide).astype(jnp.bfloat16))
-
-
-def rms_backward(d_normed, scaled, inverse, gain_wide):
-    d_scaled = d_normed * gain_wide
-    d_values = inverse * (d_scaled - scaled * jnp.mean(d_scaled * scaled, axis=-1, keepdims=True))
-    return (d_values, jnp.sum(d_normed * scaled, axis=0))
 
 
 def adam_update(weight, grad, first, second):
@@ -955,7 +1057,7 @@
     )
 
 
-def per_device(
+def layer_step(
     block_input,
     segment_ids,
     cotangent,
@@ -992,24 +1094,32 @@
     gate_up_cols = lax.all_gather(
         gate_up_weight.astype(jnp.bfloat16).reshape(-1, 2 * unit_count), "dp", axis=0, tiled=True
     )
-    down_rows = lax.all_gather(down_weight.astype(jnp.bfloat16), "dp", axis=1, tiled=True)
-    cot_all = lax.all_gather(cotangent, "seq", axis=1, tiled=True)
-    rows_in, qkv_cols, gain_all, seg_all = gather_in(
-        block_input, qkv_weight.astype(jnp.bfloat16), gain_tile, seg_tile, n_dp, n_z
-    )
+    rows_in, qkv_cols, out_line, gain_all, seg_all = gather_in(
+        block_input,
+        qkv_weight.astype(jnp.bfloat16),
+        out_weight.astype(jnp.bfloat16).T,
+        gain_tile,
+        seg_tile,
+        n_dp,
+        n_z,
+    )
+    cot_late, down_late, _ = lax.optimization_barrier(
+        (cotangent, down_weight.astype(jnp.bfloat16), gain_all)
+    )
+    cot_all = lax.all_gather(cot_late, "seq", axis=1, tiled=True)
+    down_rows = lax.all_gather(down_late, "dp", axis=1, tiled=True)
     gain_one = gain_all[:, 0, :owned].reshape(1, width)
     gain_two = gain_all[:, 0, owned : 2 * owned].reshape(1, width)
     seg_here = lax.dynamic_slice(seg_all, (z_here // 2, z_here % 2, 0), (1, 1, full_len))[0]
     tables = attn_tables(seg_here)
-    scaled_one, inverse_one, normed_one = rms_forward(rows_in.astype(jnp.float32), gain_one)
+    _, _, normed_one = rms_forward(rows_in.astype(jnp.float32), gain_one)
     qkv = jnp.dot(normed_one, qkv_cols, preferred_element_type=jnp.float32)
-    turned, lse, attended16 = attn_forward(qkv, *tables, full_len, groups)
-    out_rows = gather_out(out_weight.astype(jnp.bfloat16).T, n_dp, n_z)
+    turned, lse, attended16, out_rows = attn_forward(qkv, *tables, out_line, full_len, groups, n_dp)
     attn_part = times_transpose(attended16, out_rows)
     resid_all = share_resid(attn_part.astype(jnp.bfloat16), rows_in, n_z)
     total_rows = seqs_here * full_len
     resid = resid_all.reshape(total_rows, width).astype(jnp.float32)
-    scaled_two, inverse_two, normed_two = rms_forward(resid, gain_two)
+    _, _, normed_two = rms_forward(resid, gain_two)
     gate_up = jnp.dot(normed_two, gate_up_cols, preferred_element_type=jnp.float32)
     gate_part = gate_up[:, :unit_count]
     up_part = gate_up[:, unit_count:]
@@ -1021,25 +1131,24 @@
     d_gate = d_hidden * up_part * sigmoid_gate * (1.0 + gate_part * (1.0 - sigmoid_gate))
     d_up = d_hidden * active
     d_gate_up16 = jnp.concatenate([d_gate, d_up], 1).astype(jnp.bfloat16)
-    down_term = contract_rows(cot_rows, hidden16)
-    down_sum = lax.psum_scatter(
-        down_term.astype(jnp.bfloat16), "dp", scatter_dimension=0, tiled=True
-    ).astype(jnp.float32)
-    grad_down = down_sum.T
-    d_normed_two = times_transpose(d_gate_up16, gate_up_cols).astype(jnp.bfloat16)
+    down_term = contract_rows(cot_rows, hidden16).astype(jnp.bfloat16)
+    d_gate_up_next, down_term = lax.optimization_barrier((d_gate_up16, down_term))
+    down_sum = lax.psum_scatter(down_term, "dp", scatter_dimension=0, tiled=True)
+    grad_down = down_sum.astype(jnp.float32).T
+    gate_up_term = contract_rows(normed_two, d_gate_up_next).astype(jnp.bfloat16)
+    d_gate_up_next, gate_up_term = lax.optimization_barrier((d_gate_up16, gate_up_term))
+    gate_up_sum = lax.psum_scatter(gate_up_term, "dp", scatter_dimension=0, tiled=True)
+    grad_gate_up = gate_up_sum.reshape(gate_up_weight.shape).astype(jnp.float32)
+    d_normed_two = times_transpose(d_gate_up_next, gate_up_cols).astype(jnp.bfloat16)
     d_resid16, gain_two_part = sum_line(
         d_normed_two.reshape(resid_all.shape), resid_all, cot_all, gain_two, n_z
     )
-    gate_up_term = contract_rows(normed_two, d_gate_up16)
-    grad_gate_up = (
-        lax.psum_scatter(gate_up_term.astype(jnp.bfloat16), "dp", scatter_dimension=0, tiled=True)
-        .reshape(gate_up_weight.shape)
-        .astype(jnp.float32)
-    )
-    down_part = jnp.dot(hidden16, down_rows, preferred_element_type=jnp.float32)
+    hidden_late, _ = lax.optimization_barrier((hidden16, d_resid16))
+    down_part = jnp.dot(hidden_late, down_rows, preferred_element_type=jnp.float32)
     down_here = lax.psum_scatter(
         down_part.astype(jnp.bfloat16).reshape(resid_all.shape), "seq", scatter_dimension=1, tiled=True
-    ).astype(jnp.float32)
+    )
+    down_here = down_here.astype(jnp.float32)
     resid_here = lax.dynamic_slice_in_dim(resid_all, z_here * local_len, local_len, 1)
     output = (resid_here.astype(jnp.float32) + down_here).astype(jnp.bfloat16)
     d_attended = jnp.dot(d_resid16, out_rows, preferred_element_type=jnp.float32).astype(jnp.bfloat16)
@@ -1144,6 +1253,4 @@
         P("dp", None, "seq"),
         P("seq", "dp"),
     )
-    return jax.shard_map(
-        per_device, mesh=mesh, in_specs=in_specs, out_specs=out_specs, check_vma=False
-    )
+    return jax.shard_map(layer_step, mesh=mesh, in_specs=in_specs, out_specs=out_specs, check_vma=False)

time: 892 us -> 869 us (0.974)
  Pallas kernels: 601 us -> 493 us
  waiting for transfers between devices: 28.9 us -> 98.8 us
  local copies, waits for them, and re-layouts: 18.2 us -> 36.7 us
    reduce_scatter x3, waiting for transfers between devices: 0.01 us -> 68.9 us  [the longest x1 68.9 us: layer_step(): lax.psum_scatter(gate_up_term, 'dp', scatter_dimension=0, tiled=True)]
    pallas_call x2 -> x1, Pallas kernels: 91.4 us -> 41.7 us  [attn_forward(): pl.pallas_call(functools.partial(attn_gather_kernel, n_dp, pairs, Q_ROWS,...]
    pallas_call x1, Pallas kernels: 204 us -> 157 us  [hand_out(): pl.pallas_call(functools.partial(hand_out_kernel, n_dp, n_z), in_specs=[V...]
    pallas_call x1, Pallas kernels: 62.2 us -> 80.4 us  [share_resid(): pl.pallas_call(functools.partial(share_resid_kernel, n_z), in_specs=[VMEM...]
    unnamed x72 -> x93, local copies, waits for them, and re-layouts: 6.05 us -> 24.2 us
    pallas_call x1, Pallas kernels: 110 us -> 93.4 us  [gather_in(): pl.pallas_call(functools.partial(gather_in_kernel, n_dp, n_z), in_specs=[...]
    pallas_call x1, Pallas kernels: 111 us -> 99.9 us  [sum_line(): pl.pallas_call(functools.partial(sum_line_kernel, n_z), in_specs=[VMEM_SP...]
  transfers between devices with their start and end apart: 6 -> 6, of which waited for: 1 -> 2; matrix products, arithmetic and copies ran while one was open for 18% -> 13% of each run, Pallas kernels for 68% -> 46%
where the time goes in v3:
time: 869 us; the launch traced here: 862 us
  Pallas kernels  493 us (57%)
  matrix products  160 us (18%)
  waiting for transfers between devices  98.8 us (11%)
  other arithmetic  59.2 us (7%)
  local copies, waits for them, and re-layouts  36.7 us (4%)
  between operations  14.8 us (2%)
    pallas_call x1, Pallas kernels, hand_out(): pl.pallas_call(functools.partial(hand_out_kernel, n_dp, n_z), in_specs=[V...  157 us
    pallas_call x1, Pallas kernels, sum_line(): pl.pallas_call(functools.partial(sum_line_kernel, n_z), in_specs=[VMEM_SP...  99.9 us
    pallas_call x1, Pallas kernels, gather_in(): pl.pallas_call(functools.partial(gather_in_kernel, n_dp, n_z), in_specs=[...  93.4 us
    pallas_call x1, Pallas kernels, share_resid(): pl.pallas_call(functools.partial(share_resid_kernel, n_z), in_specs=[VMEM...  80.4 us
    reduce_scatter x1, waiting for transfers between devices, layer_step(): lax.psum_scatter(gate_up_term, 'dp', scatter_dimension=0, tiled=True)  68.9 us
    dot_general x4, matrix products, times_transpose(): lax.dot_general(left, right, (((1,), (1,)), ((), ())), preferred_element_...  59.8 us
    dot_general x4, matrix products, contract_rows(): lax.dot_general(left, right, (((0,), (0,)), ((), ())), preferred_element_...  52.3 us
    pallas_call x1, Pallas kernels, attn_forward(): pl.pallas_call(functools.partial(attn_gather_kernel, n_dp, pairs, Q_ROWS,...  41.7 us
  transfers between devices with their start and end apart: 6, of which 2 were waited for; matrix products, arithmetic and copies ran while one was open for 13% of the time, Pallas kernels for 46%

profile of v3, /device:TPU:0, one launch (start us, length us, event | category | flops | bytes accessed | tf_op | source)
XLA Modules:
  0.0 862.3 jit_solution(16249404502758461722)
XLA Ops:
  7.2 4.2 convert_element_type.127
  11.5 2.2 copy.76
  13.8 0.8 copy.65
  14.6 0.8 convert_element_type.115.w_ref
  15.4 1.1 convert_element_type.129
  16.5 0.6 pad.12.s_ref
  17.1 0.7 fusion.17.g_ref
  17.8 93.4 %gather_in.1 = (bf16[512,2048]{1,0:T(8,128)(2,1)}, bf16[2048,1536]{1,0:T(8,128)(2,1)}, bf16[512,1024]{1,0:T(8,128)(2,1)}, f32[32,8,128]{2,1,0:T(8,128)}, s32[2,8,512]{2,1,0:T(8,128)}) custom-call(bf16[2,128,2048]{2,1,0:T(8,128)(2,1)} %x_ref.1, bf16[256,768]{1,0:T(8,128)(2,1)} %convert_element_type.115.w_ref, bf16[256,512]{1,0:T(8,128)(2,1)} %bitcast.72, ...), custom_call_target="tpu_custom_call" | custom-call | bytes 200000000 | tf_op jit(solution)/shard_map/gather_in/pallas_call | solution.py:482
  111.3 0.7 all-gather.8.cloned.1.call-update
  112.0 1.6 slice_reduce_fusion.1
  113.8 0.7 reshape_squeeze.6.gain_ref
  114.5 0.7 constant_dynamic-slice_fusion.1
  115.2 0.2 convert_reduce_fusion
  115.5 1.0 fusion.13
  116.5 1.0 maximum_bitcast_fusion.cos_ref
  117.5 1.0 maximum_bitcast_fusion.1.sin_ref
  118.4 0.5 fusion.3
  118.9 8.2 fusion.10.qkv_ref
  127.1 0.6 reshape.377.seg_row_ref
  127.7 0.8 reshape.376.seg_col_ref
  128.6 41.7 %attn_forward.1 = (bf16[512,1536]{1,0:T(8,128)(2,1)}, f32[512,512]{1,0:T(8,128)}, bf16[512,1024]{1,0:T(8,128)(2,1)}, bf16[2048,1024]{1,0:T(8,128)(2,1)}) custom-call(f32[512,1536]{1,0:T(8,128)} %fusion.10.qkv_ref, f32[512,128]{1,0:T(8,128)} %maximum_bitcast_fusion.cos_ref, f32[512,128]{1,0:T(8,128)} %maximum_bitcast_fusion.1.sin_ref, ...), custom_call_target="tpu_custom_call" | custom-call | flops 2147483648 | bytes 150000000 | tf_op jit(solution)/shard_map/attn_forward/pallas_call | solution.py:217
  170.3 6.3 convolution_convert_fusion.6.part_ref
  176.6 80.4 %share_resid.1.resid_all = bf16[2,512,2048]{2,1,0:T(8,128)(2,1)} custom-call(bf16[512,2048]{1,0:T(8,128)(2,1)} %convolution_convert_fusion.6.part_ref, bf16[512,2048]{1,0:T(8,128)(2,1)} %get-tuple-element.48.x_ref), custom_call_target="tpu_custom_call" | custom-call | bytes 200000000 | tf_op jit(solution)/shard_map/share_resid/pallas_call | solution.py:586
  257.0 3.2 multiply_reduce_fusion
  260.4 3.0 fusion.1
  263.5 23.8 %fusion.26 = f32[1024,4096]{1,0:T(8,128)} fusion(bf16[1024,2048]{1,0:T(8,128)(2,1)} %fusion.1, bf16[2048,4096]{1,0:T(8,128)(2,1)} %all-gather.4.cloned.1.call-done), kind=kOutput, calls=%fused_computation.76 | convolution fusion | flops 17179869184 | bytes 37748736 | tf_op jit(solution)/shard_map/dot_general | solution.py:1123
  287.3 28.1 %all-gather.8.cloned.1.call-done = bf16[2048,2048]{1,0:T(8,128)(2,1)} async-done(((bf16[2048,256]{1,0:T(8,128)(2,1)}), bf16[2048,2048]{1,0:T(8,128)(2,1)}) %all-gather.8.cloned.1.call-update) | async-done | bytes 8388624 | tf_op jit(solution)/shard_map/all_gather | solution.py:1110
  315.4 21.9 %multiply_convert_fusion.1 = (bf16[1024,2048]{1,0:T(8,128)(2,1)}, bf16[1024,2048]{1,0:T(8,128)(2,1)}, bf16[1024,2048]{1,0:T(8,128)(2,1)}) fusion(f32[1024,4096]{1,0:T(8,128)} %fusion.26, bf16[1024,2048]{1,0:T(8,128)(2,1)} %bitcast.69, bf16[2048,2048]{1,0:T(8,128)(2,1)} %all-gather.8.cloned.1.call-done), kind=kOutput, calls=%fused_computation.6 | convolution fusion | flops 8621391872 | bytes 41943040 | tf_op jit(solution)/shard_map/dot_general | solution.py:1055
  337.3 14.1 %convolution_convert_fusion.2 = bf16[2048,2048]{1,0:T(8,128)(2,1)} fusion(bf16[1024,2048]{1,0:T(8,128)(2,1)} %bitcast.70, bf16[1024,2048]{1,0:T(8,128)(2,1)} %get-tuple-element.60), kind=kOutput, calls=%fused_computation.12 | convolution fusion | flops 8594128896 | bytes 16777216 | tf_op jit(solution)/shard_map/dot_general | solution.py:1049
  351.4 7.8 pad_maximum_fusion
  359.2 25.0 %convolution_convert_fusion = bf16[2048,4096]{1,0:T(8,128)(2,1)} fusion(bf16[1024,2048]{1,0:T(8,128)(2,1)} %fusion.1, bf16[1024,4096]{1,0:T(8,128)(2,1)} %pad_maximum_fusion), kind=kOutput, calls=%fused_computation | convolution fusion | flops 17188257792 | bytes 29360128 | tf_op jit(solution)/shard_map/dot_general | solution.py:1049
  384.2 24.2 %convolution_convert_fusion.3 = bf16[1024,2048]{1,0:T(8,128)(2,1)} fusion(bf16[1024,4096]{1,0:T(8,128)(2,1)} %pad_maximum_fusion, bf16[2048,4096]{1,0:T(8,128)(2,1)} %all-gather.4.cloned.1.call-done), kind=kOutput, calls=%fused_computation.22 | convolution fusion | flops 17181966336 | bytes 29360128 | tf_op jit(solution)/shard_map/dot_general | solution.py:1055
  408.3 99.9 %sum_line.1 = (bf16[512,2048]{1,0:T(8,128)(2,1)}, f32[8,2048]{1,0:T(8,128)}) custom-call(bf16[2,512,2048]{2,1,0:T(8,128)(2,1)} %bitcast.71, bf16[2,512,2048]{2,1,0:T(8,128)(2,1)} %share_resid.1.resid_all, bf16[2,512,2048]{2,1,0:T(8,128)(2,1)} %all-gather.6.cloned.1.call-done.cot_all, f32[1,2048]{1,0:T(1,128)} %reshape_squeeze.6.gain_ref), custom_call_target="tpu_custom_call" | custom-call | bytes 200000000 | tf_op jit(solution)/shard_map/sum_line/pallas_call | solution.py:742
  508.3 12.5 %convolution_convert_fusion.5 = bf16[1024,2048]{1,0:T(8,128)(2,1)} fusion(bf16[1024,2048]{1,0:T(8,128)(2,1)S(1)} %copy-done.39, bf16[2048,2048]{1,0:T(8,128)(2,1)} %all-gather.8.cloned.1.call-done), kind=kOutput, calls=%fused_computation.24 | convolution fusion | flops 8592031744 | bytes 16777216 | tf_op jit(solution)/shard_map/dot_general | solution.py:1147
  520.9 0.5 reduce-scatter.8.cloned.1.call-update
  521.5 0.5 reduce-scatter.6.cloned.1.call-update
  522.0 1.0 copy-done.4
  523.0 2.0 copy.70
  525.0 3.6 copy.67
  528.6 1.8 copy.68
  530.4 0.7 reshape_squeeze.7.gain_ref
  531.1 6.1 convolution_convert_fusion.4.ot_ref
  537.2 3.3 convolution_convert_fusion.8.d_out_ref
  540.5 20.5 %attn_backward.1 = bf16[512,1536]{1,0:T(8,128)(2,1)} custom-call(bf16[512,1536]{1,0:T(8,128)(2,1)} %get-tuple-element.61.turned_ref, bf16[512,1024]{1,0:T(8,128)(2,1)} %convolution_convert_fusion.8.d_out_ref, f32[512,512]{1,0:T(8,128)} %get-tuple-element.62.lse_ref, f32[512,128]{1,0:T(8,128)} %maximum_bitcast_fusion.cos_ref, ...), custom_call_target="tpu_custom_call" | custom-call | flops 5368709120 | bytes 4718592 | tf_op jit(solution)/shard_map/attn_backward/pallas_call | solution.py:243
  561.0 7.1 convolution_convert_fusion.1.qt_ref
  568.1 7.5 convolution_convert_fusion.7.dn_ref
  575.7 156.7 %hand_out.1 = (bf16[2,128,2048]{2,1,0:T(8,128)(2,1)}, f32[256,768]{1,0:T(8,128)}, f32[512,256]{1,0:T(8,128)}, f32[16,128]{1,0:T(8,128)}) custom-call(bf16[512,2048]{1,0:T(8,128)(2,1)} %convolution_convert_fusion.7.dn_ref, bf16[512,2048]{1,0:T(8,128)(2,1)} %get-tuple-element.48.x_ref, bf16[512,2048]{1,0:T(8,128)(2,1)} %get-tuple-element.59.dr_ref, ...), custom_call_target="tpu_custom_call" | custom-call | bytes 300000000 | tf_op jit(solution)/shard_map/hand_out/pallas_call | solution.py:1003
  732.5 0.9 bitcast_reduce_fusion
  733.5 0.6 multiply_subtract_fusion.4
  734.0 2.6 multiply_subtract_fusion.3
  736.6 1.9 multiply_subtract_fusion.2
  738.5 3.0 add_convert_fusion
  741.5 6.5 multiply_subtract_fusion.1
  748.0 3.0 copy.72
  751.0 0.2 convert_bitcast_fusion
  751.2 1.8 copy.71
  753.1 3.2 copy.73
  756.2 1.8 copy.74
  758.1 68.9 %reduce-scatter.6.cloned.1.call-done = bf16[256,4096]{1,0:T(8,128)(2,1)} async-done(((bf16[2048,4096]{1,0:T(8,128)(2,1)}), bf16[256,4096]{1,0:T(8,128)(2,1)}) %reduce-scatter.6.cloned.1.call-update) | async-done | bytes 2097168 | tf_op jit(solution)/shard_map/reduce_scatter | solution.py:1140
  826.9 6.6 reshape.384
  833.5 19.1 %multiply_subtract_fusion = (f32[256,2,2048]{2,1,0:T(2,128)}, f32[256,2,2048]{2,1,0:T(2,128)}, f32[256,2,2048]{2,1,0:T(2,128)}) fusion(f32[256,2,2048]{2,1,0:T(2,128)} %param.28, f32[256,2,2048]{2,1,0:T(2,128)} %reshape.384, f32[256,2,2048]{2,1,0:T(2,128)} %param.34, f32[256,2,2048]{2,1,0:T(2,128)} %param.40), kind=kLoop, calls=%fused_computation.20 | loop fusion | flops 15728640 | bytes 29360128 | tf_op jit(solution)/shard_map/sub | solution.py:1042
  852.6 1.0 copy.80
  853.5 0.9 copy.81
  854.4 0.8 copy.82
  (101 shorter events, 0.9 us)
Async XLA Ops:
  7.2 256.3 %all-gather.4.cloned.1.call-start = ((), (), s32[]{:S(2)}) async-start(), calls=%async_computation.3 | async-start | bytes 18874368 | tf_op jit(solution)/shard_map/all_gather | solution.py:1094
  11.4 2.3 copy-start.12
  11.5 3.2 copy-start.8
  11.5 4.0 copy-start.3
  13.7 2.8 copy-start.25
  13.7 3.4 copy-start.28
  13.7 3.4 copy-start.30
  13.7 273.6 %all-gather.6.cloned.1.call-start = ((), (), s32[]{:S(2)}) async-start(), calls=%async_computation.4 | async-start | bytes 5242880 | tf_op jit(solution)/shard_map/all_gather | solution.py:1109
  111.2 7.3 copy-start.1
  111.2 204.2 %all-gather.8.cloned.1.call-start = ((), (), s32[]{:S(2)}) async-start(), calls=%async_computation.5 | async-start | bytes 9437184 | tf_op jit(solution)/shard_map/all_gather | solution.py:1110
  111.9 626.6 %reduce-scatter.4.cloned.1.call-start = ((), (), s32[]{:S(2)}) async-start(), calls=%async_computation.6 | async-start | bytes 5242880 | tf_op jit(solution)/shard_map/reduce_scatter | solution.py:1148
  113.7 13.4 %copy-start.23 = (f32[2048]{0:T(1024)}, f32[2048]{0:T(1024)S(1)}, u32[]{:S(2)}) copy-start(f32[2048]{0:T(1024)S(1)} %mul.282) | copy-start | bytes 24580
  118.9 8.2 copy-start.26
  257.0 3.5 copy-start
  408.3 99.9 %copy-start.39 = (bf16[1024,2048]{1,0:T(8,128)(2,1)S(1)}, bf16[1024,2048]{1,0:T(8,128)(2,1)}, u32[]{:S(2)}) copy-start(bf16[1024,2048]{1,0:T(8,128)(2,1)} %get-tuple-element.60) | copy-start | bytes 12582916
  520.8 220.7 %reduce-scatter.8.cloned.1.call-start = ((), (), s32[]{:S(2)}) async-start(), calls=%async_computation.8 | async-start | bytes 9437184 | tf_op jit(solution)/shard_map/reduce_scatter | solution.py:1136
  521.4 1.6 copy-start.4
  521.4 305.5 %reduce-scatter.6.cloned.1.call-start = ((), (), s32[]{:S(2)}) async-start(), calls=%async_computation.7 | async-start | bytes 18874368 | tf_op jit(solution)/shard_map/reduce_scatter | solution.py:1140
  525.0 3.6 copy-start.15
  525.0 5.4 copy-start.22
  525.0 6.1 copy-start.37
  531.0 6.1 copy-start.16
  531.1 6.1 copy-start.36
  540.5 20.5 %copy-start.2 = (bf16[512,2048]{1,0:T(8,128)(2,1)S(1)}, bf16[512,2048]{1,0:T(8,128)(2,1)}, u32[]{:S(2)}) copy-start(bf16[512,2048]{1,0:T(8,128)(2,1)} %get-tuple-element.48.x_ref) | copy-start | bytes 6291460
  540.5 20.5 %copy-start.24 = (f32[2048]{0:T(1024)S(1)}, f32[2048]{0:T(1024)}, u32[]{:S(2)}) copy-start(f32[2048]{0:T(1024)} %copy-done.23) | copy-start | bytes 24580
  540.5 20.5 %copy-start.27 = (f32[512]{0:T(512)S(1)}, f32[512]{0:T(512)}, u32[]{:S(2)}) copy-start(f32[512]{0:T(512)} %copy-done.26) | copy-start | bytes 6148
  561.0 7.1 copy-start.38
  575.6 157.8 %copy-start.29 = (f32[64]{0:T(128)S(1)}, f32[64]{0:T(128)}, u32[]{:S(2)}) copy-start(f32[64]{0:T(128)} %param.27) | copy-start | bytes 772
  575.6 157.8 %copy-start.31 = (f32[64]{0:T(128)S(1)}, f32[64]{0:T(128)}, u32[]{:S(2)}) copy-start(f32[64]{0:T(128)} %param.24) | copy-start | bytes 772
  575.6 157.8 %copy-start.32 = (f32[64]{0:T(128)S(1)}, f32[64]{0:T(128)}, u32[]{:S(2)}) copy-start(f32[64]{0:T(128)} %param.33) | copy-start | bytes 772
  575.6 157.8 %copy-start.33 = (f32[64]{0:T(128)S(1)}, f32[64]{0:T(128)}, u32[]{:S(2)}) copy-start(f32[64]{0:T(128)} %param.39) | copy-start | bytes 772
  575.6 157.8 %copy-start.34 = (f32[64]{0:T(128)S(1)}, f32[64]{0:T(128)}, u32[]{:S(2)}) copy-start(f32[64]{0:T(128)} %param.36) | copy-start | bytes 772
  575.7 157.8 %copy-start.35 = (f32[64]{0:T(128)S(1)}, f32[64]{0:T(128)}, u32[]{:S(2)}) copy-start(f32[64]{0:T(128)} %param.30) | copy-start | bytes 772
  575.7 158.3 %copy-start.13 = (f32[512,256]{1,0:T(8,128)S(1)}, f32[512,256]{1,0:T(8,128)}, u32[]{:S(2)}) copy-start(f32[512,256]{1,0:T(8,128)} %param.26) | copy-start | bytes 1572868
  575.7 158.3 %copy-start.20 = (f32[512,256]{1,0:T(8,128)S(1)}, f32[512,256]{1,0:T(8,128)}, u32[]{:S(2)}) copy-start(f32[512,256]{1,0:T(8,128)} %param.32) | copy-start | bytes 1572868
  575.7 158.3 %copy-start.21 = (f32[512,256]{1,0:T(8,128)S(1)}, f32[512,256]{1,0:T(8,128)}, u32[]{:S(2)}) copy-start(f32[512,256]{1,0:T(8,128)} %param.38) | copy-start | bytes 1572868
  732.4 4.2 copy-start.9
  732.4 4.2 copy-start.10
  732.5 4.2 copy-start.18
  732.5 4.1 copy-start.19
  736.6 4.9 copy-start.5
  748.0 3.0 copy-start.7
  753.1 3.2 copy-start.6
  833.5 19.1 %copy-start.17 = (bf16[2,128,2048]{2,1,0:T(8,128)(2,1)S(1)}, bf16[2,128,2048]{2,1,0:T(8,128)(2,1)}, u32[]{:S(2)}) copy-start(bf16[2,128,2048]{2,1,0:T(8,128)(2,1)} %get-tuple-element.211) | copy-start | bytes 3145732
  833.5 20.1 %copy-start.11 = (f32[256,768]{1,0:T(8,128)S(1)}, f32[256,768]{1,0:T(8,128)}, u32[]{:S(2)}) copy-start(f32[256,768]{1,0:T(8,128)} %get-tuple-element.213) | copy-start | bytes 2359300
  833.5 20.9 %copy-start.14 = (f32[512,256]{1,0:T(8,128)S(1)}, f32[512,256]{1,0:T(8,128)}, u32[]{:S(2)}) copy-start(f32[512,256]{1,0:T(8,128)} %get-tuple-element.214) | copy-start | bytes 1572868
Sparse Core Ops, SparseCore 0:
  13.9 142.5 all-gather.3
  158.0 96.6 all-gather.5
  257.1 58.2 all-gather.7
  520.9 89.9 reduce-scatter.3
  614.2 93.0 reduce-scatter.7
  710.7 116.1 reduce-scatter.5

commit v4 on v3

--- a/solution.py
+++ b/solution.py
@@ -344,6 +344,26 @@
             self.copy(1, self.pair ^ 2, t, 1, 2).wait_recv()
             self.copy(2, self.pair ^ 2, t, 1, 1).start()
 
+    def rest(self, t):
+        if self.n_d == 4:
+            self.copy(0, self.pair ^ 1, t, 1, 1).wait_recv()
+            self.copy(1, self.pair ^ 2, t, 0, 2).wait_recv()
+        else:
+            for k in range(1, self.n_d):
+                for h in range(2):
+                    self.copy(k - 1, self.pair ^ k, t, h, k).wait_recv()
+
+    def far(self, t):
+        if self.n_d == 4:
+            for h in range(2):
+                self.copy(2, self.pair ^ 3, t, h, 1).wait_recv()
+
+    def sent(self):
+        for t in range(self.parts):
+            for h in range(2):
+                for slot in range(self.n_d - 1):
+                    self.copy(slot, self.pair, t, h, 1).wait_send()
+
     def finish(self):
         for t in range(self.parts):
             if self.n_d == 4:
@@ -500,17 +520,38 @@
     )(x_loc, w, v, gain_tile, seg_tile)
 
 
-def share_resid_kernel(n_z, part_ref, x_ref, out, got, buf, p_s, p_r, u_s, u_r, loc):
+def share_resid_kernel(n_dp, n_z, part_ref, x_ref, w_ref, out, wall, got, buf, p_s, p_r, u_s, u_r, d_s, d_r, c_s, c_r, loc):
     d, z, pair, c = place()
+    n_d = n_dp // 2
     cz = z // 2
     full = x_ref.shape[0]
     half = full // 2
     unit = half // 2
-    greet_line(n_z, d, z)
+    w_rows = w_ref.shape[0]
+    parts = 4
+    piece = w_rows // parts
+    own_copy = pltpu.make_async_copy(w_ref, wall.at[pl.ds(pl.multiple_of(d * w_rows, w_rows), w_rows)], loc.at[2])
+    own_copy.start()
+    greet_line(n_z, d, z, [(2 * (pair ^ k) + c, z) for k in range(1, n_d)])
     mine = pl.ds(pl.multiple_of(c * half, half), half)
     theirs = pl.ds(pl.multiple_of((1 - c) * half, half), half)
     swap = remote(part_ref.at[theirs], got, p_s, p_r, (2 * pair + 1 - c, z))
     swap.start()
+
+    def spot_w(owner, t, h):
+        sub = piece // 2
+        return wall.at[pl.ds(pl.multiple_of((2 * owner + c) * w_rows + (2 * t + h) * sub, sub), sub)]
+
+    def across(k, t, core):
+        at = wall.at[pl.ds(pl.multiple_of((2 * (pair ^ k) + core) * w_rows + t * piece, piece), piece)]
+        return remote(at, at, c_s.at[k, t], c_r.at[k, t], (2 * pair + 1 - c, z))
+
+    spread = Spread(n_d, pair, c, z, parts, spot_w, d_s, d_r)
+    own_copy.wait()
+    for t in range(parts):
+        spread.own(t)
+        across(0, t, c).start()
+
     swap.wait_recv()
 
     def add(r, carry):
@@ -526,7 +567,7 @@
     def sends(k, wait):
         src = buf.at[pl.ds(k * unit, unit)]
         dst = spot(z % 2, c, k)
-        for o, zz in ((0, z), (1, z - 1), (2, z + 1)):
+        for o, zz in ((1, z - 1), (2, z + 1), (0, z)):
             copy = remote(src, dst, u_s.at[o, k], u_r.at[z % 2, c, k], (2 * pair + cz, zz))
             act = copy.wait_send if wait else copy.start
             if o == 0:
@@ -546,28 +587,49 @@
     swap.wait_send()
     sends(1, False)
 
-    def relay(dist, sign, jl_wait):
+    def relay(dist, sign, k, h, begin):
         j = z + sign * dist
         ok = (j >= 2 * c) & (j <= 2 * c + 1)
         to = z - sign
         more = (to >= 0) & (to <= n_z - 1)
         jl = lax.rem(j + n_z, 2)
-
-        @pl.when(ok)
-        def _():
-            for k in range(2):
-                for h in range(2):
-                    at = spot(jl, h, k)
-                    copy = remote(at, at, u_s.at[3 + (0 if sign < 0 else 1), 4 * jl + 2 * h + k], u_r.at[jl, h, k], (2 * pair + c, to))
-                    if jl_wait:
-                        copy.wait_recv()
-                        pl.when(more)(copy.start)
-                    else:
-                        pl.when(more)(copy.wait_send)
-
-    order = [(dist, sign) for dist in range(1, n_z) for sign in (-1, 1)]
-    for dist, sign in order:
-        relay(dist, sign, True)
+        at = spot(jl, h, k)
+        copy = remote(at, at, u_s.at[3 + (0 if sign < 0 else 1), 4 * jl + 2 * h + k], u_r.at[jl, h, k], (2 * pair + c, to))
+        if begin:
+
+            @pl.when(ok)
+            def _():
+                copy.wait_recv()
+                pl.when(more)(copy.start)
+        else:
+            pl.when(ok & more)(copy.wait_send)
+
+    def take(t):
+        spread.pass_on(t)
+
+    def rest(t):
+        spread.rest(t)
+        for k in range(1, n_d):
+            if n_d != 4 or k != 3:
+                across(k, t, c).start()
+
+    def far(t):
+        if n_d == 4:
+            spread.far(t)
+            across(3, t, c).start()
+
+    links = []
+    for t in range(parts):
+        links += [(take, t), (rest, t)]
+    links += [(far, t) for t in range(parts)]
+    line = [(dist, k, h) for dist in range(1, n_z) for k in range(2) for h in range(2)]
+    for n in range(max(len(links), len(line))):
+        if n < len(line):
+            dist, k, h = line[n]
+            for sign in (-1, 1):
+                relay(dist, sign, k, h, True)
+        if n < len(links):
+            links[n][0](links[n][1])
 
     @pl.when(c == cz)
     def _():
@@ -575,27 +637,38 @@
             at = spot(z % 2, 1 - c, k)
             remote(at, at, u_s.at[0, 0], u_r.at[z % 2, 1 - c, k], (d, z)).wait_recv()
 
-    for dist, sign in order:
-        relay(dist, sign, False)
+    for dist, k, h in line:
+        for sign in (-1, 1):
+            relay(dist, sign, k, h, False)
     sends(0, True)
     sends(1, True)
-
-
-def share_resid(part, x, n_z):
+    spread.sent()
+    for k in range(n_d):
+        for t in range(parts):
+            across(k, t, c).wait_send()
+            across(k, t, 1 - c).wait_recv()
+
+
+def share_resid(part, x, w, n_dp, n_z):
     full, width = x.shape
+    n_d = n_dp // 2
     return pl.pallas_call(
-        functools.partial(share_resid_kernel, n_z),
-        in_specs=[VMEM_SPEC] * 2,
-        out_specs=ANY_SPEC,
-        out_shape=jax.ShapeDtypeStruct((2, full, width), jnp.bfloat16),
+        functools.partial(share_resid_kernel, n_dp, n_z),
+        in_specs=[VMEM_SPEC] * 3,
+        out_specs=[ANY_SPEC] * 2,
+        out_shape=[
+            jax.ShapeDtypeStruct((2, full, width), jnp.bfloat16),
+            jax.ShapeDtypeStruct((n_dp * w.shape[0], w.shape[1]), jnp.bfloat16),
+        ],
         scratch_shapes=[
             pltpu.VMEM((full // 2, width), jnp.bfloat16), pltpu.VMEM((full // 2, width), jnp.bfloat16),
-            DMA, DMA, DMA((5, 8)), DMA((2, 2, 2)), DMA((2,)),
+            DMA, DMA, DMA((5, 8)), DMA((2, 2, 2)), DMA((n_d - 1, 4, 2)), DMA((n_d - 1, 4, 2)), DMA((n_d, 4)), DMA((n_d, 4)),
+            DMA((3,)),
         ],
         compiler_params=pltpu.CompilerParams(collective_id=2, has_side_effects=True),
         cost_estimate=pl.CostEstimate(flops=0, bytes_accessed=200_000_000, transcendentals=0),
         name="share_resid",
-    )(part, x)
+    )(part, x, w)
 
 
 CHUNKS = 8
@@ -1091,9 +1164,8 @@
     gain_line = jnp.concatenate([attn_gain, mlp_gain]).astype(jnp.bfloat16).astype(jnp.float32)
     gain_tile = jnp.pad(gain_line[None], ((0, 7), (0, LANES - 2 * owned)))
     seg_tile = jnp.pad(segment_ids, ((0, 8 - seqs_here), (0, 0)))
-    gate_up_cols = lax.all_gather(
-        gate_up_weight.astype(jnp.bfloat16).reshape(-1, 2 * unit_count), "dp", axis=0, tiled=True
-    )
+    gate_up_here = gate_up_weight.astype(jnp.bfloat16).reshape(-1, 2 * unit_count)
+    down_rows = lax.all_gather(down_weight.astype(jnp.bfloat16), "dp", axis=1, tiled=True)
     rows_in, qkv_cols, out_line, gain_all, seg_all = gather_in(
         block_input,
         qkv_weight.astype(jnp.bfloat16),
@@ -1103,11 +1175,8 @@
         n_dp,
         n_z,
     )
-    cot_late, down_late, _ = lax.optimization_barrier(
-        (cotangent, down_weight.astype(jnp.bfloat16), gain_all)
-    )
+    cot_late, _ = lax.optimization_barrier((cotangent, gain_all))
     cot_all = lax.all_gather(cot_late, "seq", axis=1, tiled=True)
-    down_rows = lax.all_gather(down_late, "dp", axis=1, tiled=True)
     gain_one = gain_all[:, 0, :owned].reshape(1, width)
     gain_two = gain_all[:, 0, owned : 2 * owned].reshape(1, width)
     seg_here = lax.dynamic_slice(seg_all, (z_here // 2, z_here % 2, 0), (1, 1, full_len))[0]
@@ -1116,7 +1185,9 @@
     qkv = jnp.dot(normed_one, qkv_cols, preferred_element_type=jnp.float32)
     turned, lse, attended16, out_rows = attn_forward(qkv, *tables, out_line, full_len, groups, n_dp)
     attn_part = times_transpose(attended16, out_rows)
-    resid_all = share_resid(attn_part.astype(jnp.bfloat16), rows_in, n_z)
+    resid_all, gate_up_cols = share_resid(
+        attn_part.astype(jnp.bfloat16), rows_in, gate_up_here, n_dp, n_z
+    )
     total_rows = seqs_here * full_len
     resid = resid_all.reshape(total_rows, width).astype(jnp.float32)
     _, _, normed_two = rms_forward(resid, gain_two)
@@ -1131,22 +1202,19 @@
     d_gate = d_hidden * up_part * sigmoid_gate * (1.0 + gate_part * (1.0 - sigmoid_gate))
     d_up = d_hidden * active
     d_gate_up16 = jnp.concatenate([d_gate, d_up], 1).astype(jnp.bfloat16)
+    down_part = jnp.dot(hidden16, down_rows, preferred_element_type=jnp.float32)
+    down_here = lax.psum_scatter(
+        down_part.astype(jnp.bfloat16).reshape(resid_all.shape), "seq", scatter_dimension=1, tiled=True
+    )
+    gate_up_term = contract_rows(normed_two, d_gate_up16).astype(jnp.bfloat16)
+    gate_up_sum = lax.psum_scatter(gate_up_term, "dp", scatter_dimension=0, tiled=True)
+    grad_gate_up = gate_up_sum.reshape(gate_up_weight.shape).astype(jnp.float32)
     down_term = contract_rows(cot_rows, hidden16).astype(jnp.bfloat16)
-    d_gate_up_next, down_term = lax.optimization_barrier((d_gate_up16, down_term))
     down_sum = lax.psum_scatter(down_term, "dp", scatter_dimension=0, tiled=True)
     grad_down = down_sum.astype(jnp.float32).T
-    gate_up_term = contract_rows(normed_two, d_gate_up_next).astype(jnp.bfloat16)
-    d_gate_up_next, gate_up_term = lax.optimization_barrier((d_gate_up16, gate_up_term))
-    gate_up_sum = lax.psum_scatter(gate_up_term, "dp", scatter_dimension=0, tiled=True)
-    grad_gate_up = gate_up_sum.reshape(gate_up_weight.shape).astype(jnp.float32)
-    d_normed_two = times_transpose(d_gate_up_next, gate_up_cols).astype(jnp.bfloat16)
+    d_normed_two = times_transpose(d_gate_up16, gate_up_cols).astype(jnp.bfloat16)
     d_resid16, gain_two_part = sum_line(
         d_normed_two.reshape(resid_all.shape), resid_all, cot_all, gain_two, n_z
-    )
-    hidden_late, _ = lax.optimization_barrier((hidden16, d_resid16))
-    down_part = jnp.dot(hidden_late, down_rows, preferred_element_type=jnp.float32)
-    down_here = lax.psum_scatter(
-        down_part.astype(jnp.bfloat16).reshape(resid_all.shape), "seq", scatter_dimension=1, tiled=True
     )
     down_here = down_here.astype(jnp.float32)
     resid_here = lax.dynamic_slice_in_dim(resid_all, z_here * local_len, local_len, 1)

time: 869 us -> 815 us (0.938)
  the two profiles are of different devices: /device:TPU:0 before, /device:TPU:9 now
where the time goes in v4:
time: 815 us; the launch traced here: 808 us
  Pallas kernels  540 us (66%)
  matrix products  161 us (20%)
  other arithmetic  52.4 us (6%)
  local copies, waits for them, and re-layouts  39.9 us (5%)
  between operations  14.4 us (2%)
    pallas_call x1, Pallas kernels, hand_out(): pl.pallas_call(functools.partial(hand_out_kernel, n_dp, n_z), in_specs=[V...  194 us
    pallas_call x1, Pallas kernels, share_resid(): pl.pallas_call(functools.partial(share_resid_kernel, n_dp, n_z), in_specs...  111 us
    pallas_call x1, Pallas kernels, gather_in(): pl.pallas_call(functools.partial(gather_in_kernel, n_dp, n_z), in_specs=[...  91.9 us
    pallas_call x1, Pallas kernels, sum_line(): pl.pallas_call(functools.partial(sum_line_kernel, n_z), in_specs=[VMEM_SP...  84.1 us
    dot_general x4, matrix products, times_transpose(): lax.dot_general(left, right, (((1,), (1,)), ((), ())), preferred_element_...  60.1 us
    dot_general x4, matrix products, contract_rows(): lax.dot_general(left, right, (((0,), (0,)), ((), ())), preferred_element_...  53.1 us
    pallas_call x1, Pallas kernels, attn_forward(): pl.pallas_call(functools.partial(attn_gather_kernel, n_dp, pairs, Q_ROWS,...  37.4 us
    sub x5, other arithmetic, adam_update(): weight - learn_rate * (first_hat / (jnp.sqrt(second_hat) + adam_eps) + we...  30.3 us
  transfers between devices with their start and end apart: 5, of which 0 were waited for; matrix products, arithmetic and copies ran while one was open for 22% of the time, Pallas kernels for 55%

profile of v4, /device:TPU:9, one launch (start us, length us, event | category | flops | bytes accessed | tf_op | source)
XLA Modules:
  0.0 807.6 jit_solution(14221750468228630275)
XLA Ops:
  7.3 2.1 convert_element_type.115.w_ref
  9.3 1.9 copy.65
  11.2 0.7 convert_bitcast_fusion.2
  11.9 0.7 fusion.19.g_ref
  12.5 1.3 pad.12.s_ref
  13.8 91.9 %gather_in.1 = (bf16[512,2048]{1,0:T(8,128)(2,1)}, bf16[2048,1536]{1,0:T(8,128)(2,1)}, bf16[512,1024]{1,0:T(8,128)(2,1)}, f32[32,8,128]{2,1,0:T(8,128)}, s32[2,8,512]{2,1,0:T(8,128)}) custom-call(bf16[2,128,2048]{2,1,0:T(8,128)(2,1)} %x_ref.1, bf16[256,768]{1,0:T(8,128)(2,1)} %convert_element_type.115.w_ref, bf16[256,512]{1,0:T(8,128)(2,1)} %bitcast.70, ...), custom_call_target="tpu_custom_call" | custom-call | bytes 200000000 | tf_op jit(solution)/shard_map/gather_in/pallas_call | solution.py:502
  105.8 1.1 convert_element_type.129
  107.0 1.7 slice_reduce_fusion.1
  108.7 0.1 mul.292
  108.7 0.1 mul.282
  108.8 4.3 convert_element_type.122
  113.2 2.2 copy.75
  115.4 0.7 constant_dynamic-slice_fusion.1
  116.1 0.2 convert_reduce_fusion
  116.4 1.0 fusion.15
  117.4 1.0 maximum_bitcast_fusion.cos_ref
  118.4 1.0 maximum_bitcast_fusion.1.sin_ref
  119.3 0.5 fusion.4
  119.9 7.9 fusion.12.qkv_ref
  127.8 0.8 reshape.376.seg_col_ref
  128.6 0.6 reshape.377.seg_row_ref
  129.2 37.4 %attn_forward.1 = (bf16[512,1536]{1,0:T(8,128)(2,1)}, f32[512,512]{1,0:T(8,128)}, bf16[512,1024]{1,0:T(8,128)(2,1)}, bf16[2048,1024]{1,0:T(8,128)(2,1)}) custom-call(f32[512,1536]{1,0:T(8,128)} %fusion.12.qkv_ref, f32[512,128]{1,0:T(8,128)} %maximum_bitcast_fusion.cos_ref, f32[512,128]{1,0:T(8,128)} %maximum_bitcast_fusion.1.sin_ref, ...), custom_call_target="tpu_custom_call" | custom-call | flops 2147483648 | bytes 150000000 | tf_op jit(solution)/shard_map/attn_forward/pallas_call | solution.py:217
  166.7 6.2 convolution_convert_fusion.5.part_ref
  172.9 111.2 %share_resid.1 = (bf16[2,512,2048]{2,1,0:T(8,128)(2,1)}, bf16[2048,4096]{1,0:T(8,128)(2,1)}) custom-call(bf16[512,2048]{1,0:T(8,128)(2,1)} %convolution_convert_fusion.5.part_ref, bf16[512,2048]{1,0:T(8,128)(2,1)} %get-tuple-element.44.x_ref, bf16[256,4096]{1,0:T(8,128)(2,1)} %bitcast.64), custom_call_target="tpu_custom_call" | custom-call | bytes 200000000 | tf_op jit(solution)/shard_map/share_resid/pallas_call | solution.py:655
  284.1 3.2 multiply_reduce_fusion
  287.3 0.2 copy-done
  287.5 1.0 fusion.1
  288.6 2.1 copy-done.5
  290.6 22.3 %fusion.30 = f32[1024,4096]{1,0:T(8,128)} fusion(bf16[1024,2048]{1,0:T(8,128)(2,1)S(1)} %fusion.1, bf16[2048,4096]{1,0:T(8,128)(2,1)} %get-tuple-element.52), kind=kOutput, calls=%fused_computation.79 | convolution fusion | flops 17179869184 | bytes 37748736 | tf_op jit(solution)/shard_map/dot_general | solution.py:1194
  312.9 21.9 %multiply_convert_fusion.1 = (bf16[1024,2048]{1,0:T(8,128)(2,1)}, bf16[1024,2048]{1,0:T(8,128)(2,1)}, bf16[1024,2048]{1,0:T(8,128)(2,1)}) fusion(f32[1024,4096]{1,0:T(8,128)} %fusion.30, bf16[1024,2048]{1,0:T(8,128)(2,1)} %bitcast.67, bf16[2048,2048]{1,0:T(8,128)(2,1)} %all-gather.3.cloned.1.call-done), kind=kOutput, calls=%fused_computation.6 | convolution fusion | flops 8621391872 | bytes 41943040 | tf_op jit(solution)/shard_map/dot_general | solution.py:1128
  334.8 13.8 %convolution_convert_fusion.4 = bf16[1024,2048]{1,0:T(8,128)(2,1)} fusion(bf16[1024,2048]{1,0:T(8,128)(2,1)} %get-tuple-element.164, bf16[2048,2048]{1,0:T(8,128)(2,1)} %all-gather.3.cloned.1.call-done), kind=kOutput, calls=%fused_computation.25 | convolution fusion | flops 8592031744 | bytes 16777216 | tf_op jit(solution)/shard_map/dot_general | solution.py:1205
  348.7 14.1 %convolution_convert_fusion.1 = bf16[2048,2048]{1,0:T(8,128)(2,1)} fusion(bf16[1024,2048]{1,0:T(8,128)(2,1)} %bitcast.68, bf16[1024,2048]{1,0:T(8,128)(2,1)} %get-tuple-element.164), kind=kOutput, calls=%fused_computation.11 | convolution fusion | flops 8594128896 | bytes 16777216 | tf_op jit(solution)/shard_map/dot_general | solution.py:1122
  362.9 25.4 %convolution_convert_fusion = bf16[2048,4096]{1,0:T(8,128)(2,1)} fusion(bf16[1024,2048]{1,0:T(8,128)(2,1)} %copy-done.5, bf16[1024,2048]{1,0:T(8,128)(2,1)} %get-tuple-element.163, bf16[1024,2048]{1,0:T(8,128)(2,1)} %get-tuple-element.162), kind=kOutput, calls=%fused_computation | convolution fusion | flops 17205035008 | bytes 29360128 | tf_op jit(solution)/shard_map/dot_general | solution.py:1122
  388.4 1.5 copy-done.4
  389.9 1.8 copy.70
  391.7 0.7 reshape_squeeze.6.gain_ref
  392.4 0.7 reshape_squeeze.7.gain_ref
  393.1 2.9 copy.67
  395.9 1.8 copy.68
  397.8 24.2 %fusion.8 = bf16[1024,2048]{1,0:T(8,128)(2,1)} fusion(bf16[2048,4096]{1,0:T(8,128)(2,1)} %get-tuple-element.52, bf16[1024,2048]{1,0:T(8,128)(2,1)} %get-tuple-element.163, bf16[1024,2048]{1,0:T(8,128)(2,1)} %get-tuple-element.162), kind=kOutput, calls=%fused_computation.23 | convolution fusion | flops 17198743552 | bytes 29360128 | tf_op jit(solution)/shard_map/dot_general | solution.py:1128
  422.0 84.1 %sum_line.1 = (bf16[512,2048]{1,0:T(8,128)(2,1)}, f32[8,2048]{1,0:T(8,128)}) custom-call(bf16[2,512,2048]{2,1,0:T(8,128)(2,1)} %bitcast.69, bf16[2,512,2048]{2,1,0:T(8,128)(2,1)} %get-tuple-element.51.resid_all, bf16[2,512,2048]{2,1,0:T(8,128)(2,1)} %all-gather.5.cloned.1.call-done.cot_all, f32[1,2048]{1,0:T(1,128)} %reshape_squeeze.6.gain_ref), custom_call_target="tpu_custom_call" | custom-call | bytes 200000000 | tf_op jit(solution)/shard_map/sum_line/pallas_call | solution.py:815
  506.1 6.5 convolution_convert_fusion.3.ot_ref
  512.5 3.3 convolution_convert_fusion.7.d_out_ref
  515.9 21.1 %attn_backward.1 = bf16[512,1536]{1,0:T(8,128)(2,1)} custom-call(bf16[512,1536]{1,0:T(8,128)(2,1)} %get-tuple-element.53.turned_ref, bf16[512,1024]{1,0:T(8,128)(2,1)} %convolution_convert_fusion.7.d_out_ref, f32[512,512]{1,0:T(8,128)} %get-tuple-element.56.lse_ref, f32[512,128]{1,0:T(8,128)} %maximum_bitcast_fusion.cos_ref, ...), custom_call_target="tpu_custom_call" | custom-call | flops 5368709120 | bytes 4718592 | tf_op jit(solution)/shard_map/attn_backward/pallas_call | solution.py:243
  537.0 7.1 convolution_convert_fusion.2.qt_ref
  544.1 7.8 convolution_convert_fusion.6.dn_ref
  551.9 194.4 %hand_out.1 = (bf16[2,128,2048]{2,1,0:T(8,128)(2,1)}, f32[256,768]{1,0:T(8,128)}, f32[512,256]{1,0:T(8,128)}, f32[16,128]{1,0:T(8,128)}) custom-call(bf16[512,2048]{1,0:T(8,128)(2,1)} %convolution_convert_fusion.6.dn_ref, bf16[512,2048]{1,0:T(8,128)(2,1)} %get-tuple-element.44.x_ref, bf16[512,2048]{1,0:T(8,128)(2,1)} %get-tuple-element.55.dr_ref, ...), custom_call_target="tpu_custom_call" | custom-call | bytes 300000000 | tf_op jit(solution)/shard_map/hand_out/pallas_call | solution.py:1076
  746.4 0.9 bitcast_reduce_fusion
  747.3 0.1 constant_dynamic-slice_fusion
  747.4 0.6 multiply_subtract_fusion.4
  748.0 2.4 multiply_subtract_fusion.3
  750.4 1.8 multiply_subtract_fusion.2
  752.2 2.9 add_convert_fusion
  755.1 1.5 convert_bitcast_fusion
  756.7 1.8 copy.71
  758.5 6.5 multiply_subtract_fusion.1
  765.0 2.9 copy.72
  767.8 2.9 copy.73
  770.7 1.8 copy.74
  772.5 6.6 reshape.384
  779.1 19.1 %multiply_subtract_fusion = (f32[256,2,2048]{2,1,0:T(2,128)}, f32[256,2,2048]{2,1,0:T(2,128)}, f32[256,2,2048]{2,1,0:T(2,128)}) fusion(f32[256,2,2048]{2,1,0:T(2,128)} %param.28, f32[256,2,2048]{2,1,0:T(2,128)} %reshape.384, f32[256,2,2048]{2,1,0:T(2,128)} %param.34, f32[256,2,2048]{2,1,0:T(2,128)} %param.40), kind=kLoop, calls=%fused_computation.21 | loop fusion | flops 15728640 | bytes 29360128 | tf_op jit(solution)/shard_map/sub | solution.py:1115
  798.2 1.0 copy.80
  799.2 0.9 copy.81
  800.0 0.8 copy.82
  (85 shorter events, 0.5 us)
Async XLA Ops:
  7.2 98.6 %copy-start.3 = (f32[2048,256]{1,0:T(8,128)S(1)}, f32[2048,256]{1,0:T(8,128)}, u32[]{:S(2)}) copy-start(f32[2048,256]{1,0:T(8,128)} %param.29) | copy-start | bytes 6291460
  7.2 305.7 %all-gather.5.cloned.1.call-start = ((), (), s32[]{:S(2)}) async-start(), calls=%async_computation.5 | async-start | bytes 5242880 | tf_op jit(solution)/shard_map/all_gather | solution.py:1179
  105.7 207.2 %all-gather.3.cloned.1.call-start = ((), (), s32[]{:S(2)}) async-start(), calls=%async_computation.3 | async-start | bytes 9437184 | tf_op jit(solution)/shard_map/all_gather | solution.py:1168
  106.9 645.3 %reduce-scatter.4.cloned.1.call-start = ((), (), s32[]{:S(2)}) async-start(), calls=%async_computation.4 | async-start | bytes 5242880 | tf_op jit(solution)/shard_map/reduce_scatter | solution.py:1206
  108.8 11.0 %copy-start.21 = (f32[2048]{0:T(1024)}, f32[2048]{0:T(1024)S(1)}, u32[]{:S(2)}) copy-start(f32[2048]{0:T(1024)S(1)} %mul.282) | copy-start | bytes 24580
  113.2 6.2 copy-start.1
  119.8 8.0 copy-start.23
  284.1 3.5 copy-start
  288.6 2.1 copy-start.5
  348.7 406.5 %reduce-scatter.8.cloned.1.call-start = ((), (), s32[]{:S(2)}) async-start(), calls=%async_computation.7 | async-start | bytes 9437184 | tf_op jit(solution)/shard_map/reduce_scatter | solution.py:1213
  362.8 409.7 %reduce-scatter.6.cloned.1.call-start = ((), (), s32[]{:S(2)}) async-start(), calls=%async_computation.6 | async-start | bytes 18874368 | tf_op jit(solution)/shard_map/reduce_scatter | solution.py:1210
  388.3 1.6 copy-start.4
  388.3 3.4 copy-start.20
  388.3 4.0 copy-start.19
  391.7 4.2 copy-start.12
  421.9 84.1 %copy-start.32 = (bf16[512,1024]{1,0:T(8,128)(2,1)S(1)}, bf16[512,1024]{1,0:T(8,128)(2,1)}, u32[]{:S(2)}) copy-start(bf16[512,1024]{1,0:T(8,128)(2,1)} %get-tuple-element.49) | copy-start | bytes 3145732
  506.0 6.5 copy-start.13
  506.1 6.5 copy-start.31
  515.9 21.1 %copy-start.2 = (bf16[512,2048]{1,0:T(8,128)(2,1)S(1)}, bf16[512,2048]{1,0:T(8,128)(2,1)}, u32[]{:S(2)}) copy-start(bf16[512,2048]{1,0:T(8,128)(2,1)} %get-tuple-element.44.x_ref) | copy-start | bytes 6291460
  515.9 21.1 %copy-start.22 = (f32[2048]{0:T(1024)S(1)}, f32[2048]{0:T(1024)}, u32[]{:S(2)}) copy-start(f32[2048]{0:T(1024)} %copy-done.21) | copy-start | bytes 24580
  515.9 21.1 %copy-start.24 = (f32[512]{0:T(512)S(1)}, f32[512]{0:T(512)}, u32[]{:S(2)}) copy-start(f32[512]{0:T(512)} %copy-done.23) | copy-start | bytes 6148
  537.0 7.1 copy-start.33
  551.9 195.5 %copy-start.25 = (f32[64]{0:T(128)S(1)}, f32[64]{0:T(128)}, u32[]{:S(2)}) copy-start(f32[64]{0:T(128)} %param.27) | copy-start | bytes 772
  551.9 195.5 %copy-start.26 = (f32[64]{0:T(128)S(1)}, f32[64]{0:T(128)}, u32[]{:S(2)}) copy-start(f32[64]{0:T(128)} %param.24) | copy-start | bytes 772
  551.9 195.5 %copy-start.27 = (f32[64]{0:T(128)S(1)}, f32[64]{0:T(128)}, u32[]{:S(2)}) copy-start(f32[64]{0:T(128)} %param.33) | copy-start | bytes 772
  551.9 195.5 %copy-start.28 = (f32[64]{0:T(128)S(1)}, f32[64]{0:T(128)}, u32[]{:S(2)}) copy-start(f32[64]{0:T(128)} %param.39) | copy-start | bytes 772
  551.9 195.5 %copy-start.29 = (f32[64]{0:T(128)S(1)}, f32[64]{0:T(128)}, u32[]{:S(2)}) copy-start(f32[64]{0:T(128)} %param.36) | copy-start | bytes 772
  551.9 195.5 %copy-start.30 = (f32[64]{0:T(128)S(1)}, f32[64]{0:T(128)}, u32[]{:S(2)}) copy-start(f32[64]{0:T(128)} %param.30) | copy-start | bytes 772
  551.9 196.1 %copy-start.10 = (f32[512,256]{1,0:T(8,128)S(1)}, f32[512,256]{1,0:T(8,128)}, u32[]{:S(2)}) copy-start(f32[512,256]{1,0:T(8,128)} %param.26) | copy-start | bytes 1572868
  551.9 196.0 %copy-start.17 = (f32[512,256]{1,0:T(8,128)S(1)}, f32[512,256]{1,0:T(8,128)}, u32[]{:S(2)}) copy-start(f32[512,256]{1,0:T(8,128)} %param.32) | copy-start | bytes 1572868
  551.9 196.0 %copy-start.18 = (f32[512,256]{1,0:T(8,128)S(1)}, f32[512,256]{1,0:T(8,128)}, u32[]{:S(2)}) copy-start(f32[512,256]{1,0:T(8,128)} %param.38) | copy-start | bytes 1572868
  746.4 4.0 copy-start.7
  746.4 4.0 copy-start.8
  746.4 4.0 copy-start.15
  746.4 4.0 copy-start.16
  755.1 3.4 copy-start.6
  779.1 19.1 %copy-start.14 = (bf16[2,128,2048]{2,1,0:T(8,128)(2,1)S(1)}, bf16[2,128,2048]{2,1,0:T(8,128)(2,1)}, u32[]{:S(2)}) copy-start(bf16[2,128,2048]{2,1,0:T(8,128)(2,1)} %get-tuple-element.203) | copy-start | bytes 3145732
  779.1 20.0 %copy-start.9 = (f32[256,768]{1,0:T(8,128)S(1)}, f32[256,768]{1,0:T(8,128)}, u32[]{:S(2)}) copy-start(f32[256,768]{1,0:T(8,128)} %get-tuple-element.205) | copy-start | bytes 2359300
  779.1 20.9 %copy-start.11 = (f32[512,256]{1,0:T(8,128)S(1)}, f32[512,256]{1,0:T(8,128)}, u32[]{:S(2)}) copy-start(f32[512,256]{1,0:T(8,128)} %get-tuple-element.206) | copy-start | bytes 1572868
Sparse Core Ops, SparseCore 0:
  105.9 75.7 all-gather.4
  184.1 93.7 all-gather.2
  348.8 74.9 reduce-scatter.3
  427.1 71.8 reduce-scatter.7
  502.5 166.3 reduce-scatter.5

commit v5 on v4

--- a/solution.py
+++ b/solution.py
@@ -828,9 +828,93 @@
     )(part, resid, cot, gain)
 
 
-def hand_out_kernel(n_dp, n_z, dn_ref, x_ref, dr_ref, gain_ref, gain2_ref, qt_ref, ot_ref,
-                    ig, gq, go, gains, got, buf, q_got, q_own, q_mid, q_put, q_fin, o_got, o_own, o_mid, o_put, o_fin, g_src, g_all,
-                    p_s, p_r, i_s, i_r, q_s, q_r, qf_s, qf_r, o_s, o_r, of_s, of_r, g_s, g_r, loc):
+class Adam:
+    def __init__(self, count, sources, targets, views, bufs, sems, compute):
+        self.count, self.sources, self.targets, self.views = count, sources, targets, views
+        self.ins, self.outs = bufs[:4], bufs[4:]
+        self.in_sem, self.out_sem = sems
+        self.compute = compute
+
+    def each(self, i, slot, inward):
+        view_grad, view = self.views
+        for n in range(4):
+            if inward:
+                cut = view_grad if n == 0 else view
+                yield pltpu.make_async_copy(cut(self.sources[n], i), self.ins[n].at[slot], self.in_sem.at[slot, n])
+            else:
+                yield pltpu.make_async_copy(self.outs[n].at[slot], view(self.targets[n], i), self.out_sem.at[slot, n])
+
+    def start(self):
+        for copy in self.each(0, 0, True):
+            copy.start()
+
+    def run(self, low, high):
+        def one(i, carry):
+            slot = lax.rem(i, 2)
+
+            @pl.when(i + 1 < self.count)
+            def _():
+                for copy in self.each(i + 1, 1 - slot, True):
+                    copy.start()
+
+            for copy in self.each(i, slot, True):
+                copy.wait()
+
+            @pl.when(i >= 2)
+            def _():
+                for copy in self.each(i - 2, slot, False):
+                    copy.wait()
+
+            self.compute(slot)
+            for copy in self.each(i, slot, False):
+                copy.start()
+            return carry
+
+        lax.fori_loop(low, high, one, 0)
+
+    def end(self):
+        for i in range(max(0, self.count - 2), self.count):
+            for copy in self.each(i, i % 2, False):
+                copy.wait()
+
+
+def wide_compute(ins, outs):
+    width = ins[1].shape[-1]
+
+    def compute(slot):
+        for n in range(2):
+            grad = ins[0][slot, :, n * width : (n + 1) * width].astype(jnp.float32)
+            value = adam_update(ins[1][slot, :, n], grad, ins[2][slot, :, n], ins[3][slot, :, n])
+            outs[0][slot, :, n] = grad
+            for k in range(3):
+                outs[1 + k][slot, :, n] = value[k]
+
+    return compute
+
+
+def turned_compute(ins, outs):
+    def compute(slot):
+        grad = ins[0][slot].astype(jnp.float32).T
+        value = adam_update(ins[1][slot], grad, ins[2][slot], ins[3][slot])
+        outs[0][slot] = grad
+        for k in range(3):
+            outs[1 + k][slot] = value[k]
+
+    return compute
+
+
+WIDE_ROWS = 16
+TURNED_ROWS = 128
+
+
+def hand_out_kernel(n_dp, n_z, dn_ref, x_ref, dr_ref, gain_ref, gain2_ref, qt_ref, ot_ref, *refs):
+    wide_in, turned_in = refs[0:4], refs[4:8]
+    ig, gq, go, gains = refs[8:12]
+    wide_out, turned_out = refs[12:16], refs[16:20]
+    (got, buf, q_got, q_own, q_mid, q_put, q_fin, o_got, o_own, o_mid, o_put, o_fin, g_src, g_all) = refs[20:34]
+    wide_bufs, turned_bufs = refs[34:42], refs[42:50]
+    (p_s, p_r, i_s, i_r, q_s, q_r, qf_s, qf_r, o_s, o_r, of_s, of_r, g_s, g_r, q_loc, o_loc, loc,
+     a_in, a_out, b_in, b_out) = refs[50:]
     d, z, pair, c = place()
     n_d = n_dp // 2
     total = n_dp * n_z
@@ -843,91 +927,137 @@
     o_rows, o_cols = o_fin.shape[1:]
     relay = n_d == 4
 
-    def region(ref, rows, cols, owner, b):
-        return ref.at[pl.ds(pl.multiple_of(owner * 2 * rows, 2 * rows), 2 * rows), pl.ds(b * cols, cols)]
+    wide = Adam(
+        wide_in[1].shape[0] // WIDE_ROWS, wide_in, wide_out,
+        (lambda ref, i: ref.at[pl.ds(pl.multiple_of(i * WIDE_ROWS, WIDE_ROWS), WIDE_ROWS)],) * 2,
+        wide_bufs, (a_in, a_out), wide_compute(wide_bufs[:4], wide_bufs[4:]),
+    )
+    turned = Adam(
+        turned_in[1].shape[0] // TURNED_ROWS, turned_in, turned_out,
+        (lambda ref, i: ref.at[:, pl.ds(pl.multiple_of(i * TURNED_ROWS, TURNED_ROWS), TURNED_ROWS)],
+         lambda ref, i: ref.at[pl.ds(pl.multiple_of(i * TURNED_ROWS, TURNED_ROWS), TURNED_ROWS)]),
+        turned_bufs, (b_in, b_out), turned_compute(turned_bufs[:4], turned_bufs[4:]),
+    )
 
     class First:
-        def __init__(self, src, rows, cols, got_ref, own_ref, mid_ref, put_ref, send, recv, spare):
-            self.src, self.rows, self.cols, self.got, self.own, self.mid = src, rows, cols, got_ref, own_ref, mid_ref
-            self.put, self.send, self.recv, self.spare = put_ref, send, recv, spare
-
-        def slot(self, n, b):
-            return self.got.at[n, :, pl.ds(b * self.cols, self.cols)]
-
-        def copy(self, n, b, owner, to):
-            src = region(self.src, self.rows, self.cols, owner, b)
-            return remote(src, self.slot(n, b), self.send.at[n, b], self.recv.at[n, b], (2 * (pair ^ to) + c, z))
-
-        def load(self, b):
-            yield pltpu.make_async_copy(region(self.src, self.rows, self.cols, pair, b), self.own.at[:, pl.ds(b * self.cols, self.cols)], loc.at[self.spare + b])
+        def __init__(self, src, rows, cols, bufs, sems, spare):
+            self.src, self.rows, self.cols, self.spare = src, rows, cols, spare
+            self.got, self.own, self.mid, self.put, self.fin = bufs
+            self.send, self.recv, self.f_send, self.f_recv, self.loc = sems
+
+        def block(self, ref, b, core):
+            return ref.at[pl.ds(core * self.rows, self.rows), pl.ds(b * self.cols, self.cols)]
+
+        def source(self, owner, b, core):
+            return self.src.at[pl.ds(pl.multiple_of((2 * owner + core) * self.rows, self.rows), self.rows), pl.ds(b * self.cols, self.cols)]
+
+        def copy(self, n, b, core, owner, to):
+            return remote(self.source(owner, b, core), self.block(self.got.at[n], b, core), self.send.at[n, b, core],
+                          self.recv.at[n, b, core], (2 * (pair ^ to) + c, z))
+
+        def loads(self, b, core):
+            yield pltpu.make_async_copy(self.source(pair, b, core), self.block(self.own, b, core), self.loc.at[0, b, core])
             if relay:
-                yield pltpu.make_async_copy(region(self.src, self.rows, self.cols, pair ^ (2 >> b), b), self.mid.at[:, pl.ds(b * self.cols, self.cols)], loc.at[self.spare + 2 + b])
-
-        def begin(self, b):
-            if relay:
-                near = 1 + b
-                self.copy(1, b, pair ^ 3, near).start()
-                self.copy(0, b, pair ^ near, near).start()
-            else:
-                for k in range(1, n_d):
-                    self.copy(k - 1, b, pair ^ k, k).start()
-
-        def arrived(self, n, b):
-            remote(self.slot(n, b), self.slot(n, b), self.send.at[n, b], self.recv.at[n, b], (d, z)).wait_recv()
-
-        def middle(self, b):
+                yield pltpu.make_async_copy(self.source(pair ^ (2 >> b), b, core), self.block(self.mid, b, core), self.loc.at[1, b, core])
+
+        def begin(self, core):
+            for b in range(2):
+                if relay:
+                    self.copy(1, b, core, pair ^ 3, 1 + b).start()
+            for b in range(2):
+                if relay:
+                    self.copy(0, b, core, pair ^ (1 + b), 1 + b).start()
+                else:
+                    for k in range(1, n_d):
+                        self.copy(k - 1, b, core, pair ^ k, k).start()
+
+        def arrived(self, n, b, core):
+            at = self.block(self.got.at[n], b, core)
+            remote(at, at, self.send.at[n, b, core], self.recv.at[n, b, core], (d, z)).wait_recv()
+
+        def cut(self, b, core, r):
+            return pl.ds(pl.multiple_of(core * self.rows + r * 16, 16), 16), pl.ds(b * self.cols, self.cols)
+
+        def middle_copy(self, b, core):
+            return remote(self.block(self.mid, b, core), self.block(self.got.at[2], b, core), self.send.at[2, b, core],
+                          self.recv.at[2, b, core], (2 * (pair ^ (2 >> b)) + c, z))
+
+        def middle(self, core, between):
             if not relay:
                 return
-            self.arrived(1, b)
-            lanes = pl.ds(b * self.cols, self.cols)
-
-            def add(r, carry):
-                at = pl.ds(pl.multiple_of(r * 16, 16), 16)
-                self.mid[at, lanes] = (self.mid[at, lanes].astype(jnp.float32) + self.got[1, at, lanes].astype(jnp.float32)).astype(jnp.bfloat16)
-                return carry
-
-            lax.fori_loop(0, 2 * self.rows // 16, add, 0)
-
-        def middle_copy(self, b):
-            src = self.mid.at[:, pl.ds(b * self.cols, self.cols)]
-            return remote(src, self.slot(2, b), self.send.at[2, b], self.recv.at[2, b], (2 * (pair ^ (2 >> b)) + c, z))
-
-        def total(self, b):
+            for b in range(2):
+                self.arrived(1, b, core)
+
+                def add(r, carry):
+                    at = self.cut(b, core, r)
+                    self.mid[at] = (self.mid[at].astype(jnp.float32) + self.got[(1,) + at].astype(jnp.float32)).astype(jnp.bfloat16)
+                    return carry
+
+                lax.fori_loop(0, self.rows // 16, add, 0)
+            self.middle_copy(0, core).start()
+            between()
+            self.middle_copy(1, core).start()
+
+        def total(self, core, between):
             slots = (0, 2) if relay else range(n_d - 1)
-            for n in slots:
-                self.arrived(n, b)
-            lanes = pl.ds(b * self.cols, self.cols)
+            for b in range(2):
+                for n in slots:
+                    self.arrived(n, b, core)
+
+                def add(r, carry):
+                    at = self.cut(b, core, r)
+                    value = self.own[at].astype(jnp.float32)
+                    for n in slots:
+                        value = value + self.got[(n,) + at].astype(jnp.float32)
+                    self.put[core, b, pl.ds(pl.multiple_of(r * 16, 16), 16)] = value.astype(jnp.bfloat16)
+                    return carry
+
+                lax.fori_loop(0, self.rows // 16, add, 0)
+            self.second(0, core, False)
+            between()
+            self.second(1, core, False)
+
+        def second(self, b, core, wait):
+            here = (core == c) & (2 * c + b == z)
+            src = self.put.at[core, b]
+            copy = remote(src, self.fin.at[z], self.f_send.at[core, b], self.f_recv.at[z], (2 * pair + core, 2 * c + b))
+            keep = pltpu.make_async_copy(src, self.fin.at[z], loc.at[self.spare])
+            pl.when(jnp.logical_not(here))(copy.wait_send if wait else copy.start)
+            pl.when(here)(keep.wait if wait else keep.start)
+
+        def final(self):
             for core in range(2):
-
-                def add(r, carry):
-                    at = pl.ds(pl.multiple_of(r * 16, 16), 16)
-                    src = pl.ds(pl.multiple_of(core * self.rows + r * 16, 16), 16)
-                    value = self.own[src, lanes].astype(jnp.float32)
-                    for n in slots:
-                        value = value + self.got[n, src, lanes].astype(jnp.float32)
-                    self.put[core, b, at] = value.astype(jnp.bfloat16)
-                    return carry
-
-                lax.fori_loop(0, self.rows // 16, add, 0)
-
-        def sent(self, b):
-            for n in range(n_d - 1):
-                remote(self.slot(n, b), self.slot(n, b), self.send.at[n, b], self.recv.at[n, b], (d, z)).wait_send()
-
-    o_first = First(ot_ref, o_rows, o_cols, o_got, o_own, o_mid, o_put, o_s, o_r, 6)
-    q_first = First(qt_ref, q_rows, q_cols, q_got, q_own, q_mid, q_put, q_s, q_r, 10)
-    firsts = [(o_first, 0), (o_first, 1), (q_first, 0), (q_first, 1)]
-    for one, b in firsts:
-        for copy in one.load(b):
-            copy.start()
+                for b in range(2):
+                    self.second(b, core, True)
+            for zs in range(n_z):
+                at = self.fin.at[zs]
+                from_here = (cz == c) & (zs == z)
+                pl.when(jnp.logical_not(from_here))(remote(at, at, self.f_send.at[0, 0], self.f_recv.at[zs], (d, z)).wait_recv)
+
+        def sent(self):
+            for b in range(2):
+                for core in range(2):
+                    for n in range(n_d - 1):
+                        at = self.block(self.got.at[n], b, core)
+                        remote(at, at, self.send.at[n, b, core], self.recv.at[n, b, core], (d, z)).wait_send()
+
+    o_first = First(ot_ref, o_rows, o_cols, (o_got, o_own, o_mid, o_put, o_fin), (o_s, o_r, of_s, of_r, o_loc), 2)
+    q_first = First(qt_ref, q_rows, q_cols, (q_got, q_own, q_mid, q_put, q_fin), (q_s, q_r, qf_s, qf_r, q_loc), 3)
+    for one in (o_first, q_first):
+        for core in range(2):
+            for b in range(2):
+                for copy in one.loads(b, core):
+                    copy.start()
+    turned.start()
+    wide.start()
     greet_all(n_dp, n_z, d, z)
 
     mine = pl.ds(pl.multiple_of(c * half, half), half)
     theirs = pl.ds(pl.multiple_of((1 - c) * half, half), half)
     swap = remote(dn_ref.at[theirs], got, p_s, p_r, (2 * pair + 1 - c, z))
     swap.start()
-    for one, b in firsts:
-        one.begin(b)
+    o_first.begin(0)
+    o_first.begin(1)
 
     g_src[pl.ds(0, 8)] = jnp.zeros((8, width), jnp.float32)
     g_src[pl.ds(8, 8)] = gain2_ref[...]
@@ -954,26 +1084,29 @@
         zz = 2 * c + b
         here = (cz == c) & (zz == z)
         copy = remote(src, dst, i_s.at[b], i_r.at[z % 2], (2 * pair + cz, zz))
-        keep = pltpu.make_async_copy(src, dst, loc.at[2])
+        keep = pltpu.make_async_copy(src, dst, loc.at[0])
         pl.when(jnp.logical_not(here))(copy.wait_send if wait else copy.start)
         pl.when(here)(keep.wait if wait else keep.start)
 
+    for one in (o_first, q_first):
+        for core in range(2):
+            for b in range(2):
+                for copy in one.loads(b, core):
+                    copy.wait()
     per = quarter // 16
     lax.fori_loop(0, per, rows_of, 0)
-    lax.fori_loop(per, per + per // 2, rows_of, 0)
-    row_send(0, False)
-    lax.fori_loop(per + per // 2, 2 * per, rows_of, 0)
-    for one, b in firsts:
-        for copy in one.load(b):
-            copy.wait()
-    row_send(1, False)
+    o_first.middle(0, lambda: row_send(0, False))
+    q_first.begin(0)
+    lax.fori_loop(per, 2 * per, rows_of, 0)
+    o_first.middle(1, lambda: row_send(1, False))
+    q_first.begin(1)
 
     each = width // total
 
     def gain_tile(o):
         return g_src.at[:, pl.ds(pl.multiple_of(o * each // 128 * 128, 128), 128)]
 
-    own_gain = pltpu.make_async_copy(gain_tile(me), g_all.at[me], loc.at[3])
+    own_gain = pltpu.make_async_copy(gain_tile(me), g_all.at[me], loc.at[1])
     own_gain.start()
 
     def send_gain(o, carry):
@@ -983,64 +1116,27 @@
 
     lax.fori_loop(1, total, send_gain, 0)
 
-    def second_send(b, put_ref, fin_ref, f_s, f_r, spare, wait):
-        for core in range(2):
-            here = (core == c) & (2 * c + b == z)
-            src = put_ref.at[core, b]
-            copy = remote(src, fin_ref.at[z], f_s.at[core, b], f_r.at[z], (2 * pair + core, 2 * c + b))
-            keep = pltpu.make_async_copy(src, fin_ref.at[z], loc.at[spare])
-            pl.when(jnp.logical_not(here))(copy.wait_send if wait else copy.start)
-            pl.when(here)(keep.wait if wait else keep.start)
-
-    def last(rows, fin_ref, out_ref):
-        def add(r, carry):
-            at = pl.ds(pl.multiple_of(r * 16, 16), 16)
-            value = fin_ref[0, at].astype(jnp.float32)
-            for zs in range(1, n_z):
-                value = value + fin_ref[zs, at].astype(jnp.float32)
-            out_ref[at] = value
-            return carry
-
-        lax.fori_loop(0, rows // 16, add, 0)
-
-    o_args = (o_put, o_fin, of_s, of_r, 4)
-    q_args = (q_put, q_fin, qf_s, qf_r, 5)
-    if relay:
-        for n, (one, b) in enumerate(firsts):
-            one.middle(b)
-            if n:
-                last_one, last_b = firsts[n - 1]
-                last_one.middle_copy(last_b).start()
-    o_first.total(0)
-    if relay:
-        q_first.middle_copy(1).start()
-    o_first.total(1)
-    second_send(0, *o_args, False)
-    q_first.total(0)
-    second_send(1, *o_args, False)
-    q_first.total(1)
-    second_send(0, *q_args, False)
-
-    def arrived(fin_ref, f_s, f_r):
-        for zs in range(n_z):
-            at = fin_ref.at[zs]
-            from_here = (cz == c) & (zs == z)
-            pl.when(jnp.logical_not(from_here))(remote(at, at, f_s.at[0, 0], f_r.at[zs], (d, z)).wait_recv)
-
-    def own_done(args):
-        for b in range(2):
-            second_send(b, *args, True)
-
-    own_done(o_args)
-    arrived(o_fin, of_s, of_r)
+    def share(adam, n, parts):
+        return lambda: adam.run(n * adam.count // parts, (n + 1) * adam.count // parts)
+
+    share(turned, 0, 2)()
+    o_first.total(0, share(wide, 0, 8))
+    q_first.middle(0, share(wide, 1, 8))
+    share(turned, 1, 2)()
+    o_first.total(1, share(wide, 2, 8))
+    share(wide, 3, 8)()
+    q_first.middle(1, share(wide, 4, 8))
+    share(wide, 5, 8)()
+    q_first.total(0, share(wide, 6, 8))
+    q_first.total(1, share(wide, 7, 8))
+
+    o_first.final()
     value = o_fin[0].astype(jnp.float32)
     for zs in range(1, n_z):
         value = value + o_fin[zs].astype(jnp.float32)
     go[...] = value.T
-    second_send(1, *q_args, False)
-    own_done(q_args)
-    arrived(q_fin, qf_s, qf_r)
-    last(q_rows, q_fin, gq)
+    turned.end()
+    wide.end()
 
     many = g_all.at[pl.ds(0, total - 1)]
     gain_copy = remote(many, many, g_s, g_r, (d, z))
@@ -1058,47 +1154,68 @@
     swap.wait_send()
     for b in range(2):
         row_send(b, True)
-        o_first.sent(b)
-        q_first.sent(b)
     for i in range(2):
         from_here = (cz == c) & (2 * c + i == z)
         at = ig.at[i]
         pl.when(jnp.logical_not(from_here))(remote(at, at, i_s.at[0], i_r.at[i], (d, z)).wait_recv)
-
-
-def hand_out(dn, x, dr, gain, gain2, qt, ot, n_dp, n_z):
+    o_first.sent()
+    q_first.sent()
+    q_first.final()
+
+    def last(r, carry):
+        at = pl.ds(pl.multiple_of(r * 16, 16), 16)
+        value = q_fin[0, at].astype(jnp.float32)
+        for zs in range(1, n_z):
+            value = value + q_fin[zs, at].astype(jnp.float32)
+        gq[at] = value
+        return carry
+
+    lax.fori_loop(0, q_rows // 16, last, 0)
+
+
+def hand_out(dn, x, dr, gain, gain2, qt, ot, wide, turned, n_dp, n_z):
     full, width = x.shape
     n_d = n_dp // 2
     total = n_dp * n_z
     q_rows, q_cols = qt.shape[0] // n_dp, qt.shape[1] // 2
     o_rows, o_cols = ot.shape[0] // n_dp, ot.shape[1] // 2
     b16 = jnp.bfloat16
+    f32 = jnp.float32
+
+    def weight_bufs(rows, cols):
+        return [
+            pltpu.VMEM((n_d - 1, 2 * rows, 2 * cols), b16), pltpu.VMEM((2 * rows, 2 * cols), b16),
+            pltpu.VMEM((2 * rows, 2 * cols), b16), pltpu.VMEM((2, 2, rows, cols), b16), pltpu.VMEM((n_z, rows, cols), b16),
+        ]
+
+    wide_shape = (2, WIDE_ROWS) + wide[1].shape[1:]
+    turned_shape = (2, TURNED_ROWS, turned[1].shape[1])
+    weight_sems = [DMA((n_d - 1, 2, 2)), DMA((n_d - 1, 2, 2)), DMA((2, 2)), DMA((n_z,))]
     return pl.pallas_call(
         functools.partial(hand_out_kernel, n_dp, n_z),
-        in_specs=[VMEM_SPEC] * 5 + [ANY_SPEC] * 2,
-        out_specs=[ANY_SPEC] + [VMEM_SPEC] * 3,
+        in_specs=[VMEM_SPEC] * 5 + [ANY_SPEC] * 10,
+        out_specs=[ANY_SPEC] + [VMEM_SPEC] * 3 + [ANY_SPEC] * 8,
         out_shape=[
             jax.ShapeDtypeStruct((2, full // 4, width), b16),
-            jax.ShapeDtypeStruct((q_rows, q_cols), jnp.float32),
-            jax.ShapeDtypeStruct((o_cols, o_rows), jnp.float32),
-            jax.ShapeDtypeStruct((16, 128), jnp.float32),
-        ],
+            jax.ShapeDtypeStruct((q_rows, q_cols), f32),
+            jax.ShapeDtypeStruct((o_cols, o_rows), f32),
+            jax.ShapeDtypeStruct((16, 128), f32),
+        ]
+        + [jax.ShapeDtypeStruct(wide[1].shape, f32)] * 4
+        + [jax.ShapeDtypeStruct(turned[1].shape, f32)] * 4,
         scratch_shapes=[
             pltpu.VMEM((full // 2, width), b16), pltpu.VMEM((full // 2, width), b16),
-            pltpu.VMEM((n_d - 1, 2 * q_rows, 2 * q_cols), b16), pltpu.VMEM((2 * q_rows, 2 * q_cols), b16),
-            pltpu.VMEM((2 * q_rows, 2 * q_cols), b16),
-            pltpu.VMEM((2, 2, q_rows, q_cols), b16), pltpu.VMEM((n_z, q_rows, q_cols), b16),
-            pltpu.VMEM((n_d - 1, 2 * o_rows, 2 * o_cols), b16), pltpu.VMEM((2 * o_rows, 2 * o_cols), b16),
-            pltpu.VMEM((2 * o_rows, 2 * o_cols), b16),
-            pltpu.VMEM((2, 2, o_rows, o_cols), b16), pltpu.VMEM((n_z, o_rows, o_cols), b16),
-            pltpu.VMEM((16, width), jnp.float32), pltpu.VMEM((total, 16, 128), jnp.float32),
-            DMA, DMA, DMA((2,)), DMA((2,)), DMA((n_d - 1, 2)), DMA((n_d - 1, 2)), DMA((2, 2)), DMA((n_z,)),
-            DMA((n_d - 1, 2)), DMA((n_d - 1, 2)), DMA((2, 2)), DMA((n_z,)), DMA, DMA, DMA((14,)),
+            *weight_bufs(q_rows, q_cols), *weight_bufs(o_rows, o_cols),
+            pltpu.VMEM((16, width), f32), pltpu.VMEM((total, 16, 128), f32),
+            pltpu.VMEM((2, WIDE_ROWS, wide[0].shape[1]), b16), *[pltpu.VMEM(wide_shape, f32)] * 7,
+            pltpu.VMEM((2, turned[0].shape[0], TURNED_ROWS), b16), *[pltpu.VMEM(turned_shape, f32)] * 7,
+            DMA, DMA, DMA((2,)), DMA((2,)), *weight_sems, *weight_sems, DMA, DMA,
+            DMA((2, 2, 2)), DMA((2, 2, 2)), DMA((4,)), DMA((2, 4)), DMA((2, 4)), DMA((2, 4)), DMA((2, 4)),
         ],
-        compiler_params=pltpu.CompilerParams(collective_id=5, has_side_effects=True, vmem_limit_bytes=56 * 1024 * 1024),
+        compiler_params=pltpu.CompilerParams(collective_id=5, has_side_effects=True, vmem_limit_bytes=58 * 1024 * 1024),
         cost_estimate=pl.CostEstimate(flops=0, bytes_accessed=300_000_000, transcendentals=0),
         name="hand_out",
-    )(dn, x, dr, gain, gain2, qt, ot)
+    )(dn, x, dr, gain, gain2, qt, ot, *wide, *turned)
 
 
 def rms_forward(values, gain_wide):
@@ -1208,10 +1325,8 @@
     )
     gate_up_term = contract_rows(normed_two, d_gate_up16).astype(jnp.bfloat16)
     gate_up_sum = lax.psum_scatter(gate_up_term, "dp", scatter_dimension=0, tiled=True)
-    grad_gate_up = gate_up_sum.reshape(gate_up_weight.shape).astype(jnp.float32)
     down_term = contract_rows(cot_rows, hidden16).astype(jnp.bfloat16)
     down_sum = lax.psum_scatter(down_term, "dp", scatter_dimension=0, tiled=True)
-    grad_down = down_sum.astype(jnp.float32).T
     d_normed_two = times_transpose(d_gate_up16, gate_up_cols).astype(jnp.bfloat16)
     d_resid16, gain_two_part = sum_line(
         d_normed_two.reshape(resid_all.shape), resid_all, cot_all, gain_two, n_z
@@ -1224,9 +1339,20 @@
     d_normed_one = times_transpose(d_qkv16, qkv_cols).astype(jnp.bfloat16)
     qkv_term = contract_rows(normed_one, d_qkv16).astype(jnp.bfloat16)
     out_term = contract_rows(d_resid16, attended16).astype(jnp.bfloat16)
-    input_grad, grad_qkv, grad_out, gain_sums = hand_out(
-        d_normed_one, rows_in, d_resid16, gain_one, gain_two_part, qkv_term, out_term, n_dp, n_z
-    )
+    input_grad, grad_qkv, grad_out, gain_sums, *updated = hand_out(
+        d_normed_one,
+        rows_in,
+        d_resid16,
+        gain_one,
+        gain_two_part,
+        qkv_term,
+        out_term,
+        (gate_up_sum, gate_up_weight, first_gate_up, second_gate_up),
+        (down_sum, down_weight, first_down, second_down),
+        n_dp,
+        n_z,
+    )
+    grad_gate_up, w_gu, m_gu, v_gu, grad_down, w_down, m_down, v_down = updated
     flat = lax.axis_index("dp") * n_z + z_here
     gain_sums = lax.dynamic_slice(
         jnp.sum(gain_sums.reshape(2, 8, LANES), axis=1), (0, flat * owned % LANES), (2, owned)
@@ -1237,8 +1363,6 @@
     w_qkv, m_qkv, v_qkv = adam_update(qkv_weight, grad_qkv, first_qkv, second_qkv)
     w_out, m_out, v_out = adam_update(out_weight, grad_out, first_out, second_out)
     w_two, m_two, v_two = adam_update(mlp_gain, grad_gain_two, first_mlp_gain, second_mlp_gain)
-    w_gu, m_gu, v_gu = adam_update(gate_up_weight, grad_gate_up, first_gate_up, second_gate_up)
-    w_down, m_down, v_down = adam_update(down_weight, grad_down, first_down, second_down)
     return (
         output,
         input_grad,

time: 815 us -> 796 us (0.977)
  waiting for transfers between devices: 0.09 us -> 74.1 us
  Pallas kernels: 540 us -> 476 us
  other arithmetic: 52.4 us -> 25.1 us
    reduce_scatter x1, waiting for transfers between devices: 0.01 us -> 74 us  [layer_step(): lax.psum_scatter(gate_up_term, 'dp', scatter_dimension=0, tiled=True)]
    pallas_call x1, Pallas kernels: 194 us -> 127 us  [hand_out(): pl.pallas_call(functools.partial(hand_out_kernel, n_dp, n_z), in_specs=[V...]
    sub x5 -> x3, other arithmetic: 30.3 us -> 4.85 us  [adam_update(): weight - learn_rate * (first_hat / (jnp.sqrt(second_hat) + adam_eps) + we...]
    unnamed x81 -> x86, local copies, waits for them, and re-layouts: 26.6 us -> 31.8 us
  transfers between devices with their start and end apart: 5 -> 5, of which waited for: 0 -> 1; matrix products, arithmetic and copies ran while one was open for 22% -> 19% of each run, Pallas kernels for 55% -> 33%
where the time goes in v5:
time: 796 us; the launch traced here: 788 us
  Pallas kernels  476 us (60%)
  matrix products  160 us (20%)
  waiting for transfers between devices  74.1 us (9%)
  local copies, waits for them, and re-layouts  38 us (5%)
  other arithmetic  25.1 us (3%)
  between operations  14.7 us (2%)
    pallas_call x1, Pallas kernels, hand_out(): pl.pallas_call(functools.partial(hand_out_kernel, n_dp, n_z), in_specs=[V...  127 us
    pallas_call x1, Pallas kernels, share_resid(): pl.pallas_call(functools.partial(share_resid_kernel, n_dp, n_z), in_specs...  111 us
    pallas_call x1, Pallas kernels, gather_in(): pl.pallas_call(functools.partial(gather_in_kernel, n_dp, n_z), in_specs=[...  91.9 us
    pallas_call x1, Pallas kernels, sum_line(): pl.pallas_call(functools.partial(sum_line_kernel, n_z), in_specs=[VMEM_SP...  87.6 us
    reduce_scatter x1, waiting for transfers between devices, layer_step(): lax.psum_scatter(gate_up_term, 'dp', scatter_dimension=0, tiled=True)  74 us
    dot_general x4, matrix products, times_transpose(): lax.dot_general(left, right, (((1,), (1,)), ((), ())), preferred_element_...  59.9 us
    dot_general x4, matrix products, contract_rows(): lax.dot_general(left, right, (((0,), (0,)), ((), ())), preferred_element_...  53 us
    pallas_call x1, Pallas kernels, attn_forward(): pl.pallas_call(functools.partial(attn_gather_kernel, n_dp, pairs, Q_ROWS,...  37.5 us
  transfers between devices with their start and end apart: 5, of which 1 were waited for; matrix products, arithmetic and copies ran while one was open for 19% of the time, Pallas kernels for 33%

profile of v5, /device:TPU:9, one launch (start us, length us, event | category | flops | bytes accessed | tf_op | source)
XLA Modules:
  0.0 788.4 jit_solution(9483431620795180667)
XLA Ops:
  7.3 2.0 copy.49
  9.3 1.9 convert_element_type.108.w_ref
  11.2 0.7 convert_bitcast_fusion.1
  11.9 0.7 fusion.17.g_ref
  12.5 1.3 pad.12.s_ref
  13.8 91.9 %gather_in.1 = (bf16[512,2048]{1,0:T(8,128)(2,1)}, bf16[2048,1536]{1,0:T(8,128)(2,1)}, bf16[512,1024]{1,0:T(8,128)(2,1)}, f32[32,8,128]{2,1,0:T(8,128)}, s32[2,8,512]{2,1,0:T(8,128)}) custom-call(bf16[2,128,2048]{2,1,0:T(8,128)(2,1)} %x_ref.1, bf16[256,768]{1,0:T(8,128)(2,1)} %convert_element_type.108.w_ref, bf16[256,512]{1,0:T(8,128)(2,1)} %bitcast.62, ...), custom_call_target="tpu_custom_call" | custom-call | bytes 200000000 | tf_op jit(solution)/shard_map/gather_in/pallas_call | solution.py:502
  105.8 1.1 convert_element_type.122
  107.0 4.2 convert_element_type.115
  111.2 2.2 copy.51
  113.4 1.1 slice_reduce_fusion.1
  114.7 0.7 constant_dynamic-slice_fusion.1
  115.4 0.2 convert_reduce_fusion
  115.7 1.0 fusion.13
  116.7 1.0 maximum_bitcast_fusion.cos_ref
  117.7 1.0 maximum_bitcast_fusion.1.sin_ref
  118.6 0.5 fusion.4
  119.2 8.0 %fusion.10.qkv_ref = f32[512,1536]{1,0:T(8,128)} fusion(bf16[2048,1536]{1,0:T(8,128)(2,1)} %get-tuple-element.54, bf16[512,2048]{1,0:T(8,128)(2,1)S(1)} %copy-done.1, f32[2048]{0:T(1024)S(1)} %mul.216, f32[512]{0:T(512)S(1)} %add_rsqrt_fusion), kind=kOutput, calls=%fused_computation.32 | convolution fusion | flops 3225419776 | bytes 11544576 | tf_op jit(solution)/shard_map/dot_general | solution.py:1302
  127.1 0.6 reshape.374.seg_row_ref
  127.8 0.8 reshape.373.seg_col_ref
  128.6 37.5 %attn_forward.1 = (bf16[512,1536]{1,0:T(8,128)(2,1)}, f32[512,512]{1,0:T(8,128)}, bf16[512,1024]{1,0:T(8,128)(2,1)}, bf16[2048,1024]{1,0:T(8,128)(2,1)}) custom-call(f32[512,1536]{1,0:T(8,128)} %fusion.10.qkv_ref, f32[512,128]{1,0:T(8,128)} %maximum_bitcast_fusion.cos_ref, f32[512,128]{1,0:T(8,128)} %maximum_bitcast_fusion.1.sin_ref, ...), custom_call_target="tpu_custom_call" | custom-call | flops 2147483648 | bytes 150000000 | tf_op jit(solution)/shard_map/attn_forward/pallas_call | solution.py:217
  166.1 6.2 convolution_convert_fusion.5.part_ref
  172.3 110.9 %share_resid.1 = (bf16[2,512,2048]{2,1,0:T(8,128)(2,1)}, bf16[2048,4096]{1,0:T(8,128)(2,1)}) custom-call(bf16[512,2048]{1,0:T(8,128)(2,1)} %convolution_convert_fusion.5.part_ref, bf16[512,2048]{1,0:T(8,128)(2,1)} %get-tuple-element.52.x_ref, bf16[256,4096]{1,0:T(8,128)(2,1)} %bitcast.56), custom_call_target="tpu_custom_call" | custom-call | bytes 200000000 | tf_op jit(solution)/shard_map/share_resid/pallas_call | solution.py:655
  283.2 3.2 multiply_reduce_fusion
  286.7 1.0 fusion.1
  287.7 2.1 copy-done.8
  289.8 22.3 %fusion.26 = f32[1024,4096]{1,0:T(8,128)} fusion(bf16[1024,2048]{1,0:T(8,128)(2,1)S(1)} %fusion.1, bf16[2048,4096]{1,0:T(8,128)(2,1)} %get-tuple-element.60), kind=kOutput, calls=%fused_computation.70 | convolution fusion | flops 17179869184 | bytes 37748736 | tf_op jit(solution)/shard_map/dot_general | solution.py:1311
  312.1 22.2 %multiply_convert_fusion.1 = (bf16[1024,2048]{1,0:T(8,128)(2,1)}, bf16[1024,2048]{1,0:T(8,128)(2,1)}, bf16[1024,2048]{1,0:T(8,128)(2,1)}) fusion(f32[1024,4096]{1,0:T(8,128)} %fusion.26, bf16[1024,2048]{1,0:T(8,128)(2,1)} %bitcast.59, bf16[2048,2048]{1,0:T(8,128)(2,1)} %all-gather.3.cloned.1.call-done), kind=kOutput, calls=%fused_computation.6 | convolution fusion | flops 8621391872 | bytes 41943040 | tf_op jit(solution)/shard_map/dot_general | solution.py:1245
  334.2 13.8 %convolution_convert_fusion.4 = bf16[1024,2048]{1,0:T(8,128)(2,1)} fusion(bf16[1024,2048]{1,0:T(8,128)(2,1)} %get-tuple-element.96, bf16[2048,2048]{1,0:T(8,128)(2,1)} %all-gather.3.cloned.1.call-done), kind=kOutput, calls=%fused_computation.21 | convolution fusion | flops 8592031744 | bytes 16777216 | tf_op jit(solution)/shard_map/dot_general | solution.py:1322
  348.1 14.1 %convolution_convert_fusion.1 = bf16[2048,2048]{1,0:T(8,128)(2,1)} fusion(bf16[1024,2048]{1,0:T(8,128)(2,1)} %bitcast.60, bf16[1024,2048]{1,0:T(8,128)(2,1)} %get-tuple-element.96), kind=kOutput, calls=%fused_computation.11 | convolution fusion | flops 8594128896 | bytes 16777216 | tf_op jit(solution)/shard_map/dot_general | solution.py:1239
  362.2 25.4 %convolution_convert_fusion = bf16[2048,4096]{1,0:T(8,128)(2,1)} fusion(bf16[1024,2048]{1,0:T(8,128)(2,1)} %copy-done.8, bf16[1024,2048]{1,0:T(8,128)(2,1)} %get-tuple-element.95, bf16[1024,2048]{1,0:T(8,128)(2,1)} %get-tuple-element.94), kind=kOutput, calls=%fused_computation | convolution fusion | flops 17205035008 | bytes 29360128 | tf_op jit(solution)/shard_map/dot_general | solution.py:1239
  387.7 0.7 reshape_squeeze.7.gain_ref
  388.4 0.7 reshape_squeeze.6.gain_ref
  389.0 24.0 %fusion.7 = bf16[1024,2048]{1,0:T(8,128)(2,1)} fusion(bf16[2048,4096]{1,0:T(8,128)(2,1)} %get-tuple-element.60, bf16[1024,2048]{1,0:T(8,128)(2,1)} %get-tuple-element.95, bf16[1024,2048]{1,0:T(8,128)(2,1)} %get-tuple-element.94), kind=kOutput, calls=%fused_computation.19 | convolution fusion | flops 17198743552 | bytes 29360128 | tf_op jit(solution)/shard_map/dot_general | solution.py:1245
  413.1 87.6 %sum_line.1 = (bf16[512,2048]{1,0:T(8,128)(2,1)}, f32[8,2048]{1,0:T(8,128)}) custom-call(bf16[2,512,2048]{2,1,0:T(8,128)(2,1)} %bitcast.61, bf16[2,512,2048]{2,1,0:T(8,128)(2,1)} %get-tuple-element.59.resid_all, bf16[2,512,2048]{2,1,0:T(8,128)(2,1)} %all-gather.5.cloned.1.call-done.cot_all, f32[1,2048]{1,0:T(1,128)} %reshape_squeeze.6.gain_ref), custom_call_target="tpu_custom_call" | custom-call | bytes 200000000 | tf_op jit(solution)/shard_map/sum_line/pallas_call | solution.py:815
  500.7 6.1 convolution_convert_fusion.3.ot_ref
  506.9 3.3 convolution_convert_fusion.7.d_out_ref
  510.2 20.7 %attn_backward.1 = bf16[512,1536]{1,0:T(8,128)(2,1)} custom-call(bf16[512,1536]{1,0:T(8,128)(2,1)} %get-tuple-element.61.turned_ref, bf16[512,1024]{1,0:T(8,128)(2,1)} %convolution_convert_fusion.7.d_out_ref, f32[512,512]{1,0:T(8,128)} %get-tuple-element.64.lse_ref, f32[512,128]{1,0:T(8,128)} %maximum_bitcast_fusion.cos_ref, ...), custom_call_target="tpu_custom_call" | custom-call | flops 5368709120 | bytes 4718592 | tf_op jit(solution)/shard_map/attn_backward/pallas_call | solution.py:243
  530.9 7.4 convolution_convert_fusion.2.qt_ref
  538.3 7.5 convolution_convert_fusion.6.dn_ref
  545.8 2.9 add_convert_fusion
  548.7 74.0 %reduce-scatter.6.cloned.1.call-done.refs_0_ = bf16[256,4096]{1,0:T(8,128)(2,1)} async-done(((bf16[2048,4096]{1,0:T(8,128)(2,1)}), bf16[256,4096]{1,0:T(8,128)(2,1)}) %reduce-scatter.6.cloned.1.call-update) | async-done | bytes 2097168 | tf_op jit(solution)/shard_map/reduce_scatter | solution.py:1327
  622.7 127.5 %hand_out.1 = (bf16[2,128,2048]{2,1,0:T(8,128)(2,1)}, f32[256,768]{1,0:T(8,128)}, f32[512,256]{1,0:T(8,128)}, f32[16,128]{1,0:T(8,128)}, f32[256,2,2048]{2,1,0:T...) custom-call(bf16[512,2048]{1,0:T(8,128)(2,1)} %convolution_convert_f, ...), custom_call_target="tpu_custom_call" | custom-call | bytes 300000000 | tf_op jit(solution)/shard_map/hand_out/pallas_call | solution.py:1194
  750.2 0.9 bitcast_reduce_fusion
  751.2 2.5 multiply_subtract_fusion.1
  753.8 1.8 multiply_subtract_fusion
  755.6 0.6 multiply_subtract_fusion.2
  756.2 1.0 copy.64
  757.2 0.9 copy.65
  758.0 0.8 copy.66
  758.8 2.1 copy.67
  761.0 1.0 copy-done.16
  761.9 1.3 copy.68
  763.3 1.6 copy-done.6
  764.9 2.1 copy.69
  767.0 1.0 copy-done.15
  768.0 1.3 copy.70
  769.3 1.6 copy-done.5
  770.9 2.1 copy.71
  773.1 1.0 copy-done.14
  774.0 1.3 copy.72
  775.4 1.6 copy-done.4
  777.0 2.1 copy.73
  779.1 1.0 copy-done.13
  780.1 1.3 copy.74
  (86 shorter events, 0.9 us)
Async XLA Ops:
  7.2 98.6 %copy-start.3 = (f32[2048,256]{1,0:T(8,128)S(1)}, f32[2048,256]{1,0:T(8,128)}, u32[]{:S(2)}) copy-start(f32[2048,256]{1,0:T(8,128)} %refs_5_.1) | copy-start | bytes 6291460
  7.2 304.8 %all-gather.5.cloned.1.call-start = ((), (), s32[]{:S(2)}) async-start(), calls=%async_computation.5 | async-start | bytes 5242880 | tf_op jit(solution)/shard_map/all_gather | solution.py:1296
  105.7 206.3 %all-gather.3.cloned.1.call-start = ((), (), s32[]{:S(2)}) async-start(), calls=%async_computation.3 | async-start | bytes 9437184 | tf_op jit(solution)/shard_map/all_gather | solution.py:1285
  106.9 438.9 %reduce-scatter.4.cloned.1.call-start = ((), (), s32[]{:S(2)}) async-start(), calls=%async_computation.4 | async-start | bytes 5242880 | tf_op jit(solution)/shard_map/reduce_scatter | solution.py:1323
  111.2 7.5 copy-start.1
  114.6 12.5 %copy-start.23 = (f32[2048]{0:T(1024)}, f32[2048]{0:T(1024)S(1)}, u32[]{:S(2)}) copy-start(f32[2048]{0:T(1024)S(1)} %mul.216) | copy-start | bytes 24580
  119.1 8.0 %copy-start.25 = (f32[512]{0:T(512)}, f32[512]{0:T(512)S(1)}, u32[]{:S(2)}) copy-start(f32[512]{0:T(512)S(1)} %add_rsqrt_fusion) | copy-start | bytes 6148
  283.2 3.5 copy-start
  287.7 2.1 copy-start.8
  348.0 200.6 %reduce-scatter.8.cloned.1.call-start = ((), (), s32[]{:S(2)}) async-start(), calls=%async_computation.7 | async-start | bytes 9437184 | tf_op jit(solution)/shard_map/reduce_scatter | solution.py:1329
  362.2 260.5 %reduce-scatter.6.cloned.1.call-start = ((), (), s32[]{:S(2)}) async-start(), calls=%async_computation.6 | async-start | bytes 18874368 | tf_op jit(solution)/shard_map/reduce_scatter | solution.py:1327
  413.1 87.6 %copy-start.34 = (bf16[512,1024]{1,0:T(8,128)(2,1)S(1)}, bf16[512,1024]{1,0:T(8,128)(2,1)}, u32[]{:S(2)}) copy-start(bf16[512,1024]{1,0:T(8,128)(2,1)} %get-tuple-element.57) | copy-start | bytes 3145732
  500.7 6.2 copy-start.17
  500.7 6.2 copy-start.33
  510.2 20.7 %copy-start.2 = (bf16[512,2048]{1,0:T(8,128)(2,1)S(1)}, bf16[512,2048]{1,0:T(8,128)(2,1)}, u32[]{:S(2)}) copy-start(bf16[512,2048]{1,0:T(8,128)(2,1)} %get-tuple-element.52.x_ref) | copy-start | bytes 6291460
  510.2 20.7 %copy-start.24 = (f32[2048]{0:T(1024)S(1)}, f32[2048]{0:T(1024)}, u32[]{:S(2)}) copy-start(f32[2048]{0:T(1024)} %copy-done.23) | copy-start | bytes 24580
  510.2 20.7 %copy-start.26 = (f32[512]{0:T(512)S(1)}, f32[512]{0:T(512)}, u32[]{:S(2)}) copy-start(f32[512]{0:T(512)} %copy-done.25) | copy-start | bytes 6148
  530.9 7.4 copy-start.35
  622.7 128.5 %copy-start.11 = (f32[512,256]{1,0:T(8,128)S(1)}, f32[512,256]{1,0:T(8,128)}, u32[]{:S(2)}) copy-start(f32[512,256]{1,0:T(8,128)} %param.26) | copy-start | bytes 1572868
  622.7 128.5 %copy-start.21 = (f32[512,256]{1,0:T(8,128)S(1)}, f32[512,256]{1,0:T(8,128)}, u32[]{:S(2)}) copy-start(f32[512,256]{1,0:T(8,128)} %param.32) | copy-start | bytes 1572868
  622.7 128.5 %copy-start.22 = (f32[512,256]{1,0:T(8,128)S(1)}, f32[512,256]{1,0:T(8,128)}, u32[]{:S(2)}) copy-start(f32[512,256]{1,0:T(8,128)} %param.38) | copy-start | bytes 1572868
  750.2 3.6 copy-start.9
  750.2 3.6 copy-start.10
  750.2 3.6 copy-start.19
  750.2 3.6 copy-start.20
  751.2 4.4 copy-start.27
  751.2 4.4 copy-start.28
  751.2 4.4 copy-start.29
  751.2 4.4 copy-start.30
  751.2 4.4 copy-start.31
  751.2 4.4 copy-start.32
  751.2 4.9 copy-start.18
  753.8 4.3 copy-start.12
  753.8 5.0 copy-start.7
  758.8 3.1 copy-start.16
  761.9 2.9 copy-start.6
  764.9 3.1 copy-start.15
  768.0 2.9 copy-start.5
  770.9 3.1 copy-start.14
  774.0 2.9 copy-start.4
  777.0 3.1 copy-start.13
Sparse Core Ops, SparseCore 0:
  105.9 75.8 all-gather.4
  184.2 94.9 all-gather.2
  348.2 74.9 reduce-scatter.3
  426.5 76.5 reduce-scatter.7
  506.5 116.1 reduce-scatter.5

commit v6 on v5

--- a/solution.py
+++ b/solution.py
@@ -380,8 +380,8 @@
                         self.copy(k - 1, self.pair, t, h, k).wait_send()
 
 
-def gather_in_kernel(n_dp, n_z, x_ref, w_ref, v_ref, g_ref, s_ref, xs, wq, vo, ga, sg,
-                     x_s, x_r, f_s, f_r, w_s, w_r, v_s, v_r, d_s, d_r, g_s, g_r, s_s, s_r, loc):
+def gather_in_kernel(n_dp, n_z, x_ref, w_ref, v_ref, g_ref, s_ref, gu_ref, xs, wq, vo, ga, sg, gu16, gu_in, gu_out,
+                     x_s, x_r, f_s, f_r, w_s, w_r, v_s, v_r, d_s, d_r, g_s, g_r, s_s, s_r, loc, gu_is, gu_os):
     d, z, pair, c = place()
     n_d = n_dp // 2
     me = d * n_z + z
@@ -390,6 +390,29 @@
     half = rows // 2
     shape = w_ref.shape
     cz = z // 2
+    chunks = gu_ref.shape[0] // WIDE_ROWS
+    gu_width = gu_ref.shape[2]
+
+    def chunk_in(i, slot):
+        return pltpu.make_async_copy(gu_ref.at[pl.ds(pl.multiple_of(i * WIDE_ROWS, WIDE_ROWS), WIDE_ROWS)], gu_in.at[slot], gu_is.at[slot])
+
+    def chunk_out(i, slot):
+        return pltpu.make_async_copy(gu_out.at[slot], gu16.at[pl.ds(pl.multiple_of(i * WIDE_ROWS, WIDE_ROWS), WIDE_ROWS)], gu_os.at[slot])
+
+    def round_chunks(low, high):
+        def one(i, carry):
+            slot = lax.rem(i, 2)
+            pl.when(i + 1 < chunks)(chunk_in(i + 1, 1 - slot).start)
+            chunk_in(i, slot).wait()
+            pl.when(i >= 2)(chunk_out(i - 2, slot).wait)
+            for n in range(2):
+                gu_out[slot, :, n * gu_width : (n + 1) * gu_width] = gu_in[slot, :, n].astype(jnp.bfloat16)
+            chunk_out(i, slot).start()
+            return carry
+
+        lax.fori_loop(low, high, one, 0)
+
+    chunk_in(0, 0).start()
     greet_all(n_dp, n_z, d, z)
 
     def line_stage(src, dst, send, recv, spare, wait):
@@ -454,6 +477,7 @@
             line_stage(v_ref, block_at(vo, v_ref.shape, c, z % 2), v_s, v_r, 4, False)
         if t > 0:
             spread.pass_on(t - 1)
+        round_chunks(t * chunks // 4, (t + 1) * chunks // 4)
 
     for o in range(n_z):
         zs = lax.rem(z + o, n_z)
@@ -484,6 +508,8 @@
             mine = (core == c) & (2 * c + b == z)
             pl.when(jnp.logical_not(mine))(remote(blk, blk, v_s.at[0], v_r.at[core, b], (d, z)).wait_recv)
             pl.when(mine)(pltpu.make_async_copy(v_ref, blk, loc.at[4]).wait)
+    for i in range(max(0, chunks - 2), chunks):
+        chunk_out(i, i % 2).wait()
     seg_copy.wait_send()
     remote(s_ref, sg.at[1 - c], s_s, s_r, (d, z)).wait_recv()
     own_seg.wait()
@@ -495,29 +521,32 @@
     spread.finish()
 
 
-def gather_in(x_loc, w, v, gain_tile, seg_tile, n_dp, n_z):
+def gather_in(x_loc, w, v, gain_tile, seg_tile, wide, n_dp, n_z):
     _, rows, width = x_loc.shape
     n_d = n_dp // 2
     total = n_dp * n_z
     return pl.pallas_call(
         functools.partial(gather_in_kernel, n_dp, n_z),
-        in_specs=[VMEM_SPEC] * 5,
-        out_specs=[ANY_SPEC] * 5,
+        in_specs=[VMEM_SPEC] * 5 + [ANY_SPEC],
+        out_specs=[ANY_SPEC] * 6,
         out_shape=[
             jax.ShapeDtypeStruct((rows * n_z, width), x_loc.dtype),
             jax.ShapeDtypeStruct((w.shape[0] * n_dp, 2 * w.shape[1]), w.dtype),
             jax.ShapeDtypeStruct((v.shape[0] * 2, 2 * v.shape[1]), v.dtype),
             jax.ShapeDtypeStruct((total,) + gain_tile.shape, gain_tile.dtype),
             jax.ShapeDtypeStruct((2,) + seg_tile.shape, seg_tile.dtype),
+            jax.ShapeDtypeStruct((wide.shape[0], wide.shape[1] * wide.shape[2]), jnp.bfloat16),
         ],
         scratch_shapes=[
+            pltpu.VMEM((2, WIDE_ROWS) + wide.shape[1:], jnp.float32),
+            pltpu.VMEM((2, WIDE_ROWS, wide.shape[1] * wide.shape[2]), jnp.bfloat16),
             DMA((2, 2)), DMA((n_z,)), DMA((n_z,)), DMA((n_z,)), DMA((n_z,)), DMA((2, 2)), DMA((n_z,)), DMA((2, 2)),
-            DMA((n_d - 1, 4, 2)), DMA((n_d - 1, 4, 2)), DMA, DMA, DMA, DMA, DMA((5,)),
+            DMA((n_d - 1, 4, 2)), DMA((n_d - 1, 4, 2)), DMA, DMA, DMA, DMA, DMA((5,)), DMA((2,)), DMA((2,)),
         ],
         compiler_params=pltpu.CompilerParams(collective_id=1, has_side_effects=True),
         cost_estimate=pl.CostEstimate(flops=0, bytes_accessed=200_000_000, transcendentals=0),
         name="gather_in",
-    )(x_loc, w, v, gain_tile, seg_tile)
+    )(x_loc, w, v, gain_tile, seg_tile, wide)
 
 
 def share_resid_kernel(n_dp, n_z, part_ref, x_ref, w_ref, out, wall, got, buf, p_s, p_r, u_s, u_r, d_s, d_r, c_s, c_r, loc):
@@ -828,93 +857,65 @@
     )(part, resid, cot, gain)
 
 
-class Adam:
-    def __init__(self, count, sources, targets, views, bufs, sems, compute):
-        self.count, self.sources, self.targets, self.views = count, sources, targets, views
-        self.ins, self.outs = bufs[:4], bufs[4:]
-        self.in_sem, self.out_sem = sems
-        self.compute = compute
-
-    def each(self, i, slot, inward):
-        view_grad, view = self.views
-        for n in range(4):
-            if inward:
-                cut = view_grad if n == 0 else view
-                yield pltpu.make_async_copy(cut(self.sources[n], i), self.ins[n].at[slot], self.in_sem.at[slot, n])
-            else:
-                yield pltpu.make_async_copy(self.outs[n].at[slot], view(self.targets[n], i), self.out_sem.at[slot, n])
-
-    def start(self):
-        for copy in self.each(0, 0, True):
-            copy.start()
-
-    def run(self, low, high):
-        def one(i, carry):
-            slot = lax.rem(i, 2)
-
-            @pl.when(i + 1 < self.count)
-            def _():
-                for copy in self.each(i + 1, 1 - slot, True):
-                    copy.start()
-
-            for copy in self.each(i, slot, True):
-                copy.wait()
-
-            @pl.when(i >= 2)
-            def _():
-                for copy in self.each(i - 2, slot, False):
-                    copy.wait()
-
-            self.compute(slot)
-            for copy in self.each(i, slot, False):
-                copy.start()
-            return carry
-
-        lax.fori_loop(low, high, one, 0)
-
-    def end(self):
-        for i in range(max(0, self.count - 2), self.count):
-            for copy in self.each(i, i % 2, False):
-                copy.wait()
-
-
-def wide_compute(ins, outs):
-    width = ins[1].shape[-1]
-
-    def compute(slot):
-        for n in range(2):
-            grad = ins[0][slot, :, n * width : (n + 1) * width].astype(jnp.float32)
-            value = adam_update(ins[1][slot, :, n], grad, ins[2][slot, :, n], ins[3][slot, :, n])
-            outs[0][slot, :, n] = grad
-            for k in range(3):
-                outs[1 + k][slot, :, n] = value[k]
-
-    return compute
-
-
-def turned_compute(ins, outs):
-    def compute(slot):
-        grad = ins[0][slot].astype(jnp.float32).T
-        value = adam_update(ins[1][slot], grad, ins[2][slot], ins[3][slot])
-        outs[0][slot] = grad
-        for k in range(3):
-            outs[1 + k][slot] = value[k]
-
-    return compute
-
-
 WIDE_ROWS = 16
-TURNED_ROWS = 128
-
-
-def hand_out_kernel(n_dp, n_z, dn_ref, x_ref, dr_ref, gain_ref, gain2_ref, qt_ref, ot_ref, *refs):
-    wide_in, turned_in = refs[0:4], refs[4:8]
-    ig, gq, go, gains = refs[8:12]
-    wide_out, turned_out = refs[12:16], refs[16:20]
-    (got, buf, q_got, q_own, q_mid, q_put, q_fin, o_got, o_own, o_mid, o_put, o_fin, g_src, g_all) = refs[20:34]
-    wide_bufs, turned_bufs = refs[34:42], refs[42:50]
-    (p_s, p_r, i_s, i_r, q_s, q_r, qf_s, qf_r, o_s, o_r, of_s, of_r, g_s, g_r, q_loc, o_loc, loc,
-     a_in, a_out, b_in, b_out) = refs[50:]
+TURNED_ROWS = 256
+
+
+def adam_wide_kernel(grad_ref, w_ref, m_ref, v_ref, g_out, w_out, m_out, v_out):
+    width = w_ref.shape[-1]
+    for n in range(2):
+        grad = grad_ref[:, n * width : (n + 1) * width].astype(jnp.float32)
+        weight, first, second = adam_update(w_ref[:, n], grad, m_ref[:, n], v_ref[:, n])
+        g_out[:, n] = grad
+        w_out[:, n] = weight
+        m_out[:, n] = first
+        v_out[:, n] = second
+
+
+def adam_turned_kernel(grad_ref, w_ref, m_ref, v_ref, g_out, w_out, m_out, v_out):
+    grad = grad_ref[...].astype(jnp.float32).T
+    weight, first, second = adam_update(w_ref[...], grad, m_ref[...], v_ref[...])
+    g_out[...] = grad
+    w_out[...] = weight
+    m_out[...] = first
+    v_out[...] = second
+
+
+def adam_call(kernel, grid, grad_spec, spec, arrays):
+    shape = jax.ShapeDtypeStruct(arrays[1].shape, jnp.float32)
+    return pl.pallas_call(
+        kernel,
+        grid=(grid,),
+        in_specs=[grad_spec] + [spec] * 3,
+        out_specs=[spec] * 4,
+        out_shape=[shape] * 4,
+        cost_estimate=pl.CostEstimate(flops=20 * shape.size, bytes_accessed=30 * shape.size, transcendentals=0),
+    )(*arrays)
+
+
+def adam_wide(*arrays):
+    rows, _, width = arrays[1].shape
+    return adam_call(
+        adam_wide_kernel, rows // WIDE_ROWS,
+        pl.BlockSpec((WIDE_ROWS, 2 * width), lambda i: (i, 0)),
+        pl.BlockSpec((WIDE_ROWS, 2, width), lambda i: (i, 0, 0)),
+        arrays,
+    )
+
+
+def adam_turned(*arrays):
+    rows, cols = arrays[1].shape
+    return adam_call(
+        adam_turned_kernel, rows // TURNED_ROWS,
+        pl.BlockSpec((cols, TURNED_ROWS), lambda i: (0, i)),
+        pl.BlockSpec((TURNED_ROWS, cols), lambda i: (i, 0)),
+        arrays,
+    )
+
+
+def hand_out_kernel(n_dp, n_z, dn_ref, x_ref, dr_ref, gain_ref, gain2_ref, qt_ref, ot_ref, ig, gq, go, gains,
+                    got, buf, q_got, q_own, q_mid, q_put, q_fin, o_got, o_own, o_mid, o_put, o_fin, g_src, g_all,
+                    p_s, p_r, i_s, i_r, q_s, q_r, qf_s, qf_r, o_s, o_r, of_s, of_r, g_s, g_r, q_loc, o_loc, loc):
     d, z, pair, c = place()
     n_d = n_dp // 2
     total = n_dp * n_z
@@ -927,18 +928,6 @@
     o_rows, o_cols = o_fin.shape[1:]
     relay = n_d == 4
 
-    wide = Adam(
-        wide_in[1].shape[0] // WIDE_ROWS, wide_in, wide_out,
-        (lambda ref, i: ref.at[pl.ds(pl.multiple_of(i * WIDE_ROWS, WIDE_ROWS), WIDE_ROWS)],) * 2,
-        wide_bufs, (a_in, a_out), wide_compute(wide_bufs[:4], wide_bufs[4:]),
-    )
-    turned = Adam(
-        turned_in[1].shape[0] // TURNED_ROWS, turned_in, turned_out,
-        (lambda ref, i: ref.at[:, pl.ds(pl.multiple_of(i * TURNED_ROWS, TURNED_ROWS), TURNED_ROWS)],
-         lambda ref, i: ref.at[pl.ds(pl.multiple_of(i * TURNED_ROWS, TURNED_ROWS), TURNED_ROWS)]),
-        turned_bufs, (b_in, b_out), turned_compute(turned_bufs[:4], turned_bufs[4:]),
-    )
-
     class First:
         def __init__(self, src, rows, cols, bufs, sems, spare):
             self.src, self.rows, self.cols, self.spare = src, rows, cols, spare
@@ -1048,8 +1037,6 @@
             for b in range(2):
                 for copy in one.loads(b, core):
                     copy.start()
-    turned.start()
-    wide.start()
     greet_all(n_dp, n_z, d, z)
 
     mine = pl.ds(pl.multiple_of(c * half, half), half)
@@ -1093,6 +1080,7 @@
             for b in range(2):
                 for copy in one.loads(b, core):
                     copy.wait()
+    nothing = lambda: None
     per = quarter // 16
     lax.fori_loop(0, per, rows_of, 0)
     o_first.middle(0, lambda: row_send(0, False))
@@ -1116,27 +1104,18 @@
 
     lax.fori_loop(1, total, send_gain, 0)
 
-    def share(adam, n, parts):
-        return lambda: adam.run(n * adam.count // parts, (n + 1) * adam.count // parts)
-
-    share(turned, 0, 2)()
-    o_first.total(0, share(wide, 0, 8))
-    q_first.middle(0, share(wide, 1, 8))
-    share(turned, 1, 2)()
-    o_first.total(1, share(wide, 2, 8))
-    share(wide, 3, 8)()
-    q_first.middle(1, share(wide, 4, 8))
-    share(wide, 5, 8)()
-    q_first.total(0, share(wide, 6, 8))
-    q_first.total(1, share(wide, 7, 8))
+    o_first.total(0, nothing)
+    q_first.middle(0, nothing)
+    o_first.total(1, nothing)
+    q_first.middle(1, nothing)
+    q_first.total(0, nothing)
+    q_first.total(1, nothing)
 
     o_first.final()
     value = o_fin[0].astype(jnp.float32)
     for zs in range(1, n_z):
         value = value + o_fin[zs].astype(jnp.float32)
     go[...] = value.T
-    turned.end()
-    wide.end()
 
     many = g_all.at[pl.ds(0, total - 1)]
     gain_copy = remote(many, many, g_s, g_r, (d, z))
@@ -1173,7 +1152,7 @@
     lax.fori_loop(0, q_rows // 16, last, 0)
 
 
-def hand_out(dn, x, dr, gain, gain2, qt, ot, wide, turned, n_dp, n_z):
+def hand_out(dn, x, dr, gain, gain2, qt, ot, n_dp, n_z):
     full, width = x.shape
     n_d = n_dp // 2
     total = n_dp * n_z
@@ -1188,34 +1167,28 @@
             pltpu.VMEM((2 * rows, 2 * cols), b16), pltpu.VMEM((2, 2, rows, cols), b16), pltpu.VMEM((n_z, rows, cols), b16),
         ]
 
-    wide_shape = (2, WIDE_ROWS) + wide[1].shape[1:]
-    turned_shape = (2, TURNED_ROWS, turned[1].shape[1])
     weight_sems = [DMA((n_d - 1, 2, 2)), DMA((n_d - 1, 2, 2)), DMA((2, 2)), DMA((n_z,))]
     return pl.pallas_call(
         functools.partial(hand_out_kernel, n_dp, n_z),
-        in_specs=[VMEM_SPEC] * 5 + [ANY_SPEC] * 10,
-        out_specs=[ANY_SPEC] + [VMEM_SPEC] * 3 + [ANY_SPEC] * 8,
+        in_specs=[VMEM_SPEC] * 5 + [ANY_SPEC] * 2,
+        out_specs=[ANY_SPEC] + [VMEM_SPEC] * 3,
         out_shape=[
             jax.ShapeDtypeStruct((2, full // 4, width), b16),
             jax.ShapeDtypeStruct((q_rows, q_cols), f32),
             jax.ShapeDtypeStruct((o_cols, o_rows), f32),
             jax.ShapeDtypeStruct((16, 128), f32),
-        ]
-        + [jax.ShapeDtypeStruct(wide[1].shape, f32)] * 4
-        + [jax.ShapeDtypeStruct(turned[1].shape, f32)] * 4,
+        ],
         scratch_shapes=[
             pltpu.VMEM((full // 2, width), b16), pltpu.VMEM((full // 2, width), b16),
             *weight_bufs(q_rows, q_cols), *weight_bufs(o_rows, o_cols),
             pltpu.VMEM((16, width), f32), pltpu.VMEM((total, 16, 128), f32),
-            pltpu.VMEM((2, WIDE_ROWS, wide[0].shape[1]), b16), *[pltpu.VMEM(wide_shape, f32)] * 7,
-            pltpu.VMEM((2, turned[0].shape[0], TURNED_ROWS), b16), *[pltpu.VMEM(turned_shape, f32)] * 7,
             DMA, DMA, DMA((2,)), DMA((2,)), *weight_sems, *weight_sems, DMA, DMA,
-            DMA((2, 2, 2)), DMA((2, 2, 2)), DMA((4,)), DMA((2, 4)), DMA((2, 4)), DMA((2, 4)), DMA((2, 4)),
+            DMA((2, 2, 2)), DMA((2, 2, 2)), DMA((4,)),
         ],
         compiler_params=pltpu.CompilerParams(collective_id=5, has_side_effects=True, vmem_limit_bytes=58 * 1024 * 1024),
         cost_estimate=pl.CostEstimate(flops=0, bytes_accessed=300_000_000, transcendentals=0),
         name="hand_out",
-    )(dn, x, dr, gain, gain2, qt, ot, *wide, *turned)
+    )(dn, x, dr, gain, gain2, qt, ot)
 
 
 def rms_forward(values, gain_wide):
@@ -1281,14 +1254,14 @@
     gain_line = jnp.concatenate([attn_gain, mlp_gain]).astype(jnp.bfloat16).astype(jnp.float32)
     gain_tile = jnp.pad(gain_line[None], ((0, 7), (0, LANES - 2 * owned)))
     seg_tile = jnp.pad(segment_ids, ((0, 8 - seqs_here), (0, 0)))
-    gate_up_here = gate_up_weight.astype(jnp.bfloat16).reshape(-1, 2 * unit_count)
     down_rows = lax.all_gather(down_weight.astype(jnp.bfloat16), "dp", axis=1, tiled=True)
-    rows_in, qkv_cols, out_line, gain_all, seg_all = gather_in(
+    rows_in, qkv_cols, out_line, gain_all, seg_all, gate_up_here = gather_in(
         block_input,
         qkv_weight.astype(jnp.bfloat16),
         out_weight.astype(jnp.bfloat16).T,
         gain_tile,
         seg_tile,
+        gate_up_weight,
         n_dp,
         n_z,
     )
@@ -1320,9 +1293,7 @@
     d_up = d_hidden * active
     d_gate_up16 = jnp.concatenate([d_gate, d_up], 1).astype(jnp.bfloat16)
     down_part = jnp.dot(hidden16, down_rows, preferred_element_type=jnp.float32)
-    down_here = lax.psum_scatter(
-        down_part.astype(jnp.bfloat16).reshape(resid_all.shape), "seq", scatter_dimension=1, tiled=True
-    )
+    down16 = down_part.astype(jnp.bfloat16).reshape(resid_all.shape)
     gate_up_term = contract_rows(normed_two, d_gate_up16).astype(jnp.bfloat16)
     gate_up_sum = lax.psum_scatter(gate_up_term, "dp", scatter_dimension=0, tiled=True)
     down_term = contract_rows(cot_rows, hidden16).astype(jnp.bfloat16)
@@ -1331,7 +1302,14 @@
     d_resid16, gain_two_part = sum_line(
         d_normed_two.reshape(resid_all.shape), resid_all, cot_all, gain_two, n_z
     )
-    down_here = down_here.astype(jnp.float32)
+    down16, _ = lax.optimization_barrier((down16, d_resid16))
+    pieces = [
+        lax.dynamic_slice_in_dim(down16, (z_here + o) % n_z * local_len, local_len, 1)
+        for o in range(n_z)
+    ]
+    for o in range(1, n_z):
+        pieces[o] = lax.ppermute(pieces[o], "seq", [(i, (i + o) % n_z) for i in range(n_z)])
+    down_here = sum(piece.astype(jnp.float32) for piece in pieces)
     resid_here = lax.dynamic_slice_in_dim(resid_all, z_here * local_len, local_len, 1)
     output = (resid_here.astype(jnp.float32) + down_here).astype(jnp.bfloat16)
     d_attended = jnp.dot(d_resid16, out_rows, preferred_element_type=jnp.float32).astype(jnp.bfloat16)
@@ -1339,7 +1317,7 @@
     d_normed_one = times_transpose(d_qkv16, qkv_cols).astype(jnp.bfloat16)
     qkv_term = contract_rows(normed_one, d_qkv16).astype(jnp.bfloat16)
     out_term = contract_rows(d_resid16, attended16).astype(jnp.bfloat16)
-    input_grad, grad_qkv, grad_out, gain_sums, *updated = hand_out(
+    input_grad, grad_qkv, grad_out, gain_sums = hand_out(
         d_normed_one,
         rows_in,
         d_resid16,
@@ -1347,12 +1325,15 @@
         gain_two_part,
         qkv_term,
         out_term,
-        (gate_up_sum, gate_up_weight, first_gate_up, second_gate_up),
-        (down_sum, down_weight, first_down, second_down),
         n_dp,
         n_z,
     )
-    grad_gate_up, w_gu, m_gu, v_gu, grad_down, w_down, m_down, v_down = updated
+    grad_gate_up, w_gu, m_gu, v_gu = adam_wide(
+        gate_up_sum, gate_up_weight, first_gate_up, second_gate_up
+    )
+    grad_down, w_down, m_down, v_down = adam_turned(
+        down_sum, down_weight, first_down, second_down
+    )
     flat = lax.axis_index("dp") * n_z + z_here
     gain_sums = lax.dynamic_slice(
         jnp.sum(gain_sums.reshape(2, 8, LANES), axis=1), (0, flat * owned % LANES), (2, owned)

time: 796 us -> 727 us (0.913)
  the two profiles are of different devices: /device:TPU:9 before, /device:TPU:13 now
where the time goes in v6:
time: 727 us; the launch traced here: 720 us
  Pallas kernels  506 us (70%)
  matrix products  156 us (21%)
  other arithmetic  23.7 us (3%)
  local copies, waits for them, and re-layouts  14.7 us (2%)
  between operations  14.7 us (2%)
    pallas_call x1, Pallas kernels, hand_out(): pl.pallas_call(functools.partial(hand_out_kernel, n_dp, n_z), in_specs=[V...  131 us
    pallas_call x1, Pallas kernels, share_resid(): pl.pallas_call(functools.partial(share_resid_kernel, n_dp, n_z), in_specs...  110 us
    pallas_call x1, Pallas kernels, gather_in(): pl.pallas_call(functools.partial(gather_in_kernel, n_dp, n_z), in_specs=[...  91 us
    pallas_call x1, Pallas kernels, sum_line(): pl.pallas_call(functools.partial(sum_line_kernel, n_z), in_specs=[VMEM_SP...  86.9 us
    dot_general x4, matrix products, times_transpose(): lax.dot_general(left, right, (((1,), (1,)), ((), ())), preferred_element_...  60.1 us
    dot_general x4, matrix products, contract_rows(): lax.dot_general(left, right, (((0,), (0,)), ((), ())), preferred_element_...  50.9 us
    pallas_call x1, Pallas kernels, attn_forward(): pl.pallas_call(functools.partial(attn_gather_kernel, n_dp, pairs, Q_ROWS,...  38.1 us
    pallas_call x2, Pallas kernels, adam_call(): pl.pallas_call(kernel, grid=(grid,), in_specs=[grad_spec] + [spec] * 3, o...  27.6 us
  transfers between devices with their start and end apart: 7, of which 0 were waited for; matrix products, arithmetic and copies ran while one was open for 20% of the time, Pallas kernels for 55%

profile of v6, /device:TPU:13, one launch (start us, length us, event | category | flops | bytes accessed | tf_op | source)
XLA Modules:
  0.0 719.9 jit_solution(11285676984011637064)
XLA Ops:
  7.2 0.0 all-gather.5.cloned.1.call-start
  7.2 1.9 copy.49
  9.1 1.9 convert_element_type.114.w_ref
  11.1 0.7 convert_bitcast_fusion.1
  11.7 0.7 fusion.17.g_ref
  12.4 1.3 pad.12.s_ref
  13.7 91.0 %gather_in.1 = (bf16[512,2048]{1,0:T(8,128)(2,1)}, bf16[2048,1536]{1,0:T(8,128)(2,1)}, bf16[512,1024]{1,0:T(8,128)(2,1)}, f32[32,8,128]{2,1,0:T(8,128)}, s32[2,8...) custom-call(bf16[2,128,2048]{2,1,0:T(8,128)(2,1)} %x_ref.1, bf16[256,768]{1,0:T(8,128)(2,1)} %convert_element_type.114.w_ref, ...), custom_call_target="tpu_custom_call" | custom-call | bytes 200000000 | tf_op jit(solution)/shard_map/gather_in/pallas_call | solution.py:528
  104.7 0.0 all-gather.5.cloned.1.call-update
  104.7 0.0 all-gather.3.cloned.1.call-start
  104.8 2.8 convert_element_type.127
  107.6 0.0 all-gather.3.cloned.1.call-update
  107.6 0.0 reduce-scatter.5.cloned.1.call-start
  107.7 1.1 slice_reduce_fusion.1
  108.8 0.1 mul.228
  108.8 0.1 mul.238
  108.9 0.7 constant_dynamic-slice_fusion.4
  109.7 0.2 convert_reduce_fusion
  109.9 1.0 fusion.13
  110.9 1.0 maximum_bitcast_fusion.cos_ref
  111.9 1.0 maximum_bitcast_fusion.1.sin_ref
  112.9 0.5 fusion.4
  113.4 8.1 %fusion.10.qkv_ref = f32[512,1536]{1,0:T(8,128)} fusion(bf16[2048,1536]{1,0:T(8,128)(2,1)} %get-tuple-element.56, bf16[512,2048]{1,0:T(8,128)(2,1)S(1)} %copy-done.1, f32[2048]{0:T(1024)S(1)} %mul.228, f32[512]{0:T(512)S(1)} %add_rsqrt_fusion), kind=kOutput, calls=%fused_computation.32 | convolution fusion | flops 3225419776 | bytes 11544576 | tf_op jit(solution)/shard_map/dot_general | solution.py:1275
  121.5 0.6 reshape.371.seg_row_ref
  122.1 0.8 reshape.370.seg_col_ref
  122.9 38.1 %attn_forward.1 = (bf16[512,1536]{1,0:T(8,128)(2,1)}, f32[512,512]{1,0:T(8,128)}, bf16[512,1024]{1,0:T(8,128)(2,1)}, bf16[2048,1024]{1,0:T(8,128)(2,1)}) custom-call(f32[512,1536]{1,0:T(8,128)} %fusion.10.qkv_ref, f32[512,128]{1,0:T(8,128)} %maximum_bitcast_fusion.cos_ref, f32[512,128]{1,0:T(8,128)} %maximum_bitcast_fusion.1.sin_ref, ...), custom_call_target="tpu_custom_call" | custom-call | flops 2147483648 | bytes 150000000 | tf_op jit(solution)/shard_map/attn_forward/pallas_call | solution.py:217
  161.0 6.2 convolution_convert_fusion.5.part_ref
  167.2 110.0 %share_resid.1 = (bf16[2,512,2048]{2,1,0:T(8,128)(2,1)}, bf16[2048,4096]{1,0:T(8,128)(2,1)}) custom-call(bf16[512,2048]{1,0:T(8,128)(2,1)} %convolution_convert_fusion.5.part_ref, bf16[512,2048]{1,0:T(8,128)(2,1)} %get-tuple-element.54.x_ref, bf16[256,4096]{1,0:T(8,128)(2,1)} %get-tuple-element.61.w_ref), custom_call_target="tpu_custom_call" | custom-call | bytes 200000000 | tf_op jit(solution)/shard_map/share_resid/pallas_call | solution.py:684
  277.2 3.2 multiply_reduce_fusion
  280.5 0.2 copy-done
  280.6 1.0 fusion.1
  281.7 2.0 copy-done.3
  283.7 22.2 %fusion.26 = f32[1024,4096]{1,0:T(8,128)} fusion(bf16[1024,2048]{1,0:T(8,128)(2,1)S(1)} %fusion.1, bf16[2048,4096]{1,0:T(8,128)(2,1)} %get-tuple-element.63), kind=kOutput, calls=%fused_computation.73 | convolution fusion | flops 17179869184 | bytes 37748736 | tf_op jit(solution)/shard_map/dot_general | solution.py:1284
  305.9 22.2 %multiply_convert_fusion.1 = (bf16[1024,2048]{1,0:T(8,128)(2,1)}, bf16[1024,2048]{1,0:T(8,128)(2,1)}, bf16[1024,2048]{1,0:T(8,128)(2,1)}) fusion(f32[1024,4096]{1,0:T(8,128)} %fusion.26, bf16[1024,2048]{1,0:T(8,128)(2,1)} %bitcast.56, bf16[2048,2048]{1,0:T(8,128)(2,1)} %all-gather.3.cloned.1.call-done), kind=kOutput, calls=%fused_computation.6 | convolution fusion | flops 8621391872 | bytes 41943040 | tf_op jit(solution)/shard_map/dot_general | solution.py:1218
  328.1 14.0 %convolution_convert_fusion.1 = bf16[2048,2048]{1,0:T(8,128)(2,1)} fusion(bf16[1024,2048]{1,0:T(8,128)(2,1)} %bitcast.57, bf16[1024,2048]{1,0:T(8,128)(2,1)} %get-tuple-element.100), kind=kOutput, calls=%fused_computation.11 | convolution fusion | flops 8594128896 | bytes 16777216 | tf_op jit(solution)/shard_map/dot_general | solution.py:1212
  342.1 0.0 reduce-scatter.5.cloned.1.call-update
  342.1 0.0 reduce-scatter.3.cloned.1.call-start
  342.2 25.4 %convolution_convert_fusion = bf16[2048,4096]{1,0:T(8,128)(2,1)} fusion(bf16[1024,2048]{1,0:T(8,128)(2,1)} %copy-done.3, bf16[1024,2048]{1,0:T(8,128)(2,1)} %get-tuple-element.99, bf16[1024,2048]{1,0:T(8,128)(2,1)} %get-tuple-element.98), kind=kOutput, calls=%fused_computation | convolution fusion | flops 17205035008 | bytes 29360128 | tf_op jit(solution)/shard_map/dot_general | solution.py:1212
  367.6 0.0 reduce-scatter.3.cloned.1.call-update
  367.7 0.7 reshape_squeeze.7.gain_ref
  368.3 0.7 reshape_squeeze.6.gain_ref
  369.0 24.3 %fusion.7 = bf16[1024,2048]{1,0:T(8,128)(2,1)} fusion(bf16[2048,4096]{1,0:T(8,128)(2,1)} %get-tuple-element.63, bf16[1024,2048]{1,0:T(8,128)(2,1)} %get-tuple-element.99, bf16[1024,2048]{1,0:T(8,128)(2,1)} %get-tuple-element.98), kind=kOutput, calls=%fused_computation.19 | convolution fusion | flops 17198743552 | bytes 29360128 | tf_op jit(solution)/shard_map/dot_general | solution.py:1218
  393.3 86.9 %sum_line.1 = (bf16[512,2048]{1,0:T(8,128)(2,1)}, f32[8,2048]{1,0:T(8,128)}) custom-call(bf16[2,512,2048]{2,1,0:T(8,128)(2,1)} %bitcast.58, bf16[2,512,2048]{2,1,0:T(8,128)(2,1)} %get-tuple-element.62.resid_all, bf16[2,512,2048]{2,1,0:T(8,128)(2,1)} %all-gather.5.cloned.1.call-done.cot_all, f32[1,2048]{1,0:T(1,128)} %reshape_squeeze.6.gain_ref), custom_call_target="tpu_custom_call" | custom-call | bytes 200000000 | tf_op jit(solution)/shard_map/sum_line/pallas_call | solution.py:844
  480.2 11.5 %convolution_convert_fusion.4 = bf16[1024,2048]{1,0:T(8,128)(2,1)S(1)} fusion(bf16[1024,2048]{1,0:T(8,128)(2,1)S(1)} %copy-done.28, bf16[2048,2048]{1,0:T(8,128)(2,1)} %all-gather.3.cloned.1.call-done), kind=kOutput, calls=%fused_computation.21 | convolution fusion | flops 8592031744 | bytes 16777216 | tf_op jit(solution)/shard_map/dot_general | solution.py:1295
  491.7 1.7 constant_dynamic-slice_fusion.2
  493.4 2.6 collective-permute-start.2
  496.0 2.2 collective-permute-start.1
  498.1 4.4 convolution_convert_fusion.3.ot_ref
  502.6 3.3 convolution_convert_fusion.7.d_out_ref
  505.9 20.7 %attn_backward.1 = bf16[512,1536]{1,0:T(8,128)(2,1)} custom-call(bf16[512,1536]{1,0:T(8,128)(2,1)} %get-tuple-element.67.turned_ref, bf16[512,1024]{1,0:T(8,128)(2,1)} %convolution_convert_fusion.7.d_out_ref, f32[512,512]{1,0:T(8,128)} %get-tuple-element.68.lse_ref, f32[512,128]{1,0:T(8,128)} %maximum_bitcast_fusion.cos_ref, ...), custom_call_target="tpu_custom_call" | custom-call | flops 5368709120 | bytes 4718592 | tf_op jit(solution)/shard_map/attn_backward/pallas_call | solution.py:243
  526.6 7.1 convolution_convert_fusion.2.qt_ref
  533.7 7.5 %convolution_convert_fusion.6.dn_ref = bf16[512,2048]{1,0:T(8,128)(2,1)} fusion(bf16[512,1536]{1,0:T(8,128)(2,1)S(1)} %copy-done.27, bf16[2048,1536]{1,0:T(8,128)(2,1)} %get-tuple-element.56), kind=kOutput, calls=%fused_computation.23 | convolution fusion | flops 3222274048 | bytes 9961472 | tf_op jit(solution)/shard_map/dot_general | solution.py:1218
  541.3 131.5 %hand_out.1 = (bf16[2,128,2048]{2,1,0:T(8,128)(2,1)}, f32[256,768]{1,0:T(8,128)}, f32[512,256]{1,0:T(8,128)}, f32[16,128]{1,0:T(8,128)}) custom-call(bf16[512,2048]{1,0:T(8,128)(2,1)} %convolution_convert_fusion.6.dn_ref, bf16[512,2048]{1,0:T(8,128)(2,1)} %get-tuple-element.54.x_ref, bf16[512,2048]{1,0:T(8,128)(2,1)} %get-tuple-element.65.dr_ref, ...), custom_call_target="tpu_custom_call" | custom-call | bytes 300000000 | tf_op jit(solution)/shard_map/hand_out/pallas_call | solution.py:1171
  672.8 0.9 bitcast_reduce_fusion
  673.7 0.1 constant_dynamic-slice_fusion.3
  673.8 0.6 multiply_subtract_fusion.2
  674.3 2.4 multiply_subtract_fusion.1
  676.8 1.8 multiply_subtract_fusion
  678.6 4.1 add_convert_fusion
  682.6 9.3 %shard_map.405 = (f32[2048,256]{1,0:T(8,128)}, f32[2048,256]{1,0:T(8,128)}, f32[2048,256]{1,0:T(8,128)}, f32[2048,256]{1,0:T(8,128)}) custom-call(bf16[256,2048]{1,0:T(8,128)(2,1)} %reduce-scatter.5.cloned.1.call-done.grad_ref, f32[2048,256]{1,0:T(8,128)} %w_ref.3, f32[2048,256]{1,0:T(8,128)} %m_ref.3, f32[2048,256]{1,0:T(8,128)} %v_ref.3), custom_call_target="tpu_custom_call" | custom-call | flops 10485760 | bytes 15728640 | tf_op jit(solution)/shard_map/pallas_call | solution.py:886
  692.0 0.0 reduce-scatter.3.cloned.1.call-done.grad_ref
  692.0 18.3 %shard_map.404 = (f32[256,2,2048]{2,1,0:T(2,128)}, f32[256,2,2048]{2,1,0:T(2,128)}, f32[256,2,2048]{2,1,0:T(2,128)}, f32[256,2,2048]{2,1,0:T(2,128)}) custom-call(bf16[256,4096]{1,0:T(8,128)(2,1)} %reduce-scatter.3.cloned.1.call-done.grad_ref, f32[256,2,2048]{2,1,0:T(2,128)} %w_ref.2, f32[256,2,2048]{2,1,0:T(2,128)} %m_ref.2, f32[256,2,2048]{2,1,0:T(2,128)} %v_ref.2), custom_call_target="tpu_custom_call" | custom-call | flops 20971520 | bytes 31457280 | tf_op jit(solution)/shard_map/pallas_call | solution.py:886
  710.2 1.0 copy.55
  711.2 0.9 copy.56
  712.1 0.8 copy.57
  (68 shorter events, 0.2 us)
Async XLA Ops:
  7.2 298.7 %all-gather.5.cloned.1.call-start = ((), (), s32[]{:S(2)}) async-start(), calls=%async_computation.3 | async-start | bytes 5242880 | tf_op jit(solution)/shard_map/all_gather | solution.py:1269
  104.7 8.2 %copy-start.1 = (bf16[512,2048]{1,0:T(8,128)(2,1)S(1)}, bf16[512,2048]{1,0:T(8,128)(2,1)}, u32[]{:S(2)}) copy-start(bf16[512,2048]{1,0:T(8,128)(2,1)} %get-tuple-element.54.x_ref) | copy-start | bytes 6291460
  104.7 201.2 %all-gather.3.cloned.1.call-start = ((), (), s32[]{:S(2)}) async-start(), calls=%async_computation.2 | async-start | bytes 9437184 | tf_op jit(solution)/shard_map/all_gather | solution.py:1257
  107.6 575.0 %reduce-scatter.5.cloned.1.call-start = ((), (), s32[]{:S(2)}) async-start(), calls=%async_computation.5 | async-start | bytes 9437184 | tf_op jit(solution)/shard_map/reduce_scatter | solution.py:1300
  108.8 12.6 %copy-start.15 = (f32[2048]{0:T(1024)}, f32[2048]{0:T(1024)S(1)}, u32[]{:S(2)}) copy-start(f32[2048]{0:T(1024)S(1)} %mul.228) | copy-start | bytes 24580
  113.4 8.1 %copy-start.17 = (f32[512]{0:T(512)}, f32[512]{0:T(512)S(1)}, u32[]{:S(2)}) copy-start(f32[512]{0:T(512)S(1)} %add_rsqrt_fusion) | copy-start | bytes 6148
  277.2 3.5 copy-start
  281.7 2.0 copy-start.3
  342.1 349.8 %reduce-scatter.3.cloned.1.call-start = ((), (), s32[]{:S(2)}) async-start(), calls=%async_computation.4 | async-start | bytes 18874368 | tf_op jit(solution)/shard_map/reduce_scatter | solution.py:1298
  393.3 86.9 %copy-start.28 = (bf16[1024,2048]{1,0:T(8,128)(2,1)S(1)}, bf16[1024,2048]{1,0:T(8,128)(2,1)}, u32[]{:S(2)}) copy-start(bf16[1024,2048]{1,0:T(8,128)(2,1)} %get-tuple-element.100) | copy-start | bytes 12582916
  491.7 10.9 %copy-start.4 = (bf16[1024,2048]{1,0:T(8,128)(2,1)}, bf16[1024,2048]{1,0:T(8,128)(2,1)S(1)}, u32[]{:S(2)}) copy-start(bf16[1024,2048]{1,0:T(8,128)(2,1)S(1)} %convolution_convert_fusion.4) | copy-start | bytes 12582916
  491.7 6.5 copy-start.9
  491.7 6.4 copy-start.26
  493.4 185.2 %collective-permute-start = (bf16[2,128,2048]{2,1,0:T(8,128)(2,1)}, bf16[2,128,2048]{2,1,0:T(8,128)(2,1)S(1)}, u32[]{:S(2)}, u32[]{:S(2)}) collective-permute-start(bf16[2,128,2048]{2,1,0:T(8,128)(2,1)} %get-tuple-element.101), channel_id=1, source_target_pairs={{0,1},{1,2},{2,3},{3,0},{4,5},{5,6},{6,7},{7,4},{8,9},{9,10},{10,1... | collective-permute-start | bytes 3145736 | tf_op jit(solution)/shard_map/ppermute | solution.py:1311
  493.4 185.2 %collective-permute-start.2 = (bf16[2,128,2048]{2,1,0:T(8,128)(2,1)}, bf16[2,128,2048]{2,1,0:T(8,128)(2,1)}, u32[]{:S(2)}, u32[]{:S(2)}) collective-permute-start(bf16[2,128,2048]{2,1,0:T(8,128)(2,1)} %get-tuple-element.102), channel_id=1, source_target_pairs={{0,3},{1,0},{2,1},{3,2},{4,7},{5,4},{6,5},{7,6},{8,11},{9,8},{10,9... | collective-permute-start | bytes 3145736 | tf_op jit(solution)/shard_map/ppermute | solution.py:1311
  496.0 6.6 copy-start.25
  496.0 182.6 %collective-permute-start.1 = (bf16[2,128,2048]{2,1,0:T(8,128)(2,1)}, bf16[2,128,2048]{2,1,0:T(8,128)(2,1)}, u32[]{:S(2)}, u32[]{:S(2)}) collective-permute-start(bf16[2,128,2048]{2,1,0:T(8,128)(2,1)} %get-tuple-element.103), channel_id=1, source_target_pairs={{0,2},{1,3},{2,0},{3,1},{4,6},{5,7},{6,4},{7,5},{8,10},{9,11},{10,... | collective-permute-start | bytes 3145736 | tf_op jit(solution)/shard_map/ppermute | solution.py:1311
  505.9 20.7 %copy-start.2 = (bf16[512,2048]{1,0:T(8,128)(2,1)S(1)}, bf16[512,2048]{1,0:T(8,128)(2,1)}, u32[]{:S(2)}) copy-start(bf16[512,2048]{1,0:T(8,128)(2,1)} %get-tuple-element.54.x_ref) | copy-start | bytes 6291460
  505.9 20.7 %copy-start.16 = (f32[2048]{0:T(1024)S(1)}, f32[2048]{0:T(1024)}, u32[]{:S(2)}) copy-start(f32[2048]{0:T(1024)} %copy-done.15) | copy-start | bytes 24580
  505.9 20.7 %copy-start.18 = (f32[512]{0:T(512)S(1)}, f32[512]{0:T(512)}, u32[]{:S(2)}) copy-start(f32[512]{0:T(512)} %copy-done.17) | copy-start | bytes 6148
  526.6 7.1 copy-start.27
  541.2 132.5 %copy-start.19 = (f32[64]{0:T(128)S(1)}, f32[64]{0:T(128)}, u32[]{:S(2)}) copy-start(f32[64]{0:T(128)} %param.27) | copy-start | bytes 772
  541.2 132.5 %copy-start.20 = (f32[64]{0:T(128)S(1)}, f32[64]{0:T(128)}, u32[]{:S(2)}) copy-start(f32[64]{0:T(128)} %param.24) | copy-start | bytes 772
  541.2 132.5 %copy-start.21 = (f32[64]{0:T(128)S(1)}, f32[64]{0:T(128)}, u32[]{:S(2)}) copy-start(f32[64]{0:T(128)} %param.33) | copy-start | bytes 772
  541.2 132.5 %copy-start.22 = (f32[64]{0:T(128)S(1)}, f32[64]{0:T(128)}, u32[]{:S(2)}) copy-start(f32[64]{0:T(128)} %param.39) | copy-start | bytes 772
  541.2 132.5 %copy-start.23 = (f32[64]{0:T(128)S(1)}, f32[64]{0:T(128)}, u32[]{:S(2)}) copy-start(f32[64]{0:T(128)} %param.36) | copy-start | bytes 772
  541.2 132.5 %copy-start.24 = (f32[64]{0:T(128)S(1)}, f32[64]{0:T(128)}, u32[]{:S(2)}) copy-start(f32[64]{0:T(128)} %param.30) | copy-start | bytes 772
  541.2 133.1 %copy-start.7 = (f32[512,256]{1,0:T(8,128)S(1)}, f32[512,256]{1,0:T(8,128)}, u32[]{:S(2)}) copy-start(f32[512,256]{1,0:T(8,128)} %param.26) | copy-start | bytes 1572868
  541.2 133.1 %copy-start.13 = (f32[512,256]{1,0:T(8,128)S(1)}, f32[512,256]{1,0:T(8,128)}, u32[]{:S(2)}) copy-start(f32[512,256]{1,0:T(8,128)} %param.32) | copy-start | bytes 1572868
  541.2 133.1 %copy-start.14 = (f32[512,256]{1,0:T(8,128)S(1)}, f32[512,256]{1,0:T(8,128)}, u32[]{:S(2)}) copy-start(f32[512,256]{1,0:T(8,128)} %param.38) | copy-start | bytes 1572868
  672.7 4.0 copy-start.5
  672.8 4.0 copy-start.6
  672.8 4.0 copy-start.11
  672.8 4.0 copy-start.12
  691.9 18.3 %copy-start.10 = (bf16[2,128,2048]{2,1,0:T(8,128)(2,1)S(1)}, bf16[2,128,2048]{2,1,0:T(8,128)(2,1)}, u32[]{:S(2)}) copy-start(bf16[2,128,2048]{2,1,0:T(8,128)(2,1)} %get-tuple-element.142) | copy-start | bytes 3145732
  691.9 20.2 %copy-start.8 = (f32[512,256]{1,0:T(8,128)S(1)}, f32[512,256]{1,0:T(8,128)}, u32[]{:S(2)}) copy-start(f32[512,256]{1,0:T(8,128)} %get-tuple-element.145) | copy-start | bytes 1572868
Sparse Core Ops, SparseCore 0:
  104.8 80.2 all-gather.4
  187.6 91.3 all-gather.2
  342.3 70.5 reduce-scatter.4
  416.2 116.1 reduce-scatter.2

commit v7 on v6

--- a/solution.py
+++ b/solution.py
@@ -703,18 +703,36 @@
 CHUNKS = 8
 
 
-def sum_line_kernel(n_z, part_ref, resid_all, cot_all, gain_ref, d_out, gain_out, got, buf, resid_ref, cot_ref,
-                    s_s, s_r, p_s, p_r, loc, rows_sem):
+def sum_line_kernel(n_z, part_ref, resid_all, cot_all, gain_ref, hid_ref, down_ref, d_out, gain_out, rows_out, got, buf,
+                    resid_ref, cot_ref, hid, down, rows_buf, s_s, s_r, p_s, p_r, loc, rows_sem, mul_sem, out_sem):
     d, z, pair, c = place()
     cz = z // 2
-    full, _ = buf.shape
+    full, width = buf.shape
     rows = full // CHUNKS
     fetch = (
         pltpu.make_async_copy(resid_all.at[z % 2], resid_ref, rows_sem.at[0]),
         pltpu.make_async_copy(cot_all.at[z % 2], cot_ref, rows_sem.at[1]),
     )
-    for one in fetch:
+    factors = (pltpu.make_async_copy(hid_ref, hid, mul_sem.at[0]), pltpu.make_async_copy(down_ref, down, mul_sem.at[1]))
+    for one in fetch + factors:
         one.start()
+    tile = rows_buf.shape[2]
+    tiles = width // tile
+
+    def tile_out(j):
+        return pltpu.make_async_copy(rows_buf.at[j % 2], rows_out.at[:, pl.ds(j * tile, tile)], out_sem.at[j % 2])
+
+    def multiply(j):
+        if j >= tiles:
+            return
+        if j == 0:
+            for one in factors:
+                one.wait()
+        if j >= 2:
+            tile_out(j - 2).wait()
+        rows_buf[j % 2] = dot_n(hid[...], down[:, j * tile : (j + 1) * tile]).astype(jnp.bfloat16)
+        tile_out(j).start()
+
     greet_line(n_z, d, z)
     gain_out[...] = jnp.zeros_like(gain_out)
     own = c == cz
@@ -816,10 +834,14 @@
 
         if n > 0:
             send_step(*steps[n - 1], False)
+        if t == 0:
+            multiply(k)
         if t == 1 and k > 0:
             own_chunk(k - 1)
     send_step(*steps[-1], False)
     own_chunk(CHUNKS - 1)
+    for j in range(CHUNKS, tiles):
+        multiply(j)
 
     @pl.when(jnp.logical_not(own))
     def _():
@@ -831,6 +853,8 @@
         to_partner(CHUNKS - 1).start()
         keep(CHUNKS - 1).start()
 
+    for j in range(max(0, tiles - 2), tiles):
+        tile_out(j).wait()
     for k, t in steps:
         send_step(k, t, True)
     for k in range(CHUNKS):
@@ -839,26 +863,32 @@
         pl.when(jnp.logical_not(own))(remote(at, at, p_s.at[k], p_r.at[k], (d, z)).wait_recv)
 
 
-def sum_line(part, resid, cot, gain, n_z):
+def sum_line(part, resid, cot, gain, hidden, down, n_z):
     _, full, width = part.shape
     return pl.pallas_call(
         functools.partial(sum_line_kernel, n_z),
-        in_specs=[VMEM_SPEC, ANY_SPEC, ANY_SPEC, VMEM_SPEC],
-        out_specs=[ANY_SPEC, VMEM_SPEC],
-        out_shape=[jax.ShapeDtypeStruct((full, width), jnp.bfloat16), jax.ShapeDtypeStruct((8, width), jnp.float32)],
+        in_specs=[VMEM_SPEC, ANY_SPEC, ANY_SPEC, VMEM_SPEC, ANY_SPEC, ANY_SPEC],
+        out_specs=[ANY_SPEC, VMEM_SPEC, ANY_SPEC],
+        out_shape=[
+            jax.ShapeDtypeStruct((full, width), jnp.bfloat16),
+            jax.ShapeDtypeStruct((8, width), jnp.float32),
+            jax.ShapeDtypeStruct((hidden.shape[0], width), jnp.bfloat16),
+        ],
         scratch_shapes=[
             pltpu.VMEM((2, 2, full, width), jnp.bfloat16), pltpu.VMEM((full, width), jnp.bfloat16),
             pltpu.VMEM((full, width), jnp.bfloat16), pltpu.VMEM((full, width), jnp.bfloat16),
-            DMA((2, CHUNKS)), DMA((2, 2, CHUNKS)), DMA((CHUNKS,)), DMA((CHUNKS,)), DMA((CHUNKS,)), DMA((2,)),
+            pltpu.VMEM(hidden.shape, jnp.bfloat16), pltpu.VMEM(down.shape, jnp.bfloat16),
+            pltpu.VMEM((2, hidden.shape[0], 256), jnp.bfloat16),
+            DMA((2, CHUNKS)), DMA((2, 2, CHUNKS)), DMA((CHUNKS,)), DMA((CHUNKS,)), DMA((CHUNKS,)), DMA((2,)), DMA((2,)), DMA((2,)),
         ],
         compiler_params=pltpu.CompilerParams(collective_id=3, has_side_effects=True, vmem_limit_bytes=56 * 1024 * 1024),
         cost_estimate=pl.CostEstimate(flops=0, bytes_accessed=200_000_000, transcendentals=0),
         name="sum_line",
-    )(part, resid, cot, gain)
-
-
-WIDE_ROWS = 16
-TURNED_ROWS = 256
+    )(part, resid, cot, gain, hidden, down)
+
+
+WIDE_ROWS = 32
+TURNED_ROWS = 512
 
 
 def adam_wide_kernel(grad_ref, w_ref, m_ref, v_ref, g_out, w_out, m_out, v_out):
@@ -913,9 +943,9 @@
     )
 
 
-def hand_out_kernel(n_dp, n_z, dn_ref, x_ref, dr_ref, gain_ref, gain2_ref, qt_ref, ot_ref, ig, gq, go, gains,
-                    got, buf, q_got, q_own, q_mid, q_put, q_fin, o_got, o_own, o_mid, o_put, o_fin, g_src, g_all,
-                    p_s, p_r, i_s, i_r, q_s, q_r, qf_s, qf_r, o_s, o_r, of_s, of_r, g_s, g_r, q_loc, o_loc, loc):
+def hand_out_kernel(n_dp, n_z, dq_ref, n_ref, x_ref, dr_ref, gain_ref, gain2_ref, wq_ref, ot_ref, ig, gq, go, gains,
+                    dn_ref, wq, got, buf, q_base, q_got, q_put, q_fin, o_base, o_got, o_put, o_fin, g_src, g_all,
+                    p_s, p_r, i_s, i_r, q_s, q_r, qf_s, qf_r, o_s, o_r, of_s, of_r, g_s, g_r, loc):
     d, z, pair, c = place()
     n_d = n_dp // 2
     total = n_dp * n_z
@@ -929,25 +959,24 @@
     relay = n_d == 4
 
     class First:
-        def __init__(self, src, rows, cols, bufs, sems, spare):
-            self.src, self.rows, self.cols, self.spare = src, rows, cols, spare
-            self.got, self.own, self.mid, self.put, self.fin = bufs
-            self.send, self.recv, self.f_send, self.f_recv, self.loc = sems
+        def __init__(self, rows, cols, bufs, sems, spare):
+            self.rows, self.cols, self.spare = rows, cols, spare
+            self.base, self.got, self.put, self.fin = bufs
+            self.send, self.recv, self.f_send, self.f_recv = sems
 
         def block(self, ref, b, core):
             return ref.at[pl.ds(core * self.rows, self.rows), pl.ds(b * self.cols, self.cols)]
 
         def source(self, owner, b, core):
-            return self.src.at[pl.ds(pl.multiple_of((2 * owner + core) * self.rows, self.rows), self.rows), pl.ds(b * self.cols, self.cols)]
+            return self.base.at[pl.ds(pl.multiple_of((2 * owner + core) * self.rows, self.rows), self.rows), pl.ds(b * self.cols, self.cols)]
+
+        def cut_of(self, owner, b, core, r):
+            start = (2 * owner + core) * self.rows + r * 16
+            return pl.ds(pl.multiple_of(start, 16), 16), pl.ds(b * self.cols, self.cols)
 
         def copy(self, n, b, core, owner, to):
             return remote(self.source(owner, b, core), self.block(self.got.at[n], b, core), self.send.at[n, b, core],
                           self.recv.at[n, b, core], (2 * (pair ^ to) + c, z))
-
-        def loads(self, b, core):
-            yield pltpu.make_async_copy(self.source(pair, b, core), self.block(self.own, b, core), self.loc.at[0, b, core])
-            if relay:
-                yield pltpu.make_async_copy(self.source(pair ^ (2 >> b), b, core), self.block(self.mid, b, core), self.loc.at[1, b, core])
 
         def begin(self, core):
             for b in range(2):
@@ -968,7 +997,7 @@
             return pl.ds(pl.multiple_of(core * self.rows + r * 16, 16), 16), pl.ds(b * self.cols, self.cols)
 
         def middle_copy(self, b, core):
-            return remote(self.block(self.mid, b, core), self.block(self.got.at[2], b, core), self.send.at[2, b, core],
+            return remote(self.source(pair ^ (2 >> b), b, core), self.block(self.got.at[2], b, core), self.send.at[2, b, core],
                           self.recv.at[2, b, core], (2 * (pair ^ (2 >> b)) + c, z))
 
         def middle(self, core, between):
@@ -979,7 +1008,8 @@
 
                 def add(r, carry):
                     at = self.cut(b, core, r)
-                    self.mid[at] = (self.mid[at].astype(jnp.float32) + self.got[(1,) + at].astype(jnp.float32)).astype(jnp.bfloat16)
+                    mid = self.cut_of(pair ^ (2 >> b), b, core, r)
+                    self.base[mid] = (self.base[mid].astype(jnp.float32) + self.got[(1,) + at].astype(jnp.float32)).astype(jnp.bfloat16)
                     return carry
 
                 lax.fori_loop(0, self.rows // 16, add, 0)
@@ -995,7 +1025,7 @@
 
                 def add(r, carry):
                     at = self.cut(b, core, r)
-                    value = self.own[at].astype(jnp.float32)
+                    value = self.base[self.cut_of(pair, b, core, r)].astype(jnp.float32)
                     for n in slots:
                         value = value + self.got[(n,) + at].astype(jnp.float32)
                     self.put[core, b, pl.ds(pl.multiple_of(r * 16, 16), 16)] = value.astype(jnp.bfloat16)
@@ -1030,21 +1060,49 @@
                         at = self.block(self.got.at[n], b, core)
                         remote(at, at, self.send.at[n, b, core], self.recv.at[n, b, core], (d, z)).wait_send()
 
-    o_first = First(ot_ref, o_rows, o_cols, (o_got, o_own, o_mid, o_put, o_fin), (o_s, o_r, of_s, of_r, o_loc), 2)
-    q_first = First(qt_ref, q_rows, q_cols, (q_got, q_own, q_mid, q_put, q_fin), (q_s, q_r, qf_s, qf_r, q_loc), 3)
-    for one in (o_first, q_first):
-        for core in range(2):
-            for b in range(2):
-                for copy in one.loads(b, core):
-                    copy.start()
+    o_first = First(o_rows, o_cols, (o_base, o_got, o_put, o_fin), (o_s, o_r, of_s, of_r), 2)
+    q_first = First(q_rows, q_cols, (q_base, q_got, q_put, q_fin), (q_s, q_r, qf_s, qf_r), 3)
+    o_load = pltpu.make_async_copy(ot_ref, o_base, loc.at[4])
+    wq_load = pltpu.make_async_copy(wq_ref, wq, loc.at[5])
+    o_load.start()
+    wq_load.start()
     greet_all(n_dp, n_z, d, z)
-
+    o_load.wait()
+    o_first.begin(0)
+    o_first.begin(1)
+    nothing = lambda: None
+
+    def q_blocks(core):
+        def one(k, carry):
+            owner = pair ^ (n_d - 1 - k)
+            rows_at = pl.ds(pl.multiple_of((2 * owner + core) * q_rows, q_rows), q_rows)
+            q_base[rows_at] = dot_c(n_ref[:, rows_at], dq_ref[...]).astype(jnp.bfloat16)
+            return carry
+
+        lax.fori_loop(0, n_d, one, 0)
+
+    def dn_blocks(low, high):
+        def one(r, carry):
+            rows_at = pl.ds(pl.multiple_of(r * 256, 256), 256)
+            dn_ref[:, rows_at] = dot_t(dq_ref[...], wq[rows_at]).astype(jnp.bfloat16)
+            return carry
+
+        lax.fori_loop(low, high, one, 0)
+
+    q_blocks(0)
+    o_first.middle(0, lambda: q_blocks(1))
+    q_first.begin(0)
+    wq_load.wait()
+    dn_tiles = width // 256
+    dn_blocks(0, dn_tiles // 2)
+    o_first.middle(1, nothing)
+    q_first.begin(1)
+    dn_blocks(dn_tiles // 2, dn_tiles)
     mine = pl.ds(pl.multiple_of(c * half, half), half)
     theirs = pl.ds(pl.multiple_of((1 - c) * half, half), half)
     swap = remote(dn_ref.at[theirs], got, p_s, p_r, (2 * pair + 1 - c, z))
+    o_first.total(0, nothing)
     swap.start()
-    o_first.begin(0)
-    o_first.begin(1)
 
     g_src[pl.ds(0, 8)] = jnp.zeros((8, width), jnp.float32)
     g_src[pl.ds(8, 8)] = gain2_ref[...]
@@ -1075,19 +1133,12 @@
         pl.when(jnp.logical_not(here))(copy.wait_send if wait else copy.start)
         pl.when(here)(keep.wait if wait else keep.start)
 
-    for one in (o_first, q_first):
-        for core in range(2):
-            for b in range(2):
-                for copy in one.loads(b, core):
-                    copy.wait()
-    nothing = lambda: None
+    q_first.middle(0, nothing)
     per = quarter // 16
     lax.fori_loop(0, per, rows_of, 0)
-    o_first.middle(0, lambda: row_send(0, False))
-    q_first.begin(0)
+    o_first.total(1, lambda: row_send(0, False))
     lax.fori_loop(per, 2 * per, rows_of, 0)
-    o_first.middle(1, lambda: row_send(1, False))
-    q_first.begin(1)
+    q_first.middle(1, lambda: row_send(1, False))
 
     each = width // total
 
@@ -1104,10 +1155,6 @@
 
     lax.fori_loop(1, total, send_gain, 0)
 
-    o_first.total(0, nothing)
-    q_first.middle(0, nothing)
-    o_first.total(1, nothing)
-    q_first.middle(1, nothing)
     q_first.total(0, nothing)
     q_first.total(1, nothing)
 
@@ -1152,25 +1199,25 @@
     lax.fori_loop(0, q_rows // 16, last, 0)
 
 
-def hand_out(dn, x, dr, gain, gain2, qt, ot, n_dp, n_z):
+def hand_out(dq, normed, x, dr, gain, gain2, wq, ot, n_dp, n_z):
     full, width = x.shape
     n_d = n_dp // 2
     total = n_dp * n_z
-    q_rows, q_cols = qt.shape[0] // n_dp, qt.shape[1] // 2
+    q_rows, q_cols = wq.shape[0] // n_dp, wq.shape[1] // 2
     o_rows, o_cols = ot.shape[0] // n_dp, ot.shape[1] // 2
     b16 = jnp.bfloat16
     f32 = jnp.float32
 
     def weight_bufs(rows, cols):
         return [
-            pltpu.VMEM((n_d - 1, 2 * rows, 2 * cols), b16), pltpu.VMEM((2 * rows, 2 * cols), b16),
-            pltpu.VMEM((2 * rows, 2 * cols), b16), pltpu.VMEM((2, 2, rows, cols), b16), pltpu.VMEM((n_z, rows, cols), b16),
+            pltpu.VMEM((n_dp * rows, 2 * cols), b16), pltpu.VMEM((n_d - 1, 2 * rows, 2 * cols), b16),
+            pltpu.VMEM((2, 2, rows, cols), b16), pltpu.VMEM((n_z, rows, cols), b16),
         ]
 
     weight_sems = [DMA((n_d - 1, 2, 2)), DMA((n_d - 1, 2, 2)), DMA((2, 2)), DMA((n_z,))]
     return pl.pallas_call(
         functools.partial(hand_out_kernel, n_dp, n_z),
-        in_specs=[VMEM_SPEC] * 5 + [ANY_SPEC] * 2,
+        in_specs=[VMEM_SPEC] * 6 + [ANY_SPEC] * 2,
         out_specs=[ANY_SPEC] + [VMEM_SPEC] * 3,
         out_shape=[
             jax.ShapeDtypeStruct((2, full // 4, width), b16),
@@ -1179,16 +1226,17 @@
             jax.ShapeDtypeStruct((16, 128), f32),
         ],
         scratch_shapes=[
+            pltpu.VMEM((full, width), b16), pltpu.VMEM(wq.shape, b16),
             pltpu.VMEM((full // 2, width), b16), pltpu.VMEM((full // 2, width), b16),
             *weight_bufs(q_rows, q_cols), *weight_bufs(o_rows, o_cols),
             pltpu.VMEM((16, width), f32), pltpu.VMEM((total, 16, 128), f32),
             DMA, DMA, DMA((2,)), DMA((2,)), *weight_sems, *weight_sems, DMA, DMA,
-            DMA((2, 2, 2)), DMA((2, 2, 2)), DMA((4,)),
+            DMA((6,)),
         ],
         compiler_params=pltpu.CompilerParams(collective_id=5, has_side_effects=True, vmem_limit_bytes=58 * 1024 * 1024),
         cost_estimate=pl.CostEstimate(flops=0, bytes_accessed=300_000_000, transcendentals=0),
         name="hand_out",
-    )(dn, x, dr, gain, gain2, qt, ot)
+    )(dq, normed, x, dr, gain, gain2, wq, ot)
 
 
 def rms_forward(values, gain_wide):
@@ -1292,17 +1340,15 @@
     d_gate = d_hidden * up_part * sigmoid_gate * (1.0 + gate_part * (1.0 - sigmoid_gate))
     d_up = d_hidden * active
     d_gate_up16 = jnp.concatenate([d_gate, d_up], 1).astype(jnp.bfloat16)
-    down_part = jnp.dot(hidden16, down_rows, preferred_element_type=jnp.float32)
-    down16 = down_part.astype(jnp.bfloat16).reshape(resid_all.shape)
     gate_up_term = contract_rows(normed_two, d_gate_up16).astype(jnp.bfloat16)
     gate_up_sum = lax.psum_scatter(gate_up_term, "dp", scatter_dimension=0, tiled=True)
     down_term = contract_rows(cot_rows, hidden16).astype(jnp.bfloat16)
     down_sum = lax.psum_scatter(down_term, "dp", scatter_dimension=0, tiled=True)
     d_normed_two = times_transpose(d_gate_up16, gate_up_cols).astype(jnp.bfloat16)
-    d_resid16, gain_two_part = sum_line(
-        d_normed_two.reshape(resid_all.shape), resid_all, cot_all, gain_two, n_z
-    )
-    down16, _ = lax.optimization_barrier((down16, d_resid16))
+    d_resid16, gain_two_part, down_part = sum_line(
+        d_normed_two.reshape(resid_all.shape), resid_all, cot_all, gain_two, hidden16, down_rows, n_z
+    )
+    down16 = down_part.reshape(resid_all.shape)
     pieces = [
         lax.dynamic_slice_in_dim(down16, (z_here + o) % n_z * local_len, local_len, 1)
         for o in range(n_z)
@@ -1314,16 +1360,15 @@
     output = (resid_here.astype(jnp.float32) + down_here).astype(jnp.bfloat16)
     d_attended = jnp.dot(d_resid16, out_rows, preferred_element_type=jnp.float32).astype(jnp.bfloat16)
     d_qkv16 = attn_backward(turned, d_attended, lse, *tables, full_len, groups)
-    d_normed_one = times_transpose(d_qkv16, qkv_cols).astype(jnp.bfloat16)
-    qkv_term = contract_rows(normed_one, d_qkv16).astype(jnp.bfloat16)
     out_term = contract_rows(d_resid16, attended16).astype(jnp.bfloat16)
     input_grad, grad_qkv, grad_out, gain_sums = hand_out(
-        d_normed_one,
+        d_qkv16,
+        normed_one,
         rows_in,
         d_resid16,
         gain_one,
         gain_two_part,
-        qkv_term,
+        qkv_cols,
         out_term,
         n_dp,
         n_z,

time: 727 us -> 711 us (0.978)
  the two profiles are of different devices: /device:TPU:13 before, /device:TPU:11 now
where the time goes in v7:
time: 711 us; the launch traced here: 704 us
  Pallas kernels  511 us (72%)
  matrix products  128 us (18%)
  other arithmetic  24.3 us (3%)
  local copies, waits for them, and re-layouts  16.8 us (2%)
  between operations  14.4 us (2%)
  starting transfers between devices  9.33 us (1%)
    pallas_call x1, Pallas kernels, hand_out(): pl.pallas_call(functools.partial(hand_out_kernel, n_dp, n_z), in_specs=[V...  148 us
    pallas_call x1, Pallas kernels, share_resid(): pl.pallas_call(functools.partial(share_resid_kernel, n_dp, n_z), in_specs...  104 us
    pallas_call x1, Pallas kernels, gather_in(): pl.pallas_call(functools.partial(gather_in_kernel, n_dp, n_z), in_specs=[...  91.5 us
    pallas_call x1, Pallas kernels, sum_line(): pl.pallas_call(functools.partial(sum_line_kernel, n_z), in_specs=[VMEM_SP...  87.9 us
    dot_general x3, matrix products, times_transpose(): lax.dot_general(left, right, (((1,), (1,)), ((), ())), preferred_element_...  52.8 us
    dot_general x3, matrix products, contract_rows(): lax.dot_general(left, right, (((0,), (0,)), ((), ())), preferred_element_...  44 us
    pallas_call x1, Pallas kernels, attn_forward(): pl.pallas_call(functools.partial(attn_gather_kernel, n_dp, pairs, Q_ROWS,...  37.5 us
    dot_general x1, matrix products, layer_step(): jnp.dot(normed_two, gate_up_cols, preferred_element_type=jnp.float32)  22.3 us
  transfers between devices with their start and end apart: 7, of which 0 were waited for; matrix products, arithmetic and copies ran while one was open for 17% of the time, Pallas kernels for 58%

profile of v7, /device:TPU:11, one launch (start us, length us, event | category | flops | bytes accessed | tf_op | source)
XLA Modules:
  0.0 703.7 jit_solution(3999716106754467039)
XLA Ops:
  7.2 0.0 all-gather.3.cloned.1.call-start
  7.2 1.9 copy.49
  9.1 1.9 convert_element_type.105.w_ref
  11.0 0.7 convert_bitcast_fusion.1
  11.7 0.7 fusion.14.g_ref
  12.4 1.3 pad.12.s_ref
  13.7 91.5 %gather_in.1 = (bf16[512,2048]{1,0:T(8,128)(2,1)}, bf16[2048,1536]{1,0:T(8,128)(2,1)}, bf16[512,1024]{1,0:T(8,128)(2,1)}, f32[32,8,128]{2,1,0:T(8,128)}, s32[2,8...) custom-call(bf16[2,128,2048]{2,1,0:T(8,128)(2,1)} %x_ref.1, bf16[256,768]{1,0:T(8,128)(2,1)} %convert_element_type.105.w_ref, ...), custom_call_target="tpu_custom_call" | custom-call | bytes 200000000 | tf_op jit(solution)/shard_map/gather_in/pallas_call | solution.py:528
  105.2 0.0 all-gather.3.cloned.1.call-update
  105.2 0.0 all-gather.5.cloned.1.call-start
  105.3 2.8 convert_element_type.113
  108.1 0.0 all-gather.5.cloned.1.call-update
  108.1 0.0 reduce-scatter.5.cloned.1.call-start
  108.2 1.1 slice_reduce_fusion
  109.3 0.1 mul.238
  109.3 0.1 mul.228
  109.4 0.7 constant_dynamic-slice_fusion.4
  110.1 0.2 convert_reduce_fusion
  110.4 1.0 fusion.10
  111.4 1.0 maximum_bitcast_fusion.cos_ref
  112.4 1.0 maximum_bitcast_fusion.1.sin_ref
  113.4 0.5 fusion.4
  113.9 0.6 fusion.6.n_ref
  114.4 0.0 copy-start.2
  114.4 5.1 fusion.23.qkv_ref
  119.5 0.6 reshape.371.seg_row_ref
  120.2 0.8 reshape.370.seg_col_ref
  121.0 37.5 %attn_forward.1 = (bf16[512,1536]{1,0:T(8,128)(2,1)}, f32[512,512]{1,0:T(8,128)}, bf16[512,1024]{1,0:T(8,128)(2,1)}, bf16[2048,1024]{1,0:T(8,128)(2,1)}) custom-call(f32[512,1536]{1,0:T(8,128)} %fusion.23.qkv_ref, f32[512,128]{1,0:T(8,128)} %maximum_bitcast_fusion.cos_ref, f32[512,128]{1,0:T(8,128)} %maximum_bitcast_fusion.1.sin_ref, ...), custom_call_target="tpu_custom_call" | custom-call | flops 2147483648 | bytes 150000000 | tf_op jit(solution)/shard_map/attn_forward/pallas_call | solution.py:217
  158.5 6.3 convolution_convert_fusion.3.part_ref
  164.7 104.0 %share_resid.1 = (bf16[2,512,2048]{2,1,0:T(8,128)(2,1)}, bf16[2048,4096]{1,0:T(8,128)(2,1)}) custom-call(bf16[512,2048]{1,0:T(8,128)(2,1)} %convolution_convert_fusion.3.part_ref, bf16[512,2048]{1,0:T(8,128)(2,1)} %get-tuple-element.54.x_ref, bf16[256,4096]{1,0:T(8,128)(2,1)} %get-tuple-element.61.w_ref), custom_call_target="tpu_custom_call" | custom-call | bytes 200000000 | tf_op jit(solution)/shard_map/share_resid/pallas_call | solution.py:684
  268.8 3.2 multiply_reduce_fusion
  272.1 0.2 copy-done
  272.2 1.0 fusion.1
  273.3 0.0 copy-start.4
  273.3 2.0 copy-done.4
  275.3 22.3 %fusion.24 = f32[1024,4096]{1,0:T(8,128)} fusion(bf16[1024,2048]{1,0:T(8,128)(2,1)S(1)} %fusion.1, bf16[2048,4096]{1,0:T(8,128)(2,1)} %get-tuple-element.64), kind=kOutput, calls=%fused_computation.70 | convolution fusion | flops 17179869184 | bytes 37748736 | tf_op jit(solution)/shard_map/dot_general | solution.py:1332
  297.6 22.3 %multiply_convert_fusion.2 = (bf16[1024,2048]{1,0:T(8,128)(2,1)}, bf16[1024,2048]{1,0:T(8,128)(2,1)}, bf16[1024,2048]{1,0:T(8,128)(2,1)}) fusion(f32[1024,4096]{1,0:T(8,128)} %fusion.24, bf16[1024,2048]{1,0:T(8,128)(2,1)} %bitcast.52, bf16[2048,2048]{1,0:T(8,128)(2,1)} %all-gather.5.cloned.1.call-done.down_ref), kind=kOutput, calls=%fused_computation.7 | convolution fusion | flops 8621391872 | bytes 41943040 | tf_op jit(solution)/shard_map/dot_general | solution.py:1266
  319.8 14.0 %convolution_convert_fusion.1 = bf16[2048,2048]{1,0:T(8,128)(2,1)} fusion(bf16[1024,2048]{1,0:T(8,128)(2,1)} %bitcast.53, bf16[1024,2048]{1,0:T(8,128)(2,1)} %get-tuple-element.100.hid_ref), kind=kOutput, calls=%fused_computation.11 | convolution fusion | flops 8594128896 | bytes 16777216 | tf_op jit(solution)/shard_map/dot_general | solution.py:1260
  333.9 0.0 reduce-scatter.5.cloned.1.call-update
  333.9 0.0 reduce-scatter.3.cloned.1.call-start
  333.9 25.6 %convolution_convert_fusion = bf16[2048,4096]{1,0:T(8,128)(2,1)} fusion(bf16[1024,2048]{1,0:T(8,128)(2,1)} %copy-done.4, bf16[1024,2048]{1,0:T(8,128)(2,1)} %get-tuple-element.99, bf16[1024,2048]{1,0:T(8,128)(2,1)} %get-tuple-element.98), kind=kOutput, calls=%fused_computation | convolution fusion | flops 17205035008 | bytes 29360128 | tf_op jit(solution)/shard_map/dot_general | solution.py:1260
  359.6 0.0 reduce-scatter.3.cloned.1.call-update
  359.7 0.7 reshape_squeeze.7.gain_ref
  360.3 0.7 reshape_squeeze.6.gain_ref
  361.0 24.3 %fusion.7 = bf16[1024,2048]{1,0:T(8,128)(2,1)} fusion(bf16[2048,4096]{1,0:T(8,128)(2,1)} %get-tuple-element.64, bf16[1024,2048]{1,0:T(8,128)(2,1)} %get-tuple-element.99, bf16[1024,2048]{1,0:T(8,128)(2,1)} %get-tuple-element.98), kind=kOutput, calls=%fused_computation.18 | convolution fusion | flops 17198743552 | bytes 29360128 | tf_op jit(solution)/shard_map/dot_general | solution.py:1266
  385.3 87.9 %sum_line.1 = (bf16[512,2048]{1,0:T(8,128)(2,1)}, f32[8,2048]{1,0:T(8,128)}, bf16[1024,2048]{1,0:T(8,128)(2,1)}) custom-call(bf16[2,512,2048]{2,1,0:T(8,128)(2,1)} %bitcast.54, bf16[2,512,2048]{2,1,0:T(8,128)(2,1)} %get-tuple-element.62.resid_all, bf16[2,512,2048]{2,1,0:T(8,128)(2,1)} %all-gather.3.cloned.1.call-done.cot_all, ...), custom_call_target="tpu_custom_call" | custom-call | bytes 200000000 | tf_op jit(solution)/shard_map/sum_line/pallas_call | solution.py:868
  473.2 3.8 constant_dynamic-slice_fusion.2
  477.0 5.3 collective-permute-start
  482.3 3.9 collective-permute-start.1
  486.2 4.4 convolution_convert_fusion.2.ot_ref
  490.6 3.3 convolution_convert_fusion.4.d_out_ref
  493.9 20.3 %attn_backward.1.dq_ref = bf16[512,1536]{1,0:T(8,128)(2,1)} custom-call(bf16[512,1536]{1,0:T(8,128)(2,1)} %get-tuple-element.66.turned_ref, bf16[512,1024]{1,0:T(8,128)(2,1)} %convolution_convert_fusion.4.d_out_ref, f32[512,512]{1,0:T(8,128)} %get-tuple-element.68.lse_ref, f32[512,128]{1,0:T(8,128)} %maximum_bitcast_fusion.cos_ref, ...), custom_call_target="tpu_custom_call" | custom-call | flops 5368709120 | bytes 4718592 | tf_op jit(solution)/shard_map/attn_backward/pallas_call | solution.py:243
  514.3 147.9 %hand_out.1 = (bf16[2,128,2048]{2,1,0:T(8,128)(2,1)}, f32[256,768]{1,0:T(8,128)}, f32[512,256]{1,0:T(8,128)}, f32[16,128]{1,0:T(8,128)}) custom-call(bf16[512,1536]{1,0:T(8,128)(2,1)} %attn_backward.1.dq_ref, bf16[512,2048]{1,0:T(8,128)(2,1)} %copy-done.2, bf16[512,2048]{1,0:T(8,128)(2,1)} %get-tuple-element.54.x_ref, ...), custom_call_target="tpu_custom_call" | custom-call | bytes 300000000 | tf_op jit(solution)/shard_map/hand_out/pallas_call | solution.py:1218
  662.3 0.9 bitcast_reduce_fusion
  663.1 0.1 constant_dynamic-slice_fusion.3
  663.2 0.6 multiply_subtract_fusion.2
  663.8 2.4 multiply_subtract_fusion.1
  666.2 1.8 multiply_subtract_fusion
  668.1 4.1 add_convert_fusion
  672.1 7.3 %shard_map.405 = (f32[2048,256]{1,0:T(8,128)}, f32[2048,256]{1,0:T(8,128)}, f32[2048,256]{1,0:T(8,128)}, f32[2048,256]{1,0:T(8,128)}) custom-call(bf16[256,2048]{1,0:T(8,128)(2,1)} %reduce-scatter.5.cloned.1.call-done.grad_ref, f32[2048,256]{1,0:T(8,128)} %w_ref.3, f32[2048,256]{1,0:T(8,128)} %m_ref.3, f32[2048,256]{1,0:T(8,128)} %v_ref.3), custom_call_target="tpu_custom_call" | custom-call | flops 10485760 | bytes 15728640 | tf_op jit(solution)/shard_map/pallas_call | solution.py:916
  679.4 0.0 reduce-scatter.3.cloned.1.call-done.grad_ref
  679.4 14.9 %shard_map.404 = (f32[256,2,2048]{2,1,0:T(2,128)}, f32[256,2,2048]{2,1,0:T(2,128)}, f32[256,2,2048]{2,1,0:T(2,128)}, f32[256,2,2048]{2,1,0:T(2,128)}) custom-call(bf16[256,4096]{1,0:T(8,128)(2,1)} %reduce-scatter.3.cloned.1.call-done.grad_ref, f32[256,2,2048]{2,1,0:T(2,128)} %w_ref.2, f32[256,2,2048]{2,1,0:T(2,128)} %m_ref.2, f32[256,2,2048]{2,1,0:T(2,128)} %v_ref.2), custom_call_target="tpu_custom_call" | custom-call | flops 20971520 | bytes 31457280 | tf_op jit(solution)/shard_map/pallas_call | solution.py:916
  694.3 1.0 copy.55
  695.3 0.9 copy.56
  696.2 0.8 copy.57
  (54 shorter events, 0.2 us)
Async XLA Ops:
  7.2 290.4 %all-gather.3.cloned.1.call-start = ((), (), s32[]{:S(2)}) async-start(), calls=%async_computation.2 | async-start | bytes 5242880 | tf_op jit(solution)/shard_map/all_gather | solution.py:1317
  105.2 8.2 %copy-start.1 = (bf16[512,2048]{1,0:T(8,128)(2,1)S(1)}, bf16[512,2048]{1,0:T(8,128)(2,1)}, u32[]{:S(2)}) copy-start(bf16[512,2048]{1,0:T(8,128)(2,1)} %get-tuple-element.54.x_ref) | copy-start | bytes 6291460
  105.2 192.4 %all-gather.5.cloned.1.call-start = ((), (), s32[]{:S(2)}) async-start(), calls=%async_computation.3 | async-start | bytes 9437184 | tf_op jit(solution)/shard_map/all_gather | solution.py:1305
  108.1 564.0 %reduce-scatter.5.cloned.1.call-start = ((), (), s32[]{:S(2)}) async-start(), calls=%async_computation.5 | async-start | bytes 9437184 | tf_op jit(solution)/shard_map/reduce_scatter | solution.py:1346
  110.4 4.0 copy-start.3
  114.4 5.1 copy-start.2
  268.8 3.5 copy-start
  273.3 2.0 copy-start.4
  333.9 345.5 %reduce-scatter.3.cloned.1.call-start = ((), (), s32[]{:S(2)}) async-start(), calls=%async_computation.4 | async-start | bytes 18874368 | tf_op jit(solution)/shard_map/reduce_scatter | solution.py:1344
  473.2 13.0 %copy-start.9 = (bf16[512,2048]{1,0:T(8,128)(2,1)S(1)}, bf16[512,2048]{1,0:T(8,128)(2,1)}, u32[]{:S(2)}) copy-start(bf16[512,2048]{1,0:T(8,128)(2,1)} %get-tuple-element.67.dr_ref) | copy-start | bytes 6291460
  473.2 13.0 %copy-start.22 = (bf16[512,1024]{1,0:T(8,128)(2,1)S(1)}, bf16[512,1024]{1,0:T(8,128)(2,1)}, u32[]{:S(2)}) copy-start(bf16[512,1024]{1,0:T(8,128)(2,1)} %get-tuple-element.59) | copy-start | bytes 3145732
  477.0 191.0 %collective-permute-start = (bf16[2,128,2048]{2,1,0:T(8,128)(2,1)}, bf16[2,128,2048]{2,1,0:T(8,128)(2,1)S(1)}, u32[]{:S(2)}, u32[]{:S(2)}) collective-permute-start(bf16[2,128,2048]{2,1,0:T(8,128)(2,1)} %get-tuple-element.101), channel_id=1, source_target_pairs={{0,1},{1,2},{2,3},{3,0},{4,5},{5,6},{6,7},{7,4},{8,9},{9,10},{10,1... | collective-permute-start | bytes 3145736 | tf_op jit(solution)/shard_map/ppermute | solution.py:1357
  482.3 185.8 %collective-permute-start.2 = (bf16[2,128,2048]{2,1,0:T(8,128)(2,1)}, bf16[2,128,2048]{2,1,0:T(8,128)(2,1)}, u32[]{:S(2)}, u32[]{:S(2)}) collective-permute-start(bf16[2,128,2048]{2,1,0:T(8,128)(2,1)} %get-tuple-element.102), channel_id=1, source_target_pairs={{0,3},{1,0},{2,1},{3,2},{4,7},{5,4},{6,5},{7,6},{8,11},{9,8},{10,9... | collective-permute-start | bytes 3145736 | tf_op jit(solution)/shard_map/ppermute | solution.py:1357
  482.3 185.8 %collective-permute-start.1 = (bf16[2,128,2048]{2,1,0:T(8,128)(2,1)}, bf16[2,128,2048]{2,1,0:T(8,128)(2,1)}, u32[]{:S(2)}, u32[]{:S(2)}) collective-permute-start(bf16[2,128,2048]{2,1,0:T(8,128)(2,1)} %get-tuple-element.103), channel_id=1, source_target_pairs={{0,2},{1,3},{2,0},{3,1},{4,6},{5,7},{6,4},{7,5},{8,10},{9,11},{10,... | collective-permute-start | bytes 3145736 | tf_op jit(solution)/shard_map/ppermute | solution.py:1357
  486.2 4.4 copy-start.21
  514.2 149.0 %copy-start.15 = (f32[64]{0:T(128)S(1)}, f32[64]{0:T(128)}, u32[]{:S(2)}) copy-start(f32[64]{0:T(128)} %param.27) | copy-start | bytes 772
  514.2 149.0 %copy-start.16 = (f32[64]{0:T(128)S(1)}, f32[64]{0:T(128)}, u32[]{:S(2)}) copy-start(f32[64]{0:T(128)} %param.24) | copy-start | bytes 772
  514.2 149.0 %copy-start.17 = (f32[64]{0:T(128)S(1)}, f32[64]{0:T(128)}, u32[]{:S(2)}) copy-start(f32[64]{0:T(128)} %param.33) | copy-start | bytes 772
  514.2 149.0 %copy-start.18 = (f32[64]{0:T(128)S(1)}, f32[64]{0:T(128)}, u32[]{:S(2)}) copy-start(f32[64]{0:T(128)} %param.39) | copy-start | bytes 772
  514.2 149.0 %copy-start.19 = (f32[64]{0:T(128)S(1)}, f32[64]{0:T(128)}, u32[]{:S(2)}) copy-start(f32[64]{0:T(128)} %param.36) | copy-start | bytes 772
  514.2 149.0 %copy-start.20 = (f32[64]{0:T(128)S(1)}, f32[64]{0:T(128)}, u32[]{:S(2)}) copy-start(f32[64]{0:T(128)} %param.30) | copy-start | bytes 772
  514.2 149.5 %copy-start.7 = (f32[512,256]{1,0:T(8,128)S(1)}, f32[512,256]{1,0:T(8,128)}, u32[]{:S(2)}) copy-start(f32[512,256]{1,0:T(8,128)} %param.26) | copy-start | bytes 1572868
  514.2 149.5 %copy-start.13 = (f32[512,256]{1,0:T(8,128)S(1)}, f32[512,256]{1,0:T(8,128)}, u32[]{:S(2)}) copy-start(f32[512,256]{1,0:T(8,128)} %param.32) | copy-start | bytes 1572868
  514.3 149.5 %copy-start.14 = (f32[512,256]{1,0:T(8,128)S(1)}, f32[512,256]{1,0:T(8,128)}, u32[]{:S(2)}) copy-start(f32[512,256]{1,0:T(8,128)} %param.38) | copy-start | bytes 1572868
  662.2 4.0 copy-start.5
  662.2 4.0 copy-start.6
  662.2 4.0 copy-start.11
  662.2 4.0 copy-start.12
  679.4 14.9 %copy-start.10 = (bf16[2,128,2048]{2,1,0:T(8,128)(2,1)S(1)}, bf16[2,128,2048]{2,1,0:T(8,128)(2,1)}, u32[]{:S(2)}) copy-start(bf16[2,128,2048]{2,1,0:T(8,128)(2,1)} %get-tuple-element.142) | copy-start | bytes 3145732
  679.4 16.8 %copy-start.8 = (f32[512,256]{1,0:T(8,128)S(1)}, f32[512,256]{1,0:T(8,128)}, u32[]{:S(2)}) copy-start(f32[512,256]{1,0:T(8,128)} %get-tuple-element.145) | copy-start | bytes 1572868
Sparse Core Ops, SparseCore 0:
  105.3 82.9 all-gather.2
  190.7 85.5 all-gather.4
  334.0 70.1 reduce-scatter.4
  407.7 116.2 reduce-scatter.2

commit v8 on v7

--- a/solution.py
+++ b/solution.py
@@ -701,60 +701,115 @@
 
 
 CHUNKS = 8
-
-
-def sum_line_kernel(n_z, part_ref, resid_all, cot_all, gain_ref, hid_ref, down_ref, d_out, gain_out, rows_out, got, buf,
-                    resid_ref, cot_ref, hid, down, rows_buf, s_s, s_r, p_s, p_r, loc, rows_sem, mul_sem, out_sem):
+GROUPS = 4
+
+
+def sum_line_kernel(n_z, d_gate_ref, d_up_ref, w_ref, resid_all, cot_all, gain_ref, hid_ref, down_ref, d_out, gain_out,
+                    rows_out, left, w, part, got, buf, resid_ref, cot_ref, hid, down, rows_buf,
+                    s_s, s_r, p_s, p_r, loc, rows_sem, mul_sem, out_sem, left_sem, w_sem):
     d, z, pair, c = place()
     cz = z // 2
     full, width = buf.shape
+    inner = d_gate_ref.shape[1]
     rows = full // CHUNKS
+    group = full // GROUPS
+    per = CHUNKS // GROUPS
+    tile = 256
+    tiles = width // tile
+    lefts = []
+    for q in range(GROUPS):
+        for jl in range(2):
+            for n, src in enumerate((d_gate_ref, d_up_ref)):
+                lefts.append(pltpu.make_async_copy(
+                    src.at[pl.ds(jl * full + q * group, group)],
+                    left.at[pl.ds((2 * q + jl) * group, group), pl.ds(n * inner, inner)],
+                    left_sem.at[q, jl, n],
+                ))
+
+    def w_copy(n):
+        at = pl.ds(pl.multiple_of(n * tile, tile), tile)
+        return pltpu.make_async_copy(w_ref.at[at], w.at[at], w_sem.at[n])
+
     fetch = (
         pltpu.make_async_copy(resid_all.at[z % 2], resid_ref, rows_sem.at[0]),
         pltpu.make_async_copy(cot_all.at[z % 2], cot_ref, rows_sem.at[1]),
     )
     factors = (pltpu.make_async_copy(hid_ref, hid, mul_sem.at[0]), pltpu.make_async_copy(down_ref, down, mul_sem.at[1]))
-    for one in fetch + factors:
+    for one in lefts[:4]:
         one.start()
-    tile = rows_buf.shape[2]
-    tiles = width // tile
-
-    def tile_out(j):
-        return pltpu.make_async_copy(rows_buf.at[j % 2], rows_out.at[:, pl.ds(j * tile, tile)], out_sem.at[j % 2])
-
-    def multiply(j):
-        if j >= tiles:
-            return
-        if j == 0:
-            for one in factors:
-                one.wait()
-        if j >= 2:
-            tile_out(j - 2).wait()
-        rows_buf[j % 2] = dot_n(hid[...], down[:, j * tile : (j + 1) * tile]).astype(jnp.bfloat16)
-        tile_out(j).start()
-
+    for n in range(tiles):
+        w_copy(n).start()
+    for one in tuple(lefts[4:]) + factors + fetch:
+        one.start()
     greet_line(n_z, d, z)
     gain_out[...] = jnp.zeros_like(gain_out)
     own = c == cz
-    steps = [(k, t) for k in range(CHUNKS) for t in range(2)]
-
-    def where_is(k, t):
+
+    def compute(q, low, high):
+        if low == 0:
+            for one in lefts[4 * q : 4 * q + 4]:
+                one.wait()
+
+        def one_tile(n, carry):
+            if q == 0:
+                w_copy(n).wait()
+            at = pl.ds(pl.multiple_of(n * tile, tile), tile)
+            value = dot_t(left[pl.ds(2 * q * group, 2 * group)], w[at])
+            part[pl.ds(2 * q * group, 2 * group), at] = value.astype(jnp.bfloat16)
+            return carry
+
+        lax.fori_loop(low, high, one_tile, 0)
+
+    def tile_out(j):
+        at = pl.ds(pl.multiple_of(j * tile, tile), tile)
+        return pltpu.make_async_copy(rows_buf.at[lax.rem(j, 2)], rows_out.at[:, at], out_sem.at[lax.rem(j, 2)])
+
+    def multiply(low, high):
+        if low == 0:
+            for one in factors:
+                one.wait()
+
+        def one_tile(j, carry):
+            pl.when(j >= 2)(tile_out(j - 2).wait)
+            at = pl.ds(pl.multiple_of(j * tile, tile), tile)
+            rows_buf[lax.rem(j, 2)] = dot_n(hid[...], down[:, at]).astype(jnp.bfloat16)
+            tile_out(j).start()
+            return carry
+
+        lax.fori_loop(low, high, one_tile, 0)
+
+    def part_start(jl, k):
+        return (2 * (k // per) + jl) * group + k % per * rows
+
+    def part_at(jl, k, r):
+        return pl.ds(pl.multiple_of(part_start(jl, k) + r * 16, 16), 16)
+
+    def copy_on(k, t, side, src):
         jl = jnp.bitwise_xor(c, t)
-        return jl, 2 * c + jl, pl.ds(k * rows, rows)
-
-    def copy_on(k, t, side, src):
-        jl, _, at = where_is(k, t)
         to = z + 1 if side == 0 else z - 1
-        return remote(src, got.at[side, jl, at], s_s.at[t, k], s_r.at[side, jl, k], (2 * pair + c, to))
+        return remote(src, got.at[side, jl, pl.ds(k * rows, rows)], s_s.at[t, k], s_r.at[side, jl, k], (2 * pair + c, to))
 
     def arrived(side, jl, k):
         at = got.at[side, jl, pl.ds(k * rows, rows)]
         return remote(at, at, s_s.at[0, 0], s_r.at[side, jl, k], (d, z))
 
+    def send_step(k, t, edge_only, inner_only, wait):
+        jl = jnp.bitwise_xor(c, t)
+        j = 2 * c + jl
+        for side in range(2):
+            going = (z < j) if side == 0 else (z > j)
+            edge = (z == 0) if side == 0 else (z == n_z - 1)
+            raw = copy_on(k, t, side, part.at[pl.ds(pl.multiple_of(part_start(jl, k), rows), rows)])
+            passed = copy_on(k, t, side, got.at[side, jl, pl.ds(k * rows, rows)])
+            if not inner_only:
+                pl.when(going & edge)(raw.wait_send if wait else raw.start)
+            if not edge_only:
+                pl.when(going & jnp.logical_not(edge))(passed.wait_send if wait else passed.start)
+
     def add_in(side, jl, k):
         def one(r, carry):
             at = pl.ds(pl.multiple_of(k * rows + r * 16, 16), 16)
-            got[side, jl, at] = (got[side, jl, at].astype(jnp.float32) + part_ref[jl, at].astype(jnp.float32)).astype(jnp.bfloat16)
+            got[side, jl, at] = (got[side, jl, at].astype(jnp.float32) + part[part_at(jl, k, r)].astype(jnp.float32)).astype(jnp.bfloat16)
             return carry
 
         lax.fori_loop(0, rows // 16, one, 0)
@@ -762,10 +817,10 @@
     def finish(jl, k):
         def one(r, carry):
             at = pl.ds(pl.multiple_of(k * rows + r * 16, 16), 16)
-            total = part_ref[jl, at].astype(jnp.float32)
-            left = got[0, jl, at].astype(jnp.float32)
-            right = got[1, jl, at].astype(jnp.float32)
-            total = total + jnp.where(z > 0, left, 0.0) + jnp.where(z < n_z - 1, right, 0.0)
+            total = part[part_at(jl, k, r)].astype(jnp.float32)
+            low_side = got[0, jl, at].astype(jnp.float32)
+            high_side = got[1, jl, at].astype(jnp.float32)
+            total = total + jnp.where(z > 0, low_side, 0.0) + jnp.where(z < n_z - 1, high_side, 0.0)
             value = resid_ref[at].astype(jnp.float32)
             inverse = lax.rsqrt(jnp.mean(value * value, axis=-1, keepdims=True) + norm_eps)
             scaled = value * inverse
@@ -787,32 +842,9 @@
         at = pl.ds(k * rows, rows)
         return pltpu.make_async_copy(buf.at[at], d_out.at[at], loc.at[k])
 
-    def send_step(k, t, wait):
-        jl, j, at = where_is(k, t)
-        for side in range(2):
-            going = (z < j) if side == 0 else (z > j)
-            edge = (z == 0) if side == 0 else (z == n_z - 1)
-            edge_copy = copy_on(k, t, side, part_ref.at[jl, at])
-            inner_copy = copy_on(k, t, side, got.at[side, jl, at])
-            pl.when(going & edge)(edge_copy.wait_send if wait else edge_copy.start)
-            pl.when(going & jnp.logical_not(edge))(inner_copy.wait_send if wait else inner_copy.start)
-
-    def publish(k, wait):
-        @pl.when(own)
-        def _():
-            if wait:
-                to_partner(k).wait_send()
-                keep(k).wait()
-            else:
-                to_partner(k).start()
-                keep(k).start()
-
     def own_chunk(k):
         @pl.when(own)
         def _():
-            if k == 0:
-                for one in fetch:
-                    one.wait()
             jl = z % 2
             pl.when(z > 0)(arrived(0, jl, k).wait_recv)
             pl.when(z < n_z - 1)(arrived(1, jl, k).wait_recv)
@@ -821,32 +853,46 @@
                 to_partner(k - 1).start()
                 keep(k - 1).start()
 
+    done = 0
+    for q in range(GROUPS):
+        compute(q, 0, 1)
+        if q > 0:
+            for k in range((q - 1) * per, q * per):
+                for t in range(2):
+                    send_step(k, t, True, False, False)
+        compute(q, 1, tiles)
+    multiply(done, done + 1)
+    done += 1
+    for k in range((GROUPS - 1) * per, CHUNKS):
+        for t in range(2):
+            send_step(k, t, True, False, False)
+    for one in fetch:
+        one.wait()
+
+    steps = [(k, t) for k in range(CHUNKS) for t in range(2)]
     for n, (k, t) in enumerate(steps):
-        jl, j, at = where_is(k, t)
+        jl = jnp.bitwise_xor(c, t)
+        j = 2 * c + jl
         for side in range(2):
             going = (z < j) if side == 0 else (z > j)
-            inner = (z > 0) if side == 0 else (z < n_z - 1)
-
-            @pl.when(going & inner)
+            between = (z > 0) if side == 0 else (z < n_z - 1)
+
+            @pl.when(going & between)
             def _():
                 arrived(side, jl, k).wait_recv()
                 add_in(side, jl, k)
 
         if n > 0:
-            send_step(*steps[n - 1], False)
-        if t == 0:
-            multiply(k)
+            send_step(*steps[n - 1], False, True, False)
+        if t == 0 and done < tiles:
+            multiply(done, done + 1)
+            done += 1
         if t == 1 and k > 0:
             own_chunk(k - 1)
-    send_step(*steps[-1], False)
+    send_step(*steps[-1], False, True, False)
     own_chunk(CHUNKS - 1)
-    for j in range(CHUNKS, tiles):
-        multiply(j)
-
-    @pl.when(jnp.logical_not(own))
-    def _():
-        for one in fetch:
-            one.wait()
+    if done < tiles:
+        multiply(done, tiles)
 
     @pl.when(own)
     def _():
@@ -856,35 +902,42 @@
     for j in range(max(0, tiles - 2), tiles):
         tile_out(j).wait()
     for k, t in steps:
-        send_step(k, t, True)
+        send_step(k, t, False, False, True)
     for k in range(CHUNKS):
-        publish(k, True)
         at = d_out.at[pl.ds(k * rows, rows)]
+
+        @pl.when(own)
+        def _():
+            to_partner(k).wait_send()
+            keep(k).wait()
+
         pl.when(jnp.logical_not(own))(remote(at, at, p_s.at[k], p_r.at[k], (d, z)).wait_recv)
 
 
-def sum_line(part, resid, cot, gain, hidden, down, n_z):
-    _, full, width = part.shape
+def sum_line(d_gate, d_up, w, resid, cot, gain, hidden, down, n_z):
+    _, full, width = resid.shape
+    b16 = jnp.bfloat16
     return pl.pallas_call(
         functools.partial(sum_line_kernel, n_z),
-        in_specs=[VMEM_SPEC, ANY_SPEC, ANY_SPEC, VMEM_SPEC, ANY_SPEC, ANY_SPEC],
+        in_specs=[ANY_SPEC] * 5 + [VMEM_SPEC] + [ANY_SPEC] * 2,
         out_specs=[ANY_SPEC, VMEM_SPEC, ANY_SPEC],
         out_shape=[
-            jax.ShapeDtypeStruct((full, width), jnp.bfloat16),
+            jax.ShapeDtypeStruct((full, width), b16),
             jax.ShapeDtypeStruct((8, width), jnp.float32),
-            jax.ShapeDtypeStruct((hidden.shape[0], width), jnp.bfloat16),
+            jax.ShapeDtypeStruct((2 * full, width), b16),
         ],
         scratch_shapes=[
-            pltpu.VMEM((2, 2, full, width), jnp.bfloat16), pltpu.VMEM((full, width), jnp.bfloat16),
-            pltpu.VMEM((full, width), jnp.bfloat16), pltpu.VMEM((full, width), jnp.bfloat16),
-            pltpu.VMEM(hidden.shape, jnp.bfloat16), pltpu.VMEM(down.shape, jnp.bfloat16),
-            pltpu.VMEM((2, hidden.shape[0], 256), jnp.bfloat16),
+            pltpu.VMEM((2 * full, w.shape[1]), b16), pltpu.VMEM(w.shape, b16), pltpu.VMEM((2 * full, width), b16),
+            pltpu.VMEM((2, 2, full, width), b16), pltpu.VMEM((full, width), b16),
+            pltpu.VMEM((full, width), b16), pltpu.VMEM((full, width), b16),
+            pltpu.VMEM(hidden.shape, b16), pltpu.VMEM(down.shape, b16), pltpu.VMEM((2, 2 * full, 256), b16),
             DMA((2, CHUNKS)), DMA((2, 2, CHUNKS)), DMA((CHUNKS,)), DMA((CHUNKS,)), DMA((CHUNKS,)), DMA((2,)), DMA((2,)), DMA((2,)),
+            DMA((GROUPS, 2, 2)), DMA((width // 256,)),
         ],
-        compiler_params=pltpu.CompilerParams(collective_id=3, has_side_effects=True, vmem_limit_bytes=56 * 1024 * 1024),
+        compiler_params=pltpu.CompilerParams(collective_id=3, has_side_effects=True, vmem_limit_bytes=63 * 1024 * 1024),
         cost_estimate=pl.CostEstimate(flops=0, bytes_accessed=200_000_000, transcendentals=0),
         name="sum_line",
-    )(part, resid, cot, gain, hidden, down)
+    )(d_gate, d_up, w, resid, cot, gain, hidden, down)
 
 
 WIDE_ROWS = 32
@@ -1339,14 +1392,15 @@
     d_hidden = times_transpose(cot_rows, down_rows)
     d_gate = d_hidden * up_part * sigmoid_gate * (1.0 + gate_part * (1.0 - sigmoid_gate))
     d_up = d_hidden * active
-    d_gate_up16 = jnp.concatenate([d_gate, d_up], 1).astype(jnp.bfloat16)
+    d_gate16 = d_gate.astype(jnp.bfloat16)
+    d_up16 = d_up.astype(jnp.bfloat16)
+    d_gate_up16 = jnp.concatenate([d_gate16, d_up16], 1)
     gate_up_term = contract_rows(normed_two, d_gate_up16).astype(jnp.bfloat16)
     gate_up_sum = lax.psum_scatter(gate_up_term, "dp", scatter_dimension=0, tiled=True)
     down_term = contract_rows(cot_rows, hidden16).astype(jnp.bfloat16)
     down_sum = lax.psum_scatter(down_term, "dp", scatter_dimension=0, tiled=True)
-    d_normed_two = times_transpose(d_gate_up16, gate_up_cols).astype(jnp.bfloat16)
     d_resid16, gain_two_part, down_part = sum_line(
-        d_normed_two.reshape(resid_all.shape), resid_all, cot_all, gain_two, hidden16, down_rows, n_z
+        d_gate16, d_up16, gate_up_cols, resid_all, cot_all, gain_two, hidden16, down_rows, n_z
     )
     down16 = down_part.reshape(resid_all.shape)
     pieces = [

time: 711 us -> 701 us (0.986)
  the two profiles are of different devices: /device:TPU:11 before, /device:TPU:9 now
where the time goes in v8:
time: 701 us; the launch traced here: 694 us
  Pallas kernels  527 us (75%)
  matrix products  103 us (15%)
  other arithmetic  24.3 us (3%)
  local copies, waits for them, and re-layouts  16.8 us (2%)
  between operations  14.4 us (2%)
  starting transfers between devices  7.91 us (1%)
    pallas_call x1, Pallas kernels, hand_out(): pl.pallas_call(functools.partial(hand_out_kernel, n_dp, n_z), in_specs=[V...  159 us
    pallas_call x1, Pallas kernels, share_resid(): pl.pallas_call(functools.partial(share_resid_kernel, n_dp, n_z), in_specs...  103 us
    pallas_call x1, Pallas kernels, sum_line(): pl.pallas_call(functools.partial(sum_line_kernel, n_z), in_specs=[ANY_SPE...  93.2 us
    pallas_call x1, Pallas kernels, gather_in(): pl.pallas_call(functools.partial(gather_in_kernel, n_dp, n_z), in_specs=[...  91.9 us
    dot_general x3, matrix products, contract_rows(): lax.dot_general(left, right, (((0,), (0,)), ((), ())), preferred_element_...  43.8 us
    pallas_call x1, Pallas kernels, attn_forward(): pl.pallas_call(functools.partial(attn_gather_kernel, n_dp, pairs, Q_ROWS,...  37.6 us
    dot_general x2, matrix products, times_transpose(): lax.dot_general(left, right, (((1,), (1,)), ((), ())), preferred_element_...  28.6 us
    dot_general x1, matrix products, layer_step(): jnp.dot(normed_two, gate_up_cols, preferred_element_type=jnp.float32)  22.3 us
  transfers between devices with their start and end apart: 7, of which 0 were waited for; matrix products, arithmetic and copies ran while one was open for 14% of the time, Pallas kernels for 61%

profile of v8, /device:TPU:9, one launch (start us, length us, event | category | flops | bytes accessed | tf_op | source)
XLA Modules:
  0.0 693.6 jit_solution(841355073150820214)
XLA Ops:
  7.2 0.0 all-gather.3.cloned.1.call-start
  7.2 1.9 copy.49
  9.1 1.9 convert_element_type.107.w_ref
  11.0 0.7 convert_bitcast_fusion.1
  11.7 0.7 fusion.15.g_ref
  12.4 1.3 pad.12.s_ref
  13.7 91.9 %gather_in.1 = (bf16[512,2048]{1,0:T(8,128)(2,1)}, bf16[2048,1536]{1,0:T(8,128)(2,1)}, bf16[512,1024]{1,0:T(8,128)(2,1)}, f32[32,8,128]{2,1,0:T(8,128)}, s32[2,8...) custom-call(bf16[2,128,2048]{2,1,0:T(8,128)(2,1)} %x_ref.1, bf16[256,768]{1,0:T(8,128)(2,1)} %convert_element_type.107.w_ref, ...), custom_call_target="tpu_custom_call" | custom-call | bytes 200000000 | tf_op jit(solution)/shard_map/gather_in/pallas_call | solution.py:528
  105.6 0.0 all-gather.3.cloned.1.call-update
  105.7 0.0 all-gather.5.cloned.1.call-start
  105.7 2.8 convert_element_type.115
  108.5 0.0 all-gather.5.cloned.1.call-update
  108.5 0.0 reduce-scatter.5.cloned.1.call-start
  108.6 1.1 slice_reduce_fusion.1
  109.7 0.1 mul.228
  109.8 0.1 mul.238
  109.9 0.7 constant_dynamic-slice_fusion.4
  110.6 0.2 convert_reduce_fusion
  110.9 1.0 fusion.11
  111.9 1.0 maximum_bitcast_fusion.cos_ref
  112.8 1.0 maximum_bitcast_fusion.1.sin_ref
  113.8 0.5 fusion.6
  114.3 0.6 fusion.8.n_ref
  114.9 5.1 fusion.23.qkv_ref
  120.0 0.6 reshape.368.seg_row_ref
  120.6 0.8 reshape.367.seg_col_ref
  121.4 37.6 %attn_forward.1 = (bf16[512,1536]{1,0:T(8,128)(2,1)}, f32[512,512]{1,0:T(8,128)}, bf16[512,1024]{1,0:T(8,128)(2,1)}, bf16[2048,1024]{1,0:T(8,128)(2,1)}) custom-call(f32[512,1536]{1,0:T(8,128)} %fusion.23.qkv_ref, f32[512,128]{1,0:T(8,128)} %maximum_bitcast_fusion.cos_ref, f32[512,128]{1,0:T(8,128)} %maximum_bitcast_fusion.1.sin_ref, ...), custom_call_target="tpu_custom_call" | custom-call | flops 2147483648 | bytes 150000000 | tf_op jit(solution)/shard_map/attn_forward/pallas_call | solution.py:217
  159.1 6.3 convolution_convert_fusion.3.part_ref
  165.3 103.0 %share_resid.1 = (bf16[2,512,2048]{2,1,0:T(8,128)(2,1)}, bf16[2048,4096]{1,0:T(8,128)(2,1)}) custom-call(bf16[512,2048]{1,0:T(8,128)(2,1)} %convolution_convert_fusion.3.part_ref, bf16[512,2048]{1,0:T(8,128)(2,1)} %get-tuple-element.54.x_ref, bf16[256,4096]{1,0:T(8,128)(2,1)} %get-tuple-element.61.w_ref), custom_call_target="tpu_custom_call" | custom-call | bytes 200000000 | tf_op jit(solution)/shard_map/share_resid/pallas_call | solution.py:684
  268.4 3.2 multiply_reduce_fusion
  271.7 0.2 copy-done
  271.8 1.0 fusion.4
  272.9 0.0 copy-start.4
  272.9 2.0 copy-done.4
  274.9 22.3 %fusion.24 = f32[1024,4096]{1,0:T(8,128)} fusion(bf16[1024,2048]{1,0:T(8,128)(2,1)S(1)} %fusion.4, bf16[2048,4096]{1,0:T(8,128)(2,1)} %get-tuple-element.64.w_ref), kind=kOutput, calls=%fused_computation.69 | convolution fusion | flops 17179869184 | bytes 37748736 | tf_op jit(solution)/shard_map/dot_general | solution.py:1385
  297.2 22.4 %multiply_convert_fusion.1 = (bf16[1024,2048]{1,0:T(8,128)(2,1)}, bf16[1024,2048]{1,0:T(8,128)(2,1)}, bf16[1024,2048]{1,0:T(8,128)(2,1)}) fusion(f32[1024,4096]{1,0:T(8,128)} %fusion.24, bf16[1024,2048]{1,0:T(8,128)(2,1)} %bitcast.48, bf16[2048,2048]{1,0:T(8,128)(2,1)} %all-gather.5.cloned.1.call-done.down_ref), kind=kOutput, calls=%fused_computation.8 | convolution fusion | flops 8621391872 | bytes 41943040 | tf_op jit(solution)/shard_map/dot_general | solution.py:1319
  319.5 14.0 %convolution_convert_fusion.1 = bf16[2048,2048]{1,0:T(8,128)(2,1)} fusion(bf16[1024,2048]{1,0:T(8,128)(2,1)} %bitcast.49, bf16[1024,2048]{1,0:T(8,128)(2,1)} %get-tuple-element.100.hid_ref), kind=kOutput, calls=%fused_computation.13 | convolution fusion | flops 8594128896 | bytes 16777216 | tf_op jit(solution)/shard_map/dot_general | solution.py:1313
  333.6 0.0 reduce-scatter.5.cloned.1.call-update
  333.6 0.0 reduce-scatter.3.cloned.1.call-start
  333.6 25.4 %convolution_convert_fusion = bf16[2048,4096]{1,0:T(8,128)(2,1)} fusion(bf16[1024,2048]{1,0:T(8,128)(2,1)} %copy-done.4, bf16[1024,2048]{1,0:T(8,128)(2,1)} %get-tuple-element.98.d_up_ref, bf16[1024,2048]{1,0:T(8,128)(2,1)} %get-tuple-element.99.d_gate_ref), kind=kOutput, calls=%fused_computation | convolution fusion | flops 17205035008 | bytes 29360128 | tf_op jit(solution)/shard_map/dot_general | solution.py:1313
  359.0 0.0 reduce-scatter.3.cloned.1.call-update
  359.1 0.7 reshape_squeeze.7.gain_ref
  359.8 0.7 reshape_squeeze.6.gain_ref
  360.5 93.2 %sum_line.1 = (bf16[512,2048]{1,0:T(8,128)(2,1)}, f32[8,2048]{1,0:T(8,128)}, bf16[1024,2048]{1,0:T(8,128)(2,1)}) custom-call(bf16[1024,2048]{1,0:T(8,128)(2,1)} %get-tuple-element.99.d_gate_ref, bf16[1024,2048]{1,0:T(8,128)(2,1)} %get-tuple-element.98.d_up_ref, bf16[2048,4096]{1,0:T(8,128)(2,1)} %get-tuple-element.64.w_ref, ...), custom_call_target="tpu_custom_call" | custom-call | bytes 200000000 | tf_op jit(solution)/shard_map/sum_line/pallas_call | solution.py:920
  453.7 3.8 constant_dynamic-slice_fusion.2
  457.5 3.4 collective-permute-start
  460.9 0.0 collective-permute-start.2
  460.9 4.3 collective-permute-start.1
  465.3 4.4 convolution_convert_fusion.2.ot_ref
  469.7 3.3 convolution_convert_fusion.4.d_out_ref
  473.0 20.3 %attn_backward.1.dq_ref = bf16[512,1536]{1,0:T(8,128)(2,1)} custom-call(bf16[512,1536]{1,0:T(8,128)(2,1)} %get-tuple-element.66.turned_ref, bf16[512,1024]{1,0:T(8,128)(2,1)} %convolution_convert_fusion.4.d_out_ref, f32[512,512]{1,0:T(8,128)} %get-tuple-element.68.lse_ref, f32[512,128]{1,0:T(8,128)} %maximum_bitcast_fusion.cos_ref, ...), custom_call_target="tpu_custom_call" | custom-call | flops 5368709120 | bytes 4718592 | tf_op jit(solution)/shard_map/attn_backward/pallas_call | solution.py:243
  493.3 0.0 copy-start.17
  493.3 158.7 %hand_out.1 = (bf16[2,128,2048]{2,1,0:T(8,128)(2,1)}, f32[256,768]{1,0:T(8,128)}, f32[512,256]{1,0:T(8,128)}, f32[16,128]{1,0:T(8,128)}) custom-call(bf16[512,1536]{1,0:T(8,128)(2,1)} %attn_backward.1.dq_ref, bf16[512,2048]{1,0:T(8,128)(2,1)} %copy-done.2, bf16[512,2048]{1,0:T(8,128)(2,1)} %get-tuple-element.54.x_ref, ...), custom_call_target="tpu_custom_call" | custom-call | bytes 300000000 | tf_op jit(solution)/shard_map/hand_out/pallas_call | solution.py:1271
  652.1 0.9 bitcast_reduce_fusion
  653.0 0.1 constant_dynamic-slice_fusion.3
  653.1 0.6 multiply_subtract_fusion.2
  653.7 2.4 multiply_subtract_fusion.1
  656.1 1.8 multiply_subtract_fusion
  657.9 4.1 add_convert_fusion
  662.0 7.3 %shard_map.405 = (f32[2048,256]{1,0:T(8,128)}, f32[2048,256]{1,0:T(8,128)}, f32[2048,256]{1,0:T(8,128)}, f32[2048,256]{1,0:T(8,128)}) custom-call(bf16[256,2048]{1,0:T(8,128)(2,1)} %reduce-scatter.5.cloned.1.call-done.grad_ref, f32[2048,256]{1,0:T(8,128)} %w_ref.3, f32[2048,256]{1,0:T(8,128)} %m_ref.3, f32[2048,256]{1,0:T(8,128)} %v_ref.3), custom_call_target="tpu_custom_call" | custom-call | flops 10485760 | bytes 15728640 | tf_op jit(solution)/shard_map/pallas_call | solution.py:969
  669.3 0.0 reduce-scatter.3.cloned.1.call-done.grad_ref
  669.3 14.9 %shard_map.404 = (f32[256,2,2048]{2,1,0:T(2,128)}, f32[256,2,2048]{2,1,0:T(2,128)}, f32[256,2,2048]{2,1,0:T(2,128)}, f32[256,2,2048]{2,1,0:T(2,128)}) custom-call(bf16[256,4096]{1,0:T(8,128)(2,1)} %reduce-scatter.3.cloned.1.call-done.grad_ref, f32[256,2,2048]{2,1,0:T(2,128)} %w_ref.2, f32[256,2,2048]{2,1,0:T(2,128)} %m_ref.2, f32[256,2,2048]{2,1,0:T(2,128)} %v_ref.2), custom_call_target="tpu_custom_call" | custom-call | flops 20971520 | bytes 31457280 | tf_op jit(solution)/shard_map/pallas_call | solution.py:969
  684.2 1.0 copy.55
  685.2 0.9 copy.56
  686.1 0.8 copy.57
  (53 shorter events, 0.2 us)
Async XLA Ops:
  7.2 290.0 %all-gather.3.cloned.1.call-start = ((), (), s32[]{:S(2)}) async-start(), calls=%async_computation.2 | async-start | bytes 5242880 | tf_op jit(solution)/shard_map/all_gather | solution.py:1370
  105.6 8.2 %copy-start.1 = (bf16[512,2048]{1,0:T(8,128)(2,1)S(1)}, bf16[512,2048]{1,0:T(8,128)(2,1)}, u32[]{:S(2)}) copy-start(bf16[512,2048]{1,0:T(8,128)(2,1)} %get-tuple-element.54.x_ref) | copy-start | bytes 6291460
  105.7 191.5 %all-gather.5.cloned.1.call-start = ((), (), s32[]{:S(2)}) async-start(), calls=%async_computation.3 | async-start | bytes 9437184 | tf_op jit(solution)/shard_map/all_gather | solution.py:1358
  108.5 553.5 %reduce-scatter.5.cloned.1.call-start = ((), (), s32[]{:S(2)}) async-start(), calls=%async_computation.5 | async-start | bytes 9437184 | tf_op jit(solution)/shard_map/reduce_scatter | solution.py:1401
  110.9 4.0 copy-start.3
  114.9 5.1 copy-start.2
  268.4 3.5 copy-start
  272.9 2.0 copy-start.4
  333.6 335.7 %reduce-scatter.3.cloned.1.call-start = ((), (), s32[]{:S(2)}) async-start(), calls=%async_computation.4 | async-start | bytes 18874368 | tf_op jit(solution)/shard_map/reduce_scatter | solution.py:1399
  453.7 11.6 %copy-start.9 = (bf16[512,2048]{1,0:T(8,128)(2,1)S(1)}, bf16[512,2048]{1,0:T(8,128)(2,1)}, u32[]{:S(2)}) copy-start(bf16[512,2048]{1,0:T(8,128)(2,1)} %get-tuple-element.67.dr_ref) | copy-start | bytes 6291460
  453.7 11.6 %copy-start.22 = (bf16[512,1024]{1,0:T(8,128)(2,1)S(1)}, bf16[512,1024]{1,0:T(8,128)(2,1)}, u32[]{:S(2)}) copy-start(bf16[512,1024]{1,0:T(8,128)(2,1)} %get-tuple-element.59) | copy-start | bytes 3145732
  457.5 200.4 %collective-permute-start = (bf16[2,128,2048]{2,1,0:T(8,128)(2,1)}, bf16[2,128,2048]{2,1,0:T(8,128)(2,1)S(1)}, u32[]{:S(2)}, u32[]{:S(2)}) collective-permute-start(bf16[2,128,2048]{2,1,0:T(8,128)(2,1)} %get-tuple-element.101), channel_id=1, source_target_pairs={{0,1},{1,2},{2,3},{3,0},{4,5},{5,6},{6,7},{7,4},{8,9},{9,10},{10,1... | collective-permute-start | bytes 3145736 | tf_op jit(solution)/shard_map/ppermute | solution.py:1411
  460.9 197.0 %collective-permute-start.2 = (bf16[2,128,2048]{2,1,0:T(8,128)(2,1)}, bf16[2,128,2048]{2,1,0:T(8,128)(2,1)}, u32[]{:S(2)}, u32[]{:S(2)}) collective-permute-start(bf16[2,128,2048]{2,1,0:T(8,128)(2,1)} %get-tuple-element.102), channel_id=1, source_target_pairs={{0,3},{1,0},{2,1},{3,2},{4,7},{5,4},{6,5},{7,6},{8,11},{9,8},{10,9... | collective-permute-start | bytes 3145736 | tf_op jit(solution)/shard_map/ppermute | solution.py:1411
  460.9 197.0 %collective-permute-start.1 = (bf16[2,128,2048]{2,1,0:T(8,128)(2,1)}, bf16[2,128,2048]{2,1,0:T(8,128)(2,1)}, u32[]{:S(2)}, u32[]{:S(2)}) collective-permute-start(bf16[2,128,2048]{2,1,0:T(8,128)(2,1)} %get-tuple-element.103), channel_id=1, source_target_pairs={{0,2},{1,3},{2,0},{3,1},{4,6},{5,7},{6,4},{7,5},{8,10},{9,11},{10,... | collective-permute-start | bytes 3145736 | tf_op jit(solution)/shard_map/ppermute | solution.py:1411
  465.3 4.4 copy-start.21
  493.2 159.8 %copy-start.15 = (f32[64]{0:T(128)S(1)}, f32[64]{0:T(128)}, u32[]{:S(2)}) copy-start(f32[64]{0:T(128)} %param.27) | copy-start | bytes 772
  493.2 159.8 %copy-start.16 = (f32[64]{0:T(128)S(1)}, f32[64]{0:T(128)}, u32[]{:S(2)}) copy-start(f32[64]{0:T(128)} %param.24) | copy-start | bytes 772
  493.3 159.8 %copy-start.17 = (f32[64]{0:T(128)S(1)}, f32[64]{0:T(128)}, u32[]{:S(2)}) copy-start(f32[64]{0:T(128)} %param.33) | copy-start | bytes 772
  493.3 159.8 %copy-start.18 = (f32[64]{0:T(128)S(1)}, f32[64]{0:T(128)}, u32[]{:S(2)}) copy-start(f32[64]{0:T(128)} %param.39) | copy-start | bytes 772
  493.3 159.8 %copy-start.19 = (f32[64]{0:T(128)S(1)}, f32[64]{0:T(128)}, u32[]{:S(2)}) copy-start(f32[64]{0:T(128)} %param.36) | copy-start | bytes 772
  493.3 159.8 %copy-start.20 = (f32[64]{0:T(128)S(1)}, f32[64]{0:T(128)}, u32[]{:S(2)}) copy-start(f32[64]{0:T(128)} %param.30) | copy-start | bytes 772
  493.3 160.4 %copy-start.7 = (f32[512,256]{1,0:T(8,128)S(1)}, f32[512,256]{1,0:T(8,128)}, u32[]{:S(2)}) copy-start(f32[512,256]{1,0:T(8,128)} %param.26) | copy-start | bytes 1572868
  493.3 160.4 %copy-start.13 = (f32[512,256]{1,0:T(8,128)S(1)}, f32[512,256]{1,0:T(8,128)}, u32[]{:S(2)}) copy-start(f32[512,256]{1,0:T(8,128)} %param.32) | copy-start | bytes 1572868
  493.3 160.3 %copy-start.14 = (f32[512,256]{1,0:T(8,128)S(1)}, f32[512,256]{1,0:T(8,128)}, u32[]{:S(2)}) copy-start(f32[512,256]{1,0:T(8,128)} %param.38) | copy-start | bytes 1572868
  652.1 4.0 copy-start.5
  652.1 4.0 copy-start.6
  652.1 4.0 copy-start.11
  652.1 4.0 copy-start.12
  669.3 14.9 %copy-start.10 = (bf16[2,128,2048]{2,1,0:T(8,128)(2,1)S(1)}, bf16[2,128,2048]{2,1,0:T(8,128)(2,1)}, u32[]{:S(2)}) copy-start(bf16[2,128,2048]{2,1,0:T(8,128)(2,1)} %get-tuple-element.142) | copy-start | bytes 3145732
  669.3 16.8 %copy-start.8 = (f32[512,256]{1,0:T(8,128)S(1)}, f32[512,256]{1,0:T(8,128)}, u32[]{:S(2)}) copy-start(f32[512,256]{1,0:T(8,128)} %get-tuple-element.145) | copy-start | bytes 1572868
Sparse Core Ops, SparseCore 0:
  105.8 81.8 all-gather.2
  190.1 86.4 all-gather.4
  333.7 70.4 reduce-scatter.4
  407.6 135.7 reduce-scatter.2

commit v9 on v8

--- a/solution.py
+++ b/solution.py
@@ -381,7 +381,7 @@
 
 
 def gather_in_kernel(n_dp, n_z, x_ref, w_ref, v_ref, g_ref, s_ref, gu_ref, xs, wq, vo, ga, sg, gu16, gu_in, gu_out,
-                     x_s, x_r, f_s, f_r, w_s, w_r, v_s, v_r, d_s, d_r, g_s, g_r, s_s, s_r, loc, gu_is, gu_os):
+                     x_s, x_r, f_s, f_r, w_s, w_r, v_s, v_r, d_s, d_r, g_s, g_r, s_s, s_r, loc, gu_is, gu_os, w_f, v_f):
     d, z, pair, c = place()
     n_d = n_dp // 2
     me = d * n_z + z
@@ -416,15 +416,22 @@
     greet_all(n_dp, n_z, d, z)
 
     def line_stage(src, dst, send, recv, spare, wait):
-        for o in range(n_z):
-            copy = remote(src, dst, send.at[o], recv.at[c, z % 2], (2 * pair + cz, lax.rem(z + o, n_z)))
+        for o, zz in ((0, z), (1, z - 1), (2, z + 1)):
+            copy = remote(src, dst, send.at[o], recv.at[c, z % 2], (2 * pair + cz, zz))
             act = copy.wait_send if wait else copy.start
             if o == 0:
                 pl.when(c != cz)(act)
                 if not wait:
                     pl.when(c == cz)(pltpu.make_async_copy(src, dst, loc.at[spare]).start)
             else:
-                act()
+                pl.when(zz >= 0 if o == 1 else zz <= n_z - 1)(act)
+
+    def line_relay(blk, send, recv, core, b, wait):
+        j = 2 * c + b
+        to = jnp.where(z > j, z + 1, z - 1)
+        ok = (z != j) & (to >= 0) & (to <= n_z - 1)
+        copy = remote(blk, blk, send, recv.at[core, b], (2 * pair + c, to))
+        pl.when(ok)(copy.wait_send if wait else copy.start)
 
     my_block = block_at(wq, shape, d, z % 2)
     line_stage(w_ref, my_block, w_s, w_r, 0, False)
@@ -472,13 +479,24 @@
         arrive = remote(w_ref, blk, w_s.at[0], w_r.at[core, b], (d, z))
         pl.when(jnp.logical_not(mine))(arrive.wait_recv)
         pl.when(mine)(lambda blk=blk: pltpu.make_async_copy(w_ref, blk, loc.at[0]).wait())
+        line_relay(blk, w_f.at[t], w_r, core, b, False)
         spread.own(t)
-        if t == 1:
+        if t == 0:
             line_stage(v_ref, block_at(vo, v_ref.shape, c, z % 2), v_s, v_r, 4, False)
         if t > 0:
             spread.pass_on(t - 1)
         round_chunks(t * chunks // 4, (t + 1) * chunks // 4)
 
+    def out_unit(t, wait):
+        core, b = turn_of(t)
+        blk = block_at(vo, v_ref.shape, core, b)
+        mine = (core == c) & (2 * c + b == z)
+        if not wait:
+            pl.when(jnp.logical_not(mine))(remote(blk, blk, v_s.at[0], v_r.at[core, b], (d, z)).wait_recv)
+            pl.when(mine)(pltpu.make_async_copy(v_ref, blk, loc.at[4]).wait)
+        line_relay(blk, v_f.at[t], v_r, core, b, wait)
+
+    spread.pass_on(3)
     for o in range(n_z):
         zs = lax.rem(z + o, n_z)
         src = xs.at[pl.ds(pl.multiple_of(zs * rows + c * half, half), half)]
@@ -487,7 +505,7 @@
         pl.when(jnp.logical_not(mine))(arrive.wait_recv)
         pl.when(mine)(lambda src=src: pltpu.make_async_copy(src, src, loc.at[1]).wait())
         remote(src, src, f_s.at[zs], f_r.at[zs], (2 * pair + 1 - c, z)).start()
-    spread.pass_on(3)
+        out_unit(o, False)
 
     line_stage(w_ref, my_block, w_s, w_r, 0, True)
     line_stage(v_ref, block_at(vo, v_ref.shape, c, z % 2), v_s, v_r, 4, True)
@@ -502,12 +520,10 @@
         copy = remote(src, src, f_s.at[zs], f_r.at[zs], (d, z))
         copy.wait_send()
         copy.wait_recv()
-    for core in range(2):
-        for b in range(2):
-            blk = block_at(vo, v_ref.shape, core, b)
-            mine = (core == c) & (2 * c + b == z)
-            pl.when(jnp.logical_not(mine))(remote(blk, blk, v_s.at[0], v_r.at[core, b], (d, z)).wait_recv)
-            pl.when(mine)(pltpu.make_async_copy(v_ref, blk, loc.at[4]).wait)
+    for t in range(4):
+        core, b = turn_of(t)
+        line_relay(block_at(wq, shape, 2 * pair + core, b), w_f.at[t], w_r, core, b, True)
+        out_unit(t, True)
     for i in range(max(0, chunks - 2), chunks):
         chunk_out(i, i % 2).wait()
     seg_copy.wait_send()
@@ -540,8 +556,8 @@
         scratch_shapes=[
             pltpu.VMEM((2, WIDE_ROWS) + wide.shape[1:], jnp.float32),
             pltpu.VMEM((2, WIDE_ROWS, wide.shape[1] * wide.shape[2]), jnp.bfloat16),
-            DMA((2, 2)), DMA((n_z,)), DMA((n_z,)), DMA((n_z,)), DMA((n_z,)), DMA((2, 2)), DMA((n_z,)), DMA((2, 2)),
-            DMA((n_d - 1, 4, 2)), DMA((n_d - 1, 4, 2)), DMA, DMA, DMA, DMA, DMA((5,)), DMA((2,)), DMA((2,)),
+            DMA((2, 2)), DMA((n_z,)), DMA((n_z,)), DMA((n_z,)), DMA((3,)), DMA((2, 2)), DMA((3,)), DMA((2, 2)),
+            DMA((n_d - 1, 4, 2)), DMA((n_d - 1, 4, 2)), DMA, DMA, DMA, DMA, DMA((5,)), DMA((2,)), DMA((2,)), DMA((4,)), DMA((4,)),
         ],
         compiler_params=pltpu.CompilerParams(collective_id=1, has_side_effects=True),
         cost_estimate=pl.CostEstimate(flops=0, bytes_accessed=200_000_000, transcendentals=0),

time: 701 us -> 687 us (0.980)
  Pallas kernels: 527 us -> 514 us
    pallas_call x1, Pallas kernels: 91.9 us -> 71.6 us  [gather_in(): pl.pallas_call(functools.partial(gather_in_kernel, n_dp, n_z), in_specs=[...]
    pallas_call x1, Pallas kernels: 103 us -> 115 us  [share_resid(): pl.pallas_call(functools.partial(share_resid_kernel, n_dp, n_z), in_specs...]
  transfers between devices with their start and end apart: 7 -> 7, of which waited for: 0 -> 0; matrix products, arithmetic and copies ran while one was open for 14% -> 14% of each run, Pallas kernels for 61% -> 63%
where the time goes in v9:
time: 687 us; the launch traced here: 679 us
  Pallas kernels  514 us (75%)
  matrix products  103 us (15%)
  other arithmetic  24.3 us (4%)
  local copies, waits for them, and re-layouts  16.8 us (2%)
  between operations  14.4 us (2%)
  starting transfers between devices  7.01 us (1%)
    pallas_call x1, Pallas kernels, hand_out(): pl.pallas_call(functools.partial(hand_out_kernel, n_dp, n_z), in_specs=[V...  160 us
    pallas_call x1, Pallas kernels, share_resid(): pl.pallas_call(functools.partial(share_resid_kernel, n_dp, n_z), in_specs...  115 us
    pallas_call x1, Pallas kernels, sum_line(): pl.pallas_call(functools.partial(sum_line_kernel, n_z), in_specs=[ANY_SPE...  93.6 us
    pallas_call x1, Pallas kernels, gather_in(): pl.pallas_call(functools.partial(gather_in_kernel, n_dp, n_z), in_specs=[...  71.6 us
    dot_general x3, matrix products, contract_rows(): lax.dot_general(left, right, (((0,), (0,)), ((), ())), preferred_element_...  43.8 us
    pallas_call x1, Pallas kernels, attn_forward(): pl.pallas_call(functools.partial(attn_gather_kernel, n_dp, pairs, Q_ROWS,...  30.9 us
    dot_general x2, matrix products, times_transpose(): lax.dot_general(left, right, (((1,), (1,)), ((), ())), preferred_element_...  28.6 us
    dot_general x1, matrix products, layer_step(): jnp.dot(normed_two, gate_up_cols, preferred_element_type=jnp.float32)  22.3 us
  transfers between devices with their start and end apart: 7, of which 0 were waited for; matrix products, arithmetic and copies ran while one was open for 14% of the time, Pallas kernels for 63%

profile of v9, /device:TPU:9, one launch (start us, length us, event | category | flops | bytes accessed | tf_op | source)
XLA Modules:
  0.0 679.4 jit_solution(15576266958060290506)
XLA Ops:
  7.2 0.0 all-gather.3.cloned.1.call-start
  7.2 1.9 copy.49
  9.1 1.9 convert_element_type.107.w_ref
  11.0 0.7 convert_bitcast_fusion.1
  11.7 0.7 fusion.15.g_ref
  12.4 1.3 pad.12.s_ref
  13.7 71.6 %gather_in.1 = (bf16[512,2048]{1,0:T(8,128)(2,1)}, bf16[2048,1536]{1,0:T(8,128)(2,1)}, bf16[512,1024]{1,0:T(8,128)(2,1)}, f32[32,8,128]{2,1,0:T(8,128)}, s32[2,8...) custom-call(bf16[2,128,2048]{2,1,0:T(8,128)(2,1)} %x_ref.1, bf16[256,768]{1,0:T(8,128)(2,1)} %convert_element_type.107.w_ref, ...), custom_call_target="tpu_custom_call" | custom-call | bytes 200000000 | tf_op jit(solution)/shard_map/gather_in/pallas_call | solution.py:544
  85.4 0.0 all-gather.3.cloned.1.call-update
  85.4 0.0 all-gather.5.cloned.1.call-start
  85.4 2.8 convert_element_type.115
  88.2 0.0 all-gather.5.cloned.1.call-update
  88.3 0.0 reduce-scatter.5.cloned.1.call-start
  88.3 1.1 slice_reduce_fusion.1
  89.4 0.1 mul.228
  89.5 0.1 mul.238
  89.6 0.7 constant_dynamic-slice_fusion.4
  90.3 0.2 convert_reduce_fusion
  90.6 1.0 fusion.11
  91.6 1.0 maximum_bitcast_fusion.cos_ref
  92.6 1.0 maximum_bitcast_fusion.1.sin_ref
  93.5 0.5 fusion.6
  94.0 0.6 fusion.8.n_ref
  94.6 5.1 fusion.23.qkv_ref
  99.7 0.6 reshape.368.seg_row_ref
  100.3 0.8 reshape.367.seg_col_ref
  101.2 30.9 %attn_forward.1 = (bf16[512,1536]{1,0:T(8,128)(2,1)}, f32[512,512]{1,0:T(8,128)}, bf16[512,1024]{1,0:T(8,128)(2,1)}, bf16[2048,1024]{1,0:T(8,128)(2,1)}) custom-call(f32[512,1536]{1,0:T(8,128)} %fusion.23.qkv_ref, f32[512,128]{1,0:T(8,128)} %maximum_bitcast_fusion.cos_ref, f32[512,128]{1,0:T(8,128)} %maximum_bitcast_fusion.1.sin_ref, ...), custom_call_target="tpu_custom_call" | custom-call | flops 2147483648 | bytes 150000000 | tf_op jit(solution)/shard_map/attn_forward/pallas_call | solution.py:217
  132.1 6.2 convolution_convert_fusion.3.part_ref
  138.3 115.1 %share_resid.1 = (bf16[2,512,2048]{2,1,0:T(8,128)(2,1)}, bf16[2048,4096]{1,0:T(8,128)(2,1)}) custom-call(bf16[512,2048]{1,0:T(8,128)(2,1)} %convolution_convert_fusion.3.part_ref, bf16[512,2048]{1,0:T(8,128)(2,1)} %get-tuple-element.54.x_ref, bf16[256,4096]{1,0:T(8,128)(2,1)} %get-tuple-element.61.w_ref), custom_call_target="tpu_custom_call" | custom-call | bytes 200000000 | tf_op jit(solution)/shard_map/share_resid/pallas_call | solution.py:700
  253.3 3.2 multiply_reduce_fusion
  256.6 0.2 copy-done
  256.8 1.0 fusion.4
  257.8 2.0 copy-done.4
  259.8 22.3 %fusion.24 = f32[1024,4096]{1,0:T(8,128)} fusion(bf16[1024,2048]{1,0:T(8,128)(2,1)S(1)} %fusion.4, bf16[2048,4096]{1,0:T(8,128)(2,1)} %get-tuple-element.64.w_ref), kind=kOutput, calls=%fused_computation.69 | convolution fusion | flops 17179869184 | bytes 37748736 | tf_op jit(solution)/shard_map/dot_general | solution.py:1401
  282.1 22.4 %multiply_convert_fusion.1 = (bf16[1024,2048]{1,0:T(8,128)(2,1)}, bf16[1024,2048]{1,0:T(8,128)(2,1)}, bf16[1024,2048]{1,0:T(8,128)(2,1)}) fusion(f32[1024,4096]{1,0:T(8,128)} %fusion.24, bf16[1024,2048]{1,0:T(8,128)(2,1)} %bitcast.48, bf16[2048,2048]{1,0:T(8,128)(2,1)} %all-gather.5.cloned.1.call-done.down_ref), kind=kOutput, calls=%fused_computation.8 | convolution fusion | flops 8621391872 | bytes 41943040 | tf_op jit(solution)/shard_map/dot_general | solution.py:1335
  304.5 14.0 %convolution_convert_fusion.1 = bf16[2048,2048]{1,0:T(8,128)(2,1)} fusion(bf16[1024,2048]{1,0:T(8,128)(2,1)} %bitcast.49, bf16[1024,2048]{1,0:T(8,128)(2,1)} %get-tuple-element.100.hid_ref), kind=kOutput, calls=%fused_computation.13 | convolution fusion | flops 8594128896 | bytes 16777216 | tf_op jit(solution)/shard_map/dot_general | solution.py:1329
  318.5 0.0 reduce-scatter.5.cloned.1.call-update
  318.5 0.0 reduce-scatter.3.cloned.1.call-start
  318.6 25.4 %convolution_convert_fusion = bf16[2048,4096]{1,0:T(8,128)(2,1)} fusion(bf16[1024,2048]{1,0:T(8,128)(2,1)} %copy-done.4, bf16[1024,2048]{1,0:T(8,128)(2,1)} %get-tuple-element.98.d_up_ref, bf16[1024,2048]{1,0:T(8,128)(2,1)} %get-tuple-element.99.d_gate_ref), kind=kOutput, calls=%fused_computation | convolution fusion | flops 17205035008 | bytes 29360128 | tf_op jit(solution)/shard_map/dot_general | solution.py:1329
  343.9 0.0 reduce-scatter.3.cloned.1.call-update
  344.0 0.7 reshape_squeeze.7.gain_ref
  344.7 0.7 reshape_squeeze.6.gain_ref
  345.4 93.6 %sum_line.1 = (bf16[512,2048]{1,0:T(8,128)(2,1)}, f32[8,2048]{1,0:T(8,128)}, bf16[1024,2048]{1,0:T(8,128)(2,1)}) custom-call(bf16[1024,2048]{1,0:T(8,128)(2,1)} %get-tuple-element.99.d_gate_ref, bf16[1024,2048]{1,0:T(8,128)(2,1)} %get-tuple-element.98.d_up_ref, bf16[2048,4096]{1,0:T(8,128)(2,1)} %get-tuple-element.64.w_ref, ...), custom_call_target="tpu_custom_call" | custom-call | bytes 200000000 | tf_op jit(solution)/shard_map/sum_line/pallas_call | solution.py:936
  439.0 3.8 constant_dynamic-slice_fusion.2
  442.8 3.0 collective-permute-start
  445.8 0.4 collective-permute-start.2
  446.2 3.4 collective-permute-start.1
  449.6 4.4 convolution_convert_fusion.2.ot_ref
  454.0 3.3 convolution_convert_fusion.4.d_out_ref
  457.3 20.4 %attn_backward.1.dq_ref = bf16[512,1536]{1,0:T(8,128)(2,1)} custom-call(bf16[512,1536]{1,0:T(8,128)(2,1)} %get-tuple-element.66.turned_ref, bf16[512,1024]{1,0:T(8,128)(2,1)} %convolution_convert_fusion.4.d_out_ref, f32[512,512]{1,0:T(8,128)} %get-tuple-element.68.lse_ref, f32[512,128]{1,0:T(8,128)} %maximum_bitcast_fusion.cos_ref, ...), custom_call_target="tpu_custom_call" | custom-call | flops 5368709120 | bytes 4718592 | tf_op jit(solution)/shard_map/attn_backward/pallas_call | solution.py:243
  477.7 0.0 copy-start.17
  477.7 0.0 copy-start.18
  477.8 160.1 %hand_out.1 = (bf16[2,128,2048]{2,1,0:T(8,128)(2,1)}, f32[256,768]{1,0:T(8,128)}, f32[512,256]{1,0:T(8,128)}, f32[16,128]{1,0:T(8,128)}) custom-call(bf16[512,1536]{1,0:T(8,128)(2,1)} %attn_backward.1.dq_ref, bf16[512,2048]{1,0:T(8,128)(2,1)} %copy-done.2, bf16[512,2048]{1,0:T(8,128)(2,1)} %get-tuple-element.54.x_ref, ...), custom_call_target="tpu_custom_call" | custom-call | bytes 300000000 | tf_op jit(solution)/shard_map/hand_out/pallas_call | solution.py:1287
  637.9 0.9 bitcast_reduce_fusion
  638.8 0.1 constant_dynamic-slice_fusion.3
  638.9 0.6 multiply_subtract_fusion.2
  639.5 2.4 multiply_subtract_fusion.1
  641.9 1.8 multiply_subtract_fusion
  643.7 4.1 add_convert_fusion
  647.8 7.3 %shard_map.405 = (f32[2048,256]{1,0:T(8,128)}, f32[2048,256]{1,0:T(8,128)}, f32[2048,256]{1,0:T(8,128)}, f32[2048,256]{1,0:T(8,128)}) custom-call(bf16[256,2048]{1,0:T(8,128)(2,1)} %reduce-scatter.5.cloned.1.call-done.grad_ref, f32[2048,256]{1,0:T(8,128)} %w_ref.3, f32[2048,256]{1,0:T(8,128)} %m_ref.3, f32[2048,256]{1,0:T(8,128)} %v_ref.3), custom_call_target="tpu_custom_call" | custom-call | flops 10485760 | bytes 15728640 | tf_op jit(solution)/shard_map/pallas_call | solution.py:985
  655.1 0.0 reduce-scatter.3.cloned.1.call-done.grad_ref
  655.1 14.9 %shard_map.404 = (f32[256,2,2048]{2,1,0:T(2,128)}, f32[256,2,2048]{2,1,0:T(2,128)}, f32[256,2,2048]{2,1,0:T(2,128)}, f32[256,2,2048]{2,1,0:T(2,128)}) custom-call(bf16[256,4096]{1,0:T(8,128)(2,1)} %reduce-scatter.3.cloned.1.call-done.grad_ref, f32[256,2,2048]{2,1,0:T(2,128)} %w_ref.2, f32[256,2,2048]{2,1,0:T(2,128)} %m_ref.2, f32[256,2,2048]{2,1,0:T(2,128)} %v_ref.2), custom_call_target="tpu_custom_call" | custom-call | flops 20971520 | bytes 31457280 | tf_op jit(solution)/shard_map/pallas_call | solution.py:985
  670.0 1.0 copy.55
  671.0 0.9 copy.56
  671.9 0.8 copy.57
  (53 shorter events, 0.2 us)
Async XLA Ops:
  7.2 274.9 %all-gather.3.cloned.1.call-start = ((), (), s32[]{:S(2)}) async-start(), calls=%async_computation.2 | async-start | bytes 5242880 | tf_op jit(solution)/shard_map/all_gather | solution.py:1386
  85.3 8.2 %copy-start.1 = (bf16[512,2048]{1,0:T(8,128)(2,1)S(1)}, bf16[512,2048]{1,0:T(8,128)(2,1)}, u32[]{:S(2)}) copy-start(bf16[512,2048]{1,0:T(8,128)(2,1)} %get-tuple-element.54.x_ref) | copy-start | bytes 6291460
  85.4 196.7 %all-gather.5.cloned.1.call-start = ((), (), s32[]{:S(2)}) async-start(), calls=%async_computation.3 | async-start | bytes 9437184 | tf_op jit(solution)/shard_map/all_gather | solution.py:1374
  88.3 559.5 %reduce-scatter.5.cloned.1.call-start = ((), (), s32[]{:S(2)}) async-start(), calls=%async_computation.5 | async-start | bytes 9437184 | tf_op jit(solution)/shard_map/reduce_scatter | solution.py:1417
  90.6 4.0 copy-start.3
  94.6 5.1 copy-start.2
  253.3 3.5 copy-start
  257.8 2.0 copy-start.4
  318.5 336.6 %reduce-scatter.3.cloned.1.call-start = ((), (), s32[]{:S(2)}) async-start(), calls=%async_computation.4 | async-start | bytes 18874368 | tf_op jit(solution)/shard_map/reduce_scatter | solution.py:1415
  439.0 10.7 %copy-start.9 = (bf16[512,2048]{1,0:T(8,128)(2,1)S(1)}, bf16[512,2048]{1,0:T(8,128)(2,1)}, u32[]{:S(2)}) copy-start(bf16[512,2048]{1,0:T(8,128)(2,1)} %get-tuple-element.67.dr_ref) | copy-start | bytes 6291460
  439.0 10.7 %copy-start.22 = (bf16[512,1024]{1,0:T(8,128)(2,1)S(1)}, bf16[512,1024]{1,0:T(8,128)(2,1)}, u32[]{:S(2)}) copy-start(bf16[512,1024]{1,0:T(8,128)(2,1)} %get-tuple-element.59) | copy-start | bytes 3145732
  442.8 200.9 %collective-permute-start = (bf16[2,128,2048]{2,1,0:T(8,128)(2,1)}, bf16[2,128,2048]{2,1,0:T(8,128)(2,1)S(1)}, u32[]{:S(2)}, u32[]{:S(2)}) collective-permute-start(bf16[2,128,2048]{2,1,0:T(8,128)(2,1)} %get-tuple-element.101), channel_id=1, source_target_pairs={{0,1},{1,2},{2,3},{3,0},{4,5},{5,6},{6,7},{7,4},{8,9},{9,10},{10,1... | collective-permute-start | bytes 3145736 | tf_op jit(solution)/shard_map/ppermute | solution.py:1427
  445.8 197.9 %collective-permute-start.2 = (bf16[2,128,2048]{2,1,0:T(8,128)(2,1)}, bf16[2,128,2048]{2,1,0:T(8,128)(2,1)}, u32[]{:S(2)}, u32[]{:S(2)}) collective-permute-start(bf16[2,128,2048]{2,1,0:T(8,128)(2,1)} %get-tuple-element.102), channel_id=1, source_target_pairs={{0,3},{1,0},{2,1},{3,2},{4,7},{5,4},{6,5},{7,6},{8,11},{9,8},{10,9... | collective-permute-start | bytes 3145736 | tf_op jit(solution)/shard_map/ppermute | solution.py:1427
  446.2 197.5 %collective-permute-start.1 = (bf16[2,128,2048]{2,1,0:T(8,128)(2,1)}, bf16[2,128,2048]{2,1,0:T(8,128)(2,1)}, u32[]{:S(2)}, u32[]{:S(2)}) collective-permute-start(bf16[2,128,2048]{2,1,0:T(8,128)(2,1)} %get-tuple-element.103), channel_id=1, source_target_pairs={{0,2},{1,3},{2,0},{3,1},{4,6},{5,7},{6,4},{7,5},{8,10},{9,11},{10,... | collective-permute-start | bytes 3145736 | tf_op jit(solution)/shard_map/ppermute | solution.py:1427
  449.6 4.4 copy-start.21
  477.7 161.2 %copy-start.15 = (f32[64]{0:T(128)S(1)}, f32[64]{0:T(128)}, u32[]{:S(2)}) copy-start(f32[64]{0:T(128)} %param.27) | copy-start | bytes 772
  477.7 161.2 %copy-start.16 = (f32[64]{0:T(128)S(1)}, f32[64]{0:T(128)}, u32[]{:S(2)}) copy-start(f32[64]{0:T(128)} %param.24) | copy-start | bytes 772
  477.7 161.2 %copy-start.17 = (f32[64]{0:T(128)S(1)}, f32[64]{0:T(128)}, u32[]{:S(2)}) copy-start(f32[64]{0:T(128)} %param.33) | copy-start | bytes 772
  477.7 161.2 %copy-start.18 = (f32[64]{0:T(128)S(1)}, f32[64]{0:T(128)}, u32[]{:S(2)}) copy-start(f32[64]{0:T(128)} %param.39) | copy-start | bytes 772
  477.7 161.2 %copy-start.19 = (f32[64]{0:T(128)S(1)}, f32[64]{0:T(128)}, u32[]{:S(2)}) copy-start(f32[64]{0:T(128)} %param.36) | copy-start | bytes 772
  477.7 161.2 %copy-start.20 = (f32[64]{0:T(128)S(1)}, f32[64]{0:T(128)}, u32[]{:S(2)}) copy-start(f32[64]{0:T(128)} %param.30) | copy-start | bytes 772
  477.8 161.7 %copy-start.7 = (f32[512,256]{1,0:T(8,128)S(1)}, f32[512,256]{1,0:T(8,128)}, u32[]{:S(2)}) copy-start(f32[512,256]{1,0:T(8,128)} %param.26) | copy-start | bytes 1572868
  477.8 161.7 %copy-start.13 = (f32[512,256]{1,0:T(8,128)S(1)}, f32[512,256]{1,0:T(8,128)}, u32[]{:S(2)}) copy-start(f32[512,256]{1,0:T(8,128)} %param.32) | copy-start | bytes 1572868
  477.8 161.7 %copy-start.14 = (f32[512,256]{1,0:T(8,128)S(1)}, f32[512,256]{1,0:T(8,128)}, u32[]{:S(2)}) copy-start(f32[512,256]{1,0:T(8,128)} %param.38) | copy-start | bytes 1572868
  637.9 4.0 copy-start.5
  637.9 4.0 copy-start.6
  637.9 4.0 copy-start.11
  637.9 4.0 copy-start.12
  655.1 14.9 %copy-start.10 = (bf16[2,128,2048]{2,1,0:T(8,128)(2,1)S(1)}, bf16[2,128,2048]{2,1,0:T(8,128)(2,1)}, u32[]{:S(2)}) copy-start(bf16[2,128,2048]{2,1,0:T(8,128)(2,1)} %get-tuple-element.142) | copy-start | bytes 3145732
  655.1 16.8 %copy-start.8 = (f32[512,256]{1,0:T(8,128)S(1)}, f32[512,256]{1,0:T(8,128)}, u32[]{:S(2)}) copy-start(f32[512,256]{1,0:T(8,128)} %get-tuple-element.145) | copy-start | bytes 1572868
Sparse Core Ops, SparseCore 0:
  85.5 84.0 all-gather.2
  172.0 88.0 all-gather.4
  318.7 71.3 reduce-scatter.4
  393.4 135.7 reduce-scatter.2

commit v10 on v9

--- a/solution.py
+++ b/solution.py
@@ -380,8 +380,9 @@
                         self.copy(k - 1, self.pair, t, h, k).wait_send()
 
 
-def gather_in_kernel(n_dp, n_z, x_ref, w_ref, v_ref, g_ref, s_ref, gu_ref, xs, wq, vo, ga, sg, gu16, gu_in, gu_out,
-                     x_s, x_r, f_s, f_r, w_s, w_r, v_s, v_r, d_s, d_r, g_s, g_r, s_s, s_r, loc, gu_is, gu_os, w_f, v_f):
+def gather_in_kernel(n_dp, n_z, x_ref, w_wide, v_wide, g_ref, s_ref, gu_ref, dw_ref, xs, wq, vo, ga, sg, gu16, dw16,
+                     w_ref, v_ref, gu_in, gu_out, dw_in, dw_out,
+                     x_s, x_r, f_s, f_r, w_s, w_r, v_s, v_r, d_s, d_r, g_s, g_r, s_s, s_r, loc, gu_is, gu_os, dw_is, dw_os, w_f, v_f):
     d, z, pair, c = place()
     n_d = n_dp // 2
     me = d * n_z + z
@@ -399,20 +400,44 @@
     def chunk_out(i, slot):
         return pltpu.make_async_copy(gu_out.at[slot], gu16.at[pl.ds(pl.multiple_of(i * WIDE_ROWS, WIDE_ROWS), WIDE_ROWS)], gu_os.at[slot])
 
+    dw_rows = dw_in.shape[1]
+
+    def dw_chunk_in(i, slot):
+        return pltpu.make_async_copy(dw_ref.at[pl.ds(pl.multiple_of(i * dw_rows, dw_rows), dw_rows)], dw_in.at[slot], dw_is.at[slot])
+
+    def dw_chunk_out(i, slot):
+        return pltpu.make_async_copy(dw_out.at[slot], dw16.at[pl.ds(pl.multiple_of(i * dw_rows, dw_rows), dw_rows)], dw_os.at[slot])
+
     def round_chunks(low, high):
         def one(i, carry):
             slot = lax.rem(i, 2)
-            pl.when(i + 1 < chunks)(chunk_in(i + 1, 1 - slot).start)
+
+            @pl.when(i + 1 < chunks)
+            def _():
+                chunk_in(i + 1, 1 - slot).start()
+                dw_chunk_in(i + 1, 1 - slot).start()
+
             chunk_in(i, slot).wait()
-            pl.when(i >= 2)(chunk_out(i - 2, slot).wait)
+            dw_chunk_in(i, slot).wait()
+
+            @pl.when(i >= 2)
+            def _():
+                chunk_out(i - 2, slot).wait()
+                dw_chunk_out(i - 2, slot).wait()
+
             for n in range(2):
                 gu_out[slot, :, n * gu_width : (n + 1) * gu_width] = gu_in[slot, :, n].astype(jnp.bfloat16)
+            dw_out[slot] = dw_in[slot].astype(jnp.bfloat16)
             chunk_out(i, slot).start()
+            dw_chunk_out(i, slot).start()
             return carry
 
         lax.fori_loop(low, high, one, 0)
 
     chunk_in(0, 0).start()
+    dw_chunk_in(0, 0).start()
+    w_ref[...] = w_wide[...].astype(jnp.bfloat16)
+    v_ref[...] = v_wide[...].T.astype(jnp.bfloat16)
     greet_all(n_dp, n_z, d, z)
 
     def line_stage(src, dst, send, recv, spare, wait):
@@ -526,6 +551,7 @@
         out_unit(t, True)
     for i in range(max(0, chunks - 2), chunks):
         chunk_out(i, i % 2).wait()
+        dw_chunk_out(i, i % 2).wait()
     seg_copy.wait_send()
     remote(s_ref, sg.at[1 - c], s_s, s_r, (d, z)).wait_recv()
     own_seg.wait()
@@ -537,32 +563,37 @@
     spread.finish()
 
 
-def gather_in(x_loc, w, v, gain_tile, seg_tile, wide, n_dp, n_z):
+def gather_in(x_loc, w, v, gain_tile, seg_tile, wide, down, n_dp, n_z):
     _, rows, width = x_loc.shape
     n_d = n_dp // 2
     total = n_dp * n_z
+    b16 = jnp.bfloat16
+    down_rows = down.shape[0] * WIDE_ROWS // wide.shape[0]
     return pl.pallas_call(
         functools.partial(gather_in_kernel, n_dp, n_z),
-        in_specs=[VMEM_SPEC] * 5 + [ANY_SPEC],
-        out_specs=[ANY_SPEC] * 6,
+        in_specs=[VMEM_SPEC] * 5 + [ANY_SPEC] * 2,
+        out_specs=[ANY_SPEC] * 7,
         out_shape=[
             jax.ShapeDtypeStruct((rows * n_z, width), x_loc.dtype),
-            jax.ShapeDtypeStruct((w.shape[0] * n_dp, 2 * w.shape[1]), w.dtype),
-            jax.ShapeDtypeStruct((v.shape[0] * 2, 2 * v.shape[1]), v.dtype),
+            jax.ShapeDtypeStruct((w.shape[0] * n_dp, 2 * w.shape[1]), b16),
+            jax.ShapeDtypeStruct((v.shape[1] * 2, 2 * v.shape[0]), b16),
             jax.ShapeDtypeStruct((total,) + gain_tile.shape, gain_tile.dtype),
             jax.ShapeDtypeStruct((2,) + seg_tile.shape, seg_tile.dtype),
-            jax.ShapeDtypeStruct((wide.shape[0], wide.shape[1] * wide.shape[2]), jnp.bfloat16),
+            jax.ShapeDtypeStruct((wide.shape[0], wide.shape[1] * wide.shape[2]), b16),
+            jax.ShapeDtypeStruct(down.shape, b16),
         ],
         scratch_shapes=[
+            pltpu.VMEM(w.shape, b16), pltpu.VMEM(v.shape[::-1], b16),
             pltpu.VMEM((2, WIDE_ROWS) + wide.shape[1:], jnp.float32),
-            pltpu.VMEM((2, WIDE_ROWS, wide.shape[1] * wide.shape[2]), jnp.bfloat16),
+            pltpu.VMEM((2, WIDE_ROWS, wide.shape[1] * wide.shape[2]), b16),
+            pltpu.VMEM((2, down_rows, down.shape[1]), jnp.float32), pltpu.VMEM((2, down_rows, down.shape[1]), b16),
             DMA((2, 2)), DMA((n_z,)), DMA((n_z,)), DMA((n_z,)), DMA((3,)), DMA((2, 2)), DMA((3,)), DMA((2, 2)),
-            DMA((n_d - 1, 4, 2)), DMA((n_d - 1, 4, 2)), DMA, DMA, DMA, DMA, DMA((5,)), DMA((2,)), DMA((2,)), DMA((4,)), DMA((4,)),
+            DMA((n_d - 1, 4, 2)), DMA((n_d - 1, 4, 2)), DMA, DMA, DMA, DMA, DMA((5,)), DMA((2,)), DMA((2,)), DMA((2,)), DMA((2,)), DMA((4,)), DMA((4,)),
         ],
         compiler_params=pltpu.CompilerParams(collective_id=1, has_side_effects=True),
         cost_estimate=pl.CostEstimate(flops=0, bytes_accessed=200_000_000, transcendentals=0),
         name="gather_in",
-    )(x_loc, w, v, gain_tile, seg_tile, wide)
+    )(x_loc, w, v, gain_tile, seg_tile, wide, down)
 
 
 def share_resid_kernel(n_dp, n_z, part_ref, x_ref, w_ref, out, wall, got, buf, p_s, p_r, u_s, u_r, d_s, d_r, c_s, c_r, loc):
@@ -954,6 +985,52 @@
         cost_estimate=pl.CostEstimate(flops=0, bytes_accessed=200_000_000, transcendentals=0),
         name="sum_line",
     )(d_gate, d_up, w, resid, cot, gain, hidden, down)
+
+
+def hidden_kernel(resid_ref, gain_ref, gate_w, up_w, normed_ref, gate_ref, up_ref, hidden_ref):
+    @pl.when(pl.program_id(0) == 0)
+    def _():
+        def one(r, carry):
+            at = pl.ds(pl.multiple_of(r * 16, 16), 16)
+            value = resid_ref[at].astype(jnp.float32)
+            inverse = lax.rsqrt(jnp.mean(value * value, axis=-1, keepdims=True) + norm_eps)
+            normed_ref[at] = (value * inverse * gain_ref[...]).astype(jnp.bfloat16)
+            return carry
+
+        lax.fori_loop(0, resid_ref.shape[0] // 16, one, 0, unroll=2)
+
+    half = resid_ref.shape[0] // 4
+    for h in range(4):
+        at = slice(h * half, (h + 1) * half)
+        gate = dot_n(normed_ref[at], gate_w[...])
+        up = dot_n(normed_ref[at], up_w[...])
+        gate_ref[at] = gate.astype(jnp.bfloat16)
+        up_ref[at] = up.astype(jnp.bfloat16)
+        hidden_ref[at] = (gate * jax.nn.sigmoid(gate) * up).astype(jnp.bfloat16)
+
+
+HIDDEN_TILE = 256
+
+
+def hidden_forward(resid, gain, weights):
+    rows, width = resid.shape
+    units = weights.shape[1] // 2
+    tiles = units // HIDDEN_TILE
+    whole = lambda shape: pl.BlockSpec(shape, lambda j: (0, 0))
+    tile = pl.BlockSpec((rows, HIDDEN_TILE), lambda j: (0, j))
+    return pl.pallas_call(
+        hidden_kernel,
+        grid=(tiles,),
+        in_specs=[
+            whole((rows, width)), whole((1, width)),
+            pl.BlockSpec((width, HIDDEN_TILE), lambda j: (0, j)),
+            pl.BlockSpec((width, HIDDEN_TILE), lambda j: (0, j + tiles)),
+        ],
+        out_specs=[whole((rows, width)), tile, tile, tile],
+        out_shape=[jax.ShapeDtypeStruct((rows, width), jnp.bfloat16)] + [jax.ShapeDtypeStruct((rows, units), jnp.bfloat16)] * 3,
+        cost_estimate=pl.CostEstimate(flops=4 * rows * width * units, bytes_accessed=40_000_000, transcendentals=0),
+        name="hidden_forward",
+    )(resid, gain, weights, weights)
 
 
 WIDE_ROWS = 32
@@ -1365,20 +1442,19 @@
     n_dp = lax.axis_size("dp")
     n_z = lax.axis_size("seq")
     groups = HEADS // KV_HEADS
-    unit_count = down_weight.shape[0]
     z_here = lax.axis_index("seq")
     owned = attn_gain.shape[0]
     gain_line = jnp.concatenate([attn_gain, mlp_gain]).astype(jnp.bfloat16).astype(jnp.float32)
     gain_tile = jnp.pad(gain_line[None], ((0, 7), (0, LANES - 2 * owned)))
     seg_tile = jnp.pad(segment_ids, ((0, 8 - seqs_here), (0, 0)))
-    down_rows = lax.all_gather(down_weight.astype(jnp.bfloat16), "dp", axis=1, tiled=True)
-    rows_in, qkv_cols, out_line, gain_all, seg_all, gate_up_here = gather_in(
+    rows_in, qkv_cols, out_line, gain_all, seg_all, gate_up_here, down_here16 = gather_in(
         block_input,
-        qkv_weight.astype(jnp.bfloat16),
-        out_weight.astype(jnp.bfloat16).T,
+        qkv_weight,
+        out_weight,
         gain_tile,
         seg_tile,
         gate_up_weight,
+        down_weight,
         n_dp,
         n_z,
     )
@@ -1396,14 +1472,13 @@
         attn_part.astype(jnp.bfloat16), rows_in, gate_up_here, n_dp, n_z
     )
     total_rows = seqs_here * full_len
-    resid = resid_all.reshape(total_rows, width).astype(jnp.float32)
-    _, _, normed_two = rms_forward(resid, gain_two)
-    gate_up = jnp.dot(normed_two, gate_up_cols, preferred_element_type=jnp.float32)
-    gate_part = gate_up[:, :unit_count]
-    up_part = gate_up[:, unit_count:]
+    down_late, _ = lax.optimization_barrier((down_here16, resid_all))
+    down_rows = lax.all_gather(down_late, "dp", axis=1, tiled=True)
+    normed_two, gate16, up16, hidden16 = hidden_forward(resid_all.reshape(total_rows, width), gain_two, gate_up_cols)
+    gate_part = gate16.astype(jnp.float32)
+    up_part = up16.astype(jnp.float32)
     sigmoid_gate = jax.nn.sigmoid(gate_part)
     active = gate_part * sigmoid_gate
-    hidden16 = (active * up_part).astype(jnp.bfloat16)
     cot_rows = cot_all.reshape(total_rows, width)
     d_hidden = times_transpose(cot_rows, down_rows)
     d_gate = d_hidden * up_part * sigmoid_gate * (1.0 + gate_part * (1.0 - sigmoid_gate))
@@ -1418,14 +1493,10 @@
     d_resid16, gain_two_part, down_part = sum_line(
         d_gate16, d_up16, gate_up_cols, resid_all, cot_all, gain_two, hidden16, down_rows, n_z
     )
-    down16 = down_part.reshape(resid_all.shape)
-    pieces = [
-        lax.dynamic_slice_in_dim(down16, (z_here + o) % n_z * local_len, local_len, 1)
-        for o in range(n_z)
-    ]
-    for o in range(1, n_z):
-        pieces[o] = lax.ppermute(pieces[o], "seq", [(i, (i + o) % n_z) for i in range(n_z)])
-    down_here = sum(piece.astype(jnp.float32) for piece in pieces)
+    down_here = lax.psum_scatter(
+        down_part.reshape(resid_all.shape), "seq", scatter_dimension=1, tiled=True
+    )
+    down_here = down_here.astype(jnp.float32)
     resid_here = lax.dynamic_slice_in_dim(resid_all, z_here * local_len, local_len, 1)
     output = (resid_here.astype(jnp.float32) + down_here).astype(jnp.bfloat16)
     d_attended = jnp.dot(d_resid16, out_rows, preferred_element_type=jnp.float32).astype(jnp.bfloat16)

time: 687 us -> 664 us (0.967)
  the two profiles are of different devices: /device:TPU:9 before, /device:TPU:0 now
where the time goes in v10:
time: 664 us; the launch traced here: 660 us
  Pallas kernels  513 us (77%)
  matrix products  79.9 us (12%)
  waiting for transfers between devices  28.3 us (4%)
  between operations  14.4 us (2%)
  other arithmetic  14.2 us (2%)
  local copies, waits for them, and re-layouts  9.81 us (1%)
    pallas_call x1, Pallas kernels, hand_out(): pl.pallas_call(functools.partial(hand_out_kernel, n_dp, n_z), in_specs=[V...  140 us
    pallas_call x1, Pallas kernels, sum_line(): pl.pallas_call(functools.partial(sum_line_kernel, n_z), in_specs=[ANY_SPE...  97.8 us
    pallas_call x1, Pallas kernels, share_resid(): pl.pallas_call(functools.partial(share_resid_kernel, n_dp, n_z), in_specs...  90.3 us
    pallas_call x1, Pallas kernels, gather_in(): pl.pallas_call(functools.partial(gather_in_kernel, n_dp, n_z), in_specs=[...  73.8 us
    dot_general x3, matrix products, contract_rows(): lax.dot_general(left, right, (((0,), (0,)), ((), ())), preferred_element_...  46.1 us
    pallas_call x1, Pallas kernels, attn_forward(): pl.pallas_call(functools.partial(attn_gather_kernel, n_dp, pairs, Q_ROWS,...  39.9 us
    pallas_call x1, Pallas kernels, hidden_forward(): pl.pallas_call(hidden_kernel, grid=(tiles,), in_specs=[whole((rows, width...  28.6 us
    dot_general x2, matrix products, times_transpose(): lax.dot_general(left, right, (((1,), (1,)), ((), ())), preferred_element_...  25.3 us
  transfers between devices with their start and end apart: 5, of which 2 were waited for; matrix products, arithmetic and copies ran while one was open for 15% of the time, Pallas kernels for 64%

profile of v10, /device:TPU:0, one launch (start us, length us, event | category | flops | bytes accessed | tf_op | source)
XLA Modules:
  0.0 660.3 jit_solution(3387980716750973433)
XLA Ops:
  7.2 0.0 all-gather.3.cloned.1.call-start
  7.2 0.7 convert_bitcast_fusion
  7.9 0.7 fusion.20.g_ref
  8.6 1.3 pad.12.s_ref
  9.9 73.8 %gather_in.1 = (bf16[512,2048]{1,0:T(8,128)(2,1)}, bf16[2048,1536]{1,0:T(8,128)(2,1)}, bf16[512,1024]{1,0:T(8,128)(2,1)}, f32[32,8,128]{2,1,0:T(8,128)}, s32[2,8...) custom-call(bf16[2,128,2048]{2,1,0:T(8,128)(2,1)} %x_ref.1, f32[256,768]{1,0:T(8,128)} %w_wide.1, ...), custom_call_target="tpu_custom_call" | custom-call | bytes 200000000 | tf_op jit(solution)/shard_map/gather_in/pallas_call | solution.py:572
  83.7 0.0 all-gather.3.cloned.1.call-update
  83.7 0.2 all-gather.5.cloned.1.call-start
  84.0 1.2 slice_reduce_fusion
  85.2 0.1 mul.191
  85.3 0.7 constant_dynamic-slice_fusion.1
  86.1 0.3 convert_reduce_fusion
  86.3 1.0 fusion.16
  87.3 1.0 maximum_bitcast_fusion.cos_ref
  88.3 1.0 maximum_bitcast_fusion.1.sin_ref
  89.3 0.5 fusion.11
  89.8 0.6 fusion.13.n_ref
  90.3 0.0 copy-start.1
  90.3 5.1 fusion.28.qkv_ref
  95.4 0.6 reshape.350.seg_row_ref
  96.1 0.8 reshape.349.seg_col_ref
  96.9 39.9 %attn_forward.1 = (bf16[512,1536]{1,0:T(8,128)(2,1)}, f32[512,512]{1,0:T(8,128)}, bf16[512,1024]{1,0:T(8,128)(2,1)}, bf16[2048,1024]{1,0:T(8,128)(2,1)}) custom-call(f32[512,1536]{1,0:T(8,128)} %fusion.28.qkv_ref, f32[512,128]{1,0:T(8,128)} %maximum_bitcast_fusion.cos_ref, f32[512,128]{1,0:T(8,128)} %maximum_bitcast_fusion.1.sin_ref, ...), custom_call_target="tpu_custom_call" | custom-call | flops 2147483648 | bytes 150000000 | tf_op jit(solution)/shard_map/attn_forward/pallas_call | solution.py:217
  136.8 6.2 convolution_convert_fusion.3.part_ref
  143.0 90.3 %share_resid.1 = (bf16[2,512,2048]{2,1,0:T(8,128)(2,1)}, bf16[2048,4096]{1,0:T(8,128)(2,1)}) custom-call(bf16[512,2048]{1,0:T(8,128)(2,1)} %convolution_convert_fusion.3.part_ref, bf16[512,2048]{1,0:T(8,128)(2,1)} %get-tuple-element.60.x_ref, bf16[256,4096]{1,0:T(8,128)(2,1)} %get-tuple-element.67.w_ref), custom_call_target="tpu_custom_call" | custom-call | bytes 200000000 | tf_op jit(solution)/shard_map/share_resid/pallas_call | solution.py:731
  233.4 0.0 all-gather.5.cloned.1.call-update
  233.4 0.4 reduce-scatter.8.cloned.1.call-start
  233.8 0.7 reshape_squeeze.6.gain_ref
  234.5 28.6 %hidden_forward.1 = (bf16[1024,2048]{1,0:T(8,128)(2,1)}, bf16[1024,2048]{1,0:T(8,128)(2,1)}, bf16[1024,2048]{1,0:T(8,128)(2,1)}, bf16[1024,2048]{1,0:T(8,128)(2,1)}) custom-call(bf16[1024,2048]{1,0:T(8,128)(2,1)} %bitcast.34, f32[1,2048]{1,0:T(1,128)} %reshape_squeeze.6.gain_ref, bf16[2048,4096]{1,0:T(8,128)(2,1)} %get-tuple-element.72.gate_w.up_w.w_ref, ...), custom_call_target="tpu_custom_call" | custom-call | flops 17179869184 | bytes 40000000 | tf_op jit(solution)/shard_map/hidden_forward/pallas_call | solution.py:1021
  263.1 14.3 %convolution_convert_fusion.1 = bf16[2048,2048]{1,0:T(8,128)(2,1)} fusion(bf16[1024,2048]{1,0:T(8,128)(2,1)} %bitcast.35, bf16[1024,2048]{1,0:T(8,128)(2,1)} %get-tuple-element.75.hid_ref), kind=kOutput, calls=%fused_computation.15 | convolution fusion | flops 8594128896 | bytes 16777216 | tf_op jit(solution)/shard_map/dot_general | solution.py:1406
  277.4 0.0 reduce-scatter.8.cloned.1.call-update
  277.4 0.0 reduce-scatter.4.cloned.1.call-start
  277.5 12.3 %all-gather.5.cloned.1.call-done.down_ref = bf16[2048,2048]{1,0:T(8,128)(2,1)} async-done(((bf16[2048,256]{1,0:T(8,128)(2,1)}), bf16[2048,2048]{1,0:T(8,128)(2,1)}) %all-gather.5.cloned.1.call-update) | async-done | bytes 8388624 | tf_op jit(solution)/shard_map/all_gather | solution.py:1476
  289.8 19.1 %fusion.7 = (bf16[1024,2048]{1,0:T(8,128)(2,1)}, bf16[1024,2048]{1,0:T(8,128)(2,1)}) fusion(bf16[1024,2048]{1,0:T(8,128)(2,1)} %get-tuple-element.74, bf16[1024,2048]{1,0:T(8,128)(2,1)} %get-tuple-element.73, bf16[1024,2048]{1,0:T(8,128)(2,1)} %bitcast.36, bf16[2048,2048]{1,0:T(8,128)(2,1)} %all-gather.5.cloned.1.call-done.down_ref), kind=kOutput, calls=%fused_computation.11 | convolution fusion | flops 8621391872 | bytes 29360128 | tf_op jit(solution)/shard_map/dot_general | solution.py:1412
  308.9 97.8 %sum_line.1 = (bf16[512,2048]{1,0:T(8,128)(2,1)}, f32[8,2048]{1,0:T(8,128)}, bf16[1024,2048]{1,0:T(8,128)(2,1)}) custom-call(bf16[1024,2048]{1,0:T(8,128)(2,1)} %get-tuple-element.111.d_gate_ref, bf16[1024,2048]{1,0:T(8,128)(2,1)} %get-tuple-element.110.d_up_ref, bf16[2048,4096]{1,0:T(8,128)(2,1)} %get-tuple-element.72.gate_w.up_w.w_ref, ...), custom_call_target="tpu_custom_call" | custom-call | bytes 200000000 | tf_op jit(solution)/shard_map/sum_line/pallas_call | solution.py:967
  406.7 0.0 reduce-scatter.4.cloned.1.call-update
  406.7 0.3 reduce-scatter.6.cloned.1.call-start
  407.0 26.0 %convolution_convert_fusion = bf16[2048,4096]{1,0:T(8,128)(2,1)} fusion(bf16[1024,2048]{1,0:T(8,128)(2,1)} %get-tuple-element.85, bf16[1024,2048]{1,0:T(8,128)(2,1)} %get-tuple-element.110.d_up_ref, bf16[1024,2048]{1,0:T(8,128)(2,1)} %get-tuple-element.111.d_gate_ref), kind=kOutput, calls=%fused_computation | convolution fusion | flops 17205035008 | bytes 29360128 | tf_op jit(solution)/shard_map/dot_general | solution.py:1406
  433.0 0.0 reduce-scatter.6.cloned.1.call-update
  433.1 0.7 reshape_squeeze.7.gain_ref
  433.7 0.9 copy-done.6
  434.6 5.8 convolution_convert_fusion.2.ot_ref
  440.4 3.3 convolution_convert_fusion.4.d_out_ref
  443.7 20.3 %attn_backward.1.dq_ref = bf16[512,1536]{1,0:T(8,128)(2,1)} custom-call(bf16[512,1536]{1,0:T(8,128)(2,1)} %get-tuple-element.77.turned_ref, bf16[512,1024]{1,0:T(8,128)(2,1)} %convolution_convert_fusion.4.d_out_ref, f32[512,512]{1,0:T(8,128)} %get-tuple-element.79.lse_ref, f32[512,128]{1,0:T(8,128)} %maximum_bitcast_fusion.cos_ref, ...), custom_call_target="tpu_custom_call" | custom-call | flops 5368709120 | bytes 4718592 | tf_op jit(solution)/shard_map/attn_backward/pallas_call | solution.py:243
  464.0 0.0 copy-start.15
  464.0 0.0 copy-start.16
  464.0 0.0 copy-start.17
  464.0 0.0 copy-start.18
  464.0 0.0 copy-start.11
  464.0 0.0 copy-start.12
  464.0 139.6 %hand_out.1 = (bf16[2,128,2048]{2,1,0:T(8,128)(2,1)}, f32[256,768]{1,0:T(8,128)}, f32[512,256]{1,0:T(8,128)}, f32[16,128]{1,0:T(8,128)}) custom-call(bf16[512,1536]{1,0:T(8,128)(2,1)} %attn_backward.1.dq_ref, bf16[512,2048]{1,0:T(8,128)(2,1)} %copy-done.1, bf16[512,2048]{1,0:T(8,128)(2,1)} %get-tuple-element.60.x_ref, ...), custom_call_target="tpu_custom_call" | custom-call | bytes 300000000 | tf_op jit(solution)/shard_map/hand_out/pallas_call | solution.py:1364
  603.7 0.0 copy-start.4
  603.7 0.0 copy-start.9
  603.7 0.9 bitcast_reduce_fusion
  604.6 0.1 constant_dynamic-slice_fusion
  604.7 0.6 multiply_subtract_fusion.2
  605.2 2.4 multiply_subtract_fusion.1
  607.7 1.8 multiply_subtract_fusion
  609.5 7.7 %shard_map.405 = (f32[2048,256]{1,0:T(8,128)}, f32[2048,256]{1,0:T(8,128)}, f32[2048,256]{1,0:T(8,128)}, f32[2048,256]{1,0:T(8,128)}) custom-call(bf16[256,2048]{1,0:T(8,128)(2,1)} %reduce-scatter.8.cloned.1.call-done.grad_ref, f32[2048,256]{1,0:T(8,128)} %w_ref.3, f32[2048,256]{1,0:T(8,128)} %m_ref.3, f32[2048,256]{1,0:T(8,128)} %v_ref.3), custom_call_target="tpu_custom_call" | custom-call | flops 10485760 | bytes 15728640 | tf_op jit(solution)/shard_map/pallas_call | solution.py:1062
  617.2 0.0 reduce-scatter.4.cloned.1.call-done
  617.2 2.9 add_convert_fusion
  620.1 15.9 %reduce-scatter.6.cloned.1.call-done.grad_ref = bf16[256,4096]{1,0:T(8,128)(2,1)} async-done(((bf16[2048,4096]{1,0:T(8,128)(2,1)}), bf16[256,4096]{1,0:T(8,128)(2,1)}) %reduce-scatter.6.cloned.1.call-update) | async-done | bytes 2097168 | tf_op jit(solution)/shard_map/reduce_scatter | solution.py:1490
  636.0 14.8 %shard_map.404 = (f32[256,2,2048]{2,1,0:T(2,128)}, f32[256,2,2048]{2,1,0:T(2,128)}, f32[256,2,2048]{2,1,0:T(2,128)}, f32[256,2,2048]{2,1,0:T(2,128)}) custom-call(bf16[256,4096]{1,0:T(8,128)(2,1)} %reduce-scatter.6.cloned.1.call-done.grad_ref, f32[256,2,2048]{2,1,0:T(2,128)} %w_ref.2, f32[256,2,2048]{2,1,0:T(2,128)} %m_ref.2, f32[256,2,2048]{2,1,0:T(2,128)} %v_ref.2), custom_call_target="tpu_custom_call" | custom-call | flops 20971520 | bytes 31457280 | tf_op jit(solution)/shard_map/pallas_call | solution.py:1062
  650.8 1.0 copy.51
  651.8 0.9 copy.52
  652.7 0.8 copy.53
  (35 shorter events, 0.1 us)
Async XLA Ops:
  7.2 255.9 %all-gather.3.cloned.1.call-start = ((), (), s32[]{:S(2)}) async-start(), calls=%async_computation.3 | async-start | bytes 5242880 | tf_op jit(solution)/shard_map/all_gather | solution.py:1462
  83.7 5.6 copy-start
  83.7 206.0 %all-gather.5.cloned.1.call-start = ((), (), s32[]{:S(2)}) async-start(), calls=%async_computation.4 | async-start | bytes 9437184 | tf_op jit(solution)/shard_map/all_gather | solution.py:1476
  86.3 4.0 copy-start.2
  90.3 5.1 copy-start.1
  233.4 376.1 %reduce-scatter.8.cloned.1.call-start = ((), (), s32[]{:S(2)}) async-start(), calls=%async_computation.7 | async-start | bytes 9437184 | tf_op jit(solution)/shard_map/reduce_scatter | solution.py:1492
  277.4 339.8 %reduce-scatter.4.cloned.1.call-start = ((), (), s32[]{:S(2)}) async-start(), calls=%async_computation.5 | async-start | bytes 5242880 | tf_op jit(solution)/shard_map/reduce_scatter | solution.py:1496
  406.7 229.3 %reduce-scatter.6.cloned.1.call-start = ((), (), s32[]{:S(2)}) async-start(), calls=%async_computation.6 | async-start | bytes 18874368 | tf_op jit(solution)/shard_map/reduce_scatter | solution.py:1490
  433.0 1.6 copy-start.6
  434.6 5.8 copy-start.19
  464.0 140.7 %copy-start.13 = (f32[64]{0:T(128)S(1)}, f32[64]{0:T(128)}, u32[]{:S(2)}) copy-start(f32[64]{0:T(128)} %param.27) | copy-start | bytes 772
  464.0 140.7 %copy-start.14 = (f32[64]{0:T(128)S(1)}, f32[64]{0:T(128)}, u32[]{:S(2)}) copy-start(f32[64]{0:T(128)} %param.24) | copy-start | bytes 772
  464.0 140.7 %copy-start.15 = (f32[64]{0:T(128)S(1)}, f32[64]{0:T(128)}, u32[]{:S(2)}) copy-start(f32[64]{0:T(128)} %param.33) | copy-start | bytes 772
  464.0 140.7 %copy-start.16 = (f32[64]{0:T(128)S(1)}, f32[64]{0:T(128)}, u32[]{:S(2)}) copy-start(f32[64]{0:T(128)} %param.39) | copy-start | bytes 772
  464.0 140.7 %copy-start.17 = (f32[64]{0:T(128)S(1)}, f32[64]{0:T(128)}, u32[]{:S(2)}) copy-start(f32[64]{0:T(128)} %param.36) | copy-start | bytes 772
  464.0 140.7 %copy-start.18 = (f32[64]{0:T(128)S(1)}, f32[64]{0:T(128)}, u32[]{:S(2)}) copy-start(f32[64]{0:T(128)} %param.30) | copy-start | bytes 772
  464.0 141.2 %copy-start.7 = (f32[512,256]{1,0:T(8,128)S(1)}, f32[512,256]{1,0:T(8,128)}, u32[]{:S(2)}) copy-start(f32[512,256]{1,0:T(8,128)} %v_wide.1) | copy-start | bytes 1572868
  464.0 141.2 %copy-start.11 = (f32[512,256]{1,0:T(8,128)S(1)}, f32[512,256]{1,0:T(8,128)}, u32[]{:S(2)}) copy-start(f32[512,256]{1,0:T(8,128)} %param.32) | copy-start | bytes 1572868
  464.0 141.2 %copy-start.12 = (f32[512,256]{1,0:T(8,128)S(1)}, f32[512,256]{1,0:T(8,128)}, u32[]{:S(2)}) copy-start(f32[512,256]{1,0:T(8,128)} %param.38) | copy-start | bytes 1572868
  603.6 4.0 copy-start.3
  603.7 4.0 copy-start.4
  603.7 4.0 copy-start.9
  603.7 4.0 copy-start.10
  620.1 30.7 %copy-start.8 = (bf16[2,128,2048]{2,1,0:T(8,128)(2,1)S(1)}, bf16[2,128,2048]{2,1,0:T(8,128)(2,1)}, u32[]{:S(2)}) copy-start(bf16[2,128,2048]{2,1,0:T(8,128)(2,1)} %get-tuple-element.149) | copy-start | bytes 3145732
  620.1 32.5 %copy-start.5 = (f32[512,256]{1,0:T(8,128)S(1)}, f32[512,256]{1,0:T(8,128)}, u32[]{:S(2)}) copy-start(f32[512,256]{1,0:T(8,128)} %get-tuple-element.152) | copy-start | bytes 1572868
Sparse Core Ops, SparseCore 0:
  83.9 87.3 all-gather.2
  233.5 56.2 all-gather.4
  293.3 71.5 reduce-scatter.7
  406.8 74.3 reduce-scatter.3
  484.6 151.3 reduce-scatter.5

commit v11 on v10

--- a/solution.py
+++ b/solution.py
@@ -1493,10 +1493,14 @@
     d_resid16, gain_two_part, down_part = sum_line(
         d_gate16, d_up16, gate_up_cols, resid_all, cot_all, gain_two, hidden16, down_rows, n_z
     )
-    down_here = lax.psum_scatter(
-        down_part.reshape(resid_all.shape), "seq", scatter_dimension=1, tiled=True
-    )
-    down_here = down_here.astype(jnp.float32)
+    down16 = down_part.reshape(resid_all.shape)
+    pieces = [
+        lax.dynamic_slice_in_dim(down16, (z_here + o) % n_z * local_len, local_len, 1)
+        for o in range(n_z)
+    ]
+    for o in range(1, n_z):
+        pieces[o] = lax.ppermute(pieces[o], "seq", [(i, (i + o) % n_z) for i in range(n_z)])
+    down_here = sum(piece.astype(jnp.float32) for piece in pieces)
     resid_here = lax.dynamic_slice_in_dim(resid_all, z_here * local_len, local_len, 1)
     output = (resid_here.astype(jnp.float32) + down_here).astype(jnp.bfloat16)
     d_attended = jnp.dot(d_resid16, out_rows, preferred_element_type=jnp.float32).astype(jnp.bfloat16)

time: 664 us -> 658 us (level)
  the two profiles are of different devices: /device:TPU:0 before, /device:TPU:11 now
where the time goes in v11:
time: 658 us; the launch traced here: 654 us
  Pallas kernels  510 us (78%)
  matrix products  77.8 us (12%)
  waiting for transfers between devices  16.6 us (3%)
  other arithmetic  15.3 us (2%)
  between operations  14.4 us (2%)
  local copies, waits for them, and re-layouts  12.8 us (2%)
    pallas_call x1, Pallas kernels, hand_out(): pl.pallas_call(functools.partial(hand_out_kernel, n_dp, n_z), in_specs=[V...  146 us
    pallas_call x1, Pallas kernels, share_resid(): pl.pallas_call(functools.partial(share_resid_kernel, n_dp, n_z), in_specs...  96.1 us
    pallas_call x1, Pallas kernels, sum_line(): pl.pallas_call(functools.partial(sum_line_kernel, n_z), in_specs=[ANY_SPE...  94.8 us
    pallas_call x1, Pallas kernels, gather_in(): pl.pallas_call(functools.partial(gather_in_kernel, n_dp, n_z), in_specs=[...  71.6 us
    dot_general x3, matrix products, contract_rows(): lax.dot_general(left, right, (((0,), (0,)), ((), ())), preferred_element_...  44 us
    pallas_call x1, Pallas kernels, attn_forward(): pl.pallas_call(functools.partial(attn_gather_kernel, n_dp, pairs, Q_ROWS,...  31.4 us
    pallas_call x1, Pallas kernels, hidden_forward(): pl.pallas_call(hidden_kernel, grid=(tiles,), in_specs=[whole((rows, width...  28.2 us
    dot_general x2, matrix products, times_transpose(): lax.dot_general(left, right, (((1,), (1,)), ((), ())), preferred_element_...  25.4 us
  transfers between devices with their start and end apart: 7, of which 1 were waited for; matrix products, arithmetic and copies ran while one was open for 15% of the time, Pallas kernels for 65%

profile of v11, /device:TPU:11, one launch (start us, length us, event | category | flops | bytes accessed | tf_op | source)
XLA Modules:
  0.0 653.7 jit_solution(6375992780842996871)
XLA Ops:
  7.2 0.0 all-gather.3.cloned.1.call-start
  7.2 0.7 convert_bitcast_fusion
  7.9 0.7 fusion.20.g_ref
  8.6 1.3 pad.12.s_ref
  9.9 71.6 %gather_in.1 = (bf16[512,2048]{1,0:T(8,128)(2,1)}, bf16[2048,1536]{1,0:T(8,128)(2,1)}, bf16[512,1024]{1,0:T(8,128)(2,1)}, f32[32,8,128]{2,1,0:T(8,128)}, s32[2,8...) custom-call(bf16[2,128,2048]{2,1,0:T(8,128)(2,1)} %x_ref.1, f32[256,768]{1,0:T(8,128)} %w_wide.1, ...), custom_call_target="tpu_custom_call" | custom-call | bytes 200000000 | tf_op jit(solution)/shard_map/gather_in/pallas_call | solution.py:572
  81.5 0.0 all-gather.3.cloned.1.call-update
  81.5 0.3 all-gather.5.cloned.1.call-start
  81.9 1.3 slice_reduce_fusion
  83.2 0.1 mul.203
  83.3 0.7 constant_dynamic-slice_fusion.4
  84.0 0.2 convert_reduce_fusion
  84.3 1.0 fusion.16
  85.3 1.0 maximum_bitcast_fusion.cos_ref
  86.2 1.0 maximum_bitcast_fusion.1.sin_ref
  87.2 0.5 fusion.11
  87.7 0.6 fusion.13.n_ref
  88.3 0.0 copy-start.1
  88.3 5.1 fusion.28.qkv_ref
  93.4 0.6 reshape.350.seg_row_ref
  94.0 0.8 reshape.349.seg_col_ref
  94.8 31.4 %attn_forward.1 = (bf16[512,1536]{1,0:T(8,128)(2,1)}, f32[512,512]{1,0:T(8,128)}, bf16[512,1024]{1,0:T(8,128)(2,1)}, bf16[2048,1024]{1,0:T(8,128)(2,1)}) custom-call(f32[512,1536]{1,0:T(8,128)} %fusion.28.qkv_ref, f32[512,128]{1,0:T(8,128)} %maximum_bitcast_fusion.cos_ref, f32[512,128]{1,0:T(8,128)} %maximum_bitcast_fusion.1.sin_ref, ...), custom_call_target="tpu_custom_call" | custom-call | flops 2147483648 | bytes 150000000 | tf_op jit(solution)/shard_map/attn_forward/pallas_call | solution.py:217
  126.2 6.3 convolution_convert_fusion.3.part_ref
  132.5 96.1 %share_resid.1 = (bf16[2,512,2048]{2,1,0:T(8,128)(2,1)}, bf16[2048,4096]{1,0:T(8,128)(2,1)}) custom-call(bf16[512,2048]{1,0:T(8,128)(2,1)} %convolution_convert_fusion.3.part_ref, bf16[512,2048]{1,0:T(8,128)(2,1)} %get-tuple-element.60.x_ref, bf16[256,4096]{1,0:T(8,128)(2,1)} %get-tuple-element.67.w_ref), custom_call_target="tpu_custom_call" | custom-call | bytes 200000000 | tf_op jit(solution)/shard_map/share_resid/pallas_call | solution.py:731
  228.6 0.0 all-gather.5.cloned.1.call-update
  228.7 0.6 reduce-scatter.5.cloned.1.call-start
  229.2 0.7 reshape_squeeze.6.gain_ref
  229.9 28.2 %hidden_forward.1 = (bf16[1024,2048]{1,0:T(8,128)(2,1)}, bf16[1024,2048]{1,0:T(8,128)(2,1)}, bf16[1024,2048]{1,0:T(8,128)(2,1)}, bf16[1024,2048]{1,0:T(8,128)(2,1)}) custom-call(bf16[1024,2048]{1,0:T(8,128)(2,1)} %bitcast.34, f32[1,2048]{1,0:T(1,128)} %reshape_squeeze.6.gain_ref, bf16[2048,4096]{1,0:T(8,128)(2,1)} %get-tuple-element.72.gate_w.up_w.w_ref, ...), custom_call_target="tpu_custom_call" | custom-call | flops 17179869184 | bytes 40000000 | tf_op jit(solution)/shard_map/hidden_forward/pallas_call | solution.py:1021
  258.1 14.0 %convolution_convert_fusion.1 = bf16[2048,2048]{1,0:T(8,128)(2,1)} fusion(bf16[1024,2048]{1,0:T(8,128)(2,1)} %bitcast.35, bf16[1024,2048]{1,0:T(8,128)(2,1)} %get-tuple-element.75.hid_ref), kind=kOutput, calls=%fused_computation.15 | convolution fusion | flops 8594128896 | bytes 16777216 | tf_op jit(solution)/shard_map/dot_general | solution.py:1406
  272.2 0.0 reduce-scatter.5.cloned.1.call-update
  272.2 0.0 reduce-scatter.3.cloned.1.call-start
  272.2 16.5 %all-gather.5.cloned.1.call-done.down_ref = bf16[2048,2048]{1,0:T(8,128)(2,1)} async-done(((bf16[2048,256]{1,0:T(8,128)(2,1)}), bf16[2048,2048]{1,0:T(8,128)(2,1)}) %all-gather.5.cloned.1.call-update) | async-done | bytes 8388624 | tf_op jit(solution)/shard_map/all_gather | solution.py:1476
  288.7 19.1 %fusion.7 = (bf16[1024,2048]{1,0:T(8,128)(2,1)}, bf16[1024,2048]{1,0:T(8,128)(2,1)}) fusion(bf16[1024,2048]{1,0:T(8,128)(2,1)} %get-tuple-element.74, bf16[1024,2048]{1,0:T(8,128)(2,1)} %get-tuple-element.73, bf16[1024,2048]{1,0:T(8,128)(2,1)} %bitcast.36, bf16[2048,2048]{1,0:T(8,128)(2,1)} %all-gather.5.cloned.1.call-done.down_ref), kind=kOutput, calls=%fused_computation.11 | convolution fusion | flops 8621391872 | bytes 29360128 | tf_op jit(solution)/shard_map/dot_general | solution.py:1412
  307.8 25.6 %convolution_convert_fusion = bf16[2048,4096]{1,0:T(8,128)(2,1)} fusion(bf16[1024,2048]{1,0:T(8,128)(2,1)} %get-tuple-element.85, bf16[1024,2048]{1,0:T(8,128)(2,1)} %get-tuple-element.110.d_up_ref, bf16[1024,2048]{1,0:T(8,128)(2,1)} %get-tuple-element.111.d_gate_ref), kind=kOutput, calls=%fused_computation | convolution fusion | flops 17205035008 | bytes 29360128 | tf_op jit(solution)/shard_map/dot_general | solution.py:1406
  333.4 0.0 reduce-scatter.3.cloned.1.call-update
  333.5 0.7 reshape_squeeze.7.gain_ref
  334.2 94.8 %sum_line.1 = (bf16[512,2048]{1,0:T(8,128)(2,1)}, f32[8,2048]{1,0:T(8,128)}, bf16[1024,2048]{1,0:T(8,128)(2,1)}) custom-call(bf16[1024,2048]{1,0:T(8,128)(2,1)} %get-tuple-element.111.d_gate_ref, bf16[1024,2048]{1,0:T(8,128)(2,1)} %get-tuple-element.110.d_up_ref, bf16[2048,4096]{1,0:T(8,128)(2,1)} %get-tuple-element.72.gate_w.up_w.w_ref, ...), custom_call_target="tpu_custom_call" | custom-call | bytes 200000000 | tf_op jit(solution)/shard_map/sum_line/pallas_call | solution.py:967
  429.0 3.8 constant_dynamic-slice_fusion.2
  432.8 3.4 collective-permute-start.2
  436.2 2.1 collective-permute-start.1
  438.3 4.4 convolution_convert_fusion.2.ot_ref
  442.7 3.3 convolution_convert_fusion.4.d_out_ref
  446.0 20.3 %attn_backward.1.dq_ref = bf16[512,1536]{1,0:T(8,128)(2,1)} custom-call(bf16[512,1536]{1,0:T(8,128)(2,1)} %get-tuple-element.77.turned_ref, bf16[512,1024]{1,0:T(8,128)(2,1)} %convolution_convert_fusion.4.d_out_ref, f32[512,512]{1,0:T(8,128)} %get-tuple-element.79.lse_ref, f32[512,128]{1,0:T(8,128)} %maximum_bitcast_fusion.cos_ref, ...), custom_call_target="tpu_custom_call" | custom-call | flops 5368709120 | bytes 4718592 | tf_op jit(solution)/shard_map/attn_backward/pallas_call | solution.py:243
  466.3 0.0 copy-start.15
  466.3 0.0 copy-start.16
  466.3 0.0 copy-start.17
  466.3 0.0 copy-start.18
  466.3 0.0 copy-start.7
  466.3 0.0 copy-start.11
  466.3 0.0 copy-start.12
  466.4 145.8 %hand_out.1 = (bf16[2,128,2048]{2,1,0:T(8,128)(2,1)}, f32[256,768]{1,0:T(8,128)}, f32[512,256]{1,0:T(8,128)}, f32[16,128]{1,0:T(8,128)}) custom-call(bf16[512,1536]{1,0:T(8,128)(2,1)} %attn_backward.1.dq_ref, bf16[512,2048]{1,0:T(8,128)(2,1)} %copy-done.1, bf16[512,2048]{1,0:T(8,128)(2,1)} %get-tuple-element.60.x_ref, ...), custom_call_target="tpu_custom_call" | custom-call | bytes 300000000 | tf_op jit(solution)/shard_map/hand_out/pallas_call | solution.py:1364
  612.2 0.0 copy-start.9
  612.2 0.0 copy-start.10
  612.2 0.9 bitcast_reduce_fusion
  613.1 0.1 constant_dynamic-slice_fusion.3
  613.2 0.6 multiply_subtract_fusion.2
  613.8 2.4 multiply_subtract_fusion.1
  616.2 1.8 multiply_subtract_fusion
  618.0 4.1 add_convert_fusion
  622.1 7.3 %shard_map.405 = (f32[2048,256]{1,0:T(8,128)}, f32[2048,256]{1,0:T(8,128)}, f32[2048,256]{1,0:T(8,128)}, f32[2048,256]{1,0:T(8,128)}) custom-call(bf16[256,2048]{1,0:T(8,128)(2,1)} %reduce-scatter.5.cloned.1.call-done.grad_ref, f32[2048,256]{1,0:T(8,128)} %w_ref.3, f32[2048,256]{1,0:T(8,128)} %m_ref.3, f32[2048,256]{1,0:T(8,128)} %v_ref.3), custom_call_target="tpu_custom_call" | custom-call | flops 10485760 | bytes 15728640 | tf_op jit(solution)/shard_map/pallas_call | solution.py:1062
  629.4 0.0 reduce-scatter.3.cloned.1.call-done.grad_ref
  629.4 14.9 %shard_map.404 = (f32[256,2,2048]{2,1,0:T(2,128)}, f32[256,2,2048]{2,1,0:T(2,128)}, f32[256,2,2048]{2,1,0:T(2,128)}, f32[256,2,2048]{2,1,0:T(2,128)}) custom-call(bf16[256,4096]{1,0:T(8,128)(2,1)} %reduce-scatter.3.cloned.1.call-done.grad_ref, f32[256,2,2048]{2,1,0:T(2,128)} %w_ref.2, f32[256,2,2048]{2,1,0:T(2,128)} %m_ref.2, f32[256,2,2048]{2,1,0:T(2,128)} %v_ref.2), custom_call_target="tpu_custom_call" | custom-call | flops 20971520 | bytes 31457280 | tf_op jit(solution)/shard_map/pallas_call | solution.py:1062
  644.3 1.0 copy.51
  645.3 0.9 copy.52
  646.2 0.8 copy.53
  (41 shorter events, 0.1 us)
Async XLA Ops:
  7.2 250.9 %all-gather.3.cloned.1.call-start = ((), (), s32[]{:S(2)}) async-start(), calls=%async_computation.2 | async-start | bytes 5242880 | tf_op jit(solution)/shard_map/all_gather | solution.py:1462
  81.5 5.7 copy-start
  81.5 207.2 %all-gather.5.cloned.1.call-start = ((), (), s32[]{:S(2)}) async-start(), calls=%async_computation.3 | async-start | bytes 9437184 | tf_op jit(solution)/shard_map/all_gather | solution.py:1476
  84.3 4.0 copy-start.2
  88.3 5.1 copy-start.1
  228.7 393.4 %reduce-scatter.5.cloned.1.call-start = ((), (), s32[]{:S(2)}) async-start(), calls=%async_computation.5 | async-start | bytes 9437184 | tf_op jit(solution)/shard_map/reduce_scatter | solution.py:1492
  272.2 357.2 %reduce-scatter.3.cloned.1.call-start = ((), (), s32[]{:S(2)}) async-start(), calls=%async_computation.4 | async-start | bytes 18874368 | tf_op jit(solution)/shard_map/reduce_scatter | solution.py:1490
  429.0 9.3 %copy-start.6 = (bf16[512,2048]{1,0:T(8,128)(2,1)S(1)}, bf16[512,2048]{1,0:T(8,128)(2,1)}, u32[]{:S(2)}) copy-start(bf16[512,2048]{1,0:T(8,128)(2,1)} %get-tuple-element.78.dr_ref) | copy-start | bytes 6291460
  429.0 9.3 %copy-start.20 = (bf16[512,1024]{1,0:T(8,128)(2,1)S(1)}, bf16[512,1024]{1,0:T(8,128)(2,1)}, u32[]{:S(2)}) copy-start(bf16[512,1024]{1,0:T(8,128)(2,1)} %get-tuple-element.65) | copy-start | bytes 3145732
  432.8 185.2 %collective-permute-start = (bf16[2,128,2048]{2,1,0:T(8,128)(2,1)}, bf16[2,128,2048]{2,1,0:T(8,128)(2,1)S(1)}, u32[]{:S(2)}, u32[]{:S(2)}) collective-permute-start(bf16[2,128,2048]{2,1,0:T(8,128)(2,1)} %get-tuple-element.112), channel_id=1, source_target_pairs={{0,1},{1,2},{2,3},{3,0},{4,5},{5,6},{6,7},{7,4},{8,9},{9,10},{10,1... | collective-permute-start | bytes 3145736 | tf_op jit(solution)/shard_map/ppermute | solution.py:1502
  432.8 185.2 %collective-permute-start.2 = (bf16[2,128,2048]{2,1,0:T(8,128)(2,1)}, bf16[2,128,2048]{2,1,0:T(8,128)(2,1)}, u32[]{:S(2)}, u32[]{:S(2)}) collective-permute-start(bf16[2,128,2048]{2,1,0:T(8,128)(2,1)} %get-tuple-element.113), channel_id=1, source_target_pairs={{0,3},{1,0},{2,1},{3,2},{4,7},{5,4},{6,5},{7,6},{8,11},{9,8},{10,9... | collective-permute-start | bytes 3145736 | tf_op jit(solution)/shard_map/ppermute | solution.py:1502
  436.2 181.8 %collective-permute-start.1 = (bf16[2,128,2048]{2,1,0:T(8,128)(2,1)}, bf16[2,128,2048]{2,1,0:T(8,128)(2,1)}, u32[]{:S(2)}, u32[]{:S(2)}) collective-permute-start(bf16[2,128,2048]{2,1,0:T(8,128)(2,1)} %get-tuple-element.114), channel_id=1, source_target_pairs={{0,2},{1,3},{2,0},{3,1},{4,6},{5,7},{6,4},{7,5},{8,10},{9,11},{10,... | collective-permute-start | bytes 3145736 | tf_op jit(solution)/shard_map/ppermute | solution.py:1502
  438.3 4.4 copy-start.19
  466.3 146.9 %copy-start.13 = (f32[64]{0:T(128)S(1)}, f32[64]{0:T(128)}, u32[]{:S(2)}) copy-start(f32[64]{0:T(128)} %param.27) | copy-start | bytes 772
  466.3 146.9 %copy-start.14 = (f32[64]{0:T(128)S(1)}, f32[64]{0:T(128)}, u32[]{:S(2)}) copy-start(f32[64]{0:T(128)} %param.24) | copy-start | bytes 772
  466.3 146.9 %copy-start.15 = (f32[64]{0:T(128)S(1)}, f32[64]{0:T(128)}, u32[]{:S(2)}) copy-start(f32[64]{0:T(128)} %param.33) | copy-start | bytes 772
  466.3 146.9 %copy-start.16 = (f32[64]{0:T(128)S(1)}, f32[64]{0:T(128)}, u32[]{:S(2)}) copy-start(f32[64]{0:T(128)} %param.39) | copy-start | bytes 772
  466.3 146.9 %copy-start.17 = (f32[64]{0:T(128)S(1)}, f32[64]{0:T(128)}, u32[]{:S(2)}) copy-start(f32[64]{0:T(128)} %param.36) | copy-start | bytes 772
  466.3 146.9 %copy-start.18 = (f32[64]{0:T(128)S(1)}, f32[64]{0:T(128)}, u32[]{:S(2)}) copy-start(f32[64]{0:T(128)} %param.30) | copy-start | bytes 772
  466.3 147.4 %copy-start.7 = (f32[512,256]{1,0:T(8,128)S(1)}, f32[512,256]{1,0:T(8,128)}, u32[]{:S(2)}) copy-start(f32[512,256]{1,0:T(8,128)} %v_wide.1) | copy-start | bytes 1572868
  466.3 147.4 %copy-start.11 = (f32[512,256]{1,0:T(8,128)S(1)}, f32[512,256]{1,0:T(8,128)}, u32[]{:S(2)}) copy-start(f32[512,256]{1,0:T(8,128)} %param.32) | copy-start | bytes 1572868
  466.3 147.4 %copy-start.12 = (f32[512,256]{1,0:T(8,128)S(1)}, f32[512,256]{1,0:T(8,128)}, u32[]{:S(2)}) copy-start(f32[512,256]{1,0:T(8,128)} %param.38) | copy-start | bytes 1572868
  612.2 4.0 copy-start.3
  612.2 4.0 copy-start.4
  612.2 4.0 copy-start.9
  612.2 4.0 copy-start.10
  629.4 14.9 %copy-start.8 = (bf16[2,128,2048]{2,1,0:T(8,128)(2,1)S(1)}, bf16[2,128,2048]{2,1,0:T(8,128)(2,1)}, u32[]{:S(2)}) copy-start(bf16[2,128,2048]{2,1,0:T(8,128)(2,1)} %get-tuple-element.152) | copy-start | bytes 3145732
  629.4 16.8 %copy-start.5 = (f32[512,256]{1,0:T(8,128)S(1)}, f32[512,256]{1,0:T(8,128)}, u32[]{:S(2)}) copy-start(f32[512,256]{1,0:T(8,128)} %get-tuple-element.155) | copy-start | bytes 1572868
Sparse Core Ops, SparseCore 0:
  81.7 88.2 all-gather.2
  228.8 59.8 all-gather.4
  292.2 70.9 reduce-scatter.4
  366.6 121.1 reduce-scatter.2
